TPU v7x, 128 devices: a whole 4x4x4 slice. The times are simulated.
128 devices in a mesh: dp: 32 (over x, y, z_lo), seq: 4 (over z_hi, core).
Axes of the slice: x: 4, y: 4, z: 4 (z_hi: 2, z_lo: 2; z = z_hi * 2 + z_lo), core: 2. Of those that a mesh axis runs over, the one named last changes fastest.
Arguments:
- qkv: bfloat16 [64, 1024, 4608], P('dp', 'seq'), may hold values from -20.4 to 20.4
- gate: float32 [64, 3072], P('dp'), may hold values from 0.5 to 2.5
- cotangent: bfloat16 [64, 1024, 3072], P('dp', 'seq'), may hold values from -6 to 6
- out_weight: bfloat16 [1536, 3072], replicated, may hold values from -0.15625 to 0.15625
- clip_lengths: int32 [64], replicated, may hold values from 1 to 768, as said below
- text_lengths: int32 [64], replicated, may hold values from 1 to 256, as said below
- plan: int32 [32], replicated, may hold values from 0 to 31, as said below
Outputs:
- mixed: bfloat16 [64, 1024, 3072], P('dp', 'seq')
- gate_grad: float32 [64, 3072], P('dp')
- weight_grad: float32 [1536, 3072], P(None, ('dp', 'seq'))
- qkv_grad: bfloat16 [64, 1024, 4608], P('dp', 'seq')
Inputs may be any that keep to these rules, and one draw needn't show every extreme that they name: clip_lengths[c] counts the live video positions of source clip c = 2 g + s (group g, slot s); some clip has exactly 768. text_lengths[c] counts the live text positions of source clip c; some clip has exactly 256. plan is a permutation of 0 to 31: the second clip of group g becomes the second clip of group plan[g].
All inputs are finite; a program needn't handle non-finite values.
Results may differ from a plain program's by a relative error of at most 0.011.
Values may be sent and summed in bfloat16 or wider, within the bound.
No kernel may reach another device: no remote copies, remote signals or barrier semaphores. Data moves between devices by JAX's collectives and lax.ppermute only.
A program may use at most 128 MiB of HBM per device.

v0:
```python
import jax
import jax.numpy as jnp
from jax import lax
from jax.sharding import PartitionSpec as P

HD = 128
TXT = 256
BLOCK = 512


NEGATIVE = -1e30


def from_everyone(x, axis):
    copies = jnp.broadcast_to(x, (lax.axis_size(axis), *x.shape))
    return lax.all_to_all(copies, axis, split_axis=0, concat_axis=0, tiled=True)


def taken_together(x, axis):
    everything = from_everyone(x, axis)
    return jnp.sum(everything, axis=0)


def allowed_rows(offset, count, text_len, video_len):
    places = offset + jnp.arange(count, dtype=jnp.int32)
    return (places < text_len) | (places >= TXT) & (places < TXT + video_len)


def move_in(block_rows, inverse):
    groups = lax.axis_size("dp")
    portions = block_rows.reshape(groups, block_rows.shape[0] // groups, block_rows.shape[1])
    spread = lax.all_to_all(portions, "dp", split_axis=0, concat_axis=0, tiled=True)
    arranged = jnp.take(spread, inverse, axis=0)
    landed = lax.all_to_all(arranged, "dp", split_axis=0, concat_axis=0, tiled=True)
    return landed.reshape(block_rows.shape)


def move_out(block_rows, plan):
    groups = lax.axis_size("dp")
    portions = block_rows.reshape(groups, block_rows.shape[0] // groups, block_rows.shape[1])
    spread = lax.all_to_all(portions, "dp", split_axis=0, concat_axis=0, tiled=True)
    arranged = jnp.take(spread, plan, axis=0)
    landed = lax.all_to_all(arranged, "dp", split_axis=0, concat_axis=0, tiled=True)
    return landed.reshape(block_rows.shape)


def to_heads(tokens, seq_ways):
    clip_count, row_count, full_width = tokens.shape
    local_width = full_width // (3 * seq_ways)
    parted = tokens.reshape(clip_count, row_count, 3, seq_ways, local_width)
    exchanged = lax.all_to_all(parted, "seq", split_axis=3, concat_axis=1, tiled=True)
    return exchanged.reshape(clip_count, row_count * seq_ways, 3, local_width)


def block_scores(query_rows, key_rows, query_ok, key_ok, score_scale):
    scores = (
        jnp.einsum("qhd,khd->hqk", query_rows, key_rows, preferred_element_type=jnp.float32)
        * score_scale
    )
    live_pairs = query_ok[None, :, None] & key_ok[None, None, :]
    return (scores, live_pairs)


def attend(queries, keys_all, values_all, text_len, video_len, score_scale):
    seq_len, head_count, head_dim = queries.shape
    block_count = (TXT + video_len + BLOCK - 1) // BLOCK

    def query_step(query_block, built):
        results, log_totals = built
        offset = query_block * BLOCK
        query_rows = lax.dynamic_slice_in_dim(queries, offset, BLOCK, 0)
        query_ok = allowed_rows(offset, BLOCK, text_len, video_len)

        def scored(key_block):
            key_offset = key_block * BLOCK
            key_rows = lax.dynamic_slice_in_dim(keys_all, key_offset, BLOCK, 0)
            key_ok = allowed_rows(key_offset, BLOCK, text_len, video_len)
            scores, live_pairs = block_scores(query_rows, key_rows, query_ok, key_ok, score_scale)
            return (scores, live_pairs, key_offset)

        def stats_step(key_block, running):
            row_peak, row_total = running
            scores, live_pairs, key_offset = scored(key_block)
            masked = jnp.where(live_pairs, scores, NEGATIVE)
            new_peak = jnp.maximum(row_peak, jnp.max(masked, axis=-1))
            row_total = row_total * jnp.exp(row_peak - new_peak) + jnp.sum(
                jnp.exp(masked - new_peak[..., None]), axis=-1
            )
            return (new_peak, row_total)

        start_peak = jnp.full((head_count, BLOCK), NEGATIVE, jnp.float32)
        row_peak, row_total = lax.fori_loop(
            0, block_count, stats_step, (start_peak, jnp.zeros((head_count, BLOCK), jnp.float32))
        )
        log_total = row_peak + jnp.log(row_total)

        def value_step(key_block, partial_sums):
            scores, live_pairs, key_offset = scored(key_block)
            probs_low = jnp.exp(
                jnp.where(live_pairs, scores - log_total[..., None], NEGATIVE)
            ).astype(jnp.bfloat16)
            value_rows = lax.dynamic_slice_in_dim(values_all, key_offset, BLOCK, 0)
            return partial_sums + jnp.einsum(
                "hqk,khd->qhd", probs_low, value_rows, preferred_element_type=jnp.float32
            )

        partial_sums = lax.fori_loop(
            0, block_count, value_step, jnp.zeros((BLOCK, head_count, head_dim), jnp.float32)
        )
        results = lax.dynamic_update_slice_in_dim(
            results, partial_sums.astype(jnp.bfloat16), offset, 0
        )
        log_totals = lax.dynamic_update_slice_in_dim(log_totals, log_total, offset, 1)
        return (results, log_totals)

    initial = (
        jnp.zeros((seq_len, head_count, head_dim), jnp.bfloat16),
        jnp.zeros((head_count, seq_len), jnp.float32),
    )
    return lax.fori_loop(0, block_count, query_step, initial)


def attend_back(
    queries, keys_all, values_all, results, d_results, log_totals, text_len, video_len, score_scale
):
    seq_len, head_count, head_dim = queries.shape
    block_count = (TXT + video_len + BLOCK - 1) // BLOCK
    row_dots_all = jnp.einsum("qhd,qhd->hq", d_results, results, preferred_element_type=jnp.float32)

    def query_step(query_block, gradients):
        grad_q, grad_k, grad_v = gradients
        offset = query_block * BLOCK
        query_rows = lax.dynamic_slice_in_dim(queries, offset, BLOCK, 0)
        d_rows = lax.dynamic_slice_in_dim(d_results, offset, BLOCK, 0)
        query_ok = allowed_rows(offset, BLOCK, text_len, video_len)
        log_total = lax.dynamic_slice_in_dim(log_totals, offset, BLOCK, 1)
        row_dots = lax.dynamic_slice_in_dim(row_dots_all, offset, BLOCK, 1)

        def key_step(key_block, inner_state):
            q_sums, grad_k, grad_v = inner_state
            key_offset = key_block * BLOCK
            key_rows = lax.dynamic_slice_in_dim(keys_all, key_offset, BLOCK, 0)
            value_rows = lax.dynamic_slice_in_dim(values_all, key_offset, BLOCK, 0)
            key_ok = allowed_rows(key_offset, BLOCK, text_len, video_len)
            scores, live_pairs = block_scores(query_rows, key_rows, query_ok, key_ok, score_scale)
            probabilities = jnp.exp(jnp.where(live_pairs, scores - log_total[..., None], NEGATIVE))
            probs_low = probabilities.astype(jnp.bfloat16)
            d_probs = jnp.einsum(
                "qhd,khd->hqk", d_rows, value_rows, preferred_element_type=jnp.float32
            )
            d_scores = (probabilities * (d_probs - row_dots[..., None])).astype(jnp.bfloat16)
            q_sums = q_sums + jnp.einsum(
                "hqk,khd->qhd", d_scores, key_rows, preferred_element_type=jnp.float32
            )
            k_part = jnp.einsum(
                "hqk,qhd->khd", d_scores, query_rows, preferred_element_type=jnp.float32
            )
            v_part = jnp.einsum(
                "hqk,qhd->khd", probs_low, d_rows, preferred_element_type=jnp.float32
            )
            grad_k = lax.dynamic_update_slice_in_dim(
                grad_k,
                lax.dynamic_slice_in_dim(grad_k, key_offset, BLOCK, 0) + k_part,
                key_offset,
                0,
            )
            grad_v = lax.dynamic_update_slice_in_dim(
                grad_v,
                lax.dynamic_slice_in_dim(grad_v, key_offset, BLOCK, 0) + v_part,
                key_offset,
                0,
            )
            return (q_sums, grad_k, grad_v)

        q_start = jnp.zeros((BLOCK, head_count, head_dim), jnp.float32)
        q_sums, grad_k, grad_v = lax.fori_loop(0, block_count, key_step, (q_start, grad_k, grad_v))
        grad_q = lax.dynamic_update_slice_in_dim(grad_q, q_sums, offset, 0)
        return (grad_q, grad_k, grad_v)

    zero_grad = jnp.zeros((seq_len, head_count, head_dim), jnp.float32)
    grad_q, grad_k, grad_v = lax.fori_loop(
        0, block_count, query_step, (zero_grad, zero_grad, zero_grad)
    )
    return (
        (grad_q * score_scale).astype(jnp.bfloat16),
        (grad_k * score_scale).astype(jnp.bfloat16),
        grad_v.astype(jnp.bfloat16),
    )


def body(qkv, gate, cotangent, out_weight, clip_lengths, text_lengths, plan):
    groups = lax.axis_size("dp")
    seq_ways = lax.axis_size("seq")
    group_index = lax.axis_index("dp")
    seq_index = lax.axis_index("seq")
    ordinal = jnp.arange(groups, dtype=jnp.int32)
    inverse = jnp.sum(jnp.where(plan[None, :] == ordinal[:, None], ordinal[None, :], 0), axis=1)
    home_clip = 2 * group_index
    head_width = out_weight.shape[0]
    local_width = head_width // seq_ways
    head_count = local_width // HD
    row_count = cotangent.shape[1]
    score_scale = HD ** (-0.5)
    arrived = move_in(qkv[1], inverse)
    working = jnp.stack([qkv[0], arrived])
    clip_ids = (home_clip, 2 * inverse[group_index] + 1)
    spread_heads = to_heads(working, seq_ways)
    seq_len = spread_heads.shape[1]
    video_lens = [clip_lengths[clip_id] for clip_id in clip_ids]
    text_lens = [text_lengths[clip_id] for clip_id in clip_ids]
    sections = []
    result_list = []
    log_list = []
    for slot_index in range(2):
        triple = [
            spread_heads[slot_index, :, member].reshape(seq_len, head_count, HD)
            for member in range(3)
        ]
        results, log_totals = attend(
            triple[0],
            triple[1],
            triple[2],
            text_lens[slot_index],
            video_lens[slot_index],
            score_scale,
        )
        sections.append(triple)
        result_list.append(results)
        log_list.append(log_totals)
    attn_heads = jnp.stack(result_list).reshape(2, seq_len, 1, local_width)
    attn_back = lax.all_to_all(attn_heads, "seq", split_axis=1, concat_axis=2, tiled=True).reshape(
        2, row_count, head_width
    )
    outputs = jnp.einsum("crh,hd->crd", attn_back, out_weight, preferred_element_type=jnp.float32)
    mixed = (gate[:, None, :] * outputs).astype(jnp.bfloat16)
    gate_grad = taken_together(jnp.sum(cotangent.astype(jnp.float32) * outputs, axis=1), "seq")
    scaled = (cotangent.astype(jnp.float32) * gate[:, None, :]).astype(jnp.bfloat16)
    weight_rows = lax.dynamic_slice_in_dim(out_weight, seq_index * local_width, local_width, 0)
    flat_heads = attn_heads.reshape(2, seq_len, local_width)
    portion = lax.all_gather(scaled, "seq", axis=1, tiled=True)
    weight_part = jnp.einsum("cnh,cnd->hd", flat_heads, portion, preferred_element_type=jnp.float32)
    grad_rows = jnp.einsum(
        "cnd,hd->cnh", portion, weight_rows, preferred_element_type=jnp.float32
    ).astype(jnp.bfloat16)
    d_heads, weight_part = (grad_rows, weight_part)
    summed = lax.psum_scatter(weight_part, "dp", scatter_dimension=1, tiled=True)
    weight_grad = lax.all_to_all(summed, "seq", split_axis=1, concat_axis=0, tiled=True)
    grad_list = []
    for slot_index in range(2):
        triple = sections[slot_index]
        d_rows = d_heads[slot_index].reshape(seq_len, head_count, HD)
        grad_parts = attend_back(
            triple[0],
            triple[1],
            triple[2],
            result_list[slot_index],
            d_rows,
            log_list[slot_index],
            text_lens[slot_index],
            video_lens[slot_index],
            score_scale,
        )
        grad_list.append(
            jnp.stack([grad_part.reshape(seq_len, local_width) for grad_part in grad_parts], axis=1)
        )
    grad_heads = jnp.stack(grad_list).reshape(2, seq_len, 3, 1, local_width)
    grad_tokens = lax.all_to_all(
        grad_heads, "seq", split_axis=1, concat_axis=3, tiled=True
    ).reshape(2, row_count, 3 * head_width)
    grad_tokens = jnp.stack([grad_tokens[0], move_out(grad_tokens[1], plan)])
    return (mixed, gate_grad, weight_grad, grad_tokens)


def solution(mesh):
    in_specs = (P("dp", "seq", None), P("dp", None), P("dp", "seq", None), P(), P(), P(), P())
    out_specs = (P("dp", "seq", None), P("dp", None), P(None, ("dp", "seq")), P("dp", "seq", None))
    return jax.shard_map(body, mesh=mesh, in_specs=in_specs, out_specs=out_specs, check_vma=False)
```

profile of v0, /device:TPU:1, one launch (start us, length us, event | category | flops | bytes accessed | tf_op | source)
XLA Modules:
  0.0 709.6 jit_solution(8524687649885798854)
XLA Ops:
  7.2 4.9 fusion.183
  12.0 9.3 %all-to-all-start = ((bf16[32,8,4608]{2,1,0:T(8,128)(2,1)}), bf16[32,8,4608]{2,1,0:T(8,128)(2,1)S(1)}, u32[]{:S(2)}, u32[]{:S(2)}) async-start(bf16[32,8,4608]{2,1,0:T(8,128)(2,1)} %get-tuple-element.2898), calls=%async_computation | async-start | bytes 4718592 | tf_op jit(solution)/shard_map/all_to_all | solution.py:32
  21.5 30.6 %all-to-all-done = bf16[32,8,4608]{2,1,0:T(8,128)(2,1)S(1)} async-done(((bf16[32,8,4608]{2,1,0:T(8,128)(2,1)}), bf16[32,8,4608]{2,1,0:T(8,128)(2,1)S(1)}, u32[]{:S(2)}, u32[]{:S(2)}) %all-to-all-start) | async-done | bytes 2359328 | tf_op jit(solution)/shard_map/all_to_all | solution.py:32
  54.3 3.3 broadcast_select_fusion.1
  57.6 4.2 all-to-all-start.1
  61.9 4.3 copy.392
  66.1 25.9 %all-to-all-done.1 = bf16[32,8,4608]{2,1,0:T(8,128)(2,1)S(1)} async-done(((bf16[32,8,4608]{2,1,0:T(8,128)(2,1)}), bf16[32,8,4608]{2,1,0:T(8,128)(2,1)S(1)}, u32[]{:S(2)}, u32[]{:S(2)}) %all-to-all-start.1) | async-done | bytes 2359328 | tf_op jit(solution)/shard_map/all_to_all | solution.py:34
  94.1 5.5 copy.325
  101.8 2.5 copy.326
  104.3 8.3 %all-to-all-start.2 = ((bf16[2,256,3,4,384]{1,4,2,0,3:T(8,128)(2,1)}), bf16[2,256,3,4,384]{1,4,2,0,3:T(8,128)(2,1)}, u32[]{:S(2)}, u32[]{:S(2)}) async-start(bf16[2,256,3,4,384]{1,4,2,0,3:T(8,128)(2,1)} %copy.326), calls=%async_computation.2 | async-start | bytes 9437184 | tf_op jit(solution)/shard_map/all_to_all | solution.py:51
  117.0 49.8 %all-to-all-done.2 = bf16[2,256,3,4,384]{1,4,2,0,3:T(8,128)(2,1)} async-done(((bf16[2,256,3,4,384]{1,4,2,0,3:T(8,128)(2,1)}), bf16[2,256,3,4,384]{1,4,2,0,3:T(8,128)(2,1)}, u32[]{:S(2)}, u32[]{:S(2)}) %all-to-all-start.2) | async-done | bytes 4718624 | tf_op jit(solution)/shard_map/all_to_all | solution.py:51
  166.9 6.6 copy.327
  173.5 4.0 fusion.182
  181.5 25.5 %while.235 = (s32[]{:T(128)}, bf16[1024,3,128]{0,2,1:T(8,128)(2,1)S(1)}, f32[3,1024]{1,0:T(4,128)}, s32[]{:T(128)}, bf16[1024,3,128]{2,0,1:T(8,128)(2,1)}, /*ind...) while((s32[]{:T(128)}, ...), condition=%wide.region_16.18_spmd, body=%wide.region_9.17_spmd.sunk | while | flops 613564928 | bytes 14026645 | solution.py:120
  182.5 4.5 while.242
  187.8 6.3 while.243
  188.6 2.4 fusion.293
  191.7 2.4 fusion.293
  195.3 4.5 while.242
  200.5 6.3 while.243
  201.3 2.4 fusion.293
  204.5 2.4 fusion.293
  207.0 2.6 copy.328
  209.6 2.3 copy.331
  214.6 2.3 copy.330
  218.5 8.6 %while.232 = (s32[]{:T(128)}, bf16[1024,3,128]{0,2,1:T(8,128)(2,1)}, f32[3,1024]{1,0:T(4,128)}, s32[]{:T(128)}, bf16[1024,3,128]{2,0,1:T(8,128)(2,1)}, /*index=5...) while((s32[]{:T(128)}, bf16[1024,3,128]{0,2,1:T(8,128)(2,1)}, ...), condition=%wide.region_8.10_spmd, body=%wide.region_1.9_spmd.sunk | while | flops 613564928 | bytes 14026645 | solution.py:120
  220.0 2.3 while.240
  223.0 3.2 while.241
  223.9 2.4 fusion.301
  227.1 2.9 pad_maximum_fusion.2
  230.0 4.3 copy.338
  234.3 24.0 %all_to_all.89 = bf16[2,1024,1,384]{3,0,2,1:T(2,128)(2,1)S(1)} all-to-all(bf16[2,1024,1,384]{3,0,2,1:T(2,128)(2,1)S(1)} %copy.338), channel_id=1, replica_groups=mesh['dp'=32,'seq'=4] {'seq'}, dimensions={1} | all-to-all | bytes 3145728 | tf_op jit(solution)/shard_map/all_to_all | solution.py:231
  261.3 11.0 %fusion.166 = (f32[2,3072]{1,0:T(2,128)}, bf16[2,256,3072]{2,1,0:T(8,128)(2,1)}, bf16[2,256,3072]{2,1,0:T(8,128)(2,1)}) fusion(bf16[2,256,3072]{2,1,0:T(8,128)(2,1)} %param.31, f32[2,3072]{1,0:T(2,128)S(1)} %copy-done.29, bf16[2,256,1536]{2,1,0:T(8,128)(2,1)} %reshape.316, bf16[1536,3072]{1,0:T(8,128)(2,1)} %param.32), kind=kOutput, calls=%fused_computation.198 | convolution fusion | flops 4842842112 | bytes 20496384 | tf_op jit(solution)/shard_map/crh,hd->crd/dot_general | solution.py:234
  274.6 2.3 copy.351
  279.3 76.6 %all-gather.2.cloned.1.call-done = bf16[2,1024,3072]{2,1,0:T(8,128)(2,1)} async-done(((bf16[2,256,3072]{2,1,0:T(8,128)(2,1)}), bf16[2,1024,3072]{2,1,0:T(8,128)(2,1)}) %all-gather.2.cloned.1.call-update) | async-done | bytes 12582928 | tf_op jit(solution)/shard_map/all_gather | solution.py:240
  355.8 13.5 %fusion.171 = bf16[2,1024,384]{1,2,0:T(8,128)(2,1)S(1)} fusion(bf16[2,1024,3072]{2,1,0:T(8,128)(2,1)} %all-gather.2.cloned.1.call-done, bf16[1536,3072]{1,0:T(8,128)(2,1)} %param.32, s32[]{:T(128)S(6)} %select_n.154), kind=kOutput, calls=%fused_computation.213 | convolution fusion | flops 4832624640 | bytes 16515076 | tf_op jit(solution)/shard_map/cnd,hd->cnh/dot_general | solution.py:242
  374.0 36.1 %while.239 = (s32[]{:T(128)}, f32[1024,3,128]{0,2,1:T(8,128)}, f32[1024,3,128]{2,0,1:T(8,128)S(1)}, f32[1024,3,128]{2,0,1:T(8,128)}, s32[]{:T(128)}, /*index=5*/...) while((s32[]{:T(128)}, f32[1024,3,128]{0,2,1:T(8,128)}, ...), condition=%wide.region_27.29_spmd, body=%wide.region_24.28_spmd.sunk | while | flops 1015355392 | bytes 44485396 | solution.py:181
  378.0 13.3 %while.245 = (s32[]{:T(128)}, f32[512,3,128]{0,2,1:T(8,128)S(1)}, f32[1024,3,128]{2,0,1:T(8,128)S(1)}, f32[1024,3,128]{2,0,1:T(8,128)}, s32[]{:T(128)}, /*index=...) while((s32[]{:T(128)}, f32[512,3,128]{0,2,1:T(8,128)S(1)}, ...), condition=%wide.region_26.27_spmd.clone.clone, body=%wide.region_25.26_spmd.clone.clone.sunk | while | flops 1015355392 | bytes 39741808 | solution.py:176
  395.9 13.2 %while.245 = (s32[]{:T(128)}, f32[512,3,128]{0,2,1:T(8,128)S(1)}, f32[1024,3,128]{2,0,1:T(8,128)S(1)}, f32[1024,3,128]{2,0,1:T(8,128)}, s32[]{:T(128)}, /*index=...) while((s32[]{:T(128)}, f32[512,3,128]{0,2,1:T(8,128)S(1)}, ...), condition=%wide.region_26.27_spmd.clone.clone, body=%wide.region_25.26_spmd.clone.clone.sunk | while | flops 1015355392 | bytes 39741808 | solution.py:176
  410.1 2.6 copy.361
  414.3 2.6 multiply_convert_fusion.1
  416.9 2.4 multiply_convert_fusion.2
  422.9 11.4 %while.237 = (s32[]{:T(128)}, f32[1024,3,128]{0,2,1:T(8,128)}, f32[1024,3,128]{2,0,1:T(8,128)S(1)}, f32[1024,3,128]{2,0,1:T(8,128)}, s32[]{:T(128)}, /*index=5*/...) while((s32[]{:T(128)}, f32[1024,3,128]{0,2,1:T(8,128)}, ...), condition=%wide.region_23.25_spmd, body=%wide.region_20.24_spmd.sunk | while | flops 1015355392 | bytes 44485404 | solution.py:181
  426.7 6.7 while.244
  434.3 2.6 copy.353
  442.0 2.6 maximum_bitcast_fusion
  444.6 12.6 %copy.362 = bf16[2,1024,3,1,384]{4,0,3,2,1:T(2,128)(2,1)} copy(bf16[2,1024,3,1,384]{1,4,2,0,3:T(8,128)(2,1)} %maximum_bitcast_fusion) | data formatting | bytes 9437184 | tf_op jit(solution)/shard_map/reshape | solution.py:266
  457.3 5.5 all-to-all-start.6
  462.8 11.1 %convolution_bitcast_fusion.4 = f32[384,3072]{0,1:T(8,128)} fusion(bf16[2,1024,3072]{2,1,0:T(8,128)(2,1)} %all-gather.2.cloned.1.call-done, bf16[1,1024,384]{2,1,0:T(8,128)(2,1)S(1)} %copy-done.22, bf16[1,1024,384]{2,1,0:T(8,128)(2,1)S(1)} %copy-done.23), kind=kOutput, calls=%fused_computation.204 | convolution fusion | flops 4832624640 | bytes 18874368 | tf_op jit(solution)/shard_map/cnh,cnd->hd/dot_general | solution.py:241
  473.9 96.9 %all-to-all-done.6 = bf16[2,1024,3,1,384]{4,0,3,2,1:T(2,128)(2,1)} async-done(((bf16[2,1024,3,1,384]{4,0,3,2,1:T(2,128)(2,1)}), bf16[2,1024,3,1,384]{4,0,3,2,1:T(2,128)(2,1)}, u32[]{:S(2)}, u32[]{:S(2)}) %all-to-all-start.6) | async-done | bytes 4718624 | tf_op jit(solution)/shard_map/all_to_all | solution.py:267
  570.8 3.0 copy.363
  577.5 2.4 reshape_squeeze.39
  579.9 14.0 %all-to-all-start.7 = ((bf16[32,8,4608]{2,1,0:T(8,128)(2,1)}), bf16[32,8,4608]{2,1,0:T(8,128)(2,1)S(1)}, u32[]{:S(2)}, u32[]{:S(2)}) async-start(bf16[32,8,4608]{2,1,0:T(8,128)(2,1)} %reshape_squeeze.39), calls=%async_computation.8 | async-start | bytes 4718592 | tf_op jit(solution)/shard_map/all_to_all | solution.py:41
  593.9 28.4 %all-to-all-done.7 = bf16[32,8,4608]{2,1,0:T(8,128)(2,1)S(1)} async-done(((bf16[32,8,4608]{2,1,0:T(8,128)(2,1)}), bf16[32,8,4608]{2,1,0:T(8,128)(2,1)S(1)}, u32[]{:S(2)}, u32[]{:S(2)}) %all-to-all-start.7) | async-done | bytes 2359328 | tf_op jit(solution)/shard_map/all_to_all | solution.py:41
  622.9 9.2 %all-to-all-start.4 = ((f32[4,2,3072]{2,1,0:T(2,128)}), f32[4,2,3072]{2,1,0:T(2,128)S(1)}, u32[]{:S(2)}, u32[]{:S(2)}) async-start(f32[4,2,3072]{2,1,0:T(2,128)} %broadcast_in_dim.133), calls=%async_computation.4 | async-start | bytes 196608 | tf_op jit(solution)/shard_map/all_to_all | solution.py:16
  632.1 2.1 gather_fusion.1
  634.3 3.4 broadcast_select_fusion
  638.2 6.1 all-to-all-start.8
  645.0 4.3 copy.364
  649.3 25.0 %all-to-all-done.8 = bf16[32,8,4608]{2,1,0:T(8,128)(2,1)S(1)} async-done(((bf16[32,8,4608]{2,1,0:T(8,128)(2,1)}), bf16[32,8,4608]{2,1,0:T(8,128)(2,1)S(1)}, u32[]{:S(2)}, u32[]{:S(2)}) %all-to-all-start.8) | async-done | bytes 2359328 | tf_op jit(solution)/shard_map/all_to_all | solution.py:43
  674.3 2.5 copy.366
  676.8 13.5 %all-to-all-start.5 = ((f32[384,4,24]{0,2,1:T(8,128)}), f32[384,4,24]{0,2,1:T(8,128)S(1)}, u32[]{:S(2)}, u32[]{:S(2)}) async-start(f32[384,4,24]{0,2,1:T(8,128)} %bitcast.308), calls=%async_computation.6 | async-start | bytes 294912 | tf_op jit(solution)/shard_map/all_to_all | solution.py:247
  690.3 5.0 pad_maximum_fusion.1
  695.3 6.6 copy.367
  (260 shorter events, 112.5 us)
Async XLA Ops:
  12.0 9.4 %copy-start.30 = (s32[32]{0:T(128)S(1)}, s32[32]{0:T(128)}, u32[]{:S(2)}) copy-start(s32[32]{0:T(128)} %param.35) | copy-start | bytes 388
  12.0 40.1 %all-to-all-start = ((bf16[32,8,4608]{2,1,0:T(8,128)(2,1)}), bf16[32,8,4608]{2,1,0:T(8,128)(2,1)S(1)}, u32[]{:S(2)}, u32[]{:S(2)}) async-start(bf16[32,8,4608]{2,1,0:T(8,128)(2,1)} %get-tuple-element.2898), calls=%async_computation | async-start | bytes 4718592 | tf_op jit(solution)/shard_map/all_to_all | solution.py:32
  57.6 34.4 %all-to-all-start.1 = ((bf16[32,8,4608]{2,1,0:T(8,128)(2,1)}), bf16[32,8,4608]{2,1,0:T(8,128)(2,1)S(1)}, u32[]{:S(2)}, u32[]{:S(2)}) async-start(bf16[32,8,4608]{2,1,0:T(8,128)(2,1)} %broadcast_select_fusion.1), calls=%async_computation.1 | async-start | bytes 4718592 | tf_op jit(solution)/shard_map/all_to_all | solution.py:34
  94.1 5.5 copy-start.10
  104.3 9.5 %copy-start.27 = (s32[64]{0:T(128)S(1)}, s32[64]{0:T(128)}, u32[]{:S(2)}) copy-start(s32[64]{0:T(128)} %param.34) | copy-start | bytes 772
  104.3 9.5 %copy-start.28 = (s32[64]{0:T(128)S(1)}, s32[64]{0:T(128)}, u32[]{:S(2)}) copy-start(s32[64]{0:T(128)} %param.33) | copy-start | bytes 772
  104.3 62.6 %all-to-all-start.2 = ((bf16[2,256,3,4,384]{1,4,2,0,3:T(8,128)(2,1)}), bf16[2,256,3,4,384]{1,4,2,0,3:T(8,128)(2,1)}, u32[]{:S(2)}, u32[]{:S(2)}) async-start(bf16[2,256,3,4,384]{1,4,2,0,3:T(8,128)(2,1)} %copy.326), calls=%async_computation.2 | async-start | bytes 9437184 | tf_op jit(solution)/shard_map/all_to_all | solution.py:51
  112.5 243.3 %all-gather.2.cloned.1.call-start = ((), (), s32[]{:S(2)}) async-start(), calls=%async_computation.10 | async-start | bytes 15728640 | tf_op jit(solution)/shard_map/all_gather | solution.py:240
  207.0 6.1 copy-start.6
  207.0 4.9 copy-start.16
  227.1 7.3 %copy-start = (bf16[1024,3,128]{2,0,1:T(8,128)(2,1)}, bf16[1024,3,128]{2,0,1:T(8,128)(2,1)S(1)}, u32[]{:S(2)}) copy-start(bf16[1024,3,128]{2,0,1:T(8,128)(2,1)S(1)} %get-tuple-element.4344) | copy-start | bytes 2359300
  259.8 1.5 copy-start.29
  272.3 1.1 copy-start.17
  272.3 4.6 copy-start.7
  273.4 4.7 copy-start.4
  370.4 2.3 copy-start.3
  378.0 1.4 copy-start.8
  378.0 1.4 copy-start.25
  381.0 1.4 copy-start.11
  383.4 1.1 copy-start.12
  384.6 1.4 copy-start.8
  384.6 1.4 copy-start.25
  387.6 1.4 copy-start.11
  390.1 1.1 copy-start.12
  395.9 1.4 copy-start.8
  396.0 1.4 copy-start.25
  399.0 1.4 copy-start.11
  401.4 1.1 copy-start.12
  402.6 1.4 copy-start.8
  402.6 1.4 copy-start.25
  405.6 1.4 copy-start.11
  408.0 1.1 copy-start.12
  414.3 5.0 copy-start.2
  414.3 5.0 copy-start.5
  420.2 2.7 copy-start.1
  426.7 1.4 copy-start.9
  426.7 1.4 copy-start.24
  429.8 1.4 copy-start.14
  432.3 1.1 copy-start.15
  436.9 3.3 copy-start.13
  438.6 1.9 copy-start.18
  438.6 1.9 copy-start.19
  438.6 2.1 copy-start.20
  440.6 1.1 copy-start.21
  457.3 5.5 copy-start.22
  457.3 5.5 copy-start.23
  457.3 113.5 %all-to-all-start.6 = ((bf16[2,1024,3,1,384]{4,0,3,2,1:T(2,128)(2,1)}), bf16[2,1024,3,1,384]{4,0,3,2,1:T(2,128)(2,1)}, u32[]{:S(2)}, u32[]{:S(2)}) async-start(bf16[2,1024,3,1,384]{4,0,3,2,1:T(2,128)(2,1)} %copy.362), calls=%async_computation.7 | async-start | bytes 9437184 | tf_op jit(solution)/shard_map/all_to_all | solution.py:267
  462.8 214.0 %reduce-scatter.2.cloned.1.call-start = ((), (), s32[]{:S(2)}) async-start(), calls=%async_computation.11 | async-start | bytes 4866048 | tf_op jit(solution)/shard_map/reduce_scatter | solution.py:246
  579.9 14.0 %copy-start.31 = (s32[32]{0:T(128)S(1)}, s32[32]{0:T(128)}, u32[]{:S(2)}) copy-start(s32[32]{0:T(128)} %param.35) | copy-start | bytes 388
  579.9 42.4 %copy-start.26 = (f32[2,3072]{1,0:T(2,128)S(1)}, f32[2,3072]{1,0:T(2,128)}, u32[]{:S(2)}) copy-start(f32[2,3072]{1,0:T(2,128)} %get-tuple-element.2887) | copy-start | bytes 73732
  579.9 42.4 %all-to-all-start.7 = ((bf16[32,8,4608]{2,1,0:T(8,128)(2,1)}), bf16[32,8,4608]{2,1,0:T(8,128)(2,1)S(1)}, u32[]{:S(2)}, u32[]{:S(2)}) async-start(bf16[32,8,4608]{2,1,0:T(8,128)(2,1)} %reshape_squeeze.39), calls=%async_computation.8 | async-start | bytes 4718592 | tf_op jit(solution)/shard_map/all_to_all | solution.py:41
  622.9 15.3 %all-to-all-start.4 = ((f32[4,2,3072]{2,1,0:T(2,128)}), f32[4,2,3072]{2,1,0:T(2,128)S(1)}, u32[]{:S(2)}, u32[]{:S(2)}) async-start(f32[4,2,3072]{2,1,0:T(2,128)} %broadcast_in_dim.133), calls=%async_computation.4 | async-start | bytes 196608 | tf_op jit(solution)/shard_map/all_to_all | solution.py:16
  638.2 36.1 %all-to-all-start.8 = ((bf16[32,8,4608]{2,1,0:T(8,128)(2,1)}), bf16[32,8,4608]{2,1,0:T(8,128)(2,1)S(1)}, u32[]{:S(2)}, u32[]{:S(2)}) async-start(bf16[32,8,4608]{2,1,0:T(8,128)(2,1)} %broadcast_select_fusion), calls=%async_computation.9 | async-start | bytes 4718592 | tf_op jit(solution)/shard_map/all_to_all | solution.py:43
  676.8 25.1 %all-to-all-start.5 = ((f32[384,4,24]{0,2,1:T(8,128)}), f32[384,4,24]{0,2,1:T(8,128)S(1)}, u32[]{:S(2)}, u32[]{:S(2)}) async-start(f32[384,4,24]{0,2,1:T(8,128)} %bitcast.308), calls=%async_computation.6 | async-start | bytes 294912 | tf_op jit(solution)/shard_map/all_to_all | solution.py:247
Sparse Core Ops, SparseCore 0:
  272.5 83.3 all-gather.1
  474.1 177.7 reduce-scatter.1
where the time goes:
time: 720 us; the launch traced here: 710 us
  waiting for transfers between devices  334 us (46%)
  local copies, waits for them, and re-layouts  144 us (20%)
  matrix products  70.4 us (10%)
  starting transfers between devices  70.2 us (10%)
  other arithmetic  47.2 us (7%)
  blocking collectives  24 us (3%)
  between operations  17.9 us (2%)
    all_to_all x1, waiting for transfers between devices, body(): lax.all_to_all(grad_heads, 'seq', split_axis=1, concat_axis=3, tiled=True)  96.9 us
    all_gather x1, waiting for transfers between devices, body(): portion = lax.all_gather(scaled, 'seq', axis=1, tiled=True)  76.6 us
    all_to_all x1, waiting for transfers between devices, to_heads(): lax.all_to_all(parted, 'seq', split_axis=3, concat_axis=1, tiled=True)  49.8 us
    all_to_all x1, waiting for transfers between devices, move_in(): lax.all_to_all(portions, 'dp', split_axis=0, concat_axis=0, tiled=True)  30.6 us
    all_to_all x1, waiting for transfers between devices, move_out(): lax.all_to_all(portions, 'dp', split_axis=0, concat_axis=0, tiled=True)  28.4 us
    all_to_all x1, waiting for transfers between devices, move_in(): lax.all_to_all(arranged, 'dp', split_axis=0, concat_axis=0, tiled=True)  25.9 us
    all_to_all x1, waiting for transfers between devices, move_out(): lax.all_to_all(arranged, 'dp', split_axis=0, concat_axis=0, tiled=True)  25 us
    all_to_all x1, blocking collectives, body(): lax.all_to_all(attn_heads, 'seq', split_axis=1, concat_axis=2, tiled=True)  24 us
  transfers between devices with their start and end apart: 10, of which 8 were waited for; matrix products, arithmetic and copies ran while one was open for 8% of the time, Pallas kernels for 0%

commit v1 on v0

v1 whole, which is shorter than its diff:
```python
import functools

import jax
import jax.numpy as jnp
from jax import lax
from jax.experimental import pallas as pl
from jax.experimental.pallas import tpu as pltpu
from jax.sharding import PartitionSpec as P


HD = 128
ROWS = 256
HEADS_HALF = 6
HALF = HEADS_HALF * HD
WIDTH = 2 * HALF
TOGETHER = 2
D = 3072
NEGATIVE = -1e30
LOG2E = 1.4426950408889634
SCALE = HD**-0.5

NT = (((1,), (1,)), ((), ()))
NN = (((1,), (0,)), ((), ()))
TN = (((0,), (0,)), ((), ()))


def mm(a, b, dims):
    return lax.dot_general(a, b, dims, preferred_element_type=jnp.float32)


def cost(flops, nbytes, transcendentals=0):
    return pl.CostEstimate(
        flops=int(flops), bytes_accessed=int(nbytes), transcendentals=int(transcendentals)
    )


def swap(x, step):
    return lax.ppermute(x, "seq", [(i, i ^ step) for i in range(4)])


def prep_kernel(sp, qo, ko, vo, kc, vc, s1, s2, s3):
    s1[0] = qo[0]
    s1[1] = ko[0]
    s1[2] = vo[0]
    s2[0] = kc[0]
    s2[1] = vc[0]
    s3[0] = ko[0]
    s3[1] = vo[0]


def prep(sp, qkv, slot):
    rows = ROWS // 2

    def half(member, other):
        def index(r, sp):
            core = sp[0, 0]
            return (slot, r, 2 * member + (1 - core if other else core))

        return pl.BlockSpec((1, rows, HALF), index)

    def out(count):
        return pl.BlockSpec((count, rows, HALF), lambda r, sp: (0, r, 0))

    def shape(count):
        return jax.ShapeDtypeStruct((count, ROWS, HALF), jnp.bfloat16)

    return pl.pallas_call(
        prep_kernel,
        grid_spec=pltpu.PrefetchScalarGridSpec(
            num_scalar_prefetch=1,
            grid=(2,),
            in_specs=[half(0, True), half(1, True), half(2, True), half(1, False), half(2, False)],
            out_specs=[out(3), out(2), out(2)],
        ),
        out_shape=[shape(3), shape(2), shape(2)],
        cost_estimate=cost(1e6, 5e6),
    )(sp, qkv, qkv, qkv, qkv, qkv)


def live_limit(sp, slot, block, shape, axis):
    return lax.broadcasted_iota(jnp.int32, shape, axis) < sp[slot, 1 + block]


def key_bias(sp, slot, axis):
    shape = (ROWS, 1) if axis == 0 else (1, ROWS)
    parts = [
        jnp.where(live_limit(sp, slot, block, shape, axis), 0.0, NEGATIVE) for block in range(4)
    ]
    return jnp.concatenate(parts, axis=axis)


def fwd_kernel(slot, sp, q0, k0, v0, q1, k1, v1, k2, v2, k3, v3, att, lse):
    bias = key_bias(sp, slot, 1)
    work = []
    for head in range(TOGETHER):
        cols = slice(head * HD, (head + 1) * HD)
        keys = jnp.concatenate([k[0, :, cols] for k in (k0, k1, k2, k3)], axis=0)
        values = jnp.concatenate([v[0, :, cols] for v in (v0, v1, v2, v3)], axis=0)
        for block, q in enumerate((q0, q1)):
            work.append((head, cols, block, mm(q[0, :, cols], keys, NT), values))
    for head, cols, block, products, values in work:
        scores = products * (SCALE * LOG2E) + bias
        peak = jnp.max(scores, axis=1, keepdims=True)
        powers = jnp.exp2(scores - peak)
        total = jnp.sum(powers, axis=1, keepdims=True)
        live = live_limit(sp, slot, block, (ROWS, 1), 0)
        inverse = jnp.where(live, 1.0 / total, 0.0)
        mixed = mm(powers.astype(jnp.bfloat16), values, NN) * inverse
        att[block, :, cols] = mixed.astype(jnp.bfloat16)
        level = jnp.where(live, peak + jnp.log2(total), -NEGATIVE)
        lse[head, :, block * ROWS : (block + 1) * ROWS] = jnp.broadcast_to(level, (ROWS, HD)).T[:8]


def bwd_kernel(
    slot, sp, q0, k0, v0, q1, k1, v1, k2, v2, k3, v3, att, lse, do0, do1, own, r1, r2, r3
):
    keys = jnp.concatenate([k0[0], k1[0], k2[0], k3[0]], axis=0)
    values = jnp.concatenate([v0[0], v1[0], v2[0], v3[0]], axis=0)
    bias = key_bias(sp, slot, 0)
    grad_k = None
    grad_v = None
    for block, (q, do) in enumerate(((q0, do0), (q1, do1))):
        d_rows = do[0]
        scores = mm(keys, q[0], NT) * (SCALE * LOG2E) + bias
        level = lse[0, 0:1, block * ROWS : (block + 1) * ROWS]
        probs = jnp.exp2(scores - level)
        product = d_rows.astype(jnp.float32) * att[block].astype(jnp.float32)
        dots = jnp.sum(product.T, axis=0, keepdims=True)
        d_probs = mm(values, d_rows, NT)
        d_scores = (probs * (d_probs - dots)).astype(jnp.bfloat16)
        v_part = mm(probs.astype(jnp.bfloat16), d_rows, NN)
        k_part = mm(d_scores, q[0], NN)
        grad_k = k_part if block == 0 else grad_k + k_part
        grad_v = v_part if block == 0 else grad_v + v_part
        grad_q = (mm(keys, d_scores, TN) * SCALE).T
        if block == 0:
            own[0] = grad_q
        else:
            r1[0] = grad_q.astype(jnp.bfloat16)
    grad_k = grad_k * SCALE
    own[1] = grad_k[:ROWS]
    own[2] = grad_v[:ROWS]
    r1[1] = grad_k[ROWS : 2 * ROWS].astype(jnp.bfloat16)
    r1[2] = grad_v[ROWS : 2 * ROWS].astype(jnp.bfloat16)
    r2[0] = grad_k[2 * ROWS : 3 * ROWS].astype(jnp.bfloat16)
    r2[1] = grad_v[2 * ROWS : 3 * ROWS].astype(jnp.bfloat16)
    r3[0] = grad_k[3 * ROWS :].astype(jnp.bfloat16)
    r3[1] = grad_v[3 * ROWS :].astype(jnp.bfloat16)


def head_block(lead, index=0, heads=1):
    return pl.BlockSpec((lead, ROWS, heads * HD), lambda h, sp: (index, 0, h))


def section_specs(slot, heads=1):
    def own(member):
        return pl.BlockSpec(
            (1, ROWS, heads * HD),
            lambda h, sp: (slot, 0, (12 * member + HEADS_HALF * sp[0, 0]) // heads + h),
        )

    return [own(0), own(1), own(2)] + [head_block(1, m, heads) for m in (0, 1, 2, 0, 1, 0, 1)]


def sections(qkv, x1, x2, x3):
    return (qkv, qkv, qkv, x1, x1, x1, x2, x2, x3, x3)


LSE_SPEC = pl.BlockSpec((1, 8, 2 * ROWS), lambda h, sp: (h, 0, 0))
PAIRS = HEADS_HALF * 512 * 1024


def attend(sp, slot, qkv, received):
    return pl.pallas_call(
        functools.partial(fwd_kernel, slot),
        grid_spec=pltpu.PrefetchScalarGridSpec(
            num_scalar_prefetch=1,
            grid=(HEADS_HALF // TOGETHER,),
            in_specs=section_specs(slot, TOGETHER),
            out_specs=[
                head_block(2, 0, TOGETHER),
                pl.BlockSpec((TOGETHER, 8, 2 * ROWS), lambda h, sp: (h, 0, 0)),
            ],
        ),
        out_shape=[
            jax.ShapeDtypeStruct((2, ROWS, HALF), jnp.bfloat16),
            jax.ShapeDtypeStruct((HEADS_HALF, 8, 2 * ROWS), jnp.float32),
        ],
        cost_estimate=cost(4 * PAIRS * HD, 5e6, PAIRS),
    )(sp, *sections(qkv, *received))


def attend_back(sp, slot, qkv, received, att, lse, d_own, d_peer):
    d_own_spec = pl.BlockSpec((1, ROWS, HD), lambda h, sp: (0, 0, HEADS_HALF * sp[0, 0] + h))

    def shape(count, kind):
        return jax.ShapeDtypeStruct((count, ROWS, HALF), kind)

    return pl.pallas_call(
        functools.partial(bwd_kernel, slot),
        grid_spec=pltpu.PrefetchScalarGridSpec(
            num_scalar_prefetch=1,
            grid=(HEADS_HALF,),
            in_specs=section_specs(slot) + [head_block(2), LSE_SPEC, d_own_spec, head_block(1)],
            out_specs=[head_block(3), head_block(3), head_block(2), head_block(2)],
        ),
        out_shape=[
            shape(3, jnp.float32),
            shape(3, jnp.bfloat16),
            shape(2, jnp.bfloat16),
            shape(2, jnp.bfloat16),
        ],
        cost_estimate=cost(10 * PAIRS * HD, 1e7, PAIRS),
    )(sp, *sections(qkv, *received), att, lse, d_own, d_peer)


def join_kernel(sp, own, p1, p2, p3, *rest):
    out = rest[-1]
    core = sp[0, 0]
    member = pl.program_id(0)
    crossing = jnp.where(member > 0, 1.0, 0.0)
    mine = own[0] + crossing * p2[0].astype(jnp.float32)
    other = p1[0].astype(jnp.float32) + crossing * p3[0].astype(jnp.float32)
    first = core == 0
    out[0, :, :HALF] = jnp.where(first, mine, other).astype(jnp.bfloat16)
    out[0, :, HALF:] = jnp.where(first, other, mine).astype(jnp.bfloat16)


def join(sp, slot, own, p1, p2, p3, base):
    def piece(shift):
        return pl.BlockSpec((1, ROWS, HALF), lambda m, sp: (jnp.maximum(m - shift, 0), 0, 0))

    in_specs = [piece(0), piece(0), piece(1), piece(1)]
    args = [own, p1, p2, p3]
    aliases = {}
    if base is not None:
        in_specs.append(pl.BlockSpec(memory_space=pl.ANY))
        args.append(base)
        aliases = {5: 0}
    return pl.pallas_call(
        join_kernel,
        grid_spec=pltpu.PrefetchScalarGridSpec(
            num_scalar_prefetch=1,
            grid=(3,),
            in_specs=in_specs,
            out_specs=pl.BlockSpec((1, ROWS, WIDTH), lambda m, sp: (slot, 0, m)),
        ),
        out_shape=jax.ShapeDtypeStruct((2, ROWS, 3 * WIDTH), jnp.bfloat16),
        input_output_aliases=aliases,
        cost_estimate=cost(1e6, 1e7),
    )(sp, *args)


def pick_kernel(order, rows, out):
    def step(slot, carry):
        out[slot] = rows[order[slot]]
        return carry

    lax.fori_loop(0, rows.shape[0], step, 0)


def pick(rows, order):
    whole = pl.BlockSpec(rows.shape, lambda i, order: (0, 0, 0))
    return pl.pallas_call(
        pick_kernel,
        grid_spec=pltpu.PrefetchScalarGridSpec(
            num_scalar_prefetch=1, grid=(1,), in_specs=[whole], out_specs=whole
        ),
        out_shape=jax.ShapeDtypeStruct(rows.shape, rows.dtype),
        cost_estimate=cost(1e6, 2 * rows.size * 2),
        name="pick",
    )(order, rows)


def rows_kernel(sp, cotangent, gate, weight, send, keep, away, near, near_send, total):
    step = pl.program_id(0)
    parts = [
        (cotangent[slot].astype(jnp.float32) * gate[slot : slot + 1]).astype(jnp.bfloat16)
        for slot in range(2)
    ]

    @pl.when(step < 3)
    def _():
        send[0] = parts[0]
        send[1] = parts[1]

    @pl.when(step >= 3)
    def _():
        keep[0] = parts[0]
        keep[1] = parts[1]

    product = mm(jnp.concatenate(parts, axis=0), weight[...], NT)

    @pl.when(step == 0)
    def _():
        total[...] = product

    @pl.when((step > 0) & (step < 5))
    def _():
        total[...] += product

    @pl.when(step == 5)
    def _():
        rows = (total[...] + product).astype(jnp.bfloat16)
        near[...] = rows[:ROWS]
        away[...] = rows[ROWS:]
        near_send[0] = jnp.where(sp[0, 0] == 0, rows[:ROWS, HALF:], rows[:ROWS, :HALF])


def scaled_rows(sp, cotangent, gate, out_weight):
    cols = D // 6

    def place(step, sp):
        core = sp[0, 0]
        return jnp.where(step < 3, 3 * (1 - core), 3 * core - 3) + step

    def whole(*shape):
        return pl.BlockSpec(shape, lambda k, sp: (0,) * len(shape))

    def shape(*dims):
        return jax.ShapeDtypeStruct(dims, jnp.bfloat16)

    return pl.pallas_call(
        rows_kernel,
        grid_spec=pltpu.PrefetchScalarGridSpec(
            num_scalar_prefetch=1,
            grid=(6,),
            in_specs=[
                pl.BlockSpec((2, ROWS, cols), lambda k, sp: (0, 0, place(k, sp))),
                pl.BlockSpec((2, cols), lambda k, sp: (0, place(k, sp))),
                pl.BlockSpec((WIDTH, cols), lambda k, sp: (0, place(k, sp))),
            ],
            out_specs=[
                pl.BlockSpec((2, ROWS, cols), lambda k, sp: (0, 0, jnp.minimum(k, 2))),
                pl.BlockSpec((2, ROWS, cols), lambda k, sp: (0, 0, jnp.maximum(k - 3, 0))),
                whole(ROWS, WIDTH),
                whole(ROWS, WIDTH),
                whole(1, ROWS, HALF),
            ],
            scratch_shapes=[pltpu.VMEM((2 * ROWS, WIDTH), jnp.float32)],
        ),
        out_shape=[
            shape(2, ROWS, D // 2),
            shape(2, ROWS, D // 2),
            shape(ROWS, WIDTH),
            shape(ROWS, WIDTH),
            shape(1, ROWS, HALF),
        ],
        cost_estimate=cost(2 * 512 * WIDTH * D, 1.7e7),
        name="scaled_rows",
    )(sp, cotangent, gate, out_weight)


def project_kernel(sp, a0, a1, b0, b1, w_mine, w_other, gate, cotangent, mixed, gate_grad):
    mine = jnp.concatenate([a0[0], a1[0]], axis=0)
    other = jnp.concatenate([b0[0], b1[0]], axis=0)
    outputs = mm(mine, w_mine[...], NN) + mm(other, w_other[...], NN)
    for slot in range(2):
        rows = outputs[slot * ROWS : (slot + 1) * ROWS]
        mixed[slot] = (rows * gate[slot : slot + 1]).astype(jnp.bfloat16)
        gate_grad[slot : slot + 1] = jnp.sum(
            cotangent[slot].astype(jnp.float32) * rows, axis=0, keepdims=True
        )


def project(sp, mine, other, out_weight, gate, cotangent):
    cols = 512

    def rows(index):
        return pl.BlockSpec((1, ROWS, HALF), lambda d, sp: (index, 0, 0))

    wide = pl.BlockSpec((2, ROWS, cols), lambda d, sp: (0, 0, d))
    thin = pl.BlockSpec((2, cols), lambda d, sp: (0, d))
    return pl.pallas_call(
        project_kernel,
        grid_spec=pltpu.PrefetchScalarGridSpec(
            num_scalar_prefetch=1,
            grid=(D // cols,),
            in_specs=[
                rows(0),
                rows(0),
                rows(1),
                rows(1),
                pl.BlockSpec((HALF, cols), lambda d, sp: (sp[0, 0], d)),
                pl.BlockSpec((HALF, cols), lambda d, sp: (1 - sp[0, 0], d)),
                thin,
                wide,
            ],
            out_specs=[wide, thin],
        ),
        out_shape=[
            jax.ShapeDtypeStruct((2, ROWS, D), jnp.bfloat16),
            jax.ShapeDtypeStruct((2, D), jnp.float32),
        ],
        cost_estimate=cost(2 * 512 * WIDTH * D, 1.6e7),
        name="project",
    )(sp, mine[0], mine[1], other[0], other[1], out_weight, out_weight, gate, cotangent)


def weigh_kernel(sp, scaled_own, scaled_peer, a0, a1, b0, b1, out):
    left = jnp.concatenate(
        [scaled_own[0], scaled_peer[0], scaled_own[1], scaled_peer[1]], axis=0
    )
    mine = jnp.concatenate([a0[0], a0[1], a1[0], a1[1]], axis=0)
    other = jnp.concatenate([b0[1], b0[0], b1[1], b1[0]], axis=0)
    first = sp[0, 0] == 0
    low = jnp.where(first, mine, other)
    high = jnp.where(first, other, mine)
    out[:, :HALF] = mm(left, low, TN).astype(jnp.bfloat16)
    out[:, HALF:] = mm(left, high, TN).astype(jnp.bfloat16)


def weigh(sp, scaled, scaled_peer, mine, other):
    rows = 384
    steps = D // 2 // rows
    pair = pl.BlockSpec((2, ROWS, HALF), lambda d, sp: (0, 0, 0))
    return pl.pallas_call(
        weigh_kernel,
        grid_spec=pltpu.PrefetchScalarGridSpec(
            num_scalar_prefetch=1,
            grid=(steps,),
            in_specs=[
                pl.BlockSpec((2, ROWS, rows), lambda d, sp: (0, 0, d)),
                pl.BlockSpec((2, ROWS, rows), lambda d, sp: (0, 0, d)),
                pair,
                pair,
                pair,
                pair,
            ],
            out_specs=pl.BlockSpec((rows, WIDTH), lambda d, sp: (d, 0)),
        ),
        out_shape=jax.ShapeDtypeStruct((D // 2, WIDTH), jnp.bfloat16),
        cost_estimate=cost(2 * 1024 * WIDTH * D // 2, 1.2e7),
        name="weigh",
    )(sp, scaled, scaled_peer, mine[0], mine[1], other[0], other[1])


def plane_groups():
    return [[2 * xy + z_low for xy in range(16)] for z_low in range(2)]


def final_moves(step):
    moves = []
    for xy in range(16):
        for z_low in range(2):
            for z_high in range(2):
                for core in range(2):
                    source = 4 * (2 * xy + z_low) + 2 * z_high + core
                    target = 4 * (16 * core + xy) + ((2 * z_low + z_high) ^ step)
                    moves.append((source, target))
    return moves


def sum_kernel(sp, spread, *rest):
    total = rest[-1]
    total[...] = jnp.sum(spread[...].astype(jnp.float32), axis=0)
    count = total.shape[0] // 4
    for step, out in enumerate(rest[:-1]):
        start = pl.multiple_of((sp[1, 0] ^ step) * count, 8)
        out[...] = total[pl.ds(start, count), :].astype(jnp.bfloat16)


def sum_weights(sp, spread):
    groups, count, _ = spread.shape
    cols = 512
    quarter = pl.BlockSpec((count // 4, cols), lambda i, sp: (0, i))
    shape = jax.ShapeDtypeStruct((count // 4, WIDTH), jnp.bfloat16)
    return pl.pallas_call(
        sum_kernel,
        grid_spec=pltpu.PrefetchScalarGridSpec(
            num_scalar_prefetch=1,
            grid=(WIDTH // cols,),
            in_specs=[pl.BlockSpec((groups, count, cols), lambda i, sp: (0, 0, i))],
            out_specs=[quarter] * 4,
            scratch_shapes=[pltpu.VMEM((count, cols), jnp.float32)],
        ),
        out_shape=[shape] * 4,
        cost_estimate=cost(5e6, 5e6),
        name="sum_weights",
    )(sp, spread)


def finish_weights(quarters):
    pieces = [
        lax.ppermute(quarter, ("dp", "seq"), final_moves(step)).astype(jnp.float32)
        for step, quarter in enumerate(quarters)
    ]
    return (pieces[0] + pieces[1] + pieces[2] + pieces[3]).T


def after(value, *others):
    return lax.optimization_barrier((value, *others))[0]


def spread_out(rows):
    groups = lax.axis_size("dp")
    portions = rows.reshape(groups, -1, rows.shape[-1])
    return lax.all_to_all(portions, "dp", split_axis=0, concat_axis=0, tiled=True)


def land(arranged, shape):
    landed = lax.all_to_all(arranged, "dp", split_axis=0, concat_axis=0, tiled=True)
    return landed.reshape(shape)


def body(qkv, gate, cotangent, out_weight, clip_lengths, text_lengths, plan):
    groups = lax.axis_size("dp")
    group_index = lax.axis_index("dp")
    seq_index = lax.axis_index("seq")
    core = seq_index & 1
    z_place = 2 * (group_index & 1) + (seq_index >> 1)
    ordinal = jnp.arange(groups, dtype=jnp.int32)
    inverse = jnp.sum(jnp.where(plan[None, :] == ordinal[:, None], ordinal[None, :], 0), axis=1)

    quarters = seq_index ^ jnp.arange(4, dtype=jnp.int32)
    text = lax.dynamic_slice_in_dim(text_lengths, 2 * group_index, 2)[:, None]
    video = lax.dynamic_slice_in_dim(clip_lengths, 2 * group_index, 2)[:, None]
    limits = jnp.where(quarters[None] == 0, text, video - (quarters[None] - 1) * ROWS)
    place = jnp.stack([core, z_place]).astype(jnp.int32)[:, None]
    sp = jnp.concatenate([place, limits.astype(jnp.int32)], axis=1)
    first = core == 0

    def to_core(rows):
        other = jnp.where(first, rows[:, HALF:], rows[:, :HALF])
        return swap(other[None], 1)

    received = [None, None]
    d_own, d_peer = [None, None], [None, None]
    att, lse = [None, None], [None, None]

    s1, s2, s3 = prep(sp, qkv, 1)
    received[1] = (swap(s1, 1), swap(s2, 2), swap(s3, 3))
    scaled_send, scaled, away, near, near_send = scaled_rows(
        after(sp, s2), cotangent, gate, out_weight
    )
    d_spread = spread_out(away)
    s1, s2, s3 = prep(after(sp, away), qkv, 0)
    received[0] = (swap(s1, 1), swap(s2, 2), swap(s3, 3))
    d_own[0], d_peer[0] = near[None], swap(near_send, 1)
    scaled_peer = swap(scaled_send, 1)

    att[1], lse[1] = attend(after(sp, s2), 1, qkv, received[1])
    att_spread = spread_out(att[1].reshape(2 * ROWS, HALF))
    d_picked = pick(d_spread, after(plan, lse[1]))
    att[0], lse[0] = attend(after(sp, d_picked), 0, qkv, received[0])
    att_other = [swap(att[0], 1)]
    picked = pick(att_spread, after(inverse, lse[0]))
    moved = land(picked, (2, ROWS, HALF))
    landed = land(after(d_picked, moved), (ROWS, WIDTH))

    def back(sp, slot):
        return attend_back(
            sp, slot, qkv, received[slot], att[slot], lse[slot], d_own[slot], d_peer[slot]
        )

    own_0, *sent_0 = back(after(sp, picked), 0)
    pieces_0 = [swap(rows, 1 + i) for i, rows in enumerate(sent_0)]
    d_own[1], d_peer[1] = landed[None], to_core(landed)
    balanced = [att[0], moved]
    att_other.append(swap(moved, 1))
    partial = weigh(after(sp, sent_0[1]), scaled, scaled_peer, balanced, att_other)
    spread = lax.all_to_all(
        partial.reshape(16, WIDTH // 16, WIDTH),
        "dp",
        split_axis=0,
        concat_axis=0,
        tiled=True,
        axis_index_groups=plane_groups(),
    )
    own_1, *sent_1 = back(after(sp, partial), 1)
    pieces_1 = [swap(rows, 1 + i) for i, rows in enumerate(sent_1)]
    mixed, gate_part = project(
        after(sp, sent_1[1]), balanced, att_other, out_weight, gate, cotangent
    )
    gate_grad = gate_part + swap(gate_part, 1) + swap(gate_part, 2) + swap(gate_part, 3)
    grads = join(after(sp, gate_part), 0, own_0, *pieces_0, None)
    quarters = sum_weights(after(sp, grads), spread)
    weight_grad = finish_weights(quarters)
    grads = join(after(sp, quarters[0]), 1, own_1, *pieces_1, grads)
    return (mixed, gate_grad, weight_grad, grads)


def solution(mesh):
    in_specs = (P("dp", "seq", None), P("dp", None), P("dp", "seq", None), P(), P(), P(), P())
    out_specs = (P("dp", "seq", None), P("dp", None), P(None, ("dp", "seq")), P("dp", "seq", None))
    return jax.shard_map(body, mesh=mesh, in_specs=in_specs, out_specs=out_specs, check_vma=False)
```

time: 720 us -> 279 us (0.39)
  waiting for transfers between devices: 334 us -> 80.4 us
  local copies, waits for them, and re-layouts: 144 us -> 9 us
  Pallas kernels: 0 us -> 106 us
  matrix products: 70.4 us -> 0 us
  other arithmetic: 47.2 us -> 2.82 us
  blocking collectives: 24 us -> 0 us
  between operations: 17.9 us -> 0.94 us
    all_to_all x8 -> x5, waiting for transfers between devices: 257 us -> 11.7 us  [the longest x2 11.6 us: land(): lax.all_to_all(arranged, 'dp', split_axis=0, concat_axis=0, tiled=True)]
    pallas_call x0 -> x14, Pallas kernels: none -> 106 us  [the longest x2 25 us: attend_back(): pl.pallas_call(functools.partial(bwd_kernel, slot), grid_spec=pltpu.Prefe...]
    all_gather x1 -> x0, waiting for transfers between devices: 76.6 us -> none  [body(): portion = lax.all_gather(scaled, 'seq', axis=1, tiled=True)]
    dot_general x38 -> x0, matrix products: 70.4 us -> none  [the longest x1 13.5 us: body(): jnp.einsum('cnd,hd->cnh', portion, weight_rows, preferred_element_type=jn...]
    ppermute x0 -> x24, waiting for transfers between devices: none -> 68.8 us  [the longest x20 68.8 us: swap(): return lax.ppermute(x, 'seq', [(i, i ^ step) for i in range(4)])]
    ppermute x0 -> x24, starting transfers between devices: none -> 42.6 us  [the longest x20 28 us: swap(): return lax.ppermute(x, 'seq', [(i, i ^ step) for i in range(4)])]
    all_to_all x8 -> x5, starting transfers between devices: 70.2 us -> 33.1 us  [the longest x2 15.2 us: spread_out(): lax.all_to_all(portions, 'dp', split_axis=0, concat_axis=0, tiled=True)]
    another operation x30 -> x0, local copies, waits for them, and re-layouts: 29.8 us -> none  [the longest x3 10.1 us: body(): working = jnp.stack([qkv[0], arrived])]
  transfers between devices with their start and end apart: 10 -> 29, of which waited for: 8 -> 6; matrix products, arithmetic and copies ran while one was open for 8% -> 0% of each run, Pallas kernels for 0% -> 37%
where the time goes in v1:
time: 279 us; the launch traced here: 275 us
  Pallas kernels  106 us (38%)
  waiting for transfers between devices  80.4 us (29%)
  starting transfers between devices  75.8 us (27%)
  local copies, waits for them, and re-layouts  9 us (3%)
  other arithmetic  2.82 us (1%)
    ppermute x20, waiting for transfers between devices, swap(): return lax.ppermute(x, 'seq', [(i, i ^ step) for i in range(4)])  68.8 us
    ppermute x20, starting transfers between devices, swap(): return lax.ppermute(x, 'seq', [(i, i ^ step) for i in range(4)])  28 us
    pallas_call x2, Pallas kernels, attend_back(): pl.pallas_call(functools.partial(bwd_kernel, slot), grid_spec=pltpu.Prefe...  25 us
    pallas_call x2, Pallas kernels, attend(): pl.pallas_call(functools.partial(fwd_kernel, slot), grid_spec=pltpu.Prefe...  16.9 us
    all_to_all x2, starting transfers between devices, spread_out(): lax.all_to_all(portions, 'dp', split_axis=0, concat_axis=0, tiled=True)  15.2 us
    ppermute x4, starting transfers between devices, finish_weights(): lax.ppermute(quarter, ('dp', 'seq'), final_moves(step)).astype(jnp.float32)  14.7 us
    pallas_call x1, Pallas kernels, scaled_rows(): pl.pallas_call(rows_kernel, grid_spec=pltpu.PrefetchScalarGridSpec(num_sc...  13.6 us
    all_to_all x2, waiting for transfers between devices, land(): lax.all_to_all(arranged, 'dp', split_axis=0, concat_axis=0, tiled=True)  11.6 us
  transfers between devices with their start and end apart: 29, of which 6 were waited for; matrix products, arithmetic and copies ran while one was open for 0% of the time, Pallas kernels for 37%

profile of v1, /device:TPU:1, one launch (start us, length us, event | category | flops | bytes accessed | tf_op | source)
XLA Modules:
  0.0 275.3 jit_solution(14728029454355910535)
XLA Ops:
  0.7 0.7 dynamic_slice.7
  1.4 0.7 dynamic_slice.6
  2.1 0.1 add_bitcast_fusion.1
  2.2 0.1 copy.13
  2.3 0.1 subtract_select_fusion
  2.4 0.7 pad_add_fusion.sp
  3.0 3.6 %shard_map.102 = (bf16[3,256,768]{2,1,0:T(8,128)(2,1)}, bf16[2,256,768]{2,1,0:T(8,128)(2,1)}, bf16[2,256,768]{2,1,0:T(8,128)(2,1)}) custom-call(s32[2,5]{1,0:T(2,128)} %pad_add_fusion.sp, bf16[2,256,4608]{2,1,0:T(8,128)(2,1)} %v0.7, bf16[2,256,4608]{2,1,0:T(8,128)(2,1)} %v0.7, bf16[2,256,4608]{2,1,0:T(8,128)(2,1)} %v0.7, bf16[2,256,4608]{2,1,0:T(8,128)(2,1)} %v0.7, ...), custom_call_target="tpu_custom_call" | custom-call | flops 1000000 | bytes 5000000 | tf_op jit(solution)/shard_map/pallas_call | solution.py:67
  6.7 1.4 collective-permute-start
  8.0 3.7 %collective-permute-start.2 = (bf16[2,256,768]{2,1,0:T(8,128)(2,1)}, bf16[2,256,768]{2,1,0:T(8,128)(2,1)S(1)}, u32[]{:S(2)}, u32[]{:S(2)}) collective-permute-start(bf16[2,256,768]{2,1,0:T(8,128)(2,1)} %get-tuple-element.54), channel_id=1, source_target_pairs={{0,3},{1,2},{2,1},{3,0},{4,7},{5,6},{6,5},{7,4},{8,11},{9,10},{10,... | collective-permute-start | bytes 2359304 | tf_op jit(solution)/shard_map/ppermute | solution.py:38
  11.7 0.0 collective-permute-start.1
  11.8 13.6 %scaled_rows.1 = (bf16[2,256,1536]{2,1,0:T(8,128)(2,1)}, bf16[2,256,1536]{2,1,0:T(8,128)(2,1)}, bf16[256,1536]{1,0:T(8,128)(2,1)}, bf16[256,1536]{1,0:T(8,128)(2,1)}, bf16[1,256,768]{2,1,0:T(8,128)(2,1)}) custom-call(s32[2,5]{1,0:T(2,128)} %pad_add_fusion.sp, bf16[2,256,3072]{2,1,0:T(8,128)(2,1)} %cotangent.3, f32[2,3072]{1,0:T(2,128)} %gate.3, ...), custom_call_target="tpu_custom_call" | custom-call | flops 4831838208 | bytes 17000000 | tf_op jit(solution)/shard_map/scaled_rows/pallas_call | solution.py:323
  25.4 7.9 %all-to-all-start = ((bf16[32,8,1536]{2,1,0:T(8,128)(2,1)}), bf16[32,8,1536]{2,1,0:T(8,128)(2,1)}, u32[]{:S(2)}, u32[]{:S(2)}) async-start(bf16[32,8,1536]{2,1,0:T(8,128)(2,1)} %bitcast.23), calls=%async_computation | async-start | bytes 1572864 | tf_op jit(solution)/shard_map/all_to_all | solution.py:498
  33.2 3.7 %shard_map.103 = (bf16[3,256,768]{2,1,0:T(8,128)(2,1)}, bf16[2,256,768]{2,1,0:T(8,128)(2,1)}, bf16[2,256,768]{2,1,0:T(8,128)(2,1)}) custom-call(s32[2,5]{1,0:T(2,128)} %pad_add_fusion.sp, bf16[2,256,4608]{2,1,0:T(8,128)(2,1)} %v0.7, bf16[2,256,4608]{2,1,0:T(8,128)(2,1)} %v0.7, bf16[2,256,4608]{2,1,0:T(8,128)(2,1)} %v0.7, bf16[2,256,4608]{2,1,0:T(8,128)(2,1)} %v0.7, ...), custom_call_target="tpu_custom_call" | custom-call | flops 1000000 | bytes 5000000 | tf_op jit(solution)/shard_map/pallas_call | solution.py:67
  36.9 1.0 collective-permute-start.3
  37.9 3.3 %collective-permute-start.5 = (bf16[2,256,768]{2,1,0:T(8,128)(2,1)}, bf16[2,256,768]{2,1,0:T(8,128)(2,1)}, u32[]{:S(2)}, u32[]{:S(2)}) collective-permute-start(bf16[2,256,768]{2,1,0:T(8,128)(2,1)} %get-tuple-element.59), channel_id=1, source_target_pairs={{0,3},{1,2},{2,1},{3,0},{4,7},{5,6},{6,5},{7,4},{8,11},{9,10},{10,... | collective-permute-start | bytes 2359304 | tf_op jit(solution)/shard_map/ppermute | solution.py:38
  41.2 0.1 collective-permute-start.4
  41.3 13.3 %collective-permute-done.1.k2.v2 = bf16[2,256,768]{2,1,0:T(8,128)(2,1)} collective-permute-done((bf16[2,256,768]{2,1,0:T(8,128)(2,1)}, bf16[2,256,768]{2,1,0:T(8,128)(2,1)}, u32[]{:S(2)}, u32[]{:S(2)}) %collective-permute-start.1) | collective-permute-done | bytes 786464 | tf_op jit(solution)/shard_map/ppermute | solution.py:38
  54.7 1.0 copy-done
  55.7 8.4 %shard_map.104 = (bf16[2,256,768]{2,1,0:T(8,128)(2,1)}, f32[6,8,512]{2,1,0:T(8,128)}) custom-call(s32[2,5]{1,0:T(2,128)} %pad_add_fusion.sp, bf16[2,256,4608]{2,1,0:T(8,128)(2,1)} %v0.7, bf16[2,256,4608]{2,1,0:T(8,128)(2,1)} %v0.7, bf16[2,256,4608]{2,1,0:T(8,128)(2,1)} %v0.7, bf16[3,256,768]{2,1,0:T(8,128)(2,1)} %copy-done, bf16[3,256,768]{2,1,0:T(8,128)(2,1)} %copy-done, ...), custom_call_target="tpu_custom_call" | custom-call | flops 1610612736 | bytes 5000000 | tf_op jit(solution)/shard_map/pallas_call | solution.py:174
  64.1 0.0 copy-start.15
  64.1 7.4 %all-to-all-start.1 = ((bf16[32,16,768]{2,1,0:T(8,128)(2,1)}), bf16[32,16,768]{2,1,0:T(8,128)(2,1)S(1)}, u32[]{:S(2)}, u32[]{:S(2)}) async-start(bf16[32,16,768]{2,1,0:T(8,128)(2,1)} %bitcast.18), calls=%async_computation.1 | async-start | bytes 1572864 | tf_op jit(solution)/shard_map/all_to_all | solution.py:498
  71.5 2.0 collective-permute-start.7
  73.5 0.6 select_reduce_fusion.order
  74.1 2.9 %pick.2 = bf16[32,8,1536]{2,1,0:T(8,128)(2,1)} custom-call(s32[32]{0:T(128)} %order, bf16[32,8,1536]{2,1,0:T(8,128)(2,1)} %all-to-all-done.rows), custom_call_target="tpu_custom_call" | custom-call | flops 1000000 | bytes 1572864 | tf_op jit(solution)/shard_map/pick/pallas_call | solution.py:264
  77.0 19.8 %collective-permute-done.4.k2.v2 = bf16[2,256,768]{2,1,0:T(8,128)(2,1)} collective-permute-done((bf16[2,256,768]{2,1,0:T(8,128)(2,1)}, bf16[2,256,768]{2,1,0:T(8,128)(2,1)}, u32[]{:S(2)}, u32[]{:S(2)}) %collective-permute-start.4) | collective-permute-done | bytes 786464 | tf_op jit(solution)/shard_map/ppermute | solution.py:38
  96.8 1.1 copy-done.1
  97.9 8.5 %shard_map.105 = (bf16[2,256,768]{2,1,0:T(8,128)(2,1)}, f32[6,8,512]{2,1,0:T(8,128)}) custom-call(s32[2,5]{1,0:T(2,128)} %pad_add_fusion.sp, bf16[2,256,4608]{2,1,0:T(8,128)(2,1)} %v0.7, bf16[2,256,4608]{2,1,0:T(8,128)(2,1)} %v0.7, bf16[2,256,4608]{2,1,0:T(8,128)(2,1)} %v0.7, bf16[3,256,768]{2,1,0:T(8,128)(2,1)} %copy-done.1, ...), custom_call_target="tpu_custom_call" | custom-call | flops 1610612736 | bytes 5000000 | tf_op jit(solution)/shard_map/pallas_call | solution.py:174
  106.4 0.9 copy-done.5
  107.3 2.9 %pick.3 = bf16[32,16,768]{2,1,0:T(8,128)(2,1)} custom-call(s32[32]{0:T(128)} %select_reduce_fusion.order, bf16[32,16,768]{2,1,0:T(8,128)(2,1)} %copy-done.5), custom_call_target="tpu_custom_call" | custom-call | flops 1000000 | bytes 1572864 | tf_op jit(solution)/shard_map/pick/pallas_call | solution.py:264
  110.2 7.4 %all-to-all-start.2 = ((bf16[32,16,768]{2,1,0:T(8,128)(2,1)}), bf16[32,16,768]{2,1,0:T(8,128)(2,1)S(1)}, u32[]{:S(2)}, u32[]{:S(2)}) async-start(bf16[32,16,768]{2,1,0:T(8,128)(2,1)} %pick.3), calls=%async_computation.2 | async-start | bytes 1572864 | tf_op jit(solution)/shard_map/all_to_all | solution.py:502
  117.6 1.6 collective-permute-start.8
  119.2 11.6 %all-to-all-done.2 = bf16[32,16,768]{2,1,0:T(8,128)(2,1)S(1)} async-done(((bf16[32,16,768]{2,1,0:T(8,128)(2,1)}), bf16[32,16,768]{2,1,0:T(8,128)(2,1)S(1)}, u32[]{:S(2)}, u32[]{:S(2)}) %all-to-all-start.2) | async-done | bytes 786464 | tf_op jit(solution)/shard_map/all_to_all | solution.py:502
  130.9 2.4 collective-permute-start.9
  133.3 0.0 collective-permute-start.6
  133.3 4.1 %all-to-all-start.3 = ((bf16[32,8,1536]{2,1,0:T(8,128)(2,1)}), bf16[32,8,1536]{2,1,0:T(8,128)(2,1)S(1)}, u32[]{:S(2)}, u32[]{:S(2)}) async-start(bf16[32,8,1536]{2,1,0:T(8,128)(2,1)} %pick.2), calls=%async_computation.3 | async-start | bytes 1572864 | tf_op jit(solution)/shard_map/all_to_all | solution.py:502
  137.4 0.8 copy-done.13
  138.2 12.5 %shard_map.106 = (f32[3,256,768]{2,1,0:T(8,128)}, bf16[3,256,768]{2,1,0:T(8,128)(2,1)}, bf16[2,256,768]{2,1,0:T(8,128)(2,1)}, bf16[2,256,768]{2,1,0:T(8,128)(2,1)}) custom-call(s32[2,5]{1,0:T(2,128)} %pad_add_fusion.sp, bf16[2,256,4608]{2,1,0:T(8,128)(2,1)} %v0.7, bf16[2,256,4608]{2,1,0:T(8,128)(2,1)} %v0.7, bf16[2,256,4608]{2,1,0:T(8,128)(2,1)} %v0.7, ...), custom_call_target="tpu_custom_call" | custom-call | flops 4026531840 | bytes 10000000 | tf_op jit(solution)/shard_map/pallas_call | solution.py:199
  150.8 0.9 copy-done.11
  151.6 9.7 %weigh.1 = bf16[1536,1536]{1,0:T(8,128)(2,1)} custom-call(s32[2,5]{1,0:T(2,128)} %pad_add_fusion.sp, bf16[2,256,1536]{2,1,0:T(8,128)(2,1)} %get-tuple-element.69.scaled_own, bf16[2,256,1536]{2,1,0:T(8,128)(2,1)} %collective-permute-done.7.scaled_peer, bf16[2,256,768]{2,1,0:T(8,128)(2,1)} %get-tuple-element.64.att.a0, bf16[2,256,768]{2,1,0:T(8,128)(2,1)} %bitcast.20, ...), custom_call_target="tpu_custom_call" | custom-call | flops 4831838208 | bytes 12000000 | tf_op jit(solution)/shard_map/weigh/pallas_call | solution.py:417
  161.3 6.4 %all-to-all-start.4 = ((bf16[16,96,1536]{2,1,0:T(8,128)(2,1)}), bf16[16,96,1536]{2,1,0:T(8,128)(2,1)}, u32[]{:S(2)}, u32[]{:S(2)}) async-start(bf16[16,96,1536]{2,1,0:T(8,128)(2,1)} %bitcast.17), calls=%async_computation.4 | async-start | bytes 9437184 | tf_op jit(solution)/shard_map/all_to_all | solution.py:562
  167.8 1.2 collective-permute-start.10
  169.0 3.3 %collective-permute-start.16 = (bf16[2,256,768]{2,1,0:T(8,128)(2,1)}, bf16[2,256,768]{2,1,0:T(8,128)(2,1)S(1)}, u32[]{:S(2)}, u32[]{:S(2)}) collective-permute-start(bf16[2,256,768]{2,1,0:T(8,128)(2,1)} %get-tuple-element.80), channel_id=1, source_target_pairs={{0,3},{1,2},{2,1},{3,0},{4,7},{5,6},{6,5},{7,4},{8,11},{9,10},{10,... | collective-permute-start | bytes 2359304 | tf_op jit(solution)/shard_map/ppermute | solution.py:38
  172.3 0.4 collective-permute-start.14
  172.7 0.7 copy-done.12
  173.4 12.5 %shard_map.107 = (f32[3,256,768]{2,1,0:T(8,128)}, bf16[3,256,768]{2,1,0:T(8,128)(2,1)}, bf16[2,256,768]{2,1,0:T(8,128)(2,1)}, bf16[2,256,768]{2,1,0:T(8,128)(2,1)}) custom-call(s32[2,5]{1,0:T(2,128)} %pad_add_fusion.sp, bf16[2,256,4608]{2,1,0:T(8,128)(2,1)} %v0.7, bf16[2,256,4608]{2,1,0:T(8,128)(2,1)} %v0.7, bf16[2,256,4608]{2,1,0:T(8,128)(2,1)} %v0.7, ...), custom_call_target="tpu_custom_call" | custom-call | flops 4026531840 | bytes 10000000 | tf_op jit(solution)/shard_map/pallas_call | solution.py:199
  185.9 3.3 %collective-permute-start.23 = (bf16[2,256,768]{2,1,0:T(8,128)(2,1)}, bf16[2,256,768]{2,1,0:T(8,128)(2,1)S(1)}, u32[]{:S(2)}, u32[]{:S(2)}) collective-permute-start(bf16[2,256,768]{2,1,0:T(8,128)(2,1)} %get-tuple-element.89), channel_id=1, source_target_pairs={{0,3},{1,2},{2,1},{3,0},{4,7},{5,6},{6,5},{7,4},{8,11},{9,10},{10,... | collective-permute-start | bytes 2359304 | tf_op jit(solution)/shard_map/ppermute | solution.py:38
  189.2 0.0 collective-permute-start.22
  189.3 1.7 collective-permute-done.16.p3
  191.0 1.0 copy-done.10
  191.9 11.6 %project.1 = (bf16[2,256,3072]{2,1,0:T(8,128)(2,1)}, f32[2,3072]{1,0:T(2,128)}) custom-call(s32[2,5]{1,0:T(2,128)} %pad_add_fusion.sp, bf16[2,256,768]{2,1,0:T(8,128)(2,1)} %get-tuple-element.64.att.a0, bf16[2,256,768]{2,1,0:T(8,128)(2,1)} %bitcast.21, bf16[2,256,768]{2,1,0:T(8,128)(2,1)} %copy-done.11, bf16[2,256,768]{2,1,0:T(8,128)(2,1)} %collective-permute-done.9.b1, ...), custom_call_target="tpu_custom_call" | custom-call | flops 4831838208 | bytes 16000000 | tf_op jit(solution)/shard_map/project/pallas_call | solution.py:374
  203.6 3.7 %collective-permute-done.15.p2 = bf16[2,256,768]{2,1,0:T(8,128)(2,1)} collective-permute-done((bf16[2,256,768]{2,1,0:T(8,128)(2,1)}, bf16[2,256,768]{2,1,0:T(8,128)(2,1)}, u32[]{:S(2)}, u32[]{:S(2)}) %collective-permute-start.15) | collective-permute-done | bytes 786464 | tf_op jit(solution)/shard_map/ppermute | solution.py:38
  207.3 4.1 %collective-permute-start.13 = (f32[2,3072]{1,0:T(2,128)}, f32[2,3072]{1,0:T(2,128)S(1)}, u32[]{:S(2)}, u32[]{:S(2)}) collective-permute-start(f32[2,3072]{1,0:T(2,128)} %get-tuple-element.76), channel_id=1, source_target_pairs={{0,3},{1,2},{2,1},{3,0},{4,7},{5,6},{6,5},{7,4},{8,11},{9,10},{10,... | collective-permute-start | bytes 73736 | tf_op jit(solution)/shard_map/ppermute | solution.py:38
  211.4 30.3 %collective-permute-done.13 = f32[2,3072]{1,0:T(2,128)S(1)} collective-permute-done((f32[2,3072]{1,0:T(2,128)}, f32[2,3072]{1,0:T(2,128)S(1)}, u32[]{:S(2)}, u32[]{:S(2)}) %collective-permute-start.13) | collective-permute-done | bytes 24608 | tf_op jit(solution)/shard_map/ppermute | solution.py:38
  241.6 0.1 collective-permute-start.11
  241.8 5.7 %shard_map.108.rest_0_ = bf16[2,256,4608]{2,1,0:T(8,128)(2,1)} custom-call(s32[2,5]{1,0:T(2,128)} %pad_add_fusion.sp, f32[3,256,768]{2,1,0:T(8,128)} %get-tuple-element.78.own, bf16[3,256,768]{2,1,0:T(8,128)(2,1)} %copy-done.8, bf16[2,256,768]{2,1,0:T(8,128)(2,1)} %collective-permute-done.15.p2, bf16[2,256,768]{2,1,0:T(8,128)(2,1)} %copy-done.10), custom_call_target="tpu_custom_call" | custom-call | flops 1000000 | bytes 10000000 | tf_op jit(solution)/shard_map/pallas_call | solution.py:240
  247.5 5.0 %sum_weights.1 = (bf16[24,1536]{1,0:T(8,128)(2,1)}, bf16[24,1536]{1,0:T(8,128)(2,1)}, bf16[24,1536]{1,0:T(8,128)(2,1)}, bf16[24,1536]{1,0:T(8,128)(2,1)}) custom-call(s32[2,5]{1,0:T(2,128)} %pad_add_fusion.sp, bf16[16,96,1536]{2,1,0:T(8,128)(2,1)} %all-to-all-done.4.spread), custom_call_target="tpu_custom_call" | custom-call | flops 5000000 | bytes 5000000 | tf_op jit(solution)/shard_map/sum_weights/pallas_call | solution.py:468
  252.5 3.2 %collective-permute-start.18 = (bf16[24,1536]{1,0:T(8,128)(2,1)}, bf16[24,1536]{1,0:T(8,128)(2,1)S(1)}, u32[]{:S(2)}, u32[]{:S(2)}) collective-permute-start(bf16[24,1536]{1,0:T(8,128)(2,1)} %get-tuple-element.83), channel_id=1, source_target_pairs={{0,1},{1,65},{2,0},{3,64},{4,3},{5,67},{6,2},{7,66},{8,5},{9,69},{... | collective-permute-start | bytes 221192 | tf_op jit(solution)/shard_map/ppermute | solution.py:485
  255.6 3.2 %collective-permute-start.19 = (bf16[24,1536]{1,0:T(8,128)(2,1)}, bf16[24,1536]{1,0:T(8,128)(2,1)S(1)}, u32[]{:S(2)}, u32[]{:S(2)}) collective-permute-start(bf16[24,1536]{1,0:T(8,128)(2,1)} %get-tuple-element.84), channel_id=1, source_target_pairs={{0,2},{1,66},{2,3},{3,67},{4,0},{5,64},{6,1},{7,65},{8,6},{9,70},{... | collective-permute-start | bytes 221192 | tf_op jit(solution)/shard_map/ppermute | solution.py:485
  258.9 4.9 %collective-permute-start.20 = (bf16[24,1536]{1,0:T(8,128)(2,1)}, bf16[24,1536]{1,0:T(8,128)(2,1)S(1)}, u32[]{:S(2)}, u32[]{:S(2)}) collective-permute-start(bf16[24,1536]{1,0:T(8,128)(2,1)} %get-tuple-element.85), channel_id=1, source_target_pairs={{0,3},{1,67},{2,2},{3,66},{4,1},{5,65},{6,0},{7,64},{8,7},{9,71},{... | collective-permute-start | bytes 221192 | tf_op jit(solution)/shard_map/ppermute | solution.py:485
  263.8 3.4 %collective-permute-start.17 = (bf16[24,1536]{1,0:T(8,128)(2,1)}, bf16[24,1536]{1,0:T(8,128)(2,1)S(1)}, u32[]{:S(2)}, u32[]{:S(2)}) collective-permute-start(bf16[24,1536]{1,0:T(8,128)(2,1)} %get-tuple-element.82), channel_id=1, source_target_pairs={{0,0},{1,64},{2,1},{3,65},{4,2},{5,66},{6,3},{7,67},{8,4},{9,68},{... | collective-permute-start | bytes 221192 | tf_op jit(solution)/shard_map/ppermute | solution.py:485
  267.2 0.6 add_add_fusion
  267.8 1.1 copy-done.7
  268.9 5.7 %shard_map.109 = bf16[2,256,4608]{2,1,0:T(8,128)(2,1)} custom-call(s32[2,5]{1,0:T(2,128)} %pad_add_fusion.sp, f32[3,256,768]{2,1,0:T(8,128)} %get-tuple-element.87.own, bf16[3,256,768]{2,1,0:T(8,128)(2,1)} %copy-done.7, bf16[2,256,768]{2,1,0:T(8,128)(2,1)} %collective-permute-done.22.p2, ...), custom_call_target="tpu_custom_call", output_to_operand_aliasing={{}: (5, {})} | custom-call | flops 1000000 | bytes 10000000 | tf_op jit(solution)/shard_map/pallas_call | solution.py:240
  274.6 0.7 add_bitcast_fusion
  (52 shorter events, 0.2 us)
Async XLA Ops:
  6.7 48.0 %collective-permute-start = (bf16[3,256,768]{2,1,0:T(8,128)(2,1)}, bf16[3,256,768]{2,1,0:T(8,128)(2,1)S(1)}, u32[]{:S(2)}, u32[]{:S(2)}) collective-permute-start(bf16[3,256,768]{2,1,0:T(8,128)(2,1)} %get-tuple-element.53), channel_id=1, source_target_pairs={{0,1},{1,0},{2,3},{3,2},{4,5},{5,4},{6,7},{7,6},{8,9},{9,8},{10,11... | collective-permute-start | bytes 3538952 | tf_op jit(solution)/shard_map/ppermute | solution.py:38
  8.0 33.2 %collective-permute-start.2 = (bf16[2,256,768]{2,1,0:T(8,128)(2,1)}, bf16[2,256,768]{2,1,0:T(8,128)(2,1)S(1)}, u32[]{:S(2)}, u32[]{:S(2)}) collective-permute-start(bf16[2,256,768]{2,1,0:T(8,128)(2,1)} %get-tuple-element.54), channel_id=1, source_target_pairs={{0,3},{1,2},{2,1},{3,0},{4,7},{5,6},{6,5},{7,4},{8,11},{9,10},{10,... | collective-permute-start | bytes 2359304 | tf_op jit(solution)/shard_map/ppermute | solution.py:38
  11.7 42.9 %collective-permute-start.1 = (bf16[2,256,768]{2,1,0:T(8,128)(2,1)}, bf16[2,256,768]{2,1,0:T(8,128)(2,1)}, u32[]{:S(2)}, u32[]{:S(2)}) collective-permute-start(bf16[2,256,768]{2,1,0:T(8,128)(2,1)} %get-tuple-element.47), channel_id=1, source_target_pairs={{0,2},{1,3},{2,0},{3,1},{4,6},{5,7},{6,4},{7,5},{8,10},{9,11},{10,... | collective-permute-start | bytes 2359304 | tf_op jit(solution)/shard_map/ppermute | solution.py:38
  25.4 38.8 %all-to-all-start = ((bf16[32,8,1536]{2,1,0:T(8,128)(2,1)}), bf16[32,8,1536]{2,1,0:T(8,128)(2,1)}, u32[]{:S(2)}, u32[]{:S(2)}) async-start(bf16[32,8,1536]{2,1,0:T(8,128)(2,1)} %bitcast.23), calls=%async_computation | async-start | bytes 1572864 | tf_op jit(solution)/shard_map/all_to_all | solution.py:498
  36.9 59.9 %collective-permute-start.3 = (bf16[3,256,768]{2,1,0:T(8,128)(2,1)}, bf16[3,256,768]{2,1,0:T(8,128)(2,1)S(1)}, u32[]{:S(2)}, u32[]{:S(2)}) collective-permute-start(bf16[3,256,768]{2,1,0:T(8,128)(2,1)} %get-tuple-element.58), channel_id=1, source_target_pairs={{0,1},{1,0},{2,3},{3,2},{4,5},{5,4},{6,7},{7,6},{8,9},{9,8},{10,11... | collective-permute-start | bytes 3538952 | tf_op jit(solution)/shard_map/ppermute | solution.py:38
  37.9 39.1 %collective-permute-start.5 = (bf16[2,256,768]{2,1,0:T(8,128)(2,1)}, bf16[2,256,768]{2,1,0:T(8,128)(2,1)}, u32[]{:S(2)}, u32[]{:S(2)}) collective-permute-start(bf16[2,256,768]{2,1,0:T(8,128)(2,1)} %get-tuple-element.59), channel_id=1, source_target_pairs={{0,3},{1,2},{2,1},{3,0},{4,7},{5,6},{6,5},{7,4},{8,11},{9,10},{10,... | collective-permute-start | bytes 2359304 | tf_op jit(solution)/shard_map/ppermute | solution.py:38
  41.2 13.5 %copy-start.2 = (bf16[2,256,768]{2,1,0:T(8,128)(2,1)}, bf16[2,256,768]{2,1,0:T(8,128)(2,1)S(1)}, u32[]{:S(2)}) copy-start(bf16[2,256,768]{2,1,0:T(8,128)(2,1)S(1)} %collective-permute-done.2.k3.v3) | copy-start | bytes 2359300
  41.2 55.6 %collective-permute-start.4 = (bf16[2,256,768]{2,1,0:T(8,128)(2,1)}, bf16[2,256,768]{2,1,0:T(8,128)(2,1)}, u32[]{:S(2)}, u32[]{:S(2)}) collective-permute-start(bf16[2,256,768]{2,1,0:T(8,128)(2,1)} %get-tuple-element.51), channel_id=1, source_target_pairs={{0,2},{1,3},{2,0},{3,1},{4,6},{5,7},{6,4},{7,5},{8,10},{9,11},{10,... | collective-permute-start | bytes 2359304 | tf_op jit(solution)/shard_map/ppermute | solution.py:38
  54.7 1.0 copy-start
  64.1 9.4 %copy-start.15 = (s32[32]{0:T(128)S(1)}, s32[32]{0:T(128)}, u32[]{:S(2)}) copy-start(s32[32]{0:T(128)} %order) | copy-start | bytes 388
  64.1 42.3 %all-to-all-start.1 = ((bf16[32,16,768]{2,1,0:T(8,128)(2,1)}), bf16[32,16,768]{2,1,0:T(8,128)(2,1)S(1)}, u32[]{:S(2)}, u32[]{:S(2)}) async-start(bf16[32,16,768]{2,1,0:T(8,128)(2,1)} %bitcast.18), calls=%async_computation.1 | async-start | bytes 1572864 | tf_op jit(solution)/shard_map/all_to_all | solution.py:498
  71.5 79.2 %collective-permute-start.7 = (bf16[2,256,1536]{2,1,0:T(8,128)(2,1)}, bf16[2,256,1536]{2,1,0:T(8,128)(2,1)}, u32[]{:S(2)}, u32[]{:S(2)}) collective-permute-start(bf16[2,256,1536]{2,1,0:T(8,128)(2,1)} %get-tuple-element.70), channel_id=1, source_target_pairs={{0,1},{1,0},{2,3},{3,2},{4,5},{5,4},{6,7},{7,6},{8,9},{9,8},{10,11... | collective-permute-start | bytes 4718600 | tf_op jit(solution)/shard_map/ppermute | solution.py:38
  96.8 1.1 copy-start.1
  106.4 11.2 %copy-start.4 = (bf16[2,256,768]{2,1,0:T(8,128)(2,1)S(1)}, bf16[2,256,768]{2,1,0:T(8,128)(2,1)}, u32[]{:S(2)}) copy-start(bf16[2,256,768]{2,1,0:T(8,128)(2,1)} %get-tuple-element.64.att.a0) | copy-start | bytes 2359300
  106.4 0.9 copy-start.5
  110.2 20.7 %all-to-all-start.2 = ((bf16[32,16,768]{2,1,0:T(8,128)(2,1)}), bf16[32,16,768]{2,1,0:T(8,128)(2,1)S(1)}, u32[]{:S(2)}, u32[]{:S(2)}) async-start(bf16[32,16,768]{2,1,0:T(8,128)(2,1)} %pick.3), calls=%async_computation.2 | async-start | bytes 1572864 | tf_op jit(solution)/shard_map/all_to_all | solution.py:502
  117.6 33.1 %collective-permute-start.8 = (bf16[2,256,768]{2,1,0:T(8,128)(2,1)S(1)}, bf16[2,256,768]{2,1,0:T(8,128)(2,1)S(1)}, u32[]{:S(2)}, u32[]{:S(2)}) collective-permute-start(bf16[2,256,768]{2,1,0:T(8,128)(2,1)S(1)} %copy-done.4), channel_id=1, source_target_pairs={{0,1},{1,0},{2,3},{3,2},{4,5},{5,4},{6,7},{7,6},{8,9},{9,8},{10,11... | collective-permute-start | bytes 2359304 | tf_op jit(solution)/shard_map/ppermute | solution.py:38
  130.9 19.8 %copy-start.6 = (bf16[32,16,768]{2,1,0:T(8,128)(2,1)}, bf16[32,16,768]{2,1,0:T(8,128)(2,1)S(1)}, u32[]{:S(2)}) copy-start(bf16[32,16,768]{2,1,0:T(8,128)(2,1)S(1)} %all-to-all-done.2) | copy-start | bytes 2359300
  130.9 19.9 %collective-permute-start.9 = (bf16[2,256,768]{2,1,0:T(8,128)(2,1)S(1)}, bf16[2,256,768]{2,1,0:T(8,128)(2,1)}, u32[]{:S(2)}, u32[]{:S(2)}) collective-permute-start(bf16[2,256,768]{2,1,0:T(8,128)(2,1)S(1)} %bitcast.19), channel_id=1, source_target_pairs={{0,1},{1,0},{2,3},{3,2},{4,5},{5,4},{6,7},{7,6},{8,9},{9,8},{10,11... | collective-permute-start | bytes 2359304 | tf_op jit(solution)/shard_map/ppermute | solution.py:38
  133.3 4.1 %collective-permute-start.6 = (bf16[1,256,768]{2,1,0:T(8,128)(2,1)}, bf16[1,256,768]{2,1,0:T(8,128)(2,1)S(1)}, u32[]{:S(2)}, u32[]{:S(2)}) collective-permute-start(bf16[1,256,768]{2,1,0:T(8,128)(2,1)} %get-tuple-element.66), channel_id=1, source_target_pairs={{0,1},{1,0},{2,3},{3,2},{4,5},{5,4},{6,7},{7,6},{8,9},{9,8},{10,11... | collective-permute-start | bytes 1179656 | tf_op jit(solution)/shard_map/ppermute | solution.py:38
  133.3 28.0 %all-to-all-start.3 = ((bf16[32,8,1536]{2,1,0:T(8,128)(2,1)}), bf16[32,8,1536]{2,1,0:T(8,128)(2,1)S(1)}, u32[]{:S(2)}, u32[]{:S(2)}) async-start(bf16[32,8,1536]{2,1,0:T(8,128)(2,1)} %pick.2), calls=%async_computation.3 | async-start | bytes 1572864 | tf_op jit(solution)/shard_map/all_to_all | solution.py:502
  137.4 0.8 copy-start.13
  150.7 0.9 copy-start.11
  161.3 6.4 %copy-start.3 = (bf16[32,8,1536]{2,1,0:T(8,128)(2,1)}, bf16[32,8,1536]{2,1,0:T(8,128)(2,1)S(1)}, u32[]{:S(2)}) copy-start(bf16[32,8,1536]{2,1,0:T(8,128)(2,1)S(1)} %all-to-all-done.3) | copy-start | bytes 2359300
  161.3 86.1 %all-to-all-start.4 = ((bf16[16,96,1536]{2,1,0:T(8,128)(2,1)}), bf16[16,96,1536]{2,1,0:T(8,128)(2,1)}, u32[]{:S(2)}, u32[]{:S(2)}) async-start(bf16[16,96,1536]{2,1,0:T(8,128)(2,1)} %bitcast.17), calls=%async_computation.4 | async-start | bytes 9437184 | tf_op jit(solution)/shard_map/all_to_all | solution.py:562
  167.8 4.9 %collective-permute-start.10 = (bf16[1,256,768]{2,1,0:T(8,128)(2,1)S(1)}, bf16[1,256,768]{2,1,0:T(8,128)(2,1)S(1)}, u32[]{:S(2)}, u32[]{:S(2)}) collective-permute-start(bf16[1,256,768]{2,1,0:T(8,128)(2,1)S(1)} %fusion), channel_id=1, source_target_pairs={{0,1},{1,0},{2,3},{3,2},{4,5},{5,4},{6,7},{7,6},{8,9},{9,8},{10,11... | collective-permute-start | bytes 1179656 | tf_op jit(solution)/shard_map/ppermute | solution.py:38
  169.0 22.0 %collective-permute-start.16 = (bf16[2,256,768]{2,1,0:T(8,128)(2,1)}, bf16[2,256,768]{2,1,0:T(8,128)(2,1)S(1)}, u32[]{:S(2)}, u32[]{:S(2)}) collective-permute-start(bf16[2,256,768]{2,1,0:T(8,128)(2,1)} %get-tuple-element.80), channel_id=1, source_target_pairs={{0,3},{1,2},{2,1},{3,0},{4,7},{5,6},{6,5},{7,4},{8,11},{9,10},{10,... | collective-permute-start | bytes 2359304 | tf_op jit(solution)/shard_map/ppermute | solution.py:38
  172.3 39.1 %collective-permute-start.14 = (bf16[3,256,768]{2,1,0:T(8,128)(2,1)}, bf16[3,256,768]{2,1,0:T(8,128)(2,1)S(1)}, u32[]{:S(2)}, u32[]{:S(2)}) collective-permute-start(bf16[3,256,768]{2,1,0:T(8,128)(2,1)} %get-tuple-element.79), channel_id=1, source_target_pairs={{0,1},{1,0},{2,3},{3,2},{4,5},{5,4},{6,7},{7,6},{8,9},{9,8},{10,11... | collective-permute-start | bytes 3538952 | tf_op jit(solution)/shard_map/ppermute | solution.py:38
  172.7 34.6 %collective-permute-start.15 = (bf16[2,256,768]{2,1,0:T(8,128)(2,1)}, bf16[2,256,768]{2,1,0:T(8,128)(2,1)}, u32[]{:S(2)}, u32[]{:S(2)}) collective-permute-start(bf16[2,256,768]{2,1,0:T(8,128)(2,1)} %get-tuple-element.67), channel_id=1, source_target_pairs={{0,2},{1,3},{2,0},{3,1},{4,6},{5,7},{6,4},{7,5},{8,10},{9,11},{10,... | collective-permute-start | bytes 2359304 | tf_op jit(solution)/shard_map/ppermute | solution.py:38
  172.7 0.7 copy-start.12
  185.9 72.9 %collective-permute-start.23 = (bf16[2,256,768]{2,1,0:T(8,128)(2,1)}, bf16[2,256,768]{2,1,0:T(8,128)(2,1)S(1)}, u32[]{:S(2)}, u32[]{:S(2)}) collective-permute-start(bf16[2,256,768]{2,1,0:T(8,128)(2,1)} %get-tuple-element.89), channel_id=1, source_target_pairs={{0,3},{1,2},{2,1},{3,0},{4,7},{5,6},{6,5},{7,4},{8,11},{9,10},{10,... | collective-permute-start | bytes 2359304 | tf_op jit(solution)/shard_map/ppermute | solution.py:38
  189.2 74.5 %collective-permute-start.22 = (bf16[2,256,768]{2,1,0:T(8,128)(2,1)}, bf16[2,256,768]{2,1,0:T(8,128)(2,1)}, u32[]{:S(2)}, u32[]{:S(2)}) collective-permute-start(bf16[2,256,768]{2,1,0:T(8,128)(2,1)} %get-tuple-element.73), channel_id=1, source_target_pairs={{0,2},{1,3},{2,0},{3,1},{4,6},{5,7},{6,4},{7,5},{8,10},{9,11},{10,... | collective-permute-start | bytes 2359304 | tf_op jit(solution)/shard_map/ppermute | solution.py:38
  191.0 1.0 copy-start.10
  191.9 75.9 %collective-permute-start.21 = (bf16[3,256,768]{2,1,0:T(8,128)(2,1)}, bf16[3,256,768]{2,1,0:T(8,128)(2,1)S(1)}, u32[]{:S(2)}, u32[]{:S(2)}) collective-permute-start(bf16[3,256,768]{2,1,0:T(8,128)(2,1)} %get-tuple-element.88), channel_id=1, source_target_pairs={{0,1},{1,0},{2,3},{3,2},{4,5},{5,4},{6,7},{7,6},{8,9},{9,8},{10,11... | collective-permute-start | bytes 3538952 | tf_op jit(solution)/shard_map/ppermute | solution.py:38
  207.3 34.4 %collective-permute-start.13 = (f32[2,3072]{1,0:T(2,128)}, f32[2,3072]{1,0:T(2,128)S(1)}, u32[]{:S(2)}, u32[]{:S(2)}) collective-permute-start(f32[2,3072]{1,0:T(2,128)} %get-tuple-element.76), channel_id=1, source_target_pairs={{0,3},{1,2},{2,1},{3,0},{4,7},{5,6},{6,5},{7,4},{8,11},{9,10},{10,... | collective-permute-start | bytes 73736 | tf_op jit(solution)/shard_map/ppermute | solution.py:38
  211.4 30.4 %copy-start.8 = (bf16[3,256,768]{2,1,0:T(8,128)(2,1)}, bf16[3,256,768]{2,1,0:T(8,128)(2,1)S(1)}, u32[]{:S(2)}) copy-start(bf16[3,256,768]{2,1,0:T(8,128)(2,1)S(1)} %collective-permute-done.14.p1) | copy-start | bytes 3538948
  211.4 41.1 %collective-permute-start.12 = (f32[2,3072]{1,0:T(2,128)}, f32[2,3072]{1,0:T(2,128)S(1)}, u32[]{:S(2)}, u32[]{:S(2)}) collective-permute-start(f32[2,3072]{1,0:T(2,128)} %get-tuple-element.76), channel_id=1, source_target_pairs={{0,2},{1,3},{2,0},{3,1},{4,6},{5,7},{6,4},{7,5},{8,10},{9,11},{10,... | collective-permute-start | bytes 73736 | tf_op jit(solution)/shard_map/ppermute | solution.py:38
  241.6 14.0 %collective-permute-start.11 = (f32[2,3072]{1,0:T(2,128)}, f32[2,3072]{1,0:T(2,128)S(1)}, u32[]{:S(2)}, u32[]{:S(2)}) collective-permute-start(f32[2,3072]{1,0:T(2,128)} %get-tuple-element.76), channel_id=1, source_target_pairs={{0,1},{1,0},{2,3},{3,2},{4,5},{5,4},{6,7},{7,6},{8,9},{9,8},{10,11... | collective-permute-start | bytes 73736 | tf_op jit(solution)/shard_map/ppermute | solution.py:38
  247.5 19.7 %copy-start.14 = (f32[2,3072]{1,0:T(2,128)S(1)}, f32[2,3072]{1,0:T(2,128)}, u32[]{:S(2)}) copy-start(f32[2,3072]{1,0:T(2,128)} %get-tuple-element.76) | copy-start | bytes 73732
  252.5 22.1 %collective-permute-start.18 = (bf16[24,1536]{1,0:T(8,128)(2,1)}, bf16[24,1536]{1,0:T(8,128)(2,1)S(1)}, u32[]{:S(2)}, u32[]{:S(2)}) collective-permute-start(bf16[24,1536]{1,0:T(8,128)(2,1)} %get-tuple-element.83), channel_id=1, source_target_pairs={{0,1},{1,65},{2,0},{3,64},{4,3},{5,67},{6,2},{7,66},{8,5},{9,69},{... | collective-permute-start | bytes 221192 | tf_op jit(solution)/shard_map/ppermute | solution.py:485
  255.6 18.9 %collective-permute-start.19 = (bf16[24,1536]{1,0:T(8,128)(2,1)}, bf16[24,1536]{1,0:T(8,128)(2,1)S(1)}, u32[]{:S(2)}, u32[]{:S(2)}) collective-permute-start(bf16[24,1536]{1,0:T(8,128)(2,1)} %get-tuple-element.84), channel_id=1, source_target_pairs={{0,2},{1,66},{2,3},{3,67},{4,0},{5,64},{6,1},{7,65},{8,6},{9,70},{... | collective-permute-start | bytes 221192 | tf_op jit(solution)/shard_map/ppermute | solution.py:485
  258.9 9.0 %copy-start.9 = (bf16[2,256,768]{2,1,0:T(8,128)(2,1)}, bf16[2,256,768]{2,1,0:T(8,128)(2,1)S(1)}, u32[]{:S(2)}) copy-start(bf16[2,256,768]{2,1,0:T(8,128)(2,1)S(1)} %collective-permute-done.23.p3) | copy-start | bytes 2359300
  258.9 15.7 %collective-permute-start.20 = (bf16[24,1536]{1,0:T(8,128)(2,1)}, bf16[24,1536]{1,0:T(8,128)(2,1)S(1)}, u32[]{:S(2)}, u32[]{:S(2)}) collective-permute-start(bf16[24,1536]{1,0:T(8,128)(2,1)} %get-tuple-element.85), channel_id=1, source_target_pairs={{0,3},{1,67},{2,2},{3,66},{4,1},{5,65},{6,0},{7,64},{8,7},{9,71},{... | collective-permute-start | bytes 221192 | tf_op jit(solution)/shard_map/ppermute | solution.py:485
  263.8 10.8 %collective-permute-start.17 = (bf16[24,1536]{1,0:T(8,128)(2,1)}, bf16[24,1536]{1,0:T(8,128)(2,1)S(1)}, u32[]{:S(2)}, u32[]{:S(2)}) collective-permute-start(bf16[24,1536]{1,0:T(8,128)(2,1)} %get-tuple-element.82), channel_id=1, source_target_pairs={{0,0},{1,64},{2,1},{3,65},{4,2},{5,66},{6,3},{7,67},{8,4},{9,68},{... | collective-permute-start | bytes 221192 | tf_op jit(solution)/shard_map/ppermute | solution.py:485
  267.8 1.1 copy-start.7

commit v2 on v1

--- a/solution.py
+++ b/solution.py
@@ -14,6 +14,7 @@
 HALF = HEADS_HALF * HD
 WIDTH = 2 * HALF
 TOGETHER = 2
+SHARE = 96
 D = 3072
 NEGATIVE = -1e30
 LOG2E = 1.4426950408889634
@@ -397,46 +398,96 @@
     )(sp, mine[0], mine[1], other[0], other[1], out_weight, out_weight, gate, cotangent)
 
 
-def weigh_kernel(sp, scaled_own, scaled_peer, a0, a1, b0, b1, out):
+def weigh_kernel(sp, scaled_own, scaled_peer, a0, a1, b0, b1, *rest):
+    outs, product = rest[:8], rest[8]
+    step = pl.program_id(0)
     left = jnp.concatenate(
         [scaled_own[0], scaled_peer[0], scaled_own[1], scaled_peer[1]], axis=0
     )
     mine = jnp.concatenate([a0[0], a0[1], a1[0], a1[1]], axis=0)
     other = jnp.concatenate([b0[1], b0[0], b1[1], b1[0]], axis=0)
     first = sp[0, 0] == 0
-    low = jnp.where(first, mine, other)
-    high = jnp.where(first, other, mine)
-    out[:, :HALF] = mm(left, low, TN).astype(jnp.bfloat16)
-    out[:, HALF:] = mm(left, high, TN).astype(jnp.bfloat16)
+    by_x = mm(left, jnp.where(first, mine, other), TN).astype(jnp.bfloat16)
+    for x_step in range(4):
+
+        @pl.when(step == x_step)
+        def _():
+            outs[x_step][...] = by_x
+
+    product[...] = mm(left, jnp.where(first, other, mine), TN)
+    for y_step in range(4):
+        start = pl.multiple_of((sp[1, 5] ^ y_step) * SHARE, 8)
+        rows = product[pl.ds(start, SHARE), :].astype(jnp.bfloat16)
+        outs[4 + y_step][sp[0, 5] ^ step] = rows
 
 
 def weigh(sp, scaled, scaled_peer, mine, other):
-    rows = 384
-    steps = D // 2 // rows
+    rows = D // 8
     pair = pl.BlockSpec((2, ROWS, HALF), lambda d, sp: (0, 0, 0))
+    wide = pl.BlockSpec((2, ROWS, rows), lambda d, sp: (0, 0, sp[0, 5] ^ d))
     return pl.pallas_call(
         weigh_kernel,
         grid_spec=pltpu.PrefetchScalarGridSpec(
             num_scalar_prefetch=1,
-            grid=(steps,),
-            in_specs=[
-                pl.BlockSpec((2, ROWS, rows), lambda d, sp: (0, 0, d)),
-                pl.BlockSpec((2, ROWS, rows), lambda d, sp: (0, 0, d)),
-                pair,
-                pair,
-                pair,
-                pair,
-            ],
-            out_specs=pl.BlockSpec((rows, WIDTH), lambda d, sp: (d, 0)),
-        ),
-        out_shape=jax.ShapeDtypeStruct((D // 2, WIDTH), jnp.bfloat16),
+            grid=(4,),
+            in_specs=[wide, wide, pair, pair, pair, pair],
+            out_specs=[pl.BlockSpec((rows, HALF), lambda d, sp: (0, 0))] * 4
+            + [pl.BlockSpec((4, SHARE, HALF), lambda d, sp: (0, 0, 0))] * 4,
+            scratch_shapes=[pltpu.VMEM((rows, HALF), jnp.float32)],
+        ),
+        out_shape=[jax.ShapeDtypeStruct((rows, HALF), jnp.bfloat16)] * 4
+        + [jax.ShapeDtypeStruct((4, SHARE, HALF), jnp.bfloat16)] * 4,
         cost_estimate=cost(2 * 1024 * WIDTH * D // 2, 1.2e7),
         name="weigh",
     )(sp, scaled, scaled_peer, mine[0], mine[1], other[0], other[1])
 
 
-def plane_groups():
-    return [[2 * xy + z_low for xy in range(16)] for z_low in range(2)]
+def along_x(x, step):
+    return lax.ppermute(x, "dp", [(g, g ^ (step << 3)) for g in range(32)])
+
+
+def along_y(x, step):
+    return lax.ppermute(x, "dp", [(g, g ^ (step << 1)) for g in range(32)])
+
+
+def add_up(refs):
+    total = refs[0][...].astype(jnp.float32)
+    for ref in refs[1:]:
+        total = total + ref[...].astype(jnp.float32)
+    return total
+
+
+def part_kernel(sp, *refs):
+    by_x, by_y, outs, total = refs[:4], refs[4:8], refs[8:16], refs[16]
+    total[...] = add_up(by_x)
+    for step in range(4):
+        start = pl.multiple_of((sp[1, 5] ^ step) * SHARE, 8)
+        outs[step][...] = total[pl.ds(start, SHARE), :].astype(jnp.bfloat16)
+    for step in range(4):
+        place = sp[0, 5] ^ step
+        rows = by_y[0][place].astype(jnp.float32)
+        for ref in by_y[1:]:
+            rows = rows + ref[place].astype(jnp.float32)
+        outs[4 + step][...] = rows.astype(jnp.bfloat16)
+
+
+def sum_parts(sp, by_x, by_y):
+    cols = HALF // 2
+    share = pl.BlockSpec((SHARE, cols), lambda i, sp: (0, i))
+    return pl.pallas_call(
+        part_kernel,
+        grid_spec=pltpu.PrefetchScalarGridSpec(
+            num_scalar_prefetch=1,
+            grid=(2,),
+            in_specs=[pl.BlockSpec((4 * SHARE, cols), lambda i, sp: (0, i))] * 4
+            + [pl.BlockSpec((4, SHARE, cols), lambda i, sp: (0, 0, i))] * 4,
+            out_specs=[share] * 8,
+            scratch_shapes=[pltpu.VMEM((4 * SHARE, cols), jnp.float32)],
+        ),
+        out_shape=[jax.ShapeDtypeStruct((SHARE, HALF), jnp.bfloat16)] * 8,
+        cost_estimate=cost(5e6, 6e6),
+        name="sum_parts",
+    )(sp, *by_x, *by_y)
 
 
 def final_moves(step):
@@ -451,33 +502,33 @@
     return moves
 
 
-def sum_kernel(sp, spread, *rest):
-    total = rest[-1]
-    total[...] = jnp.sum(spread[...].astype(jnp.float32), axis=0)
-    count = total.shape[0] // 4
-    for step, out in enumerate(rest[:-1]):
+def sum_kernel(sp, *refs):
+    low, high, outs, total = refs[:4], refs[4:8], refs[8:12], refs[12]
+    total[:, :HALF] = add_up(low)
+    total[:, HALF:] = add_up(high)
+    count = SHARE // 4
+    for step, out in enumerate(outs):
         start = pl.multiple_of((sp[1, 0] ^ step) * count, 8)
         out[...] = total[pl.ds(start, count), :].astype(jnp.bfloat16)
 
 
-def sum_weights(sp, spread):
-    groups, count, _ = spread.shape
-    cols = 512
-    quarter = pl.BlockSpec((count // 4, cols), lambda i, sp: (0, i))
-    shape = jax.ShapeDtypeStruct((count // 4, WIDTH), jnp.bfloat16)
+def sum_weights(sp, low, high):
+    def whole(rows, cols):
+        return pl.BlockSpec((rows, cols), lambda i, sp: (0, 0))
+
     return pl.pallas_call(
         sum_kernel,
         grid_spec=pltpu.PrefetchScalarGridSpec(
             num_scalar_prefetch=1,
-            grid=(WIDTH // cols,),
-            in_specs=[pl.BlockSpec((groups, count, cols), lambda i, sp: (0, 0, i))],
-            out_specs=[quarter] * 4,
-            scratch_shapes=[pltpu.VMEM((count, cols), jnp.float32)],
-        ),
-        out_shape=[shape] * 4,
-        cost_estimate=cost(5e6, 5e6),
+            grid=(1,),
+            in_specs=[whole(SHARE, HALF)] * 8,
+            out_specs=[whole(SHARE // 4, WIDTH)] * 4,
+            scratch_shapes=[pltpu.VMEM((SHARE, WIDTH), jnp.float32)],
+        ),
+        out_shape=[jax.ShapeDtypeStruct((SHARE // 4, WIDTH), jnp.bfloat16)] * 4,
+        cost_estimate=cost(1e6, 2e6),
         name="sum_weights",
-    )(sp, spread)
+    )(sp, *low, *high)
 
 
 def finish_weights(quarters):
@@ -517,7 +568,8 @@
     video = lax.dynamic_slice_in_dim(clip_lengths, 2 * group_index, 2)[:, None]
     limits = jnp.where(quarters[None] == 0, text, video - (quarters[None] - 1) * ROWS)
     place = jnp.stack([core, z_place]).astype(jnp.int32)[:, None]
-    sp = jnp.concatenate([place, limits.astype(jnp.int32)], axis=1)
+    plane = jnp.stack([group_index >> 3, (group_index >> 1) & 3]).astype(jnp.int32)[:, None]
+    sp = jnp.concatenate([place, limits.astype(jnp.int32), plane], axis=1)
     first = core == 0
 
     def to_core(rows):
@@ -535,48 +587,49 @@
     )
     d_spread = spread_out(away)
     s1, s2, s3 = prep(after(sp, away), qkv, 0)
-    received[0] = (swap(s1, 1), swap(s2, 2), swap(s3, 3))
+    near_keys = (swap(s1, 1), swap(s3, 3))
+    received[0] = (near_keys[0], swap(s2, 2), near_keys[1])
     d_own[0], d_peer[0] = near[None], swap(near_send, 1)
     scaled_peer = swap(scaled_send, 1)
 
-    att[1], lse[1] = attend(after(sp, s2), 1, qkv, received[1])
-    att_spread = spread_out(att[1].reshape(2 * ROWS, HALF))
-    d_picked = pick(d_spread, after(plan, lse[1]))
-    att[0], lse[0] = attend(after(sp, d_picked), 0, qkv, received[0])
-    att_other = [swap(att[0], 1)]
-    picked = pick(att_spread, after(inverse, lse[0]))
-    moved = land(picked, (2, ROWS, HALF))
-    landed = land(after(d_picked, moved), (ROWS, WIDTH))
+    d_picked = pick(d_spread, after(plan, s2))
+    landed = land(d_picked, (ROWS, WIDTH))
+    att[1], lse[1] = attend(after(sp, d_picked), 1, qkv, received[1])
+    d_own[1], d_peer[1] = landed[None], to_core(landed)
+    att_spread = spread_out(after(att[1], landed).reshape(2 * ROWS, HALF))
 
     def back(sp, slot):
         return attend_back(
             sp, slot, qkv, received[slot], att[slot], lse[slot], d_own[slot], d_peer[slot]
         )
 
+    own_1, r1, r2, r3 = back(sp, 1)
+    pieces_1 = (swap(r1, 1), swap(r3, 3))
+    pieces_1 = (pieces_1[0], swap(r2, 2), pieces_1[1])
+    att[0], lse[0] = attend(after(sp, r2), 0, qkv, received[0])
+    att_other = [swap(att[0], 1)]
+    picked = pick(att_spread, after(inverse, lse[0]))
+    moved = land(picked, (2, ROWS, HALF))
     own_0, *sent_0 = back(after(sp, picked), 0)
     pieces_0 = [swap(rows, 1 + i) for i, rows in enumerate(sent_0)]
-    d_own[1], d_peer[1] = landed[None], to_core(landed)
     balanced = [att[0], moved]
     att_other.append(swap(moved, 1))
-    partial = weigh(after(sp, sent_0[1]), scaled, scaled_peer, balanced, att_other)
-    spread = lax.all_to_all(
-        partial.reshape(16, WIDTH // 16, WIDTH),
-        "dp",
-        split_axis=0,
-        concat_axis=0,
-        tiled=True,
-        axis_index_groups=plane_groups(),
-    )
-    own_1, *sent_1 = back(after(sp, partial), 1)
-    pieces_1 = [swap(rows, 1 + i) for i, rows in enumerate(sent_1)]
+    *partial, = weigh(after(sp, sent_0[1]), scaled, scaled_peer, balanced, att_other)
+    by_x, by_y = partial[:4], partial[4:]
+    for step in (2, 1, 3):
+        by_x[step] = along_x(by_x[step], step)
+        by_y[step] = along_y(by_y[step], step)
     mixed, gate_part = project(
-        after(sp, sent_1[1]), balanced, att_other, out_weight, gate, cotangent
+        after(sp, partial[0]), balanced, att_other, out_weight, gate, cotangent
     )
     gate_grad = gate_part + swap(gate_part, 1) + swap(gate_part, 2) + swap(gate_part, 3)
-    grads = join(after(sp, gate_part), 0, own_0, *pieces_0, None)
-    quarters = sum_weights(after(sp, grads), spread)
+    grads = join(after(sp, gate_part), 1, own_1, *pieces_1, None)
+    parts = list(sum_parts(after(sp, grads), by_x, by_y))
+    low = parts[:1] + [along_y(parts[step], step) for step in (1, 2, 3)]
+    high = parts[4:5] + [along_x(parts[4 + step], step) for step in (1, 2, 3)]
+    quarters = sum_weights(sp, low, high)
     weight_grad = finish_weights(quarters)
-    grads = join(after(sp, quarters[0]), 1, own_1, *pieces_1, grads)
+    grads = join(after(sp, quarters[0]), 0, own_0, *pieces_0, grads)
     return (mixed, gate_grad, weight_grad, grads)
 
 

time: 279 us -> 302 us (1.082)
  waiting for transfers between devices: 80.4 us -> 98.9 us
  Pallas kernels: 106 us -> 111 us
    ppermute x0 -> x12, waiting for transfers between devices: none -> 35 us  [the longest x6 27.6 us: along_x(): return lax.ppermute(x, 'dp', [(g, g ^ step << 3) for g in range(32)])]
    ppermute x20, waiting for transfers between devices: 68.8 us -> 45.2 us  [swap(): return lax.ppermute(x, 'seq', [(i, i ^ step) for i in range(4)])]
    ppermute x0 -> x12, starting transfers between devices: none -> 9.08 us  [the longest x6 5.69 us: along_y(): return lax.ppermute(x, 'dp', [(g, g ^ step << 1) for g in range(32)])]
    all_to_all x1 -> x0, starting transfers between devices: 6.42 us -> none  [body(): lax.all_to_all(partial.reshape(16, WIDTH // 16, WIDTH), 'dp', split_axis=...]
    all_to_all x2, waiting for transfers between devices: 0.01 us -> 5.53 us  [spread_out(): lax.all_to_all(portions, 'dp', split_axis=0, concat_axis=0, tiled=True)]
    pallas_call x0 -> x1, Pallas kernels: none -> 4.08 us  [sum_parts(): pl.pallas_call(part_kernel, grid_spec=pltpu.PrefetchScalarGridSpec(num_sc...]
    unnamed x32 -> x48, local copies, waits for them, and re-layouts: 7.45 us -> 7.24 us
  transfers between devices with their start and end apart: 29 -> 40, of which waited for: 6 -> 14; matrix products, arithmetic and copies ran while one was open for 0% -> 1% of each run, Pallas kernels for 37% -> 32%
where the time goes in v2:
time: 302 us; the launch traced here: 298 us
  Pallas kernels  111 us (37%)
  waiting for transfers between devices  98.9 us (33%)
  starting transfers between devices  74 us (25%)
  local copies, waits for them, and re-layouts  8.89 us (3%)
  other arithmetic  4.02 us (1%)
    ppermute x20, waiting for transfers between devices, swap(): return lax.ppermute(x, 'seq', [(i, i ^ step) for i in range(4)])  45.2 us
    ppermute x6, waiting for transfers between devices, along_x(): return lax.ppermute(x, 'dp', [(g, g ^ step << 3) for g in range(32)])  27.6 us
    ppermute x20, starting transfers between devices, swap(): return lax.ppermute(x, 'seq', [(i, i ^ step) for i in range(4)])  26 us
    pallas_call x2, Pallas kernels, attend_back(): pl.pallas_call(functools.partial(bwd_kernel, slot), grid_spec=pltpu.Prefe...  25 us
    pallas_call x2, Pallas kernels, attend(): pl.pallas_call(functools.partial(fwd_kernel, slot), grid_spec=pltpu.Prefe...  16.9 us
    all_to_all x2, starting transfers between devices, spread_out(): lax.all_to_all(portions, 'dp', split_axis=0, concat_axis=0, tiled=True)  15.6 us
    pallas_call x1, Pallas kernels, scaled_rows(): pl.pallas_call(rows_kernel, grid_spec=pltpu.PrefetchScalarGridSpec(num_sc...  13.6 us
    all_to_all x2, waiting for transfers between devices, land(): lax.all_to_all(arranged, 'dp', split_axis=0, concat_axis=0, tiled=True)  13.1 us
  transfers between devices with their start and end apart: 40, of which 14 were waited for; matrix products, arithmetic and copies ran while one was open for 1% of the time, Pallas kernels for 32%

profile of v2, /device:TPU:1, one launch (start us, length us, event | category | flops | bytes accessed | tf_op | source)
XLA Modules:
  0.0 298.1 jit_solution(3297760779299636989)
XLA Ops:
  0.7 0.7 dynamic_slice.7
  3.2 3.6 %shard_map.102 = (bf16[3,256,768]{2,1,0:T(8,128)(2,1)}, bf16[2,256,768]{2,1,0:T(8,128)(2,1)}, bf16[2,256,768]{2,1,0:T(8,128)(2,1)}) custom-call(s32[2,6]{1,0:T(2,128)} %pad_add_fusion.sp, bf16[2,256,4608]{2,1,0:T(8,128)(2,1)} %v0.7, bf16[2,256,4608]{2,1,0:T(8,128)(2,1)} %v0.7, bf16[2,256,4608]{2,1,0:T(8,128)(2,1)} %v0.7, bf16[2,256,4608]{2,1,0:T(8,128)(2,1)} %v0.7, ...), custom_call_target="tpu_custom_call" | custom-call | flops 1000000 | bytes 5000000 | tf_op jit(solution)/shard_map/pallas_call | solution.py:68
  6.8 13.6 %scaled_rows.1 = (bf16[2,256,1536]{2,1,0:T(8,128)(2,1)}, bf16[2,256,1536]{2,1,0:T(8,128)(2,1)}, bf16[256,1536]{1,0:T(8,128)(2,1)}, bf16[256,1536]{1,0:T(8,128)(2,1)}, bf16[1,256,768]{2,1,0:T(8,128)(2,1)}) custom-call(s32[2,6]{1,0:T(2,128)} %pad_add_fusion.sp, bf16[2,256,3072]{2,1,0:T(8,128)(2,1)} %cotangent.3, f32[2,3072]{1,0:T(2,128)} %gate.3, ...), custom_call_target="tpu_custom_call" | custom-call | flops 4831838208 | bytes 17000000 | tf_op jit(solution)/shard_map/scaled_rows/pallas_call | solution.py:324
  20.5 9.2 %all-to-all-start = ((bf16[32,8,1536]{2,1,0:T(8,128)(2,1)}), bf16[32,8,1536]{2,1,0:T(8,128)(2,1)S(1)}, u32[]{:S(2)}, u32[]{:S(2)}) async-start(bf16[32,8,1536]{2,1,0:T(8,128)(2,1)} %bitcast.23), calls=%async_computation | async-start | bytes 1572864 | tf_op jit(solution)/shard_map/all_to_all | solution.py:549
  29.7 1.0 collective-permute-start
  30.7 3.3 %collective-permute-start.2 = (bf16[2,256,768]{2,1,0:T(8,128)(2,1)}, bf16[2,256,768]{2,1,0:T(8,128)(2,1)}, u32[]{:S(2)}, u32[]{:S(2)}) collective-permute-start(bf16[2,256,768]{2,1,0:T(8,128)(2,1)} %get-tuple-element.64), channel_id=1, source_target_pairs={{0,3},{1,2},{2,1},{3,0},{4,7},{5,6},{6,5},{7,4},{8,11},{9,10},{10,... | collective-permute-start | bytes 2359304 | tf_op jit(solution)/shard_map/ppermute | solution.py:39
  34.0 3.6 %shard_map.103 = (bf16[3,256,768]{2,1,0:T(8,128)(2,1)}, bf16[2,256,768]{2,1,0:T(8,128)(2,1)}, bf16[2,256,768]{2,1,0:T(8,128)(2,1)}) custom-call(s32[2,6]{1,0:T(2,128)} %pad_add_fusion.sp, bf16[2,256,4608]{2,1,0:T(8,128)(2,1)} %v0.7, bf16[2,256,4608]{2,1,0:T(8,128)(2,1)} %v0.7, bf16[2,256,4608]{2,1,0:T(8,128)(2,1)} %v0.7, bf16[2,256,4608]{2,1,0:T(8,128)(2,1)} %v0.7, ...), custom_call_target="tpu_custom_call" | custom-call | flops 1000000 | bytes 5000000 | tf_op jit(solution)/shard_map/pallas_call | solution.py:68
  37.6 5.5 %all-to-all-done.rows = bf16[32,8,1536]{2,1,0:T(8,128)(2,1)S(1)} async-done(((bf16[32,8,1536]{2,1,0:T(8,128)(2,1)}), bf16[32,8,1536]{2,1,0:T(8,128)(2,1)S(1)}, u32[]{:S(2)}, u32[]{:S(2)}) %all-to-all-start) | async-done | bytes 786464 | tf_op jit(solution)/shard_map/all_to_all | solution.py:549
  43.2 0.9 copy-done.5
  44.1 3.0 pick.2
  47.0 4.6 %all-to-all-start.1 = ((bf16[32,8,1536]{2,1,0:T(8,128)(2,1)}), bf16[32,8,1536]{2,1,0:T(8,128)(2,1)}, u32[]{:S(2)}, u32[]{:S(2)}) async-start(bf16[32,8,1536]{2,1,0:T(8,128)(2,1)} %pick.2), calls=%async_computation.1 | async-start | bytes 1572864 | tf_op jit(solution)/shard_map/all_to_all | solution.py:553
  51.7 3.3 %collective-permute-start.1 = (bf16[2,256,768]{2,1,0:T(8,128)(2,1)}, bf16[2,256,768]{2,1,0:T(8,128)(2,1)}, u32[]{:S(2)}, u32[]{:S(2)}) collective-permute-start(bf16[2,256,768]{2,1,0:T(8,128)(2,1)} %get-tuple-element.63), channel_id=1, source_target_pairs={{0,2},{1,3},{2,0},{3,1},{4,6},{5,7},{6,4},{7,5},{8,10},{9,11},{10,... | collective-permute-start | bytes 2359304 | tf_op jit(solution)/shard_map/ppermute | solution.py:39
  55.0 2.7 collective-permute-start.4
  57.6 9.6 %collective-permute-done.2.k3.v3 = bf16[2,256,768]{2,1,0:T(8,128)(2,1)} collective-permute-done((bf16[2,256,768]{2,1,0:T(8,128)(2,1)}, bf16[2,256,768]{2,1,0:T(8,128)(2,1)}, u32[]{:S(2)}, u32[]{:S(2)}) %collective-permute-start.2) | collective-permute-done | bytes 786464 | tf_op jit(solution)/shard_map/ppermute | solution.py:39
  67.2 2.0 collective-permute-start.6
  69.2 1.2 fusion
  70.4 15.3 %collective-permute-done.1.k2.v2 = bf16[2,256,768]{2,1,0:T(8,128)(2,1)} collective-permute-done((bf16[2,256,768]{2,1,0:T(8,128)(2,1)}, bf16[2,256,768]{2,1,0:T(8,128)(2,1)}, u32[]{:S(2)}, u32[]{:S(2)}) %collective-permute-start.1) | collective-permute-done | bytes 786464 | tf_op jit(solution)/shard_map/ppermute | solution.py:39
  86.3 1.0 copy-done.1
  87.4 8.4 %shard_map.104 = (bf16[2,256,768]{2,1,0:T(8,128)(2,1)}, f32[6,8,512]{2,1,0:T(8,128)}) custom-call(s32[2,6]{1,0:T(2,128)} %pad_add_fusion.sp, bf16[2,256,4608]{2,1,0:T(8,128)(2,1)} %v0.7, bf16[2,256,4608]{2,1,0:T(8,128)(2,1)} %v0.7, bf16[2,256,4608]{2,1,0:T(8,128)(2,1)} %v0.7, bf16[3,256,768]{2,1,0:T(8,128)(2,1)} %copy-done.1, ...), custom_call_target="tpu_custom_call" | custom-call | flops 1610612736 | bytes 5000000 | tf_op jit(solution)/shard_map/pallas_call | solution.py:175
  95.8 6.4 %all-to-all-start.2 = ((bf16[32,16,768]{2,1,0:T(8,128)(2,1)}), bf16[32,16,768]{2,1,0:T(8,128)(2,1)S(1)}, u32[]{:S(2)}, u32[]{:S(2)}) async-start(bf16[32,16,768]{2,1,0:T(8,128)(2,1)} %bitcast.18), calls=%async_computation.2 | async-start | bytes 1572864 | tf_op jit(solution)/shard_map/all_to_all | solution.py:549
  103.2 12.5 %shard_map.105 = (f32[3,256,768]{2,1,0:T(8,128)}, bf16[3,256,768]{2,1,0:T(8,128)(2,1)}, bf16[2,256,768]{2,1,0:T(8,128)(2,1)}, bf16[2,256,768]{2,1,0:T(8,128)(2,1)}) custom-call(s32[2,6]{1,0:T(2,128)} %pad_add_fusion.sp, bf16[2,256,4608]{2,1,0:T(8,128)(2,1)} %v0.7, bf16[2,256,4608]{2,1,0:T(8,128)(2,1)} %v0.7, bf16[2,256,4608]{2,1,0:T(8,128)(2,1)} %v0.7, ...), custom_call_target="tpu_custom_call" | custom-call | flops 4026531840 | bytes 10000000 | tf_op jit(solution)/shard_map/pallas_call | solution.py:200
  115.7 11.5 %collective-permute-done.6.k3.v3 = bf16[2,256,768]{2,1,0:T(8,128)(2,1)} collective-permute-done((bf16[2,256,768]{2,1,0:T(8,128)(2,1)}, bf16[2,256,768]{2,1,0:T(8,128)(2,1)}, u32[]{:S(2)}, u32[]{:S(2)}) %collective-permute-start.6) | collective-permute-done | bytes 786464 | tf_op jit(solution)/shard_map/ppermute | solution.py:39
  127.2 0.9 copy-done.2
  128.1 1.0 copy-done
  129.2 8.4 %shard_map.106 = (bf16[2,256,768]{2,1,0:T(8,128)(2,1)}, f32[6,8,512]{2,1,0:T(8,128)}) custom-call(s32[2,6]{1,0:T(2,128)} %pad_add_fusion.sp, bf16[2,256,4608]{2,1,0:T(8,128)(2,1)} %v0.7, bf16[2,256,4608]{2,1,0:T(8,128)(2,1)} %v0.7, bf16[2,256,4608]{2,1,0:T(8,128)(2,1)} %v0.7, bf16[3,256,768]{2,1,0:T(8,128)(2,1)} %copy-done, bf16[3,256,768]{2,1,0:T(8,128)(2,1)} %copy-done, ...), custom_call_target="tpu_custom_call" | custom-call | flops 1610612736 | bytes 5000000 | tf_op jit(solution)/shard_map/pallas_call | solution.py:175
  137.6 0.9 copy-done.4
  138.5 2.9 pick.3
  141.4 6.4 %all-to-all-start.3 = ((bf16[32,16,768]{2,1,0:T(8,128)(2,1)}), bf16[32,16,768]{2,1,0:T(8,128)(2,1)S(1)}, u32[]{:S(2)}, u32[]{:S(2)}) async-start(bf16[32,16,768]{2,1,0:T(8,128)(2,1)} %pick.3), calls=%async_computation.3 | async-start | bytes 1572864 | tf_op jit(solution)/shard_map/all_to_all | solution.py:553
  148.4 13.1 %all-to-all-done.3 = bf16[32,16,768]{2,1,0:T(8,128)(2,1)S(1)} async-done(((bf16[32,16,768]{2,1,0:T(8,128)(2,1)}), bf16[32,16,768]{2,1,0:T(8,128)(2,1)S(1)}, u32[]{:S(2)}, u32[]{:S(2)}) %all-to-all-start.3) | async-done | bytes 786464 | tf_op jit(solution)/shard_map/all_to_all | solution.py:553
  161.5 2.0 collective-permute-start.10
  163.5 0.9 collective-permute-start.15
  164.4 1.6 collective-permute-done.7.do1
  166.0 1.2 collective-permute-start.16
  167.3 12.5 %shard_map.107 = (f32[3,256,768]{2,1,0:T(8,128)}, bf16[3,256,768]{2,1,0:T(8,128)(2,1)}, bf16[2,256,768]{2,1,0:T(8,128)(2,1)}, bf16[2,256,768]{2,1,0:T(8,128)(2,1)}) custom-call(s32[2,6]{1,0:T(2,128)} %pad_add_fusion.sp, bf16[2,256,4608]{2,1,0:T(8,128)(2,1)} %v0.7, bf16[2,256,4608]{2,1,0:T(8,128)(2,1)} %v0.7, bf16[2,256,4608]{2,1,0:T(8,128)(2,1)} %v0.7, ...), custom_call_target="tpu_custom_call" | custom-call | flops 4026531840 | bytes 10000000 | tf_op jit(solution)/shard_map/pallas_call | solution.py:200
  179.9 12.7 %weigh.1 = (bf16[384,768]{1,0:T(8,128)(2,1)}, bf16[384,768]{1,0:T(8,128)(2,1)}, bf16[384,768]{1,0:T(8,128)(2,1)}, bf16[384,768]{1,0:T(8,128)(2,1)}, bf16[4,96,76...) custom-call(s32[2,6]{1,0:T(2,128)} %pad_add_fusion.sp, ...), custom_call_target="tpu_custom_call" | custom-call | flops 4831838208 | bytes 12000000 | tf_op jit(solution)/shard_map/weigh/pallas_call | solution.py:428
  192.5 1.7 collective-permute-start.18
  194.2 7.2 %collective-permute-done.16.p3 = bf16[2,256,768]{2,1,0:T(8,128)(2,1)} collective-permute-done((bf16[2,256,768]{2,1,0:T(8,128)(2,1)}, bf16[2,256,768]{2,1,0:T(8,128)(2,1)}, u32[]{:S(2)}, u32[]{:S(2)}) %collective-permute-start.16) | collective-permute-done | bytes 786464 | tf_op jit(solution)/shard_map/ppermute | solution.py:39
  202.9 0.8 collective-permute-start.35
  203.7 3.5 %collective-permute-done.17.refs_1_ = bf16[384,768]{1,0:T(8,128)(2,1)S(1)} collective-permute-done((bf16[384,768]{1,0:T(8,128)(2,1)}, bf16[384,768]{1,0:T(8,128)(2,1)S(1)}, u32[]{:S(2)}, u32[]{:S(2)}) %collective-permute-start.17) | collective-permute-done | bytes 589856 | tf_op jit(solution)/shard_map/ppermute | solution.py:446
  207.9 12.4 %collective-permute-done.18.refs_2_ = bf16[384,768]{1,0:T(8,128)(2,1)S(1)} collective-permute-done((bf16[384,768]{1,0:T(8,128)(2,1)}, bf16[384,768]{1,0:T(8,128)(2,1)S(1)}, u32[]{:S(2)}, u32[]{:S(2)}) %collective-permute-start.18) | collective-permute-done | bytes 589856 | tf_op jit(solution)/shard_map/ppermute | solution.py:446
  220.3 0.8 collective-permute-start.22
  221.1 9.7 %collective-permute-done.19.refs_3_ = bf16[384,768]{1,0:T(8,128)(2,1)S(1)} collective-permute-done((bf16[384,768]{1,0:T(8,128)(2,1)}, bf16[384,768]{1,0:T(8,128)(2,1)S(1)}, u32[]{:S(2)}, u32[]{:S(2)}) %collective-permute-start.19) | collective-permute-done | bytes 589856 | tf_op jit(solution)/shard_map/ppermute | solution.py:446
  230.8 0.9 collective-permute-start.34
  231.7 0.8 copy-done.14
  232.6 0.8 collective-permute-start.33
  233.3 11.6 %project.1 = (bf16[2,256,3072]{2,1,0:T(8,128)(2,1)}, f32[2,3072]{1,0:T(2,128)}) custom-call(s32[2,6]{1,0:T(2,128)} %pad_add_fusion.sp, bf16[2,256,768]{2,1,0:T(8,128)(2,1)} %get-tuple-element.81.att.a0, bf16[2,256,768]{2,1,0:T(8,128)(2,1)} %bitcast.21, bf16[2,256,768]{2,1,0:T(8,128)(2,1)} %collective-permute-done.9.b0, ...), custom_call_target="tpu_custom_call" | custom-call | flops 4831838208 | bytes 16000000 | tf_op jit(solution)/shard_map/project/pallas_call | solution.py:375
  244.9 5.7 %shard_map.108.rest_0_ = bf16[2,256,4608]{2,1,0:T(8,128)(2,1)} custom-call(s32[2,6]{1,0:T(2,128)} %pad_add_fusion.sp, f32[3,256,768]{2,1,0:T(8,128)} %get-tuple-element.93.own, bf16[3,256,768]{2,1,0:T(8,128)(2,1)} %copy-done.8, bf16[2,256,768]{2,1,0:T(8,128)(2,1)} %copy-done.10, bf16[2,256,768]{2,1,0:T(8,128)(2,1)} %collective-permute-done.16.p3), custom_call_target="tpu_custom_call" | custom-call | flops 1000000 | bytes 10000000 | tf_op jit(solution)/shard_map/pallas_call | solution.py:241
  250.6 4.1 %sum_parts.1 = (bf16[96,768]{1,0:T(8,128)(2,1)}, bf16[96,768]{1,0:T(8,128)(2,1)}, bf16[96,768]{1,0:T(8,128)(2,1)}, bf16[96,768]{1,0:T(8,128)(2,1)}, bf16[96,768]...) custom-call(s32[2,6]{1,0:T(2,128)} %pad_add_fusion.sp, ...), custom_call_target="tpu_custom_call" | custom-call | flops 5000000 | bytes 6000000 | tf_op jit(solution)/shard_map/sum_parts/pallas_call | solution.py:477
  255.1 1.1 collective-permute-start.24
  256.2 2.5 collective-permute-start.25
  258.7 1.7 collective-permute-done.23.refs_1_
  260.4 3.1 %collective-permute-done.24.refs_2_ = bf16[96,768]{1,0:T(8,128)(2,1)S(1)} collective-permute-done((bf16[96,768]{1,0:T(8,128)(2,1)}, bf16[96,768]{1,0:T(8,128)(2,1)S(1)}, u32[]{:S(2)}, u32[]{:S(2)}) %collective-permute-start.24) | collective-permute-done | bytes 147488 | tf_op jit(solution)/shard_map/ppermute | solution.py:450
  263.6 2.5 collective-permute-done.25.refs_3_
  266.1 1.2 collective-permute-start.28
  267.3 3.3 %collective-permute-start.13 = (f32[2,3072]{1,0:T(2,128)S(1)}, f32[2,3072]{1,0:T(2,128)S(1)}, u32[]{:S(2)}, u32[]{:S(2)}) collective-permute-start(f32[2,3072]{1,0:T(2,128)S(1)} %copy-done.22), channel_id=1, source_target_pairs={{0,3},{1,2},{2,1},{3,0},{4,7},{5,6},{6,5},{7,4},{8,11},{9,10},{10,... | collective-permute-start | bytes 73736 | tf_op jit(solution)/shard_map/ppermute | solution.py:39
  270.5 1.3 collective-permute-start.12
  271.8 1.9 collective-permute-done.28.refs_7_
  273.8 0.9 collective-permute-start.11
  274.7 2.9 sum_weights.1
  277.9 3.9 %collective-permute-start.31 = (bf16[24,1536]{1,0:T(8,128)(2,1)}, bf16[24,1536]{1,0:T(8,128)(2,1)S(1)}, u32[]{:S(2)}, u32[]{:S(2)}) collective-permute-start(bf16[24,1536]{1,0:T(8,128)(2,1)} %get-tuple-element.114), channel_id=1, source_target_pairs={{0,2},{1,66},{2,3},{3,67},{4,0},{5,64},{6,1},{7,65},{8,6},{9,70},{... | collective-permute-start | bytes 221192 | tf_op jit(solution)/shard_map/ppermute | solution.py:536
  281.8 4.3 %collective-permute-start.32 = (bf16[24,1536]{1,0:T(8,128)(2,1)}, bf16[24,1536]{1,0:T(8,128)(2,1)S(1)}, u32[]{:S(2)}, u32[]{:S(2)}) collective-permute-start(bf16[24,1536]{1,0:T(8,128)(2,1)} %get-tuple-element.115), channel_id=1, source_target_pairs={{0,3},{1,67},{2,2},{3,66},{4,1},{5,65},{6,0},{7,64},{8,7},{9,71},{... | collective-permute-start | bytes 221192 | tf_op jit(solution)/shard_map/ppermute | solution.py:536
  286.1 3.9 %collective-permute-start.29 = (bf16[24,1536]{1,0:T(8,128)(2,1)}, bf16[24,1536]{1,0:T(8,128)(2,1)S(1)}, u32[]{:S(2)}, u32[]{:S(2)}) collective-permute-start(bf16[24,1536]{1,0:T(8,128)(2,1)} %get-tuple-element.112), channel_id=1, source_target_pairs={{0,0},{1,64},{2,1},{3,65},{4,2},{5,66},{6,3},{7,67},{8,4},{9,68},{... | collective-permute-start | bytes 221192 | tf_op jit(solution)/shard_map/ppermute | solution.py:536
  290.7 1.0 copy-done.7
  291.7 5.7 %shard_map.109 = bf16[2,256,4608]{2,1,0:T(8,128)(2,1)} custom-call(s32[2,6]{1,0:T(2,128)} %pad_add_fusion.sp, f32[3,256,768]{2,1,0:T(8,128)} %get-tuple-element.117.own, bf16[3,256,768]{2,1,0:T(8,128)(2,1)} %copy-done.7, bf16[2,256,768]{2,1,0:T(8,128)(2,1)} %collective-permute-done.34.p2, ...), custom_call_target="tpu_custom_call", output_to_operand_aliasing={{}: (5, {})} | custom-call | flops 1000000 | bytes 10000000 | tf_op jit(solution)/shard_map/pallas_call | solution.py:241
  (93 shorter events, 8.4 us)
Async XLA Ops:
  20.5 22.7 %all-to-all-start = ((bf16[32,8,1536]{2,1,0:T(8,128)(2,1)}), bf16[32,8,1536]{2,1,0:T(8,128)(2,1)S(1)}, u32[]{:S(2)}, u32[]{:S(2)}) async-start(bf16[32,8,1536]{2,1,0:T(8,128)(2,1)} %bitcast.23), calls=%async_computation | async-start | bytes 1572864 | tf_op jit(solution)/shard_map/all_to_all | solution.py:549
  29.7 56.6 %collective-permute-start = (bf16[3,256,768]{2,1,0:T(8,128)(2,1)}, bf16[3,256,768]{2,1,0:T(8,128)(2,1)S(1)}, u32[]{:S(2)}, u32[]{:S(2)}) collective-permute-start(bf16[3,256,768]{2,1,0:T(8,128)(2,1)} %get-tuple-element.62), channel_id=1, source_target_pairs={{0,1},{1,0},{2,3},{3,2},{4,5},{5,4},{6,7},{7,6},{8,9},{9,8},{10,11... | collective-permute-start | bytes 3538952 | tf_op jit(solution)/shard_map/ppermute | solution.py:39
  30.7 36.5 %collective-permute-start.2 = (bf16[2,256,768]{2,1,0:T(8,128)(2,1)}, bf16[2,256,768]{2,1,0:T(8,128)(2,1)}, u32[]{:S(2)}, u32[]{:S(2)}) collective-permute-start(bf16[2,256,768]{2,1,0:T(8,128)(2,1)} %get-tuple-element.64), channel_id=1, source_target_pairs={{0,3},{1,2},{2,1},{3,0},{4,7},{5,6},{6,5},{7,4},{8,11},{9,10},{10,... | collective-permute-start | bytes 2359304 | tf_op jit(solution)/shard_map/ppermute | solution.py:39
  43.2 0.9 copy-start.5
  47.0 22.2 %all-to-all-start.1 = ((bf16[32,8,1536]{2,1,0:T(8,128)(2,1)}), bf16[32,8,1536]{2,1,0:T(8,128)(2,1)}, u32[]{:S(2)}, u32[]{:S(2)}) async-start(bf16[32,8,1536]{2,1,0:T(8,128)(2,1)} %pick.2), calls=%async_computation.1 | async-start | bytes 1572864 | tf_op jit(solution)/shard_map/all_to_all | solution.py:553
  51.7 33.9 %collective-permute-start.1 = (bf16[2,256,768]{2,1,0:T(8,128)(2,1)}, bf16[2,256,768]{2,1,0:T(8,128)(2,1)}, u32[]{:S(2)}, u32[]{:S(2)}) collective-permute-start(bf16[2,256,768]{2,1,0:T(8,128)(2,1)} %get-tuple-element.63), channel_id=1, source_target_pairs={{0,2},{1,3},{2,0},{3,1},{4,6},{5,7},{6,4},{7,5},{8,10},{9,11},{10,... | collective-permute-start | bytes 2359304 | tf_op jit(solution)/shard_map/ppermute | solution.py:39
  55.0 72.3 %collective-permute-start.4 = (bf16[3,256,768]{2,1,0:T(8,128)(2,1)}, bf16[3,256,768]{2,1,0:T(8,128)(2,1)S(1)}, u32[]{:S(2)}, u32[]{:S(2)}) collective-permute-start(bf16[3,256,768]{2,1,0:T(8,128)(2,1)} %get-tuple-element.75), channel_id=1, source_target_pairs={{0,1},{1,0},{2,3},{3,2},{4,5},{5,4},{6,7},{7,6},{8,9},{9,8},{10,11... | collective-permute-start | bytes 3538952 | tf_op jit(solution)/shard_map/ppermute | solution.py:39
  57.6 69.6 %collective-permute-start.5 = (bf16[2,256,768]{2,1,0:T(8,128)(2,1)}, bf16[2,256,768]{2,1,0:T(8,128)(2,1)S(1)}, u32[]{:S(2)}, u32[]{:S(2)}) collective-permute-start(bf16[2,256,768]{2,1,0:T(8,128)(2,1)} %get-tuple-element.68), channel_id=1, source_target_pairs={{0,2},{1,3},{2,0},{3,1},{4,6},{5,7},{6,4},{7,5},{8,10},{9,11},{10,... | collective-permute-start | bytes 2359304 | tf_op jit(solution)/shard_map/ppermute | solution.py:39
  67.2 60.0 %collective-permute-start.6 = (bf16[2,256,768]{2,1,0:T(8,128)(2,1)}, bf16[2,256,768]{2,1,0:T(8,128)(2,1)}, u32[]{:S(2)}, u32[]{:S(2)}) collective-permute-start(bf16[2,256,768]{2,1,0:T(8,128)(2,1)} %get-tuple-element.76), channel_id=1, source_target_pairs={{0,3},{1,2},{2,1},{3,0},{4,7},{5,6},{6,5},{7,4},{8,11},{9,10},{10,... | collective-permute-start | bytes 2359304 | tf_op jit(solution)/shard_map/ppermute | solution.py:39
  85.6 17.6 %collective-permute-start.3 = (bf16[1,256,768]{2,1,0:T(8,128)(2,1)S(1)}, bf16[1,256,768]{2,1,0:T(8,128)(2,1)}, u32[]{:S(2)}, u32[]{:S(2)}) collective-permute-start(bf16[1,256,768]{2,1,0:T(8,128)(2,1)S(1)} %fusion), channel_id=1, source_target_pairs={{0,1},{1,0},{2,3},{3,2},{4,5},{5,4},{6,7},{7,6},{8,9},{9,8},{10,11... | collective-permute-start | bytes 1179656 | tf_op jit(solution)/shard_map/ppermute | solution.py:39
  86.3 1.0 copy-start.1
  95.8 6.8 %copy-start.23 = (s32[32]{0:T(128)S(1)}, s32[32]{0:T(128)}, u32[]{:S(2)}) copy-start(s32[32]{0:T(128)} %order) | copy-start | bytes 388
  95.8 41.8 %all-to-all-start.2 = ((bf16[32,16,768]{2,1,0:T(8,128)(2,1)}), bf16[32,16,768]{2,1,0:T(8,128)(2,1)S(1)}, u32[]{:S(2)}, u32[]{:S(2)}) async-start(bf16[32,16,768]{2,1,0:T(8,128)(2,1)} %bitcast.18), calls=%async_computation.2 | async-start | bytes 1572864 | tf_op jit(solution)/shard_map/all_to_all | solution.py:549
  102.2 65.0 %collective-permute-start.8 = (bf16[2,256,1536]{2,1,0:T(8,128)(2,1)}, bf16[2,256,1536]{2,1,0:T(8,128)(2,1)}, u32[]{:S(2)}, u32[]{:S(2)}) collective-permute-start(bf16[2,256,1536]{2,1,0:T(8,128)(2,1)} %get-tuple-element.87), channel_id=1, source_target_pairs={{0,1},{1,0},{2,3},{3,2},{4,5},{5,4},{6,7},{7,6},{8,9},{9,8},{10,11... | collective-permute-start | bytes 4718600 | tf_op jit(solution)/shard_map/ppermute | solution.py:39
  127.2 0.9 copy-start.2
  128.1 1.0 copy-start
  137.6 10.2 %copy-start.3 = (bf16[2,256,768]{2,1,0:T(8,128)(2,1)S(1)}, bf16[2,256,768]{2,1,0:T(8,128)(2,1)}, u32[]{:S(2)}) copy-start(bf16[2,256,768]{2,1,0:T(8,128)(2,1)} %get-tuple-element.81.att.a0) | copy-start | bytes 2359300
  137.6 0.9 copy-start.4
  141.4 20.1 %all-to-all-start.3 = ((bf16[32,16,768]{2,1,0:T(8,128)(2,1)}), bf16[32,16,768]{2,1,0:T(8,128)(2,1)S(1)}, u32[]{:S(2)}, u32[]{:S(2)}) async-start(bf16[32,16,768]{2,1,0:T(8,128)(2,1)} %pick.3), calls=%async_computation.3 | async-start | bytes 1572864 | tf_op jit(solution)/shard_map/all_to_all | solution.py:553
  147.8 32.0 %collective-permute-start.9 = (bf16[2,256,768]{2,1,0:T(8,128)(2,1)S(1)}, bf16[2,256,768]{2,1,0:T(8,128)(2,1)}, u32[]{:S(2)}, u32[]{:S(2)}) collective-permute-start(bf16[2,256,768]{2,1,0:T(8,128)(2,1)S(1)} %copy-done.3), channel_id=1, source_target_pairs={{0,1},{1,0},{2,3},{3,2},{4,5},{5,4},{6,7},{7,6},{8,9},{9,8},{10,11... | collective-permute-start | bytes 2359304 | tf_op jit(solution)/shard_map/ppermute | solution.py:39
  161.5 18.3 %copy-start.6 = (bf16[32,16,768]{2,1,0:T(8,128)(2,1)}, bf16[32,16,768]{2,1,0:T(8,128)(2,1)S(1)}, u32[]{:S(2)}) copy-start(bf16[32,16,768]{2,1,0:T(8,128)(2,1)S(1)} %all-to-all-done.3) | copy-start | bytes 2359300
  161.5 18.3 %collective-permute-start.10 = (bf16[2,256,768]{2,1,0:T(8,128)(2,1)S(1)}, bf16[2,256,768]{2,1,0:T(8,128)(2,1)}, u32[]{:S(2)}, u32[]{:S(2)}) collective-permute-start(bf16[2,256,768]{2,1,0:T(8,128)(2,1)S(1)} %bitcast.19), channel_id=1, source_target_pairs={{0,1},{1,0},{2,3},{3,2},{4,5},{5,4},{6,7},{7,6},{8,9},{9,8},{10,11... | collective-permute-start | bytes 2359304 | tf_op jit(solution)/shard_map/ppermute | solution.py:39
  163.5 2.5 collective-permute-start.7
  163.5 38.5 %collective-permute-start.15 = (bf16[2,256,768]{2,1,0:T(8,128)(2,1)}, bf16[2,256,768]{2,1,0:T(8,128)(2,1)S(1)}, u32[]{:S(2)}, u32[]{:S(2)}) collective-permute-start(bf16[2,256,768]{2,1,0:T(8,128)(2,1)} %get-tuple-element.73), channel_id=1, source_target_pairs={{0,2},{1,3},{2,0},{3,1},{4,6},{5,7},{6,4},{7,5},{8,10},{9,11},{10,... | collective-permute-start | bytes 2359304 | tf_op jit(solution)/shard_map/ppermute | solution.py:39
  166.0 1.2 copy-start.15
  166.0 35.5 %collective-permute-start.16 = (bf16[2,256,768]{2,1,0:T(8,128)(2,1)}, bf16[2,256,768]{2,1,0:T(8,128)(2,1)}, u32[]{:S(2)}, u32[]{:S(2)}) collective-permute-start(bf16[2,256,768]{2,1,0:T(8,128)(2,1)} %get-tuple-element.95), channel_id=1, source_target_pairs={{0,3},{1,2},{2,1},{3,0},{4,7},{5,6},{6,5},{7,4},{8,11},{9,10},{10,... | collective-permute-start | bytes 2359304 | tf_op jit(solution)/shard_map/ppermute | solution.py:39
  167.2 35.1 %collective-permute-start.14 = (bf16[3,256,768]{2,1,0:T(8,128)(2,1)}, bf16[3,256,768]{2,1,0:T(8,128)(2,1)S(1)}, u32[]{:S(2)}, u32[]{:S(2)}) collective-permute-start(bf16[3,256,768]{2,1,0:T(8,128)(2,1)} %get-tuple-element.94), channel_id=1, source_target_pairs={{0,1},{1,0},{2,3},{3,2},{4,5},{5,4},{6,7},{7,6},{8,9},{9,8},{10,11... | collective-permute-start | bytes 3538952 | tf_op jit(solution)/shard_map/ppermute | solution.py:39
  192.5 14.7 %collective-permute-start.17 = (bf16[384,768]{1,0:T(8,128)(2,1)}, bf16[384,768]{1,0:T(8,128)(2,1)S(1)}, u32[]{:S(2)}, u32[]{:S(2)}) collective-permute-start(bf16[384,768]{1,0:T(8,128)(2,1)} %get-tuple-element.97), channel_id=1, source_target_pairs={{0,32},{4,36},{8,40},{12,44},{16,48},{20,52},{24,56},{28,60},{32,0... | collective-permute-start | bytes 1769480 | tf_op jit(solution)/shard_map/ppermute | solution.py:446
  192.5 27.7 %collective-permute-start.18 = (bf16[384,768]{1,0:T(8,128)(2,1)}, bf16[384,768]{1,0:T(8,128)(2,1)S(1)}, u32[]{:S(2)}, u32[]{:S(2)}) collective-permute-start(bf16[384,768]{1,0:T(8,128)(2,1)} %get-tuple-element.98), channel_id=1, source_target_pairs={{0,64},{4,68},{8,72},{12,76},{16,80},{20,84},{24,88},{28,92},{32,9... | collective-permute-start | bytes 1769480 | tf_op jit(solution)/shard_map/ppermute | solution.py:446
  201.5 29.3 %collective-permute-start.19 = (bf16[384,768]{1,0:T(8,128)(2,1)}, bf16[384,768]{1,0:T(8,128)(2,1)S(1)}, u32[]{:S(2)}, u32[]{:S(2)}) collective-permute-start(bf16[384,768]{1,0:T(8,128)(2,1)} %get-tuple-element.99), channel_id=1, source_target_pairs={{0,96},{4,100},{8,104},{12,108},{16,112},{20,116},{24,120},{28,124... | collective-permute-start | bytes 1769480 | tf_op jit(solution)/shard_map/ppermute | solution.py:446
  202.0 0.9 copy-start.10
  202.0 29.7 %collective-permute-start.20 = (bf16[4,96,768]{2,1,0:T(8,128)(2,1)}, bf16[4,96,768]{2,1,0:T(8,128)(2,1)S(1)}, u32[]{:S(2)}, u32[]{:S(2)}) collective-permute-start(bf16[4,96,768]{2,1,0:T(8,128)(2,1)} %get-tuple-element.101), channel_id=1, source_target_pairs={{0,8},{4,12},{8,0},{12,4},{16,24},{20,28},{24,16},{28,20},{32,40},... | collective-permute-start | bytes 1769480 | tf_op jit(solution)/shard_map/ppermute | solution.py:450
  202.9 42.0 %copy-start.8 = (bf16[3,256,768]{2,1,0:T(8,128)(2,1)}, bf16[3,256,768]{2,1,0:T(8,128)(2,1)S(1)}, u32[]{:S(2)}) copy-start(bf16[3,256,768]{2,1,0:T(8,128)(2,1)S(1)} %collective-permute-done.14.p1) | copy-start | bytes 3538948
  202.9 53.3 %collective-permute-start.35 = (bf16[2,256,768]{2,1,0:T(8,128)(2,1)}, bf16[2,256,768]{2,1,0:T(8,128)(2,1)S(1)}, u32[]{:S(2)}, u32[]{:S(2)}) collective-permute-start(bf16[2,256,768]{2,1,0:T(8,128)(2,1)} %get-tuple-element.119), channel_id=1, source_target_pairs={{0,3},{1,2},{2,1},{3,0},{4,7},{5,6},{6,5},{7,4},{8,11},{9,10},{10,... | collective-permute-start | bytes 2359304 | tf_op jit(solution)/shard_map/ppermute | solution.py:39
  207.2 24.5 %copy-start.11 = (bf16[384,768]{1,0:T(8,128)(2,1)}, bf16[384,768]{1,0:T(8,128)(2,1)S(1)}, u32[]{:S(2)}) copy-start(bf16[384,768]{1,0:T(8,128)(2,1)S(1)} %collective-permute-done.17.refs_1_) | copy-start | bytes 1769476
  207.2 43.4 %collective-permute-start.21 = (bf16[4,96,768]{2,1,0:T(8,128)(2,1)}, bf16[4,96,768]{2,1,0:T(8,128)(2,1)}, u32[]{:S(2)}, u32[]{:S(2)}) collective-permute-start(bf16[4,96,768]{2,1,0:T(8,128)(2,1)} %get-tuple-element.102), channel_id=1, source_target_pairs={{0,16},{4,20},{8,24},{12,28},{16,0},{20,4},{24,8},{28,12},{32,48},... | collective-permute-start | bytes 1769480 | tf_op jit(solution)/shard_map/ppermute | solution.py:450
  220.3 11.4 %copy-start.12 = (bf16[384,768]{1,0:T(8,128)(2,1)}, bf16[384,768]{1,0:T(8,128)(2,1)S(1)}, u32[]{:S(2)}) copy-start(bf16[384,768]{1,0:T(8,128)(2,1)S(1)} %collective-permute-done.18.refs_2_) | copy-start | bytes 1769476
  220.3 30.4 %collective-permute-start.22 = (bf16[4,96,768]{2,1,0:T(8,128)(2,1)}, bf16[4,96,768]{2,1,0:T(8,128)(2,1)}, u32[]{:S(2)}, u32[]{:S(2)}) collective-permute-start(bf16[4,96,768]{2,1,0:T(8,128)(2,1)} %get-tuple-element.103), channel_id=1, source_target_pairs={{0,24},{4,28},{8,16},{12,20},{16,8},{20,12},{24,0},{28,4},{32,56},... | collective-permute-start | bytes 1769480 | tf_op jit(solution)/shard_map/ppermute | solution.py:450
  230.8 0.9 copy-start.13
  230.8 46.9 %collective-permute-start.34 = (bf16[2,256,768]{2,1,0:T(8,128)(2,1)}, bf16[2,256,768]{2,1,0:T(8,128)(2,1)}, u32[]{:S(2)}, u32[]{:S(2)}) collective-permute-start(bf16[2,256,768]{2,1,0:T(8,128)(2,1)} %get-tuple-element.84), channel_id=1, source_target_pairs={{0,2},{1,3},{2,0},{3,1},{4,6},{5,7},{6,4},{7,5},{8,10},{9,11},{10,... | collective-permute-start | bytes 2359304 | tf_op jit(solution)/shard_map/ppermute | solution.py:39
  231.7 0.8 copy-start.14
  232.6 58.1 %collective-permute-start.33 = (bf16[3,256,768]{2,1,0:T(8,128)(2,1)}, bf16[3,256,768]{2,1,0:T(8,128)(2,1)S(1)}, u32[]{:S(2)}, u32[]{:S(2)}) collective-permute-start(bf16[3,256,768]{2,1,0:T(8,128)(2,1)} %get-tuple-element.118), channel_id=1, source_target_pairs={{0,1},{1,0},{2,3},{3,2},{4,5},{5,4},{6,7},{7,6},{8,9},{9,8},{10,11... | collective-permute-start | bytes 3538952 | tf_op jit(solution)/shard_map/ppermute | solution.py:39
  250.6 16.6 %copy-start.22 = (f32[2,3072]{1,0:T(2,128)S(1)}, f32[2,3072]{1,0:T(2,128)}, u32[]{:S(2)}) copy-start(f32[2,3072]{1,0:T(2,128)} %get-tuple-element.91) | copy-start | bytes 73732
  254.7 5.7 %collective-permute-start.23 = (bf16[96,768]{1,0:T(8,128)(2,1)}, bf16[96,768]{1,0:T(8,128)(2,1)S(1)}, u32[]{:S(2)}, u32[]{:S(2)}) collective-permute-start(bf16[96,768]{1,0:T(8,128)(2,1)} %get-tuple-element.105), channel_id=1, source_target_pairs={{0,8},{4,12},{8,0},{12,4},{16,24},{20,28},{24,16},{28,20},{32,40},... | collective-permute-start | bytes 442376 | tf_op jit(solution)/shard_map/ppermute | solution.py:450
  255.1 8.4 %collective-permute-start.24 = (bf16[96,768]{1,0:T(8,128)(2,1)}, bf16[96,768]{1,0:T(8,128)(2,1)S(1)}, u32[]{:S(2)}, u32[]{:S(2)}) collective-permute-start(bf16[96,768]{1,0:T(8,128)(2,1)} %get-tuple-element.106), channel_id=1, source_target_pairs={{0,16},{4,20},{8,24},{12,28},{16,0},{20,4},{24,8},{28,12},{32,48},... | collective-permute-start | bytes 442376 | tf_op jit(solution)/shard_map/ppermute | solution.py:450
  256.2 34.5 %copy-start.9 = (bf16[2,256,768]{2,1,0:T(8,128)(2,1)}, bf16[2,256,768]{2,1,0:T(8,128)(2,1)S(1)}, u32[]{:S(2)}) copy-start(bf16[2,256,768]{2,1,0:T(8,128)(2,1)S(1)} %collective-permute-done.35.p3) | copy-start | bytes 2359300
  256.2 9.9 %collective-permute-start.25 = (bf16[96,768]{1,0:T(8,128)(2,1)}, bf16[96,768]{1,0:T(8,128)(2,1)S(1)}, u32[]{:S(2)}, u32[]{:S(2)}) collective-permute-start(bf16[96,768]{1,0:T(8,128)(2,1)} %get-tuple-element.107), channel_id=1, source_target_pairs={{0,24},{4,28},{8,16},{12,20},{16,8},{20,12},{24,0},{28,4},{32,56},... | collective-permute-start | bytes 442376 | tf_op jit(solution)/shard_map/ppermute | solution.py:450
  260.4 14.3 %copy-start.16 = (bf16[96,768]{1,0:T(8,128)(2,1)}, bf16[96,768]{1,0:T(8,128)(2,1)S(1)}, u32[]{:S(2)}) copy-start(bf16[96,768]{1,0:T(8,128)(2,1)S(1)} %collective-permute-done.23.refs_1_) | copy-start | bytes 442372
  260.4 6.8 %collective-permute-start.26 = (bf16[96,768]{1,0:T(8,128)(2,1)}, bf16[96,768]{1,0:T(8,128)(2,1)S(1)}, u32[]{:S(2)}, u32[]{:S(2)}) collective-permute-start(bf16[96,768]{1,0:T(8,128)(2,1)} %get-tuple-element.109), channel_id=1, source_target_pairs={{0,32},{4,36},{8,40},{12,44},{16,48},{20,52},{24,56},{28,60},{32,0... | collective-permute-start | bytes 442376 | tf_op jit(solution)/shard_map/ppermute | solution.py:446
  263.6 11.1 %copy-start.17 = (bf16[96,768]{1,0:T(8,128)(2,1)}, bf16[96,768]{1,0:T(8,128)(2,1)S(1)}, u32[]{:S(2)}) copy-start(bf16[96,768]{1,0:T(8,128)(2,1)S(1)} %collective-permute-done.24.refs_2_) | copy-start | bytes 442372
  263.6 7.0 %collective-permute-start.27 = (bf16[96,768]{1,0:T(8,128)(2,1)}, bf16[96,768]{1,0:T(8,128)(2,1)S(1)}, u32[]{:S(2)}, u32[]{:S(2)}) collective-permute-start(bf16[96,768]{1,0:T(8,128)(2,1)} %get-tuple-element.110), channel_id=1, source_target_pairs={{0,64},{4,68},{8,72},{12,76},{16,80},{20,84},{24,88},{28,92},{32,9... | collective-permute-start | bytes 442376 | tf_op jit(solution)/shard_map/ppermute | solution.py:446
  266.1 8.6 %copy-start.18 = (bf16[96,768]{1,0:T(8,128)(2,1)}, bf16[96,768]{1,0:T(8,128)(2,1)S(1)}, u32[]{:S(2)}) copy-start(bf16[96,768]{1,0:T(8,128)(2,1)S(1)} %collective-permute-done.25.refs_3_) | copy-start | bytes 442372
  266.1 7.7 %collective-permute-start.28 = (bf16[96,768]{1,0:T(8,128)(2,1)}, bf16[96,768]{1,0:T(8,128)(2,1)S(1)}, u32[]{:S(2)}, u32[]{:S(2)}) collective-permute-start(bf16[96,768]{1,0:T(8,128)(2,1)} %get-tuple-element.111), channel_id=1, source_target_pairs={{0,96},{4,100},{8,104},{12,108},{16,112},{20,116},{24,120},{28,124... | collective-permute-start | bytes 442376 | tf_op jit(solution)/shard_map/ppermute | solution.py:446
  267.3 7.4 %copy-start.19 = (bf16[96,768]{1,0:T(8,128)(2,1)}, bf16[96,768]{1,0:T(8,128)(2,1)S(1)}, u32[]{:S(2)}) copy-start(bf16[96,768]{1,0:T(8,128)(2,1)S(1)} %collective-permute-done.26.refs_5_) | copy-start | bytes 442372
  267.3 10.6 %collective-permute-start.13 = (f32[2,3072]{1,0:T(2,128)S(1)}, f32[2,3072]{1,0:T(2,128)S(1)}, u32[]{:S(2)}, u32[]{:S(2)}) collective-permute-start(f32[2,3072]{1,0:T(2,128)S(1)} %copy-done.22), channel_id=1, source_target_pairs={{0,3},{1,2},{2,1},{3,0},{4,7},{5,6},{6,5},{7,4},{8,11},{9,10},{10,... | collective-permute-start | bytes 73736 | tf_op jit(solution)/shard_map/ppermute | solution.py:39
  270.5 4.2 %copy-start.20 = (bf16[96,768]{1,0:T(8,128)(2,1)}, bf16[96,768]{1,0:T(8,128)(2,1)S(1)}, u32[]{:S(2)}) copy-start(bf16[96,768]{1,0:T(8,128)(2,1)S(1)} %collective-permute-done.27.refs_6_) | copy-start | bytes 442372
  270.5 11.3 %collective-permute-start.12 = (f32[2,3072]{1,0:T(2,128)S(1)}, f32[2,3072]{1,0:T(2,128)S(1)}, u32[]{:S(2)}, u32[]{:S(2)}) collective-permute-start(f32[2,3072]{1,0:T(2,128)S(1)} %copy-done.22), channel_id=1, source_target_pairs={{0,2},{1,3},{2,0},{3,1},{4,6},{5,7},{6,4},{7,5},{8,10},{9,11},{10,... | collective-permute-start | bytes 73736 | tf_op jit(solution)/shard_map/ppermute | solution.py:39
  273.8 0.9 copy-start.21
  273.8 12.3 %collective-permute-start.11 = (f32[2,3072]{1,0:T(2,128)S(1)}, f32[2,3072]{1,0:T(2,128)S(1)}, u32[]{:S(2)}, u32[]{:S(2)}) collective-permute-start(f32[2,3072]{1,0:T(2,128)S(1)} %copy-done.22), channel_id=1, source_target_pairs={{0,1},{1,0},{2,3},{3,2},{4,5},{5,4},{6,7},{7,6},{8,9},{9,8},{10,11... | collective-permute-start | bytes 73736 | tf_op jit(solution)/shard_map/ppermute | solution.py:39
  277.7 19.7 %collective-permute-start.30 = (bf16[24,1536]{1,0:T(8,128)(2,1)}, bf16[24,1536]{1,0:T(8,128)(2,1)S(1)}, u32[]{:S(2)}, u32[]{:S(2)}) collective-permute-start(bf16[24,1536]{1,0:T(8,128)(2,1)} %get-tuple-element.113), channel_id=1, source_target_pairs={{0,1},{1,65},{2,0},{3,64},{4,3},{5,67},{6,2},{7,66},{8,5},{9,69},{... | collective-permute-start | bytes 221192 | tf_op jit(solution)/shard_map/ppermute | solution.py:536
  277.9 19.5 %collective-permute-start.31 = (bf16[24,1536]{1,0:T(8,128)(2,1)}, bf16[24,1536]{1,0:T(8,128)(2,1)S(1)}, u32[]{:S(2)}, u32[]{:S(2)}) collective-permute-start(bf16[24,1536]{1,0:T(8,128)(2,1)} %get-tuple-element.114), channel_id=1, source_target_pairs={{0,2},{1,66},{2,3},{3,67},{4,0},{5,64},{6,1},{7,65},{8,6},{9,70},{... | collective-permute-start | bytes 221192 | tf_op jit(solution)/shard_map/ppermute | solution.py:536
  281.8 15.6 %collective-permute-start.32 = (bf16[24,1536]{1,0:T(8,128)(2,1)}, bf16[24,1536]{1,0:T(8,128)(2,1)S(1)}, u32[]{:S(2)}, u32[]{:S(2)}) collective-permute-start(bf16[24,1536]{1,0:T(8,128)(2,1)} %get-tuple-element.115), channel_id=1, source_target_pairs={{0,3},{1,67},{2,2},{3,66},{4,1},{5,65},{6,0},{7,64},{8,7},{9,71},{... | collective-permute-start | bytes 221192 | tf_op jit(solution)/shard_map/ppermute | solution.py:536
  286.1 11.3 %collective-permute-start.29 = (bf16[24,1536]{1,0:T(8,128)(2,1)}, bf16[24,1536]{1,0:T(8,128)(2,1)S(1)}, u32[]{:S(2)}, u32[]{:S(2)}) collective-permute-start(bf16[24,1536]{1,0:T(8,128)(2,1)} %get-tuple-element.112), channel_id=1, source_target_pairs={{0,0},{1,64},{2,1},{3,65},{4,2},{5,66},{6,3},{7,67},{8,4},{9,68},{... | collective-permute-start | bytes 221192 | tf_op jit(solution)/shard_map/ppermute | solution.py:536
  290.7 1.0 copy-start.7

commit v3 on v2

--- a/solution.py
+++ b/solution.py
@@ -14,6 +14,7 @@
 HALF = HEADS_HALF * HD
 WIDTH = 2 * HALF
 TOGETHER = 2
+TOGETHER_BACK = 2
 SHARE = 96
 D = 3072
 NEGATIVE = -1e30
@@ -115,38 +116,42 @@
 def bwd_kernel(
     slot, sp, q0, k0, v0, q1, k1, v1, k2, v2, k3, v3, att, lse, do0, do1, own, r1, r2, r3
 ):
-    keys = jnp.concatenate([k0[0], k1[0], k2[0], k3[0]], axis=0)
-    values = jnp.concatenate([v0[0], v1[0], v2[0], v3[0]], axis=0)
     bias = key_bias(sp, slot, 0)
-    grad_k = None
-    grad_v = None
-    for block, (q, do) in enumerate(((q0, do0), (q1, do1))):
-        d_rows = do[0]
-        scores = mm(keys, q[0], NT) * (SCALE * LOG2E) + bias
-        level = lse[0, 0:1, block * ROWS : (block + 1) * ROWS]
-        probs = jnp.exp2(scores - level)
-        product = d_rows.astype(jnp.float32) * att[block].astype(jnp.float32)
-        dots = jnp.sum(product.T, axis=0, keepdims=True)
-        d_probs = mm(values, d_rows, NT)
-        d_scores = (probs * (d_probs - dots)).astype(jnp.bfloat16)
-        v_part = mm(probs.astype(jnp.bfloat16), d_rows, NN)
-        k_part = mm(d_scores, q[0], NN)
-        grad_k = k_part if block == 0 else grad_k + k_part
-        grad_v = v_part if block == 0 else grad_v + v_part
-        grad_q = (mm(keys, d_scores, TN) * SCALE).T
-        if block == 0:
-            own[0] = grad_q
-        else:
-            r1[0] = grad_q.astype(jnp.bfloat16)
-    grad_k = grad_k * SCALE
-    own[1] = grad_k[:ROWS]
-    own[2] = grad_v[:ROWS]
-    r1[1] = grad_k[ROWS : 2 * ROWS].astype(jnp.bfloat16)
-    r1[2] = grad_v[ROWS : 2 * ROWS].astype(jnp.bfloat16)
-    r2[0] = grad_k[2 * ROWS : 3 * ROWS].astype(jnp.bfloat16)
-    r2[1] = grad_v[2 * ROWS : 3 * ROWS].astype(jnp.bfloat16)
-    r3[0] = grad_k[3 * ROWS :].astype(jnp.bfloat16)
-    r3[1] = grad_v[3 * ROWS :].astype(jnp.bfloat16)
+    low = jnp.bfloat16
+    for head in range(TOGETHER_BACK):
+        cols = slice(head * HD, (head + 1) * HD)
+        keys = jnp.concatenate([k[0, :, cols] for k in (k0, k1, k2, k3)], axis=0)
+        values = jnp.concatenate([v[0, :, cols] for v in (v0, v1, v2, v3)], axis=0)
+        grad_k = None
+        grad_v = None
+        for block, (q, do) in enumerate(((q0, do0), (q1, do1))):
+            q_rows = q[0, :, cols]
+            d_rows = do[0, :, cols]
+            scores = mm(keys, q_rows, NT) * (SCALE * LOG2E) + bias
+            level = lse[head, 0:1, block * ROWS : (block + 1) * ROWS]
+            probs = jnp.exp2(scores - level)
+            product = d_rows.astype(jnp.float32) * att[block, :, cols].astype(jnp.float32)
+            dots = jnp.sum(product.T, axis=0, keepdims=True)
+            d_probs = mm(values, d_rows, NT)
+            d_scores = (probs * (d_probs - dots)).astype(low)
+            v_part = mm(probs.astype(low), d_rows, NN)
+            k_part = mm(d_scores, q_rows, NN)
+            grad_k = k_part if block == 0 else grad_k + k_part
+            grad_v = v_part if block == 0 else grad_v + v_part
+            grad_q = (mm(keys, d_scores, TN) * SCALE).T
+            if block == 0:
+                own[0, :, cols] = grad_q
+            else:
+                r1[0, :, cols] = grad_q.astype(low)
+        grad_k = grad_k * SCALE
+        own[1, :, cols] = grad_k[:ROWS]
+        own[2, :, cols] = grad_v[:ROWS]
+        r1[1, :, cols] = grad_k[ROWS : 2 * ROWS].astype(low)
+        r1[2, :, cols] = grad_v[ROWS : 2 * ROWS].astype(low)
+        r2[0, :, cols] = grad_k[2 * ROWS : 3 * ROWS].astype(low)
+        r2[1, :, cols] = grad_v[2 * ROWS : 3 * ROWS].astype(low)
+        r3[0, :, cols] = grad_k[3 * ROWS :].astype(low)
+        r3[1, :, cols] = grad_v[3 * ROWS :].astype(low)
 
 
 def head_block(lead, index=0, heads=1):
@@ -167,7 +172,6 @@
     return (qkv, qkv, qkv, x1, x1, x1, x2, x2, x3, x3)
 
 
-LSE_SPEC = pl.BlockSpec((1, 8, 2 * ROWS), lambda h, sp: (h, 0, 0))
 PAIRS = HEADS_HALF * 512 * 1024
 
 
@@ -192,18 +196,30 @@
 
 
 def attend_back(sp, slot, qkv, received, att, lse, d_own, d_peer):
-    d_own_spec = pl.BlockSpec((1, ROWS, HD), lambda h, sp: (0, 0, HEADS_HALF * sp[0, 0] + h))
+    heads = TOGETHER_BACK
+    d_own_spec = pl.BlockSpec(
+        (1, ROWS, heads * HD), lambda h, sp: (0, 0, HEADS_HALF // heads * sp[0, 0] + h)
+    )
 
     def shape(count, kind):
         return jax.ShapeDtypeStruct((count, ROWS, HALF), kind)
 
+    def piece(count):
+        return head_block(count, 0, heads)
+
     return pl.pallas_call(
         functools.partial(bwd_kernel, slot),
         grid_spec=pltpu.PrefetchScalarGridSpec(
             num_scalar_prefetch=1,
-            grid=(HEADS_HALF,),
-            in_specs=section_specs(slot) + [head_block(2), LSE_SPEC, d_own_spec, head_block(1)],
-            out_specs=[head_block(3), head_block(3), head_block(2), head_block(2)],
+            grid=(HEADS_HALF // heads,),
+            in_specs=section_specs(slot, heads)
+            + [
+                piece(2),
+                pl.BlockSpec((heads, 8, 2 * ROWS), lambda h, sp: (h, 0, 0)),
+                d_own_spec,
+                piece(1),
+            ],
+            out_specs=[piece(3), piece(3), piece(2), piece(2)],
         ),
         out_shape=[
             shape(3, jnp.float32),
@@ -273,82 +289,62 @@
     )(order, rows)
 
 
-def rows_kernel(sp, cotangent, gate, weight, send, keep, away, near, near_send, total):
+def rows_kernel(slot, sp, cotangent, gate, weight, send, keep, rows, total):
     step = pl.program_id(0)
-    parts = [
-        (cotangent[slot].astype(jnp.float32) * gate[slot : slot + 1]).astype(jnp.bfloat16)
-        for slot in range(2)
-    ]
-
-    @pl.when(step < 3)
+    scaled = (cotangent[0].astype(jnp.float32) * gate[slot : slot + 1]).astype(jnp.bfloat16)
+
+    @pl.when(step < 2)
     def _():
-        send[0] = parts[0]
-        send[1] = parts[1]
-
-    @pl.when(step >= 3)
+        send[...] = scaled
+
+    @pl.when(step >= 2)
     def _():
-        keep[0] = parts[0]
-        keep[1] = parts[1]
-
-    product = mm(jnp.concatenate(parts, axis=0), weight[...], NT)
+        keep[...] = scaled
+
+    product = mm(scaled, weight[...], NT)
 
     @pl.when(step == 0)
     def _():
         total[...] = product
 
-    @pl.when((step > 0) & (step < 5))
+    @pl.when((step > 0) & (step < 3))
     def _():
         total[...] += product
 
-    @pl.when(step == 5)
+    @pl.when(step == 3)
     def _():
-        rows = (total[...] + product).astype(jnp.bfloat16)
-        near[...] = rows[:ROWS]
-        away[...] = rows[ROWS:]
-        near_send[0] = jnp.where(sp[0, 0] == 0, rows[:ROWS, HALF:], rows[:ROWS, :HALF])
-
-
-def scaled_rows(sp, cotangent, gate, out_weight):
-    cols = D // 6
+        rows[...] = (total[...] + product).astype(jnp.bfloat16)
+
+
+def scaled_rows(sp, slot, cotangent, gate, out_weight):
+    cols = D // 4
 
     def place(step, sp):
         core = sp[0, 0]
-        return jnp.where(step < 3, 3 * (1 - core), 3 * core - 3) + step
-
-    def whole(*shape):
-        return pl.BlockSpec(shape, lambda k, sp: (0,) * len(shape))
-
-    def shape(*dims):
-        return jax.ShapeDtypeStruct(dims, jnp.bfloat16)
-
-    return pl.pallas_call(
-        rows_kernel,
-        grid_spec=pltpu.PrefetchScalarGridSpec(
-            num_scalar_prefetch=1,
-            grid=(6,),
+        return jnp.where(step < 2, 2 * (1 - core), 2 * core - 2) + step
+
+    def shape(cols):
+        return jax.ShapeDtypeStruct((ROWS, cols), jnp.bfloat16)
+
+    return pl.pallas_call(
+        functools.partial(rows_kernel, slot),
+        grid_spec=pltpu.PrefetchScalarGridSpec(
+            num_scalar_prefetch=1,
+            grid=(4,),
             in_specs=[
-                pl.BlockSpec((2, ROWS, cols), lambda k, sp: (0, 0, place(k, sp))),
+                pl.BlockSpec((1, ROWS, cols), lambda k, sp: (slot, 0, place(k, sp))),
                 pl.BlockSpec((2, cols), lambda k, sp: (0, place(k, sp))),
                 pl.BlockSpec((WIDTH, cols), lambda k, sp: (0, place(k, sp))),
             ],
             out_specs=[
-                pl.BlockSpec((2, ROWS, cols), lambda k, sp: (0, 0, jnp.minimum(k, 2))),
-                pl.BlockSpec((2, ROWS, cols), lambda k, sp: (0, 0, jnp.maximum(k - 3, 0))),
-                whole(ROWS, WIDTH),
-                whole(ROWS, WIDTH),
-                whole(1, ROWS, HALF),
+                pl.BlockSpec((ROWS, cols), lambda k, sp: (0, jnp.minimum(k, 1))),
+                pl.BlockSpec((ROWS, cols), lambda k, sp: (0, jnp.maximum(k - 2, 0))),
+                pl.BlockSpec((ROWS, WIDTH), lambda k, sp: (0, 0)),
             ],
-            scratch_shapes=[pltpu.VMEM((2 * ROWS, WIDTH), jnp.float32)],
-        ),
-        out_shape=[
-            shape(2, ROWS, D // 2),
-            shape(2, ROWS, D // 2),
-            shape(ROWS, WIDTH),
-            shape(ROWS, WIDTH),
-            shape(1, ROWS, HALF),
-        ],
-        cost_estimate=cost(2 * 512 * WIDTH * D, 1.7e7),
-        name="scaled_rows",
+            scratch_shapes=[pltpu.VMEM((ROWS, WIDTH), jnp.float32)],
+        ),
+        out_shape=[shape(D // 2), shape(D // 2), shape(WIDTH)],
+        cost_estimate=cost(2 * 256 * WIDTH * D, 1.3e7),
     )(sp, cotangent, gate, out_weight)
 
 
@@ -365,7 +361,7 @@
 
 
 def project(sp, mine, other, out_weight, gate, cotangent):
-    cols = 512
+    cols = 1024
 
     def rows(index):
         return pl.BlockSpec((1, ROWS, HALF), lambda d, sp: (index, 0, 0))
@@ -398,12 +394,10 @@
     )(sp, mine[0], mine[1], other[0], other[1], out_weight, out_weight, gate, cotangent)
 
 
-def weigh_kernel(sp, scaled_own, scaled_peer, a0, a1, b0, b1, *rest):
+def weigh_kernel(sp, own0, peer0, own1, peer1, a0, a1, b0, b1, *rest):
     outs, product = rest[:8], rest[8]
     step = pl.program_id(0)
-    left = jnp.concatenate(
-        [scaled_own[0], scaled_peer[0], scaled_own[1], scaled_peer[1]], axis=0
-    )
+    left = jnp.concatenate([own0[...], peer0[...], own1[...], peer1[...]], axis=0)
     mine = jnp.concatenate([a0[0], a0[1], a1[0], a1[1]], axis=0)
     other = jnp.concatenate([b0[1], b0[0], b1[1], b1[0]], axis=0)
     first = sp[0, 0] == 0
@@ -421,16 +415,16 @@
         outs[4 + y_step][sp[0, 5] ^ step] = rows
 
 
-def weigh(sp, scaled, scaled_peer, mine, other):
+def weigh(sp, scaled, mine, other):
     rows = D // 8
     pair = pl.BlockSpec((2, ROWS, HALF), lambda d, sp: (0, 0, 0))
-    wide = pl.BlockSpec((2, ROWS, rows), lambda d, sp: (0, 0, sp[0, 5] ^ d))
+    wide = pl.BlockSpec((ROWS, rows), lambda d, sp: (0, sp[0, 5] ^ d))
     return pl.pallas_call(
         weigh_kernel,
         grid_spec=pltpu.PrefetchScalarGridSpec(
             num_scalar_prefetch=1,
             grid=(4,),
-            in_specs=[wide, wide, pair, pair, pair, pair],
+            in_specs=[wide] * 4 + [pair] * 4,
             out_specs=[pl.BlockSpec((rows, HALF), lambda d, sp: (0, 0))] * 4
             + [pl.BlockSpec((4, SHARE, HALF), lambda d, sp: (0, 0, 0))] * 4,
             scratch_shapes=[pltpu.VMEM((rows, HALF), jnp.float32)],
@@ -439,7 +433,7 @@
         + [jax.ShapeDtypeStruct((4, SHARE, HALF), jnp.bfloat16)] * 4,
         cost_estimate=cost(2 * 1024 * WIDTH * D // 2, 1.2e7),
         name="weigh",
-    )(sp, scaled, scaled_peer, mine[0], mine[1], other[0], other[1])
+    )(sp, *scaled, mine[0], mine[1], other[0], other[1])
 
 
 def along_x(x, step):
@@ -580,21 +574,20 @@
     d_own, d_peer = [None, None], [None, None]
     att, lse = [None, None], [None, None]
 
-    s1, s2, s3 = prep(sp, qkv, 1)
+    cp = core.astype(jnp.int32).reshape(1, 1)
+    send_1, keep_1, away = scaled_rows(cp, 1, cotangent, gate, out_weight)
+    d_spread = spread_out(away)
+    s1, s2, s3 = prep(after(cp, away), qkv, 1)
     received[1] = (swap(s1, 1), swap(s2, 2), swap(s3, 3))
-    scaled_send, scaled, away, near, near_send = scaled_rows(
-        after(sp, s2), cotangent, gate, out_weight
-    )
-    d_spread = spread_out(away)
-    s1, s2, s3 = prep(after(sp, away), qkv, 0)
-    near_keys = (swap(s1, 1), swap(s3, 3))
-    received[0] = (near_keys[0], swap(s2, 2), near_keys[1])
-    d_own[0], d_peer[0] = near[None], swap(near_send, 1)
-    scaled_peer = swap(scaled_send, 1)
-
-    d_picked = pick(d_spread, after(plan, s2))
+    send_0, keep_0, near = scaled_rows(after(cp, s2), 0, cotangent, gate, out_weight)
+    d_own[0], d_peer[0] = near[None], to_core(near)
+    scaled = (keep_0, swap(send_0, 1), keep_1, swap(send_1, 1))
+    d_picked = pick(d_spread, after(plan, near))
     landed = land(d_picked, (ROWS, WIDTH))
-    att[1], lse[1] = attend(after(sp, d_picked), 1, qkv, received[1])
+    s1, s2, s3 = prep(after(cp, d_picked), qkv, 0)
+    received[0] = (swap(s1, 1), swap(s2, 2), swap(s3, 3))
+    sp = after(sp, s2)
+    att[1], lse[1] = attend(sp, 1, qkv, received[1])
     d_own[1], d_peer[1] = landed[None], to_core(landed)
     att_spread = spread_out(after(att[1], landed).reshape(2 * ROWS, HALF))
 
@@ -614,7 +607,7 @@
     pieces_0 = [swap(rows, 1 + i) for i, rows in enumerate(sent_0)]
     balanced = [att[0], moved]
     att_other.append(swap(moved, 1))
-    *partial, = weigh(after(sp, sent_0[1]), scaled, scaled_peer, balanced, att_other)
+    *partial, = weigh(after(sp, sent_0[1]), scaled, balanced, att_other)
     by_x, by_y = partial[:4], partial[4:]
     for step in (2, 1, 3):
         by_x[step] = along_x(by_x[step], step)
@@ -627,9 +620,9 @@
     parts = list(sum_parts(after(sp, grads), by_x, by_y))
     low = parts[:1] + [along_y(parts[step], step) for step in (1, 2, 3)]
     high = parts[4:5] + [along_x(parts[4 + step], step) for step in (1, 2, 3)]
-    quarters = sum_weights(sp, low, high)
+    grads = join(after(sp, parts[0]), 0, own_0, *pieces_0, grads)
+    quarters = sum_weights(after(sp, grads), low, high)
     weight_grad = finish_weights(quarters)
-    grads = join(after(sp, quarters[0]), 0, own_0, *pieces_0, grads)
     return (mixed, gate_grad, weight_grad, grads)
 
 

time: 302 us -> 312 us (1.033)
  the two profiles are of different devices: /device:TPU:1 before, /device:TPU:18 now
where the time goes in v3:
time: 312 us; the launch traced here: 311 us
  Pallas kernels  112 us (36%)
  waiting for transfers between devices  111 us (36%)
  starting transfers between devices  78.2 us (25%)
  local copies, waits for them, and re-layouts  5.23 us (2%)
  other arithmetic  4.04 us (1%)
    ppermute x21, waiting for transfers between devices, swap(): return lax.ppermute(x, 'seq', [(i, i ^ step) for i in range(4)])  50.8 us
    ppermute x6, waiting for transfers between devices, along_x(): return lax.ppermute(x, 'dp', [(g, g ^ step << 3) for g in range(32)])  24.8 us
    pallas_call x2, Pallas kernels, attend_back(): pl.pallas_call(functools.partial(bwd_kernel, slot), grid_spec=pltpu.Prefe...  24.1 us
    pallas_call x2, Pallas kernels, attend(): pl.pallas_call(functools.partial(fwd_kernel, slot), grid_spec=pltpu.Prefe...  16.8 us
    pallas_call x2, Pallas kernels, scaled_rows(): pl.pallas_call(functools.partial(rows_kernel, slot), grid_spec=pltpu.Pref...  16.8 us
    all_to_all x2, starting transfers between devices, spread_out(): lax.all_to_all(portions, 'dp', split_axis=0, concat_axis=0, tiled=True)  16.4 us
    ppermute x21, starting transfers between devices, swap(): return lax.ppermute(x, 'seq', [(i, i ^ step) for i in range(4)])  16.1 us
    ppermute x4, starting transfers between devices, finish_weights(): lax.ppermute(quarter, ('dp', 'seq'), final_moves(step)).astype(jnp.float32)  15.7 us
  transfers between devices with their start and end apart: 41, of which 14 were waited for; matrix products, arithmetic and copies ran while one was open for 1% of the time, Pallas kernels for 32%

profile of v3, /device:TPU:18, one launch (start us, length us, event | category | flops | bytes accessed | tf_op | source)
XLA Modules:
  0.0 311.0 jit_solution(13193554054249414501)
XLA Ops:
  0.6 8.4 %shard_map.102 = (bf16[256,1536]{1,0:T(8,128)(2,1)}, bf16[256,1536]{1,0:T(8,128)(2,1)}, bf16[256,1536]{1,0:T(8,128)(2,1)}) custom-call(s32[1,1]{1,0:T(1,128)} %bitcast.6.sp, bf16[2,256,3072]{2,1,0:T(8,128)(2,1)} %cotangent.5, f32[2,3072]{1,0:T(2,128)} %gate.5, bf16[1536,3072]{1,0:T(8,128)(2,1)} %w_other.1), custom_call_target="tpu_custom_call" | custom-call | flops 2415919104 | bytes 13000000 | tf_op jit(solution)/shard_map/pallas_call | solution.py:329
  9.0 8.7 %all-to-all-start = ((bf16[32,8,1536]{2,1,0:T(8,128)(2,1)}), bf16[32,8,1536]{2,1,0:T(8,128)(2,1)S(1)}, u32[]{:S(2)}, u32[]{:S(2)}) async-start(bf16[32,8,1536]{2,1,0:T(8,128)(2,1)} %bitcast.26), calls=%async_computation | async-start | bytes 1572864 | tf_op jit(solution)/shard_map/all_to_all | solution.py:543
  17.8 3.0 shard_map.103
  20.7 8.4 %shard_map.104 = (bf16[256,1536]{1,0:T(8,128)(2,1)}, bf16[256,1536]{1,0:T(8,128)(2,1)}, bf16[256,1536]{1,0:T(8,128)(2,1)}) custom-call(s32[1,1]{1,0:T(1,128)} %bitcast.6.sp, bf16[2,256,3072]{2,1,0:T(8,128)(2,1)} %cotangent.5, f32[2,3072]{1,0:T(2,128)} %gate.5, bf16[1536,3072]{1,0:T(8,128)(2,1)} %w_other.1), custom_call_target="tpu_custom_call" | custom-call | flops 2415919104 | bytes 13000000 | tf_op jit(solution)/shard_map/pallas_call | solution.py:329
  29.5 0.9 copy-done.5
  30.4 2.9 pick.2
  33.3 8.0 %all-to-all-start.1 = ((bf16[32,8,1536]{2,1,0:T(8,128)(2,1)}), bf16[32,8,1536]{2,1,0:T(8,128)(2,1)}, u32[]{:S(2)}, u32[]{:S(2)}) async-start(bf16[32,8,1536]{2,1,0:T(8,128)(2,1)} %pick.2), calls=%async_computation.1 | async-start | bytes 1572864 | tf_op jit(solution)/shard_map/all_to_all | solution.py:547
  41.3 3.7 %collective-permute-start.1 = (bf16[2,256,768]{2,1,0:T(8,128)(2,1)}, bf16[2,256,768]{2,1,0:T(8,128)(2,1)}, u32[]{:S(2)}, u32[]{:S(2)}) collective-permute-start(bf16[2,256,768]{2,1,0:T(8,128)(2,1)} %get-tuple-element.67), channel_id=1, source_target_pairs={{0,2},{1,3},{2,0},{3,1},{4,6},{5,7},{6,4},{7,5},{8,10},{9,11},{10,... | collective-permute-start | bytes 2359304 | tf_op jit(solution)/shard_map/ppermute | solution.py:40
  45.4 2.9 shard_map.105
  48.7 3.0 collective-permute-start.6
  51.7 2.1 all-to-all-done.1
  53.9 1.2 fusion
  55.0 32.4 %collective-permute-done.2.k3.v3 = bf16[2,256,768]{2,1,0:T(8,128)(2,1)} collective-permute-done((bf16[2,256,768]{2,1,0:T(8,128)(2,1)}, bf16[2,256,768]{2,1,0:T(8,128)(2,1)}, u32[]{:S(2)}, u32[]{:S(2)}) %collective-permute-start.2) | collective-permute-done | bytes 786464 | tf_op jit(solution)/shard_map/ppermute | solution.py:40
  88.5 0.6 pad_add_fusion.sp
  89.1 1.0 copy-done.1
  90.1 8.4 %shard_map.106 = (bf16[2,256,768]{2,1,0:T(8,128)(2,1)}, f32[6,8,512]{2,1,0:T(8,128)}) custom-call(s32[2,6]{1,0:T(2,128)} %pad_add_fusion.sp, bf16[2,256,4608]{2,1,0:T(8,128)(2,1)} %v0.7, bf16[2,256,4608]{2,1,0:T(8,128)(2,1)} %v0.7, bf16[2,256,4608]{2,1,0:T(8,128)(2,1)} %v0.7, bf16[3,256,768]{2,1,0:T(8,128)(2,1)} %copy-done.1, ...), custom_call_target="tpu_custom_call" | custom-call | flops 1610612736 | bytes 5000000 | tf_op jit(solution)/shard_map/pallas_call | solution.py:179
  98.5 7.7 %all-to-all-start.2 = ((bf16[32,16,768]{2,1,0:T(8,128)(2,1)}), bf16[32,16,768]{2,1,0:T(8,128)(2,1)}, u32[]{:S(2)}, u32[]{:S(2)}) async-start(bf16[32,16,768]{2,1,0:T(8,128)(2,1)} %bitcast.21), calls=%async_computation.2 | async-start | bytes 1572864 | tf_op jit(solution)/shard_map/all_to_all | solution.py:543
  106.2 0.6 select_reduce_fusion.order
  106.9 12.0 %shard_map.107 = (f32[3,256,768]{2,1,0:T(8,128)}, bf16[3,256,768]{2,1,0:T(8,128)(2,1)}, bf16[2,256,768]{2,1,0:T(8,128)(2,1)}, bf16[2,256,768]{2,1,0:T(8,128)(2,1)}) custom-call(s32[2,6]{1,0:T(2,128)} %pad_add_fusion.sp, bf16[2,256,4608]{2,1,0:T(8,128)(2,1)} %v0.7, bf16[2,256,4608]{2,1,0:T(8,128)(2,1)} %v0.7, bf16[2,256,4608]{2,1,0:T(8,128)(2,1)} %v0.7, ...), custom_call_target="tpu_custom_call" | custom-call | flops 4026531840 | bytes 10000000 | tf_op jit(solution)/shard_map/pallas_call | solution.py:210
  118.9 10.9 %collective-permute-done.5.k2.v2 = bf16[2,256,768]{2,1,0:T(8,128)(2,1)} collective-permute-done((bf16[2,256,768]{2,1,0:T(8,128)(2,1)}, bf16[2,256,768]{2,1,0:T(8,128)(2,1)}, u32[]{:S(2)}, u32[]{:S(2)}) %collective-permute-start.5) | collective-permute-done | bytes 786464 | tf_op jit(solution)/shard_map/ppermute | solution.py:40
  129.8 1.0 copy-done
  130.8 8.4 %shard_map.108 = (bf16[2,256,768]{2,1,0:T(8,128)(2,1)}, f32[6,8,512]{2,1,0:T(8,128)}) custom-call(s32[2,6]{1,0:T(2,128)} %pad_add_fusion.sp, bf16[2,256,4608]{2,1,0:T(8,128)(2,1)} %v0.7, bf16[2,256,4608]{2,1,0:T(8,128)(2,1)} %v0.7, bf16[2,256,4608]{2,1,0:T(8,128)(2,1)} %v0.7, bf16[3,256,768]{2,1,0:T(8,128)(2,1)} %copy-done, bf16[3,256,768]{2,1,0:T(8,128)(2,1)} %copy-done, ...), custom_call_target="tpu_custom_call" | custom-call | flops 1610612736 | bytes 5000000 | tf_op jit(solution)/shard_map/pallas_call | solution.py:179
  139.3 3.0 pick.3
  142.3 7.5 %all-to-all-start.3 = ((bf16[32,16,768]{2,1,0:T(8,128)(2,1)}), bf16[32,16,768]{2,1,0:T(8,128)(2,1)S(1)}, u32[]{:S(2)}, u32[]{:S(2)}) async-start(bf16[32,16,768]{2,1,0:T(8,128)(2,1)} %pick.3), calls=%async_computation.3 | async-start | bytes 1572864 | tf_op jit(solution)/shard_map/all_to_all | solution.py:547
  151.0 10.7 %all-to-all-done.3 = bf16[32,16,768]{2,1,0:T(8,128)(2,1)S(1)} async-done(((bf16[32,16,768]{2,1,0:T(8,128)(2,1)}), bf16[32,16,768]{2,1,0:T(8,128)(2,1)S(1)}, u32[]{:S(2)}, u32[]{:S(2)}) %all-to-all-start.3) | async-done | bytes 786464 | tf_op jit(solution)/shard_map/all_to_all | solution.py:547
  162.5 1.1 collective-permute-start.16
  163.6 2.2 collective-permute-start.17
  165.8 12.1 %shard_map.109 = (f32[3,256,768]{2,1,0:T(8,128)}, bf16[3,256,768]{2,1,0:T(8,128)(2,1)}, bf16[2,256,768]{2,1,0:T(8,128)(2,1)}, bf16[2,256,768]{2,1,0:T(8,128)(2,1)}) custom-call(s32[2,6]{1,0:T(2,128)} %pad_add_fusion.sp, bf16[2,256,4608]{2,1,0:T(8,128)(2,1)} %v0.7, bf16[2,256,4608]{2,1,0:T(8,128)(2,1)} %v0.7, bf16[2,256,4608]{2,1,0:T(8,128)(2,1)} %v0.7, ...), custom_call_target="tpu_custom_call" | custom-call | flops 4026531840 | bytes 10000000 | tf_op jit(solution)/shard_map/pallas_call | solution.py:210
  177.9 12.9 %weigh.1 = (bf16[384,768]{1,0:T(8,128)(2,1)}, bf16[384,768]{1,0:T(8,128)(2,1)}, bf16[384,768]{1,0:T(8,128)(2,1)}, bf16[384,768]{1,0:T(8,128)(2,1)}, bf16[4,96,76...) custom-call(s32[2,6]{1,0:T(2,128)} %pad_add_fusion.sp, ...), custom_call_target="tpu_custom_call" | custom-call | flops 4831838208 | bytes 12000000 | tf_op jit(solution)/shard_map/weigh/pallas_call | solution.py:422
  190.8 1.2 collective-permute-start.18
  192.0 1.1 collective-permute-start.19
  193.1 7.4 %collective-permute-done.17.p3 = bf16[2,256,768]{2,1,0:T(8,128)(2,1)} collective-permute-done((bf16[2,256,768]{2,1,0:T(8,128)(2,1)}, bf16[2,256,768]{2,1,0:T(8,128)(2,1)}, u32[]{:S(2)}, u32[]{:S(2)}) %collective-permute-start.17) | collective-permute-done | bytes 786464 | tf_op jit(solution)/shard_map/ppermute | solution.py:40
  200.6 0.8 collective-permute-start.20
  201.4 0.8 collective-permute-start.21
  202.3 4.9 %collective-permute-done.18.refs_1_ = bf16[384,768]{1,0:T(8,128)(2,1)S(1)} collective-permute-done((bf16[384,768]{1,0:T(8,128)(2,1)}, bf16[384,768]{1,0:T(8,128)(2,1)S(1)}, u32[]{:S(2)}, u32[]{:S(2)}) %collective-permute-start.18) | collective-permute-done | bytes 589856 | tf_op jit(solution)/shard_map/ppermute | solution.py:440
  207.2 0.8 copy-done.11
  208.1 11.6 %collective-permute-done.19.refs_2_ = bf16[384,768]{1,0:T(8,128)(2,1)} collective-permute-done((bf16[384,768]{1,0:T(8,128)(2,1)}, bf16[384,768]{1,0:T(8,128)(2,1)}, u32[]{:S(2)}, u32[]{:S(2)}) %collective-permute-start.19) | collective-permute-done | bytes 589856 | tf_op jit(solution)/shard_map/ppermute | solution.py:440
  219.7 1.1 collective-permute-start.25
  220.8 8.2 %collective-permute-done.20.refs_3_ = bf16[384,768]{1,0:T(8,128)(2,1)} collective-permute-done((bf16[384,768]{1,0:T(8,128)(2,1)}, bf16[384,768]{1,0:T(8,128)(2,1)}, u32[]{:S(2)}, u32[]{:S(2)}) %collective-permute-start.20) | collective-permute-done | bytes 589856 | tf_op jit(solution)/shard_map/ppermute | solution.py:440
  229.1 1.2 collective-permute-start.22
  230.2 1.1 collective-permute-start.23
  231.3 11.0 %project.1 = (bf16[2,256,3072]{2,1,0:T(8,128)(2,1)}, f32[2,3072]{1,0:T(2,128)}) custom-call(s32[2,6]{1,0:T(2,128)} %pad_add_fusion.sp, bf16[2,256,768]{2,1,0:T(8,128)(2,1)} %get-tuple-element.86.att.a0, bf16[2,256,768]{2,1,0:T(8,128)(2,1)} %bitcast.25, bf16[2,256,768]{2,1,0:T(8,128)(2,1)} %collective-permute-done.10.b0, ...), custom_call_target="tpu_custom_call" | custom-call | flops 4831838208 | bytes 16000000 | tf_op jit(solution)/shard_map/project/pallas_call | solution.py:371
  242.4 5.7 %shard_map.110.rest_0_ = bf16[2,256,4608]{2,1,0:T(8,128)(2,1)} custom-call(s32[2,6]{1,0:T(2,128)} %pad_add_fusion.sp, f32[3,256,768]{2,1,0:T(8,128)} %get-tuple-element.98.own, bf16[3,256,768]{2,1,0:T(8,128)(2,1)} %copy-done.8, bf16[2,256,768]{2,1,0:T(8,128)(2,1)} %copy-done.10, bf16[2,256,768]{2,1,0:T(8,128)(2,1)} %collective-permute-done.17.p3), custom_call_target="tpu_custom_call" | custom-call | flops 1000000 | bytes 10000000 | tf_op jit(solution)/shard_map/pallas_call | solution.py:257
  248.1 9.6 %collective-permute-done.23.refs_7_ = bf16[4,96,768]{2,1,0:T(8,128)(2,1)} collective-permute-done((bf16[4,96,768]{2,1,0:T(8,128)(2,1)}, bf16[4,96,768]{2,1,0:T(8,128)(2,1)}, u32[]{:S(2)}, u32[]{:S(2)}) %collective-permute-start.23) | collective-permute-done | bytes 589856 | tf_op jit(solution)/shard_map/ppermute | solution.py:444
  257.6 4.2 %sum_parts.1 = (bf16[96,768]{1,0:T(8,128)(2,1)}, bf16[96,768]{1,0:T(8,128)(2,1)}, bf16[96,768]{1,0:T(8,128)(2,1)}, bf16[96,768]{1,0:T(8,128)(2,1)}, bf16[96,768]...) custom-call(s32[2,6]{1,0:T(2,128)} %pad_add_fusion.sp, ...), custom_call_target="tpu_custom_call" | custom-call | flops 5000000 | bytes 6000000 | tf_op jit(solution)/shard_map/sum_parts/pallas_call | solution.py:471
  261.8 1.5 collective-permute-start.27
  263.3 1.1 collective-permute-start.28
  264.5 0.9 collective-permute-start.29
  265.4 3.0 collective-permute-start.30
  268.7 1.5 collective-permute-start.32
  270.2 1.3 collective-permute-done.28.refs_2_
  271.6 1.4 collective-permute-done.29.refs_3_
  272.9 1.1 collective-permute-start.13
  274.1 0.9 collective-permute-start.12
  274.9 5.7 %shard_map.111 = bf16[2,256,4608]{2,1,0:T(8,128)(2,1)} custom-call(s32[2,6]{1,0:T(2,128)} %pad_add_fusion.sp, f32[3,256,768]{2,1,0:T(8,128)} %get-tuple-element.111.own, bf16[3,256,768]{2,1,0:T(8,128)(2,1)} %copy-done.7, bf16[2,256,768]{2,1,0:T(8,128)(2,1)} %collective-permute-done.25.p2, ...), custom_call_target="tpu_custom_call", output_to_operand_aliasing={{}: (5, {})} | custom-call | flops 1000000 | bytes 10000000 | tf_op jit(solution)/shard_map/pallas_call | solution.py:257
  280.7 0.6 copy-done.17
  281.4 2.9 sum_weights.1
  284.3 7.3 %collective-permute-start.33 = (bf16[24,1536]{1,0:T(8,128)(2,1)}, bf16[24,1536]{1,0:T(8,128)(2,1)S(1)}, u32[]{:S(2)}, u32[]{:S(2)}) collective-permute-start(bf16[24,1536]{1,0:T(8,128)(2,1)} %get-tuple-element.122), channel_id=1, source_target_pairs={{0,0},{1,64},{2,1},{3,65},{4,2},{5,66},{6,3},{7,67},{8,4},{9,68},{... | collective-permute-start | bytes 221192 | tf_op jit(solution)/shard_map/ppermute | solution.py:530
  291.8 6.1 %collective-permute-start.35 = (bf16[24,1536]{1,0:T(8,128)(2,1)}, bf16[24,1536]{1,0:T(8,128)(2,1)S(1)}, u32[]{:S(2)}, u32[]{:S(2)}) collective-permute-start(bf16[24,1536]{1,0:T(8,128)(2,1)} %get-tuple-element.124), channel_id=1, source_target_pairs={{0,2},{1,66},{2,3},{3,67},{4,0},{5,64},{6,1},{7,65},{8,6},{9,70},{... | collective-permute-start | bytes 221192 | tf_op jit(solution)/shard_map/ppermute | solution.py:530
  297.9 2.1 collective-permute-start.36
  300.0 0.6 add_add_fusion
  300.6 2.4 collective-permute-done.34
  303.0 7.3 %collective-permute-done.36 = bf16[24,1536]{1,0:T(8,128)(2,1)S(1)} collective-permute-done((bf16[24,1536]{1,0:T(8,128)(2,1)}, bf16[24,1536]{1,0:T(8,128)(2,1)S(1)}, u32[]{:S(2)}, u32[]{:S(2)}) %collective-permute-start.36) | collective-permute-done | bytes 73760 | tf_op jit(solution)/shard_map/ppermute | solution.py:530
  310.3 0.7 add_bitcast_fusion
  (95 shorter events, 5.0 us)
Async XLA Ops:
  9.0 20.5 %all-to-all-start = ((bf16[32,8,1536]{2,1,0:T(8,128)(2,1)}), bf16[32,8,1536]{2,1,0:T(8,128)(2,1)S(1)}, u32[]{:S(2)}, u32[]{:S(2)}) async-start(bf16[32,8,1536]{2,1,0:T(8,128)(2,1)} %bitcast.26), calls=%async_computation | async-start | bytes 1572864 | tf_op jit(solution)/shard_map/all_to_all | solution.py:543
  20.7 68.4 %collective-permute-start = (bf16[3,256,768]{2,1,0:T(8,128)(2,1)}, bf16[3,256,768]{2,1,0:T(8,128)(2,1)S(1)}, u32[]{:S(2)}, u32[]{:S(2)}) collective-permute-start(bf16[3,256,768]{2,1,0:T(8,128)(2,1)} %get-tuple-element.74), channel_id=1, source_target_pairs={{0,1},{1,0},{2,3},{3,2},{4,5},{5,4},{6,7},{7,6},{8,9},{9,8},{10,11... | collective-permute-start | bytes 3538952 | tf_op jit(solution)/shard_map/ppermute | solution.py:40
  29.2 15.8 %copy-start.21 = (s32[64]{0:T(128)S(1)}, s32[64]{0:T(128)}, u32[]{:S(2)}) copy-start(s32[64]{0:T(128)} %param.11) | copy-start | bytes 772
  29.2 15.9 %copy-start.22 = (s32[64]{0:T(128)S(1)}, s32[64]{0:T(128)}, u32[]{:S(2)}) copy-start(s32[64]{0:T(128)} %param.12) | copy-start | bytes 772
  29.5 0.9 copy-start.5
  33.3 20.6 %all-to-all-start.1 = ((bf16[32,8,1536]{2,1,0:T(8,128)(2,1)}), bf16[32,8,1536]{2,1,0:T(8,128)(2,1)}, u32[]{:S(2)}, u32[]{:S(2)}) async-start(bf16[32,8,1536]{2,1,0:T(8,128)(2,1)} %pick.2), calls=%async_computation.1 | async-start | bytes 1572864 | tf_op jit(solution)/shard_map/all_to_all | solution.py:547
  41.3 46.7 %collective-permute-start.1 = (bf16[2,256,768]{2,1,0:T(8,128)(2,1)}, bf16[2,256,768]{2,1,0:T(8,128)(2,1)}, u32[]{:S(2)}, u32[]{:S(2)}) collective-permute-start(bf16[2,256,768]{2,1,0:T(8,128)(2,1)} %get-tuple-element.67), channel_id=1, source_target_pairs={{0,2},{1,3},{2,0},{3,1},{4,6},{5,7},{6,4},{7,5},{8,10},{9,11},{10,... | collective-permute-start | bytes 2359304 | tf_op jit(solution)/shard_map/ppermute | solution.py:40
  45.0 42.4 %collective-permute-start.2 = (bf16[2,256,768]{2,1,0:T(8,128)(2,1)}, bf16[2,256,768]{2,1,0:T(8,128)(2,1)}, u32[]{:S(2)}, u32[]{:S(2)}) collective-permute-start(bf16[2,256,768]{2,1,0:T(8,128)(2,1)} %get-tuple-element.75), channel_id=1, source_target_pairs={{0,3},{1,2},{2,1},{3,0},{4,7},{5,6},{6,5},{7,4},{8,11},{9,10},{10,... | collective-permute-start | bytes 2359304 | tf_op jit(solution)/shard_map/ppermute | solution.py:40
  48.3 81.5 %collective-permute-start.4 = (bf16[3,256,768]{2,1,0:T(8,128)(2,1)}, bf16[3,256,768]{2,1,0:T(8,128)(2,1)S(1)}, u32[]{:S(2)}, u32[]{:S(2)}) collective-permute-start(bf16[3,256,768]{2,1,0:T(8,128)(2,1)} %get-tuple-element.80), channel_id=1, source_target_pairs={{0,1},{1,0},{2,3},{3,2},{4,5},{5,4},{6,7},{7,6},{8,9},{9,8},{10,11... | collective-permute-start | bytes 3538952 | tf_op jit(solution)/shard_map/ppermute | solution.py:40
  48.7 70.2 %collective-permute-start.6 = (bf16[2,256,768]{2,1,0:T(8,128)(2,1)}, bf16[2,256,768]{2,1,0:T(8,128)(2,1)S(1)}, u32[]{:S(2)}, u32[]{:S(2)}) collective-permute-start(bf16[2,256,768]{2,1,0:T(8,128)(2,1)} %get-tuple-element.81), channel_id=1, source_target_pairs={{0,3},{1,2},{2,1},{3,0},{4,7},{5,6},{6,5},{7,4},{8,11},{9,10},{10,... | collective-permute-start | bytes 2359304 | tf_op jit(solution)/shard_map/ppermute | solution.py:40
  87.4 42.4 %collective-permute-start.5 = (bf16[2,256,768]{2,1,0:T(8,128)(2,1)}, bf16[2,256,768]{2,1,0:T(8,128)(2,1)}, u32[]{:S(2)}, u32[]{:S(2)}) collective-permute-start(bf16[2,256,768]{2,1,0:T(8,128)(2,1)} %get-tuple-element.72), channel_id=1, source_target_pairs={{0,2},{1,3},{2,0},{3,1},{4,6},{5,7},{6,4},{7,5},{8,10},{9,11},{10,... | collective-permute-start | bytes 2359304 | tf_op jit(solution)/shard_map/ppermute | solution.py:40
  88.0 18.9 %collective-permute-start.3 = (bf16[1,256,768]{2,1,0:T(8,128)(2,1)S(1)}, bf16[1,256,768]{2,1,0:T(8,128)(2,1)}, u32[]{:S(2)}, u32[]{:S(2)}) collective-permute-start(bf16[1,256,768]{2,1,0:T(8,128)(2,1)S(1)} %fusion), channel_id=1, source_target_pairs={{0,1},{1,0},{2,3},{3,2},{4,5},{5,4},{6,7},{7,6},{8,9},{9,8},{10,11... | collective-permute-start | bytes 1179656 | tf_op jit(solution)/shard_map/ppermute | solution.py:40
  89.1 17.1 %copy-start.20 = (s32[32]{0:T(128)S(1)}, s32[32]{0:T(128)}, u32[]{:S(2)}) copy-start(s32[32]{0:T(128)} %order) | copy-start | bytes 388
  89.1 1.0 copy-start.1
  98.5 40.7 %all-to-all-start.2 = ((bf16[32,16,768]{2,1,0:T(8,128)(2,1)}), bf16[32,16,768]{2,1,0:T(8,128)(2,1)}, u32[]{:S(2)}, u32[]{:S(2)}) async-start(bf16[32,16,768]{2,1,0:T(8,128)(2,1)} %bitcast.21), calls=%async_computation.2 | async-start | bytes 1572864 | tf_op jit(solution)/shard_map/all_to_all | solution.py:543
  118.9 10.9 %copy-start.2 = (bf16[2,256,768]{2,1,0:T(8,128)(2,1)}, bf16[2,256,768]{2,1,0:T(8,128)(2,1)S(1)}, u32[]{:S(2)}) copy-start(bf16[2,256,768]{2,1,0:T(8,128)(2,1)S(1)} %collective-permute-done.6.k3.v3) | copy-start | bytes 2359300
  129.8 1.0 copy-start
  139.2 11.1 %copy-start.3 = (bf16[256,1536]{1,0:T(8,128)(2,1)S(1)}, bf16[256,1536]{1,0:T(8,128)(2,1)}, u32[]{:S(2)}) copy-start(bf16[256,1536]{1,0:T(8,128)(2,1)} %get-tuple-element.69) | copy-start | bytes 2359300
  139.3 11.3 %copy-start.4 = (bf16[2,256,768]{2,1,0:T(8,128)(2,1)S(1)}, bf16[2,256,768]{2,1,0:T(8,128)(2,1)}, u32[]{:S(2)}) copy-start(bf16[2,256,768]{2,1,0:T(8,128)(2,1)} %get-tuple-element.86.att.a0) | copy-start | bytes 2359300
  142.3 19.4 %all-to-all-start.3 = ((bf16[32,16,768]{2,1,0:T(8,128)(2,1)}), bf16[32,16,768]{2,1,0:T(8,128)(2,1)S(1)}, u32[]{:S(2)}, u32[]{:S(2)}) async-start(bf16[32,16,768]{2,1,0:T(8,128)(2,1)} %pick.3), calls=%async_computation.3 | async-start | bytes 1572864 | tf_op jit(solution)/shard_map/all_to_all | solution.py:547
  149.8 12.7 %collective-permute-start.9 = (bf16[256,1536]{1,0:T(8,128)(2,1)}, bf16[256,1536]{1,0:T(8,128)(2,1)}, u32[]{:S(2)}, u32[]{:S(2)}) collective-permute-start(bf16[256,1536]{1,0:T(8,128)(2,1)} %get-tuple-element.92), channel_id=1, source_target_pairs={{0,1},{1,0},{2,3},{3,2},{4,5},{5,4},{6,7},{7,6},{8,9},{9,8},{10,11... | collective-permute-start | bytes 2359304 | tf_op jit(solution)/shard_map/ppermute | solution.py:40
  149.9 13.8 %collective-permute-start.8 = (bf16[256,1536]{1,0:T(8,128)(2,1)}, bf16[256,1536]{1,0:T(8,128)(2,1)}, u32[]{:S(2)}, u32[]{:S(2)}) collective-permute-start(bf16[256,1536]{1,0:T(8,128)(2,1)} %get-tuple-element.90), channel_id=1, source_target_pairs={{0,1},{1,0},{2,3},{3,2},{4,5},{5,4},{6,7},{7,6},{8,9},{9,8},{10,11... | collective-permute-start | bytes 2359304 | tf_op jit(solution)/shard_map/ppermute | solution.py:40
  150.4 11.3 %collective-permute-start.7 = (bf16[1,256,768]{2,1,0:T(8,128)(2,1)S(1)}, bf16[1,256,768]{2,1,0:T(8,128)(2,1)S(1)}, u32[]{:S(2)}, u32[]{:S(2)}) collective-permute-start(bf16[1,256,768]{2,1,0:T(8,128)(2,1)S(1)} %select_bitcast_fusion), channel_id=1, source_target_pairs={{0,1},{1,0},{2,3},{3,2},{4,5},{5,4},{6,7},{7,6},{8,9},{9,8},{10,11... | collective-permute-start | bytes 1179656 | tf_op jit(solution)/shard_map/ppermute | solution.py:40
  150.6 27.3 %collective-permute-start.10 = (bf16[2,256,768]{2,1,0:T(8,128)(2,1)S(1)}, bf16[2,256,768]{2,1,0:T(8,128)(2,1)}, u32[]{:S(2)}, u32[]{:S(2)}) collective-permute-start(bf16[2,256,768]{2,1,0:T(8,128)(2,1)S(1)} %copy-done.4), channel_id=1, source_target_pairs={{0,1},{1,0},{2,3},{3,2},{4,5},{5,4},{6,7},{7,6},{8,9},{9,8},{10,11... | collective-permute-start | bytes 2359304 | tf_op jit(solution)/shard_map/ppermute | solution.py:40
  161.7 16.2 %copy-start.6 = (bf16[32,16,768]{2,1,0:T(8,128)(2,1)}, bf16[32,16,768]{2,1,0:T(8,128)(2,1)S(1)}, u32[]{:S(2)}) copy-start(bf16[32,16,768]{2,1,0:T(8,128)(2,1)S(1)} %all-to-all-done.3) | copy-start | bytes 2359300
  161.7 16.2 %collective-permute-start.11 = (bf16[2,256,768]{2,1,0:T(8,128)(2,1)S(1)}, bf16[2,256,768]{2,1,0:T(8,128)(2,1)}, u32[]{:S(2)}, u32[]{:S(2)}) collective-permute-start(bf16[2,256,768]{2,1,0:T(8,128)(2,1)S(1)} %bitcast.23), channel_id=1, source_target_pairs={{0,1},{1,0},{2,3},{3,2},{4,5},{5,4},{6,7},{7,6},{8,9},{9,8},{10,11... | collective-permute-start | bytes 2359304 | tf_op jit(solution)/shard_map/ppermute | solution.py:40
  161.7 0.8 copy-start.12
  161.7 40.5 %collective-permute-start.15 = (bf16[3,256,768]{2,1,0:T(8,128)(2,1)}, bf16[3,256,768]{2,1,0:T(8,128)(2,1)S(1)}, u32[]{:S(2)}, u32[]{:S(2)}) collective-permute-start(bf16[3,256,768]{2,1,0:T(8,128)(2,1)} %get-tuple-element.99), channel_id=1, source_target_pairs={{0,1},{1,0},{2,3},{3,2},{4,5},{5,4},{6,7},{7,6},{8,9},{9,8},{10,11... | collective-permute-start | bytes 3538952 | tf_op jit(solution)/shard_map/ppermute | solution.py:40
  162.5 38.9 %collective-permute-start.16 = (bf16[2,256,768]{2,1,0:T(8,128)(2,1)}, bf16[2,256,768]{2,1,0:T(8,128)(2,1)S(1)}, u32[]{:S(2)}, u32[]{:S(2)}) collective-permute-start(bf16[2,256,768]{2,1,0:T(8,128)(2,1)} %get-tuple-element.78), channel_id=1, source_target_pairs={{0,2},{1,3},{2,0},{3,1},{4,6},{5,7},{6,4},{7,5},{8,10},{9,11},{10,... | collective-permute-start | bytes 2359304 | tf_op jit(solution)/shard_map/ppermute | solution.py:40
  163.6 36.9 %collective-permute-start.17 = (bf16[2,256,768]{2,1,0:T(8,128)(2,1)}, bf16[2,256,768]{2,1,0:T(8,128)(2,1)}, u32[]{:S(2)}, u32[]{:S(2)}) collective-permute-start(bf16[2,256,768]{2,1,0:T(8,128)(2,1)} %get-tuple-element.100), channel_id=1, source_target_pairs={{0,3},{1,2},{2,1},{3,0},{4,7},{5,6},{6,5},{7,4},{8,11},{9,10},{10,... | collective-permute-start | bytes 2359304 | tf_op jit(solution)/shard_map/ppermute | solution.py:40
  190.8 16.4 %collective-permute-start.18 = (bf16[384,768]{1,0:T(8,128)(2,1)}, bf16[384,768]{1,0:T(8,128)(2,1)S(1)}, u32[]{:S(2)}, u32[]{:S(2)}) collective-permute-start(bf16[384,768]{1,0:T(8,128)(2,1)} %get-tuple-element.102), channel_id=1, source_target_pairs={{0,32},{4,36},{8,40},{12,44},{16,48},{20,52},{24,56},{28,60},{32,0... | collective-permute-start | bytes 1769480 | tf_op jit(solution)/shard_map/ppermute | solution.py:440
  192.0 27.7 %collective-permute-start.19 = (bf16[384,768]{1,0:T(8,128)(2,1)}, bf16[384,768]{1,0:T(8,128)(2,1)}, u32[]{:S(2)}, u32[]{:S(2)}) collective-permute-start(bf16[384,768]{1,0:T(8,128)(2,1)} %get-tuple-element.103), channel_id=1, source_target_pairs={{0,64},{4,68},{8,72},{12,76},{16,80},{20,84},{24,88},{28,92},{32,9... | collective-permute-start | bytes 1769480 | tf_op jit(solution)/shard_map/ppermute | solution.py:440
  200.6 28.5 %collective-permute-start.20 = (bf16[384,768]{1,0:T(8,128)(2,1)}, bf16[384,768]{1,0:T(8,128)(2,1)}, u32[]{:S(2)}, u32[]{:S(2)}) collective-permute-start(bf16[384,768]{1,0:T(8,128)(2,1)} %get-tuple-element.104), channel_id=1, source_target_pairs={{0,96},{4,100},{8,104},{12,108},{16,112},{20,116},{24,120},{28,124... | collective-permute-start | bytes 1769480 | tf_op jit(solution)/shard_map/ppermute | solution.py:440
  201.4 0.9 copy-start.10
  201.4 28.9 %collective-permute-start.21 = (bf16[4,96,768]{2,1,0:T(8,128)(2,1)}, bf16[4,96,768]{2,1,0:T(8,128)(2,1)}, u32[]{:S(2)}, u32[]{:S(2)}) collective-permute-start(bf16[4,96,768]{2,1,0:T(8,128)(2,1)} %get-tuple-element.106), channel_id=1, source_target_pairs={{0,8},{4,12},{8,0},{12,4},{16,24},{20,28},{24,16},{28,20},{32,40},... | collective-permute-start | bytes 1769480 | tf_op jit(solution)/shard_map/ppermute | solution.py:444
  202.3 40.1 %copy-start.8 = (bf16[3,256,768]{2,1,0:T(8,128)(2,1)}, bf16[3,256,768]{2,1,0:T(8,128)(2,1)S(1)}, u32[]{:S(2)}) copy-start(bf16[3,256,768]{2,1,0:T(8,128)(2,1)S(1)} %collective-permute-done.15.p1) | copy-start | bytes 3538948
  202.3 66.1 %collective-permute-start.24 = (bf16[3,256,768]{2,1,0:T(8,128)(2,1)}, bf16[3,256,768]{2,1,0:T(8,128)(2,1)S(1)}, u32[]{:S(2)}, u32[]{:S(2)}) collective-permute-start(bf16[3,256,768]{2,1,0:T(8,128)(2,1)} %get-tuple-element.112), channel_id=1, source_target_pairs={{0,1},{1,0},{2,3},{3,2},{4,5},{5,4},{6,7},{7,6},{8,9},{9,8},{10,11... | collective-permute-start | bytes 3538952 | tf_op jit(solution)/shard_map/ppermute | solution.py:40
  207.2 0.8 copy-start.11
  208.1 56.4 %collective-permute-start.26 = (bf16[2,256,768]{2,1,0:T(8,128)(2,1)}, bf16[2,256,768]{2,1,0:T(8,128)(2,1)S(1)}, u32[]{:S(2)}, u32[]{:S(2)}) collective-permute-start(bf16[2,256,768]{2,1,0:T(8,128)(2,1)} %get-tuple-element.113), channel_id=1, source_target_pairs={{0,3},{1,2},{2,1},{3,0},{4,7},{5,6},{6,5},{7,4},{8,11},{9,10},{10,... | collective-permute-start | bytes 2359304 | tf_op jit(solution)/shard_map/ppermute | solution.py:40
  219.7 45.7 %collective-permute-start.25 = (bf16[2,256,768]{2,1,0:T(8,128)(2,1)}, bf16[2,256,768]{2,1,0:T(8,128)(2,1)}, u32[]{:S(2)}, u32[]{:S(2)}) collective-permute-start(bf16[2,256,768]{2,1,0:T(8,128)(2,1)} %get-tuple-element.87), channel_id=1, source_target_pairs={{0,2},{1,3},{2,0},{3,1},{4,6},{5,7},{6,4},{7,5},{8,10},{9,11},{10,... | collective-permute-start | bytes 2359304 | tf_op jit(solution)/shard_map/ppermute | solution.py:40
  229.1 19.0 %collective-permute-start.22 = (bf16[4,96,768]{2,1,0:T(8,128)(2,1)}, bf16[4,96,768]{2,1,0:T(8,128)(2,1)}, u32[]{:S(2)}, u32[]{:S(2)}) collective-permute-start(bf16[4,96,768]{2,1,0:T(8,128)(2,1)} %get-tuple-element.107), channel_id=1, source_target_pairs={{0,16},{4,20},{8,24},{12,28},{16,0},{20,4},{24,8},{28,12},{32,48},... | collective-permute-start | bytes 1769480 | tf_op jit(solution)/shard_map/ppermute | solution.py:444
  230.2 27.4 %collective-permute-start.23 = (bf16[4,96,768]{2,1,0:T(8,128)(2,1)}, bf16[4,96,768]{2,1,0:T(8,128)(2,1)}, u32[]{:S(2)}, u32[]{:S(2)}) collective-permute-start(bf16[4,96,768]{2,1,0:T(8,128)(2,1)} %get-tuple-element.108), channel_id=1, source_target_pairs={{0,24},{4,28},{8,16},{12,20},{16,8},{20,12},{24,0},{28,4},{32,56},... | collective-permute-start | bytes 1769480 | tf_op jit(solution)/shard_map/ppermute | solution.py:444
  257.6 13.9 %copy-start.19 = (f32[2,3072]{1,0:T(2,128)S(1)}, f32[2,3072]{1,0:T(2,128)}, u32[]{:S(2)}) copy-start(f32[2,3072]{1,0:T(2,128)} %get-tuple-element.96) | copy-start | bytes 73732
  261.8 6.9 %collective-permute-start.27 = (bf16[96,768]{1,0:T(8,128)(2,1)}, bf16[96,768]{1,0:T(8,128)(2,1)S(1)}, u32[]{:S(2)}, u32[]{:S(2)}) collective-permute-start(bf16[96,768]{1,0:T(8,128)(2,1)} %get-tuple-element.115), channel_id=1, source_target_pairs={{0,8},{4,12},{8,0},{12,4},{16,24},{20,28},{24,16},{28,20},{32,40},... | collective-permute-start | bytes 442376 | tf_op jit(solution)/shard_map/ppermute | solution.py:444
  263.3 8.2 %collective-permute-start.28 = (bf16[96,768]{1,0:T(8,128)(2,1)}, bf16[96,768]{1,0:T(8,128)(2,1)S(1)}, u32[]{:S(2)}, u32[]{:S(2)}) collective-permute-start(bf16[96,768]{1,0:T(8,128)(2,1)} %get-tuple-element.116), channel_id=1, source_target_pairs={{0,16},{4,20},{8,24},{12,28},{16,0},{20,4},{24,8},{28,12},{32,48},... | collective-permute-start | bytes 442376 | tf_op jit(solution)/shard_map/ppermute | solution.py:444
  264.5 10.5 %copy-start.9 = (bf16[2,256,768]{2,1,0:T(8,128)(2,1)}, bf16[2,256,768]{2,1,0:T(8,128)(2,1)S(1)}, u32[]{:S(2)}) copy-start(bf16[2,256,768]{2,1,0:T(8,128)(2,1)S(1)} %collective-permute-done.26.p3) | copy-start | bytes 2359300
  264.5 8.5 %collective-permute-start.29 = (bf16[96,768]{1,0:T(8,128)(2,1)}, bf16[96,768]{1,0:T(8,128)(2,1)S(1)}, u32[]{:S(2)}, u32[]{:S(2)}) collective-permute-start(bf16[96,768]{1,0:T(8,128)(2,1)} %get-tuple-element.117), channel_id=1, source_target_pairs={{0,24},{4,28},{8,16},{12,20},{16,8},{20,12},{24,0},{28,4},{32,56},... | collective-permute-start | bytes 442376 | tf_op jit(solution)/shard_map/ppermute | solution.py:444
  265.4 8.7 %collective-permute-start.30 = (bf16[96,768]{1,0:T(8,128)(2,1)}, bf16[96,768]{1,0:T(8,128)(2,1)S(1)}, u32[]{:S(2)}, u32[]{:S(2)}) collective-permute-start(bf16[96,768]{1,0:T(8,128)(2,1)} %get-tuple-element.119), channel_id=1, source_target_pairs={{0,32},{4,36},{8,40},{12,44},{16,48},{20,52},{24,56},{28,60},{32,0... | collective-permute-start | bytes 442376 | tf_op jit(solution)/shard_map/ppermute | solution.py:440
  268.4 6.6 %copy-start.7 = (bf16[3,256,768]{2,1,0:T(8,128)(2,1)}, bf16[3,256,768]{2,1,0:T(8,128)(2,1)S(1)}, u32[]{:S(2)}) copy-start(bf16[3,256,768]{2,1,0:T(8,128)(2,1)S(1)} %collective-permute-done.24.p1) | copy-start | bytes 3538948
  268.4 12.3 %collective-permute-start.31 = (bf16[96,768]{1,0:T(8,128)(2,1)}, bf16[96,768]{1,0:T(8,128)(2,1)S(1)}, u32[]{:S(2)}, u32[]{:S(2)}) collective-permute-start(bf16[96,768]{1,0:T(8,128)(2,1)} %get-tuple-element.120), channel_id=1, source_target_pairs={{0,64},{4,68},{8,72},{12,76},{16,80},{20,84},{24,88},{28,92},{32,9... | collective-permute-start | bytes 442376 | tf_op jit(solution)/shard_map/ppermute | solution.py:440
  268.7 11.9 %copy-start.13 = (bf16[96,768]{1,0:T(8,128)(2,1)}, bf16[96,768]{1,0:T(8,128)(2,1)S(1)}, u32[]{:S(2)}) copy-start(bf16[96,768]{1,0:T(8,128)(2,1)S(1)} %collective-permute-done.27.refs_1_) | copy-start | bytes 442372
  268.7 12.0 %collective-permute-start.32 = (bf16[96,768]{1,0:T(8,128)(2,1)}, bf16[96,768]{1,0:T(8,128)(2,1)S(1)}, u32[]{:S(2)}, u32[]{:S(2)}) collective-permute-start(bf16[96,768]{1,0:T(8,128)(2,1)} %get-tuple-element.121), channel_id=1, source_target_pairs={{0,96},{4,100},{8,104},{12,108},{16,112},{20,116},{24,120},{28,124... | collective-permute-start | bytes 442376 | tf_op jit(solution)/shard_map/ppermute | solution.py:440
  271.6 9.1 %copy-start.14 = (bf16[96,768]{1,0:T(8,128)(2,1)}, bf16[96,768]{1,0:T(8,128)(2,1)S(1)}, u32[]{:S(2)}) copy-start(bf16[96,768]{1,0:T(8,128)(2,1)S(1)} %collective-permute-done.28.refs_2_) | copy-start | bytes 442372
  271.6 20.2 %collective-permute-start.14 = (f32[2,3072]{1,0:T(2,128)S(1)}, f32[2,3072]{1,0:T(2,128)S(1)}, u32[]{:S(2)}, u32[]{:S(2)}) collective-permute-start(f32[2,3072]{1,0:T(2,128)S(1)} %copy-done.19), channel_id=1, source_target_pairs={{0,3},{1,2},{2,1},{3,0},{4,7},{5,6},{6,5},{7,4},{8,11},{9,10},{10,... | collective-permute-start | bytes 73736 | tf_op jit(solution)/shard_map/ppermute | solution.py:40
  272.9 7.7 %copy-start.15 = (bf16[96,768]{1,0:T(8,128)(2,1)}, bf16[96,768]{1,0:T(8,128)(2,1)S(1)}, u32[]{:S(2)}) copy-start(bf16[96,768]{1,0:T(8,128)(2,1)S(1)} %collective-permute-done.29.refs_3_) | copy-start | bytes 442372
  272.9 24.9 %collective-permute-start.13 = (f32[2,3072]{1,0:T(2,128)S(1)}, f32[2,3072]{1,0:T(2,128)S(1)}, u32[]{:S(2)}, u32[]{:S(2)}) collective-permute-start(f32[2,3072]{1,0:T(2,128)S(1)} %copy-done.19), channel_id=1, source_target_pairs={{0,2},{1,3},{2,0},{3,1},{4,6},{5,7},{6,4},{7,5},{8,10},{9,11},{10,... | collective-permute-start | bytes 73736 | tf_op jit(solution)/shard_map/ppermute | solution.py:40
  274.1 6.6 %copy-start.16 = (bf16[96,768]{1,0:T(8,128)(2,1)}, bf16[96,768]{1,0:T(8,128)(2,1)S(1)}, u32[]{:S(2)}) copy-start(bf16[96,768]{1,0:T(8,128)(2,1)S(1)} %collective-permute-done.30.refs_5_) | copy-start | bytes 442372
  274.1 25.9 %collective-permute-start.12 = (f32[2,3072]{1,0:T(2,128)S(1)}, f32[2,3072]{1,0:T(2,128)S(1)}, u32[]{:S(2)}, u32[]{:S(2)}) collective-permute-start(f32[2,3072]{1,0:T(2,128)S(1)} %copy-done.19), channel_id=1, source_target_pairs={{0,1},{1,0},{2,3},{3,2},{4,5},{5,4},{6,7},{7,6},{8,9},{9,8},{10,11... | collective-permute-start | bytes 73736 | tf_op jit(solution)/shard_map/ppermute | solution.py:40
  280.7 0.7 copy-start.17
  280.7 0.7 copy-start.18
  284.3 16.3 %collective-permute-start.33 = (bf16[24,1536]{1,0:T(8,128)(2,1)}, bf16[24,1536]{1,0:T(8,128)(2,1)S(1)}, u32[]{:S(2)}, u32[]{:S(2)}) collective-permute-start(bf16[24,1536]{1,0:T(8,128)(2,1)} %get-tuple-element.122), channel_id=1, source_target_pairs={{0,0},{1,64},{2,1},{3,65},{4,2},{5,66},{6,3},{7,67},{8,4},{9,68},{... | collective-permute-start | bytes 221192 | tf_op jit(solution)/shard_map/ppermute | solution.py:530
  291.6 11.5 %collective-permute-start.34 = (bf16[24,1536]{1,0:T(8,128)(2,1)}, bf16[24,1536]{1,0:T(8,128)(2,1)S(1)}, u32[]{:S(2)}, u32[]{:S(2)}) collective-permute-start(bf16[24,1536]{1,0:T(8,128)(2,1)} %get-tuple-element.123), channel_id=1, source_target_pairs={{0,1},{1,65},{2,0},{3,64},{4,3},{5,67},{6,2},{7,66},{8,5},{9,69},{... | collective-permute-start | bytes 221192 | tf_op jit(solution)/shard_map/ppermute | solution.py:530
  291.8 11.3 %collective-permute-start.35 = (bf16[24,1536]{1,0:T(8,128)(2,1)}, bf16[24,1536]{1,0:T(8,128)(2,1)S(1)}, u32[]{:S(2)}, u32[]{:S(2)}) collective-permute-start(bf16[24,1536]{1,0:T(8,128)(2,1)} %get-tuple-element.124), channel_id=1, source_target_pairs={{0,2},{1,66},{2,3},{3,67},{4,0},{5,64},{6,1},{7,65},{8,6},{9,70},{... | collective-permute-start | bytes 221192 | tf_op jit(solution)/shard_map/ppermute | solution.py:530
  297.9 12.5 %collective-permute-start.36 = (bf16[24,1536]{1,0:T(8,128)(2,1)}, bf16[24,1536]{1,0:T(8,128)(2,1)S(1)}, u32[]{:S(2)}, u32[]{:S(2)}) collective-permute-start(bf16[24,1536]{1,0:T(8,128)(2,1)} %get-tuple-element.125), channel_id=1, source_target_pairs={{0,3},{1,67},{2,2},{3,66},{4,1},{5,65},{6,0},{7,64},{8,7},{9,71},{... | collective-permute-start | bytes 221192 | tf_op jit(solution)/shard_map/ppermute | solution.py:530

commit v4 on v3

--- a/solution.py
+++ b/solution.py
@@ -400,15 +400,14 @@
     left = jnp.concatenate([own0[...], peer0[...], own1[...], peer1[...]], axis=0)
     mine = jnp.concatenate([a0[0], a0[1], a1[0], a1[1]], axis=0)
     other = jnp.concatenate([b0[1], b0[0], b1[1], b1[0]], axis=0)
-    first = sp[0, 0] == 0
-    by_x = mm(left, jnp.where(first, mine, other), TN).astype(jnp.bfloat16)
+    by_x = mm(left, mine, TN).astype(jnp.bfloat16)
     for x_step in range(4):
 
         @pl.when(step == x_step)
         def _():
             outs[x_step][...] = by_x
 
-    product[...] = mm(left, jnp.where(first, other, mine), TN)
+    product[...] = mm(left, other, TN)
     for y_step in range(4):
         start = pl.multiple_of((sp[1, 5] ^ y_step) * SHARE, 8)
         rows = product[pl.ds(start, SHARE), :].astype(jnp.bfloat16)
@@ -498,8 +497,11 @@
 
 def sum_kernel(sp, *refs):
     low, high, outs, total = refs[:4], refs[4:8], refs[8:12], refs[12]
-    total[:, :HALF] = add_up(low)
-    total[:, HALF:] = add_up(high)
+    first = sp[0, 0] == 0
+    mine = add_up(low)
+    other = add_up(high)
+    total[:, :HALF] = jnp.where(first, mine, other)
+    total[:, HALF:] = jnp.where(first, other, mine)
     count = SHARE // 4
     for step, out in enumerate(outs):
         start = pl.multiple_of((sp[1, 0] ^ step) * count, 8)
@@ -575,18 +577,19 @@
     att, lse = [None, None], [None, None]
 
     cp = core.astype(jnp.int32).reshape(1, 1)
-    send_1, keep_1, away = scaled_rows(cp, 1, cotangent, gate, out_weight)
+    s1, s2, s3 = prep(cp, qkv, 1)
+    received[1] = (swap(s1, 1), swap(s2, 2), swap(s3, 3))
+    send_1, keep_1, away = scaled_rows(after(cp, s2), 1, cotangent, gate, out_weight)
     d_spread = spread_out(away)
-    s1, s2, s3 = prep(after(cp, away), qkv, 1)
-    received[1] = (swap(s1, 1), swap(s2, 2), swap(s3, 3))
+    s1, s2, s3 = prep(after(cp, away), qkv, 0)
+    near_keys = (swap(s1, 1), swap(s3, 3))
+    received[0] = (near_keys[0], swap(s2, 2), near_keys[1])
     send_0, keep_0, near = scaled_rows(after(cp, s2), 0, cotangent, gate, out_weight)
     d_own[0], d_peer[0] = near[None], to_core(near)
     scaled = (keep_0, swap(send_0, 1), keep_1, swap(send_1, 1))
     d_picked = pick(d_spread, after(plan, near))
     landed = land(d_picked, (ROWS, WIDTH))
-    s1, s2, s3 = prep(after(cp, d_picked), qkv, 0)
-    received[0] = (swap(s1, 1), swap(s2, 2), swap(s3, 3))
-    sp = after(sp, s2)
+    sp = after(sp, d_picked)
     att[1], lse[1] = attend(sp, 1, qkv, received[1])
     d_own[1], d_peer[1] = landed[None], to_core(landed)
     att_spread = spread_out(after(att[1], landed).reshape(2 * ROWS, HALF))

time: 312 us -> 324 us (1.038)
  the two profiles are of different devices: /device:TPU:18 before, /device:TPU:1 now
where the time goes in v4:
time: 324 us; the launch traced here: 319 us
  Pallas kernels  112 us (35%)
  waiting for transfers between devices  106 us (33%)
  starting transfers between devices  88 us (27%)
  local copies, waits for them, and re-layouts  7.98 us (2%)
  other arithmetic  4.04 us (1%)
    ppermute x21, waiting for transfers between devices, swap(): return lax.ppermute(x, 'seq', [(i, i ^ step) for i in range(4)])  56.1 us
    ppermute x21, starting transfers between devices, swap(): return lax.ppermute(x, 'seq', [(i, i ^ step) for i in range(4)])  33.9 us
    pallas_call x2, Pallas kernels, attend_back(): pl.pallas_call(functools.partial(bwd_kernel, slot), grid_spec=pltpu.Prefe...  24.1 us
    ppermute x6, waiting for transfers between devices, along_x(): return lax.ppermute(x, 'dp', [(g, g ^ step << 3) for g in range(32)])  17.7 us
    all_to_all x2, waiting for transfers between devices, land(): lax.all_to_all(arranged, 'dp', split_axis=0, concat_axis=0, tiled=True)  17.4 us
    pallas_call x2, Pallas kernels, scaled_rows(): pl.pallas_call(functools.partial(rows_kernel, slot), grid_spec=pltpu.Pref...  16.9 us
    pallas_call x2, Pallas kernels, attend(): pl.pallas_call(functools.partial(fwd_kernel, slot), grid_spec=pltpu.Prefe...  16.9 us
    all_to_all x2, starting transfers between devices, spread_out(): lax.all_to_all(portions, 'dp', split_axis=0, concat_axis=0, tiled=True)  15.3 us
  transfers between devices with their start and end apart: 41, of which 11 were waited for; matrix products, arithmetic and copies ran while one was open for 1% of the time, Pallas kernels for 31%

profile of v4, /device:TPU:1, one launch (start us, length us, event | category | flops | bytes accessed | tf_op | source)
XLA Modules:
  0.0 319.1 jit_solution(11373855929258761228)
XLA Ops:
  0.6 3.0 shard_map.102
  3.6 8.5 %shard_map.103 = (bf16[256,1536]{1,0:T(8,128)(2,1)}, bf16[256,1536]{1,0:T(8,128)(2,1)}, bf16[256,1536]{1,0:T(8,128)(2,1)}) custom-call(s32[1,1]{1,0:T(1,128)} %bitcast.6.sp, bf16[2,256,3072]{2,1,0:T(8,128)(2,1)} %cotangent.5, f32[2,3072]{1,0:T(2,128)} %gate.5, bf16[1536,3072]{1,0:T(8,128)(2,1)} %w_other.1), custom_call_target="tpu_custom_call" | custom-call | flops 2415919104 | bytes 13000000 | tf_op jit(solution)/shard_map/pallas_call | solution.py:329
  12.1 9.2 %all-to-all-start = ((bf16[32,8,1536]{2,1,0:T(8,128)(2,1)}), bf16[32,8,1536]{2,1,0:T(8,128)(2,1)S(1)}, u32[]{:S(2)}, u32[]{:S(2)}) async-start(bf16[32,8,1536]{2,1,0:T(8,128)(2,1)} %bitcast.26), calls=%async_computation | async-start | bytes 1572864 | tf_op jit(solution)/shard_map/all_to_all | solution.py:545
  21.3 1.0 collective-permute-start
  22.3 2.9 shard_map.104
  25.3 8.4 %shard_map.105 = (bf16[256,1536]{1,0:T(8,128)(2,1)}, bf16[256,1536]{1,0:T(8,128)(2,1)}, bf16[256,1536]{1,0:T(8,128)(2,1)}) custom-call(s32[1,1]{1,0:T(1,128)} %bitcast.6.sp, bf16[2,256,3072]{2,1,0:T(8,128)(2,1)} %cotangent.5, f32[2,3072]{1,0:T(2,128)} %gate.5, bf16[1536,3072]{1,0:T(8,128)(2,1)} %w_other.1), custom_call_target="tpu_custom_call" | custom-call | flops 2415919104 | bytes 13000000 | tf_op jit(solution)/shard_map/pallas_call | solution.py:329
  33.7 1.1 all-to-all-done.rows
  34.8 0.9 copy-done.6
  35.7 2.9 pick.2
  38.5 7.0 %all-to-all-start.1 = ((bf16[32,8,1536]{2,1,0:T(8,128)(2,1)}), bf16[32,8,1536]{2,1,0:T(8,128)(2,1)}, u32[]{:S(2)}, u32[]{:S(2)}) async-start(bf16[32,8,1536]{2,1,0:T(8,128)(2,1)} %pick.2), calls=%async_computation.1 | async-start | bytes 1572864 | tf_op jit(solution)/shard_map/all_to_all | solution.py:549
  45.6 3.4 %collective-permute-start.1 = (bf16[2,256,768]{2,1,0:T(8,128)(2,1)}, bf16[2,256,768]{2,1,0:T(8,128)(2,1)}, u32[]{:S(2)}, u32[]{:S(2)}) collective-permute-start(bf16[2,256,768]{2,1,0:T(8,128)(2,1)} %get-tuple-element.65), channel_id=1, source_target_pairs={{0,2},{1,3},{2,0},{3,1},{4,6},{5,7},{6,4},{7,5},{8,10},{9,11},{10,... | collective-permute-start | bytes 2359304 | tf_op jit(solution)/shard_map/ppermute | solution.py:40
  49.1 3.7 %collective-permute-start.2 = (bf16[2,256,768]{2,1,0:T(8,128)(2,1)}, bf16[2,256,768]{2,1,0:T(8,128)(2,1)}, u32[]{:S(2)}, u32[]{:S(2)}) collective-permute-start(bf16[2,256,768]{2,1,0:T(8,128)(2,1)} %get-tuple-element.75), channel_id=1, source_target_pairs={{0,3},{1,2},{2,1},{3,0},{4,7},{5,6},{6,5},{7,4},{8,11},{9,10},{10,... | collective-permute-start | bytes 2359304 | tf_op jit(solution)/shard_map/ppermute | solution.py:40
  53.3 6.1 %all-to-all-done.1 = bf16[32,8,1536]{2,1,0:T(8,128)(2,1)} async-done(((bf16[32,8,1536]{2,1,0:T(8,128)(2,1)}), bf16[32,8,1536]{2,1,0:T(8,128)(2,1)}, u32[]{:S(2)}, u32[]{:S(2)}) %all-to-all-start.1) | async-done | bytes 786464 | tf_op jit(solution)/shard_map/all_to_all | solution.py:549
  59.4 1.2 fusion
  60.6 48.4 %collective-permute-done.2.k3.v3 = bf16[2,256,768]{2,1,0:T(8,128)(2,1)} collective-permute-done((bf16[2,256,768]{2,1,0:T(8,128)(2,1)}, bf16[2,256,768]{2,1,0:T(8,128)(2,1)}, u32[]{:S(2)}, u32[]{:S(2)}) %collective-permute-start.2) | collective-permute-done | bytes 786464 | tf_op jit(solution)/shard_map/ppermute | solution.py:40
  109.0 1.8 collective-permute-start.6
  110.9 0.7 pad_add_fusion.sp
  111.6 1.0 copy-done.1
  112.6 8.4 %shard_map.106 = (bf16[2,256,768]{2,1,0:T(8,128)(2,1)}, f32[6,8,512]{2,1,0:T(8,128)}) custom-call(s32[2,6]{1,0:T(2,128)} %pad_add_fusion.sp, bf16[2,256,4608]{2,1,0:T(8,128)(2,1)} %v0.7, bf16[2,256,4608]{2,1,0:T(8,128)(2,1)} %v0.7, bf16[2,256,4608]{2,1,0:T(8,128)(2,1)} %v0.7, bf16[3,256,768]{2,1,0:T(8,128)(2,1)} %copy-done.1, ...), custom_call_target="tpu_custom_call" | custom-call | flops 1610612736 | bytes 5000000 | tf_op jit(solution)/shard_map/pallas_call | solution.py:179
  121.0 6.1 %all-to-all-start.2 = ((bf16[32,16,768]{2,1,0:T(8,128)(2,1)}), bf16[32,16,768]{2,1,0:T(8,128)(2,1)S(1)}, u32[]{:S(2)}, u32[]{:S(2)}) async-start(bf16[32,16,768]{2,1,0:T(8,128)(2,1)} %bitcast.21), calls=%async_computation.2 | async-start | bytes 1572864 | tf_op jit(solution)/shard_map/all_to_all | solution.py:545
  127.8 12.1 %shard_map.107 = (f32[3,256,768]{2,1,0:T(8,128)}, bf16[3,256,768]{2,1,0:T(8,128)(2,1)}, bf16[2,256,768]{2,1,0:T(8,128)(2,1)}, bf16[2,256,768]{2,1,0:T(8,128)(2,1)}) custom-call(s32[2,6]{1,0:T(2,128)} %pad_add_fusion.sp, bf16[2,256,4608]{2,1,0:T(8,128)(2,1)} %v0.7, bf16[2,256,4608]{2,1,0:T(8,128)(2,1)} %v0.7, bf16[2,256,4608]{2,1,0:T(8,128)(2,1)} %v0.7, ...), custom_call_target="tpu_custom_call" | custom-call | flops 4026531840 | bytes 10000000 | tf_op jit(solution)/shard_map/pallas_call | solution.py:210
  139.9 0.9 copy-done.2
  140.8 1.0 copy-done
  141.8 8.4 %shard_map.108 = (bf16[2,256,768]{2,1,0:T(8,128)(2,1)}, f32[6,8,512]{2,1,0:T(8,128)}) custom-call(s32[2,6]{1,0:T(2,128)} %pad_add_fusion.sp, bf16[2,256,4608]{2,1,0:T(8,128)(2,1)} %v0.7, bf16[2,256,4608]{2,1,0:T(8,128)(2,1)} %v0.7, bf16[2,256,4608]{2,1,0:T(8,128)(2,1)} %v0.7, bf16[3,256,768]{2,1,0:T(8,128)(2,1)} %copy-done, bf16[3,256,768]{2,1,0:T(8,128)(2,1)} %copy-done, ...), custom_call_target="tpu_custom_call" | custom-call | flops 1610612736 | bytes 5000000 | tf_op jit(solution)/shard_map/pallas_call | solution.py:179
  150.3 0.9 copy-done.5
  151.2 2.9 pick.3
  154.1 7.6 %all-to-all-start.3 = ((bf16[32,16,768]{2,1,0:T(8,128)(2,1)}), bf16[32,16,768]{2,1,0:T(8,128)(2,1)S(1)}, u32[]{:S(2)}, u32[]{:S(2)}) async-start(bf16[32,16,768]{2,1,0:T(8,128)(2,1)} %pick.3), calls=%async_computation.3 | async-start | bytes 1572864 | tf_op jit(solution)/shard_map/all_to_all | solution.py:549
  161.7 1.3 collective-permute-start.9
  163.7 11.3 %all-to-all-done.3 = bf16[32,16,768]{2,1,0:T(8,128)(2,1)S(1)} async-done(((bf16[32,16,768]{2,1,0:T(8,128)(2,1)}), bf16[32,16,768]{2,1,0:T(8,128)(2,1)S(1)}, u32[]{:S(2)}, u32[]{:S(2)}) %all-to-all-start.3) | async-done | bytes 786464 | tf_op jit(solution)/shard_map/all_to_all | solution.py:549
  175.1 2.3 collective-permute-start.11
  177.5 0.6 copy-done.13
  178.2 3.3 %collective-permute-start.16 = (bf16[2,256,768]{2,1,0:T(8,128)(2,1)}, bf16[2,256,768]{2,1,0:T(8,128)(2,1)S(1)}, u32[]{:S(2)}, u32[]{:S(2)}) collective-permute-start(bf16[2,256,768]{2,1,0:T(8,128)(2,1)} %get-tuple-element.78), channel_id=1, source_target_pairs={{0,2},{1,3},{2,0},{3,1},{4,6},{5,7},{6,4},{7,5},{8,10},{9,11},{10,... | collective-permute-start | bytes 2359304 | tf_op jit(solution)/shard_map/ppermute | solution.py:40
  181.7 12.0 %shard_map.109 = (f32[3,256,768]{2,1,0:T(8,128)}, bf16[3,256,768]{2,1,0:T(8,128)(2,1)}, bf16[2,256,768]{2,1,0:T(8,128)(2,1)}, bf16[2,256,768]{2,1,0:T(8,128)(2,1)}) custom-call(s32[2,6]{1,0:T(2,128)} %pad_add_fusion.sp, bf16[2,256,4608]{2,1,0:T(8,128)(2,1)} %v0.7, bf16[2,256,4608]{2,1,0:T(8,128)(2,1)} %v0.7, bf16[2,256,4608]{2,1,0:T(8,128)(2,1)} %v0.7, ...), custom_call_target="tpu_custom_call" | custom-call | flops 4026531840 | bytes 10000000 | tf_op jit(solution)/shard_map/pallas_call | solution.py:210
  193.8 13.4 %weigh.1 = (bf16[384,768]{1,0:T(8,128)(2,1)}, bf16[384,768]{1,0:T(8,128)(2,1)}, bf16[384,768]{1,0:T(8,128)(2,1)}, bf16[384,768]{1,0:T(8,128)(2,1)}, bf16[4,96,76...) custom-call(s32[2,6]{1,0:T(2,128)} %pad_add_fusion.sp, ...), custom_call_target="tpu_custom_call" | custom-call | flops 4831838208 | bytes 12000000 | tf_op jit(solution)/shard_map/weigh/pallas_call | solution.py:421
  207.1 1.7 collective-permute-start.19
  208.9 7.6 %collective-permute-done.17.p3 = bf16[2,256,768]{2,1,0:T(8,128)(2,1)} collective-permute-done((bf16[2,256,768]{2,1,0:T(8,128)(2,1)}, bf16[2,256,768]{2,1,0:T(8,128)(2,1)}, u32[]{:S(2)}, u32[]{:S(2)}) %collective-permute-start.17) | collective-permute-done | bytes 786464 | tf_op jit(solution)/shard_map/ppermute | solution.py:40
  217.3 0.7 copy-done.11
  218.0 0.7 collective-permute-start.24
  218.7 3.2 collective-permute-done.18.refs_1_
  221.9 0.8 copy-done.12
  222.7 4.7 %collective-permute-start.26 = (bf16[2,256,768]{2,1,0:T(8,128)(2,1)}, bf16[2,256,768]{2,1,0:T(8,128)(2,1)S(1)}, u32[]{:S(2)}, u32[]{:S(2)}) collective-permute-start(bf16[2,256,768]{2,1,0:T(8,128)(2,1)} %get-tuple-element.113), channel_id=1, source_target_pairs={{0,3},{1,2},{2,1},{3,0},{4,7},{5,6},{6,5},{7,4},{8,11},{9,10},{10,... | collective-permute-start | bytes 2359304 | tf_op jit(solution)/shard_map/ppermute | solution.py:40
  227.4 7.4 %collective-permute-done.19.refs_2_ = bf16[384,768]{1,0:T(8,128)(2,1)} collective-permute-done((bf16[384,768]{1,0:T(8,128)(2,1)}, bf16[384,768]{1,0:T(8,128)(2,1)}, u32[]{:S(2)}, u32[]{:S(2)}) %collective-permute-start.19) | collective-permute-done | bytes 589856 | tf_op jit(solution)/shard_map/ppermute | solution.py:439
  234.8 3.2 %collective-permute-start.25 = (bf16[2,256,768]{2,1,0:T(8,128)(2,1)}, bf16[2,256,768]{2,1,0:T(8,128)(2,1)}, u32[]{:S(2)}, u32[]{:S(2)}) collective-permute-start(bf16[2,256,768]{2,1,0:T(8,128)(2,1)} %get-tuple-element.87), channel_id=1, source_target_pairs={{0,2},{1,3},{2,0},{3,1},{4,6},{5,7},{6,4},{7,5},{8,10},{9,11},{10,... | collective-permute-start | bytes 2359304 | tf_op jit(solution)/shard_map/ppermute | solution.py:40
  238.1 7.1 %collective-permute-done.20.refs_3_ = bf16[384,768]{1,0:T(8,128)(2,1)} collective-permute-done((bf16[384,768]{1,0:T(8,128)(2,1)}, bf16[384,768]{1,0:T(8,128)(2,1)}, u32[]{:S(2)}, u32[]{:S(2)}) %collective-permute-start.20) | collective-permute-done | bytes 589856 | tf_op jit(solution)/shard_map/ppermute | solution.py:439
  245.8 2.1 collective-permute-start.23
  247.9 11.0 %project.1 = (bf16[2,256,3072]{2,1,0:T(8,128)(2,1)}, f32[2,3072]{1,0:T(2,128)}) custom-call(s32[2,6]{1,0:T(2,128)} %pad_add_fusion.sp, bf16[2,256,768]{2,1,0:T(8,128)(2,1)} %get-tuple-element.86.att.a0, bf16[2,256,768]{2,1,0:T(8,128)(2,1)} %bitcast.25, bf16[2,256,768]{2,1,0:T(8,128)(2,1)} %collective-permute-done.10.b0, ...), custom_call_target="tpu_custom_call" | custom-call | flops 4831838208 | bytes 16000000 | tf_op jit(solution)/shard_map/project/pallas_call | solution.py:371
  258.9 5.7 %shard_map.110.rest_0_ = bf16[2,256,4608]{2,1,0:T(8,128)(2,1)} custom-call(s32[2,6]{1,0:T(2,128)} %pad_add_fusion.sp, f32[3,256,768]{2,1,0:T(8,128)} %get-tuple-element.98.own, bf16[3,256,768]{2,1,0:T(8,128)(2,1)} %copy-done.9, bf16[2,256,768]{2,1,0:T(8,128)(2,1)} %copy-done.11, bf16[2,256,768]{2,1,0:T(8,128)(2,1)} %collective-permute-done.17.p3), custom_call_target="tpu_custom_call" | custom-call | flops 1000000 | bytes 10000000 | tf_op jit(solution)/shard_map/pallas_call | solution.py:257
  264.6 10.3 %collective-permute-done.23.refs_7_ = bf16[4,96,768]{2,1,0:T(8,128)(2,1)} collective-permute-done((bf16[4,96,768]{2,1,0:T(8,128)(2,1)}, bf16[4,96,768]{2,1,0:T(8,128)(2,1)}, u32[]{:S(2)}, u32[]{:S(2)}) %collective-permute-start.23) | collective-permute-done | bytes 589856 | tf_op jit(solution)/shard_map/ppermute | solution.py:443
  274.9 4.2 %sum_parts.1 = (bf16[96,768]{1,0:T(8,128)(2,1)}, bf16[96,768]{1,0:T(8,128)(2,1)}, bf16[96,768]{1,0:T(8,128)(2,1)}, bf16[96,768]{1,0:T(8,128)(2,1)}, bf16[96,768]...) custom-call(s32[2,6]{1,0:T(2,128)} %pad_add_fusion.sp, ...), custom_call_target="tpu_custom_call" | custom-call | flops 5000000 | bytes 6000000 | tf_op jit(solution)/shard_map/sum_parts/pallas_call | solution.py:470
  279.2 1.4 collective-permute-start.28
  280.6 2.5 collective-permute-start.29
  283.0 1.7 collective-permute-start.31
  284.8 2.1 collective-permute-start.32
  287.4 4.7 %collective-permute-start.14 = (f32[2,3072]{1,0:T(2,128)S(1)}, f32[2,3072]{1,0:T(2,128)S(1)}, u32[]{:S(2)}, u32[]{:S(2)}) collective-permute-start(f32[2,3072]{1,0:T(2,128)S(1)} %copy-done.20), channel_id=1, source_target_pairs={{0,3},{1,2},{2,1},{3,0},{4,7},{5,6},{6,5},{7,4},{8,11},{9,10},{10,... | collective-permute-start | bytes 73736 | tf_op jit(solution)/shard_map/ppermute | solution.py:40
  292.1 0.9 collective-permute-start.13
  293.1 1.5 collective-permute-start.12
  294.6 5.7 %shard_map.111 = bf16[2,256,4608]{2,1,0:T(8,128)(2,1)} custom-call(s32[2,6]{1,0:T(2,128)} %pad_add_fusion.sp, f32[3,256,768]{2,1,0:T(8,128)} %get-tuple-element.111.own, bf16[3,256,768]{2,1,0:T(8,128)(2,1)} %copy-done.8, bf16[2,256,768]{2,1,0:T(8,128)(2,1)} %collective-permute-done.25.p2, ...), custom_call_target="tpu_custom_call", output_to_operand_aliasing={{}: (5, {})} | custom-call | flops 1000000 | bytes 10000000 | tf_op jit(solution)/shard_map/pallas_call | solution.py:257
  301.0 3.0 sum_weights.1
  304.0 1.9 collective-permute-start.33
  305.9 2.3 collective-permute-start.34
  308.2 4.3 %collective-permute-start.35 = (bf16[24,1536]{1,0:T(8,128)(2,1)}, bf16[24,1536]{1,0:T(8,128)(2,1)S(1)}, u32[]{:S(2)}, u32[]{:S(2)}) collective-permute-start(bf16[24,1536]{1,0:T(8,128)(2,1)} %get-tuple-element.124), channel_id=1, source_target_pairs={{0,2},{1,66},{2,3},{3,67},{4,0},{5,64},{6,1},{7,65},{8,6},{9,70},{... | collective-permute-start | bytes 221192 | tf_op jit(solution)/shard_map/ppermute | solution.py:532
  312.5 2.7 collective-permute-start.36
  315.9 2.5 collective-permute-done.36
  318.4 0.7 add_bitcast_fusion
  (97 shorter events, 6.0 us)
Async XLA Ops:
  12.1 22.6 %all-to-all-start = ((bf16[32,8,1536]{2,1,0:T(8,128)(2,1)}), bf16[32,8,1536]{2,1,0:T(8,128)(2,1)S(1)}, u32[]{:S(2)}, u32[]{:S(2)}) async-start(bf16[32,8,1536]{2,1,0:T(8,128)(2,1)} %bitcast.26), calls=%async_computation | async-start | bytes 1572864 | tf_op jit(solution)/shard_map/all_to_all | solution.py:545
  21.3 90.3 %collective-permute-start = (bf16[3,256,768]{2,1,0:T(8,128)(2,1)}, bf16[3,256,768]{2,1,0:T(8,128)(2,1)S(1)}, u32[]{:S(2)}, u32[]{:S(2)}) collective-permute-start(bf16[3,256,768]{2,1,0:T(8,128)(2,1)} %get-tuple-element.74), channel_id=1, source_target_pairs={{0,1},{1,0},{2,3},{3,2},{4,5},{5,4},{6,7},{7,6},{8,9},{9,8},{10,11... | collective-permute-start | bytes 3538952 | tf_op jit(solution)/shard_map/ppermute | solution.py:40
  33.7 19.1 %copy-start.22 = (s32[64]{0:T(128)S(1)}, s32[64]{0:T(128)}, u32[]{:S(2)}) copy-start(s32[64]{0:T(128)} %param.11) | copy-start | bytes 772
  33.7 19.2 %copy-start.23 = (s32[64]{0:T(128)S(1)}, s32[64]{0:T(128)}, u32[]{:S(2)}) copy-start(s32[64]{0:T(128)} %param.12) | copy-start | bytes 772
  34.8 0.9 copy-start.6
  38.5 20.9 %all-to-all-start.1 = ((bf16[32,8,1536]{2,1,0:T(8,128)(2,1)}), bf16[32,8,1536]{2,1,0:T(8,128)(2,1)}, u32[]{:S(2)}, u32[]{:S(2)}) async-start(bf16[32,8,1536]{2,1,0:T(8,128)(2,1)} %pick.2), calls=%async_computation.1 | async-start | bytes 1572864 | tf_op jit(solution)/shard_map/all_to_all | solution.py:549
  45.6 65.2 %collective-permute-start.1 = (bf16[2,256,768]{2,1,0:T(8,128)(2,1)}, bf16[2,256,768]{2,1,0:T(8,128)(2,1)}, u32[]{:S(2)}, u32[]{:S(2)}) collective-permute-start(bf16[2,256,768]{2,1,0:T(8,128)(2,1)} %get-tuple-element.65), channel_id=1, source_target_pairs={{0,2},{1,3},{2,0},{3,1},{4,6},{5,7},{6,4},{7,5},{8,10},{9,11},{10,... | collective-permute-start | bytes 2359304 | tf_op jit(solution)/shard_map/ppermute | solution.py:40
  49.0 90.9 %collective-permute-start.5 = (bf16[2,256,768]{2,1,0:T(8,128)(2,1)}, bf16[2,256,768]{2,1,0:T(8,128)(2,1)S(1)}, u32[]{:S(2)}, u32[]{:S(2)}) collective-permute-start(bf16[2,256,768]{2,1,0:T(8,128)(2,1)} %get-tuple-element.69), channel_id=1, source_target_pairs={{0,2},{1,3},{2,0},{3,1},{4,6},{5,7},{6,4},{7,5},{8,10},{9,11},{10,... | collective-permute-start | bytes 2359304 | tf_op jit(solution)/shard_map/ppermute | solution.py:40
  49.1 59.9 %collective-permute-start.2 = (bf16[2,256,768]{2,1,0:T(8,128)(2,1)}, bf16[2,256,768]{2,1,0:T(8,128)(2,1)}, u32[]{:S(2)}, u32[]{:S(2)}) collective-permute-start(bf16[2,256,768]{2,1,0:T(8,128)(2,1)} %get-tuple-element.75), channel_id=1, source_target_pairs={{0,3},{1,2},{2,1},{3,0},{4,7},{5,6},{6,5},{7,4},{8,11},{9,10},{10,... | collective-permute-start | bytes 2359304 | tf_op jit(solution)/shard_map/ppermute | solution.py:40
  52.7 87.2 %collective-permute-start.4 = (bf16[3,256,768]{2,1,0:T(8,128)(2,1)}, bf16[3,256,768]{2,1,0:T(8,128)(2,1)S(1)}, u32[]{:S(2)}, u32[]{:S(2)}) collective-permute-start(bf16[3,256,768]{2,1,0:T(8,128)(2,1)} %get-tuple-element.80), channel_id=1, source_target_pairs={{0,1},{1,0},{2,3},{3,2},{4,5},{5,4},{6,7},{7,6},{8,9},{9,8},{10,11... | collective-permute-start | bytes 3538952 | tf_op jit(solution)/shard_map/ppermute | solution.py:40
  109.0 30.9 %collective-permute-start.6 = (bf16[2,256,768]{2,1,0:T(8,128)(2,1)}, bf16[2,256,768]{2,1,0:T(8,128)(2,1)}, u32[]{:S(2)}, u32[]{:S(2)}) collective-permute-start(bf16[2,256,768]{2,1,0:T(8,128)(2,1)} %get-tuple-element.81), channel_id=1, source_target_pairs={{0,3},{1,2},{2,1},{3,0},{4,7},{5,6},{6,5},{7,4},{8,11},{9,10},{10,... | collective-permute-start | bytes 2359304 | tf_op jit(solution)/shard_map/ppermute | solution.py:40
  110.8 17.0 %collective-permute-start.3 = (bf16[1,256,768]{2,1,0:T(8,128)(2,1)S(1)}, bf16[1,256,768]{2,1,0:T(8,128)(2,1)}, u32[]{:S(2)}, u32[]{:S(2)}) collective-permute-start(bf16[1,256,768]{2,1,0:T(8,128)(2,1)S(1)} %fusion), channel_id=1, source_target_pairs={{0,1},{1,0},{2,3},{3,2},{4,5},{5,4},{6,7},{7,6},{8,9},{9,8},{10,11... | collective-permute-start | bytes 1179656 | tf_op jit(solution)/shard_map/ppermute | solution.py:40
  111.6 15.6 %copy-start.21 = (s32[32]{0:T(128)S(1)}, s32[32]{0:T(128)}, u32[]{:S(2)}) copy-start(s32[32]{0:T(128)} %order) | copy-start | bytes 388
  111.6 1.0 copy-start.1
  121.0 29.2 %all-to-all-start.2 = ((bf16[32,16,768]{2,1,0:T(8,128)(2,1)}), bf16[32,16,768]{2,1,0:T(8,128)(2,1)S(1)}, u32[]{:S(2)}, u32[]{:S(2)}) async-start(bf16[32,16,768]{2,1,0:T(8,128)(2,1)} %bitcast.21), calls=%async_computation.2 | async-start | bytes 1572864 | tf_op jit(solution)/shard_map/all_to_all | solution.py:545
  139.9 0.9 copy-start.2
  140.8 1.0 copy-start
  150.2 12.8 %copy-start.3 = (bf16[256,1536]{1,0:T(8,128)(2,1)S(1)}, bf16[256,1536]{1,0:T(8,128)(2,1)}, u32[]{:S(2)}) copy-start(bf16[256,1536]{1,0:T(8,128)(2,1)} %get-tuple-element.71) | copy-start | bytes 2359300
  150.3 13.4 %copy-start.4 = (bf16[2,256,768]{2,1,0:T(8,128)(2,1)S(1)}, bf16[2,256,768]{2,1,0:T(8,128)(2,1)}, u32[]{:S(2)}) copy-start(bf16[2,256,768]{2,1,0:T(8,128)(2,1)} %get-tuple-element.86.att.a0) | copy-start | bytes 2359300
  150.3 0.9 copy-start.5
  154.1 21.0 %all-to-all-start.3 = ((bf16[32,16,768]{2,1,0:T(8,128)(2,1)}), bf16[32,16,768]{2,1,0:T(8,128)(2,1)S(1)}, u32[]{:S(2)}, u32[]{:S(2)}) async-start(bf16[32,16,768]{2,1,0:T(8,128)(2,1)} %pick.3), calls=%async_computation.3 | async-start | bytes 1572864 | tf_op jit(solution)/shard_map/all_to_all | solution.py:549
  161.7 16.5 %collective-permute-start.9 = (bf16[256,1536]{1,0:T(8,128)(2,1)}, bf16[256,1536]{1,0:T(8,128)(2,1)}, u32[]{:S(2)}, u32[]{:S(2)}) collective-permute-start(bf16[256,1536]{1,0:T(8,128)(2,1)} %get-tuple-element.92), channel_id=1, source_target_pairs={{0,1},{1,0},{2,3},{3,2},{4,5},{5,4},{6,7},{7,6},{8,9},{9,8},{10,11... | collective-permute-start | bytes 2359304 | tf_op jit(solution)/shard_map/ppermute | solution.py:40
  163.0 18.5 %collective-permute-start.8 = (bf16[256,1536]{1,0:T(8,128)(2,1)}, bf16[256,1536]{1,0:T(8,128)(2,1)}, u32[]{:S(2)}, u32[]{:S(2)}) collective-permute-start(bf16[256,1536]{1,0:T(8,128)(2,1)} %get-tuple-element.90), channel_id=1, source_target_pairs={{0,1},{1,0},{2,3},{3,2},{4,5},{5,4},{6,7},{7,6},{8,9},{9,8},{10,11... | collective-permute-start | bytes 2359304 | tf_op jit(solution)/shard_map/ppermute | solution.py:40
  163.1 14.3 %collective-permute-start.7 = (bf16[1,256,768]{2,1,0:T(8,128)(2,1)S(1)}, bf16[1,256,768]{2,1,0:T(8,128)(2,1)S(1)}, u32[]{:S(2)}, u32[]{:S(2)}) collective-permute-start(bf16[1,256,768]{2,1,0:T(8,128)(2,1)S(1)} %select_bitcast_fusion), channel_id=1, source_target_pairs={{0,1},{1,0},{2,3},{3,2},{4,5},{5,4},{6,7},{7,6},{8,9},{9,8},{10,11... | collective-permute-start | bytes 1179656 | tf_op jit(solution)/shard_map/ppermute | solution.py:40
  163.6 30.1 %collective-permute-start.10 = (bf16[2,256,768]{2,1,0:T(8,128)(2,1)S(1)}, bf16[2,256,768]{2,1,0:T(8,128)(2,1)}, u32[]{:S(2)}, u32[]{:S(2)}) collective-permute-start(bf16[2,256,768]{2,1,0:T(8,128)(2,1)S(1)} %copy-done.4), channel_id=1, source_target_pairs={{0,1},{1,0},{2,3},{3,2},{4,5},{5,4},{6,7},{7,6},{8,9},{9,8},{10,11... | collective-permute-start | bytes 2359304 | tf_op jit(solution)/shard_map/ppermute | solution.py:40
  175.1 18.6 %copy-start.7 = (bf16[32,16,768]{2,1,0:T(8,128)(2,1)}, bf16[32,16,768]{2,1,0:T(8,128)(2,1)S(1)}, u32[]{:S(2)}) copy-start(bf16[32,16,768]{2,1,0:T(8,128)(2,1)S(1)} %all-to-all-done.3) | copy-start | bytes 2359300
  175.1 18.7 %collective-permute-start.11 = (bf16[2,256,768]{2,1,0:T(8,128)(2,1)S(1)}, bf16[2,256,768]{2,1,0:T(8,128)(2,1)}, u32[]{:S(2)}, u32[]{:S(2)}) collective-permute-start(bf16[2,256,768]{2,1,0:T(8,128)(2,1)S(1)} %bitcast.23), channel_id=1, source_target_pairs={{0,1},{1,0},{2,3},{3,2},{4,5},{5,4},{6,7},{7,6},{8,9},{9,8},{10,11... | collective-permute-start | bytes 2359304 | tf_op jit(solution)/shard_map/ppermute | solution.py:40
  177.4 0.7 copy-start.13
  177.4 39.9 %collective-permute-start.15 = (bf16[3,256,768]{2,1,0:T(8,128)(2,1)}, bf16[3,256,768]{2,1,0:T(8,128)(2,1)S(1)}, u32[]{:S(2)}, u32[]{:S(2)}) collective-permute-start(bf16[3,256,768]{2,1,0:T(8,128)(2,1)} %get-tuple-element.99), channel_id=1, source_target_pairs={{0,1},{1,0},{2,3},{3,2},{4,5},{5,4},{6,7},{7,6},{8,9},{9,8},{10,11... | collective-permute-start | bytes 3538952 | tf_op jit(solution)/shard_map/ppermute | solution.py:40
  178.2 39.0 %collective-permute-start.16 = (bf16[2,256,768]{2,1,0:T(8,128)(2,1)}, bf16[2,256,768]{2,1,0:T(8,128)(2,1)S(1)}, u32[]{:S(2)}, u32[]{:S(2)}) collective-permute-start(bf16[2,256,768]{2,1,0:T(8,128)(2,1)} %get-tuple-element.78), channel_id=1, source_target_pairs={{0,2},{1,3},{2,0},{3,1},{4,6},{5,7},{6,4},{7,5},{8,10},{9,11},{10,... | collective-permute-start | bytes 2359304 | tf_op jit(solution)/shard_map/ppermute | solution.py:40
  181.5 35.0 %collective-permute-start.17 = (bf16[2,256,768]{2,1,0:T(8,128)(2,1)}, bf16[2,256,768]{2,1,0:T(8,128)(2,1)}, u32[]{:S(2)}, u32[]{:S(2)}) collective-permute-start(bf16[2,256,768]{2,1,0:T(8,128)(2,1)} %get-tuple-element.100), channel_id=1, source_target_pairs={{0,3},{1,2},{2,1},{3,0},{4,7},{5,6},{6,5},{7,4},{8,11},{9,10},{10,... | collective-permute-start | bytes 2359304 | tf_op jit(solution)/shard_map/ppermute | solution.py:40
  207.1 14.7 %collective-permute-start.18 = (bf16[384,768]{1,0:T(8,128)(2,1)}, bf16[384,768]{1,0:T(8,128)(2,1)S(1)}, u32[]{:S(2)}, u32[]{:S(2)}) collective-permute-start(bf16[384,768]{1,0:T(8,128)(2,1)} %get-tuple-element.102), channel_id=1, source_target_pairs={{0,32},{4,36},{8,40},{12,44},{16,48},{20,52},{24,56},{28,60},{32,0... | collective-permute-start | bytes 1769480 | tf_op jit(solution)/shard_map/ppermute | solution.py:439
  207.1 27.7 %collective-permute-start.19 = (bf16[384,768]{1,0:T(8,128)(2,1)}, bf16[384,768]{1,0:T(8,128)(2,1)}, u32[]{:S(2)}, u32[]{:S(2)}) collective-permute-start(bf16[384,768]{1,0:T(8,128)(2,1)} %get-tuple-element.103), channel_id=1, source_target_pairs={{0,64},{4,68},{8,72},{12,76},{16,80},{20,84},{24,88},{28,92},{32,9... | collective-permute-start | bytes 1769480 | tf_op jit(solution)/shard_map/ppermute | solution.py:439
  216.5 28.7 %collective-permute-start.20 = (bf16[384,768]{1,0:T(8,128)(2,1)}, bf16[384,768]{1,0:T(8,128)(2,1)}, u32[]{:S(2)}, u32[]{:S(2)}) collective-permute-start(bf16[384,768]{1,0:T(8,128)(2,1)} %get-tuple-element.104), channel_id=1, source_target_pairs={{0,96},{4,100},{8,104},{12,108},{16,112},{20,116},{24,120},{28,124... | collective-permute-start | bytes 1769480 | tf_op jit(solution)/shard_map/ppermute | solution.py:439
  217.1 0.9 copy-start.11
  217.1 28.7 %collective-permute-start.21 = (bf16[4,96,768]{2,1,0:T(8,128)(2,1)}, bf16[4,96,768]{2,1,0:T(8,128)(2,1)}, u32[]{:S(2)}, u32[]{:S(2)}) collective-permute-start(bf16[4,96,768]{2,1,0:T(8,128)(2,1)} %get-tuple-element.106), channel_id=1, source_target_pairs={{0,8},{4,12},{8,0},{12,4},{16,24},{20,28},{24,16},{28,20},{32,40},... | collective-permute-start | bytes 1769480 | tf_op jit(solution)/shard_map/ppermute | solution.py:443
  218.0 40.9 %copy-start.9 = (bf16[3,256,768]{2,1,0:T(8,128)(2,1)}, bf16[3,256,768]{2,1,0:T(8,128)(2,1)S(1)}, u32[]{:S(2)}) copy-start(bf16[3,256,768]{2,1,0:T(8,128)(2,1)S(1)} %collective-permute-done.15.p1) | copy-start | bytes 3538948
  218.0 65.0 %collective-permute-start.24 = (bf16[3,256,768]{2,1,0:T(8,128)(2,1)}, bf16[3,256,768]{2,1,0:T(8,128)(2,1)S(1)}, u32[]{:S(2)}, u32[]{:S(2)}) collective-permute-start(bf16[3,256,768]{2,1,0:T(8,128)(2,1)} %get-tuple-element.112), channel_id=1, source_target_pairs={{0,1},{1,0},{2,3},{3,2},{4,5},{5,4},{6,7},{7,6},{8,9},{9,8},{10,11... | collective-permute-start | bytes 3538952 | tf_op jit(solution)/shard_map/ppermute | solution.py:40
  221.9 0.8 copy-start.12
  222.7 57.9 %collective-permute-start.26 = (bf16[2,256,768]{2,1,0:T(8,128)(2,1)}, bf16[2,256,768]{2,1,0:T(8,128)(2,1)S(1)}, u32[]{:S(2)}, u32[]{:S(2)}) collective-permute-start(bf16[2,256,768]{2,1,0:T(8,128)(2,1)} %get-tuple-element.113), channel_id=1, source_target_pairs={{0,3},{1,2},{2,1},{3,0},{4,7},{5,6},{6,5},{7,4},{8,11},{9,10},{10,... | collective-permute-start | bytes 2359304 | tf_op jit(solution)/shard_map/ppermute | solution.py:40
  234.8 48.2 %collective-permute-start.25 = (bf16[2,256,768]{2,1,0:T(8,128)(2,1)}, bf16[2,256,768]{2,1,0:T(8,128)(2,1)}, u32[]{:S(2)}, u32[]{:S(2)}) collective-permute-start(bf16[2,256,768]{2,1,0:T(8,128)(2,1)} %get-tuple-element.87), channel_id=1, source_target_pairs={{0,2},{1,3},{2,0},{3,1},{4,6},{5,7},{6,4},{7,5},{8,10},{9,11},{10,... | collective-permute-start | bytes 2359304 | tf_op jit(solution)/shard_map/ppermute | solution.py:40
  245.2 19.4 %collective-permute-start.22 = (bf16[4,96,768]{2,1,0:T(8,128)(2,1)}, bf16[4,96,768]{2,1,0:T(8,128)(2,1)}, u32[]{:S(2)}, u32[]{:S(2)}) collective-permute-start(bf16[4,96,768]{2,1,0:T(8,128)(2,1)} %get-tuple-element.107), channel_id=1, source_target_pairs={{0,16},{4,20},{8,24},{12,28},{16,0},{20,4},{24,8},{28,12},{32,48},... | collective-permute-start | bytes 1769480 | tf_op jit(solution)/shard_map/ppermute | solution.py:443
  245.8 29.1 %collective-permute-start.23 = (bf16[4,96,768]{2,1,0:T(8,128)(2,1)}, bf16[4,96,768]{2,1,0:T(8,128)(2,1)}, u32[]{:S(2)}, u32[]{:S(2)}) collective-permute-start(bf16[4,96,768]{2,1,0:T(8,128)(2,1)} %get-tuple-element.108), channel_id=1, source_target_pairs={{0,24},{4,28},{8,16},{12,20},{16,8},{20,12},{24,0},{28,4},{32,56},... | collective-permute-start | bytes 1769480 | tf_op jit(solution)/shard_map/ppermute | solution.py:443
  274.9 12.5 %copy-start.20 = (f32[2,3072]{1,0:T(2,128)S(1)}, f32[2,3072]{1,0:T(2,128)}, u32[]{:S(2)}) copy-start(f32[2,3072]{1,0:T(2,128)} %get-tuple-element.96) | copy-start | bytes 73732
  279.1 5.7 %collective-permute-start.27 = (bf16[96,768]{1,0:T(8,128)(2,1)}, bf16[96,768]{1,0:T(8,128)(2,1)S(1)}, u32[]{:S(2)}, u32[]{:S(2)}) collective-permute-start(bf16[96,768]{1,0:T(8,128)(2,1)} %get-tuple-element.115), channel_id=1, source_target_pairs={{0,8},{4,12},{8,0},{12,4},{16,24},{20,28},{24,16},{28,20},{32,40},... | collective-permute-start | bytes 442376 | tf_op jit(solution)/shard_map/ppermute | solution.py:443
  279.2 8.2 %collective-permute-start.28 = (bf16[96,768]{1,0:T(8,128)(2,1)}, bf16[96,768]{1,0:T(8,128)(2,1)S(1)}, u32[]{:S(2)}, u32[]{:S(2)}) collective-permute-start(bf16[96,768]{1,0:T(8,128)(2,1)} %get-tuple-element.116), channel_id=1, source_target_pairs={{0,16},{4,20},{8,24},{12,28},{16,0},{20,4},{24,8},{28,12},{32,48},... | collective-permute-start | bytes 442376 | tf_op jit(solution)/shard_map/ppermute | solution.py:443
  280.6 14.0 %copy-start.10 = (bf16[2,256,768]{2,1,0:T(8,128)(2,1)}, bf16[2,256,768]{2,1,0:T(8,128)(2,1)S(1)}, u32[]{:S(2)}) copy-start(bf16[2,256,768]{2,1,0:T(8,128)(2,1)S(1)} %collective-permute-done.26.p3) | copy-start | bytes 2359300
  280.6 11.6 %collective-permute-start.29 = (bf16[96,768]{1,0:T(8,128)(2,1)}, bf16[96,768]{1,0:T(8,128)(2,1)S(1)}, u32[]{:S(2)}, u32[]{:S(2)}) collective-permute-start(bf16[96,768]{1,0:T(8,128)(2,1)} %get-tuple-element.117), channel_id=1, source_target_pairs={{0,24},{4,28},{8,16},{12,20},{16,8},{20,12},{24,0},{28,4},{32,56},... | collective-permute-start | bytes 442376 | tf_op jit(solution)/shard_map/ppermute | solution.py:443
  283.0 10.1 %collective-permute-start.30 = (bf16[96,768]{1,0:T(8,128)(2,1)}, bf16[96,768]{1,0:T(8,128)(2,1)S(1)}, u32[]{:S(2)}, u32[]{:S(2)}) collective-permute-start(bf16[96,768]{1,0:T(8,128)(2,1)} %get-tuple-element.119), channel_id=1, source_target_pairs={{0,32},{4,36},{8,40},{12,44},{16,48},{20,52},{24,56},{28,60},{32,0... | collective-permute-start | bytes 442376 | tf_op jit(solution)/shard_map/ppermute | solution.py:439
  283.0 11.5 %copy-start.8 = (bf16[3,256,768]{2,1,0:T(8,128)(2,1)}, bf16[3,256,768]{2,1,0:T(8,128)(2,1)S(1)}, u32[]{:S(2)}) copy-start(bf16[3,256,768]{2,1,0:T(8,128)(2,1)S(1)} %collective-permute-done.24.p1) | copy-start | bytes 3538948
  283.0 17.2 %collective-permute-start.31 = (bf16[96,768]{1,0:T(8,128)(2,1)}, bf16[96,768]{1,0:T(8,128)(2,1)S(1)}, u32[]{:S(2)}, u32[]{:S(2)}) collective-permute-start(bf16[96,768]{1,0:T(8,128)(2,1)} %get-tuple-element.120), channel_id=1, source_target_pairs={{0,64},{4,68},{8,72},{12,76},{16,80},{20,84},{24,88},{28,92},{32,9... | collective-permute-start | bytes 442376 | tf_op jit(solution)/shard_map/ppermute | solution.py:439
  284.8 15.4 %copy-start.14 = (bf16[96,768]{1,0:T(8,128)(2,1)}, bf16[96,768]{1,0:T(8,128)(2,1)S(1)}, u32[]{:S(2)}) copy-start(bf16[96,768]{1,0:T(8,128)(2,1)S(1)} %collective-permute-done.27.refs_1_) | copy-start | bytes 442372
  284.8 15.5 %collective-permute-start.32 = (bf16[96,768]{1,0:T(8,128)(2,1)}, bf16[96,768]{1,0:T(8,128)(2,1)S(1)}, u32[]{:S(2)}, u32[]{:S(2)}) collective-permute-start(bf16[96,768]{1,0:T(8,128)(2,1)} %get-tuple-element.121), channel_id=1, source_target_pairs={{0,96},{4,100},{8,104},{12,108},{16,112},{20,116},{24,120},{28,124... | collective-permute-start | bytes 442376 | tf_op jit(solution)/shard_map/ppermute | solution.py:439
  287.4 12.8 %copy-start.15 = (bf16[96,768]{1,0:T(8,128)(2,1)}, bf16[96,768]{1,0:T(8,128)(2,1)S(1)}, u32[]{:S(2)}) copy-start(bf16[96,768]{1,0:T(8,128)(2,1)S(1)} %collective-permute-done.28.refs_2_) | copy-start | bytes 442372
  287.4 20.8 %collective-permute-start.14 = (f32[2,3072]{1,0:T(2,128)S(1)}, f32[2,3072]{1,0:T(2,128)S(1)}, u32[]{:S(2)}, u32[]{:S(2)}) collective-permute-start(f32[2,3072]{1,0:T(2,128)S(1)} %copy-done.20), channel_id=1, source_target_pairs={{0,3},{1,2},{2,1},{3,0},{4,7},{5,6},{6,5},{7,4},{8,11},{9,10},{10,... | collective-permute-start | bytes 73736 | tf_op jit(solution)/shard_map/ppermute | solution.py:40
  292.1 8.1 %copy-start.16 = (bf16[96,768]{1,0:T(8,128)(2,1)}, bf16[96,768]{1,0:T(8,128)(2,1)S(1)}, u32[]{:S(2)}) copy-start(bf16[96,768]{1,0:T(8,128)(2,1)S(1)} %collective-permute-done.29.refs_3_) | copy-start | bytes 442372
  292.1 20.4 %collective-permute-start.13 = (f32[2,3072]{1,0:T(2,128)S(1)}, f32[2,3072]{1,0:T(2,128)S(1)}, u32[]{:S(2)}, u32[]{:S(2)}) collective-permute-start(f32[2,3072]{1,0:T(2,128)S(1)} %copy-done.20), channel_id=1, source_target_pairs={{0,2},{1,3},{2,0},{3,1},{4,6},{5,7},{6,4},{7,5},{8,10},{9,11},{10,... | collective-permute-start | bytes 73736 | tf_op jit(solution)/shard_map/ppermute | solution.py:40
  293.1 7.2 %copy-start.17 = (bf16[96,768]{1,0:T(8,128)(2,1)}, bf16[96,768]{1,0:T(8,128)(2,1)S(1)}, u32[]{:S(2)}) copy-start(bf16[96,768]{1,0:T(8,128)(2,1)S(1)} %collective-permute-done.30.refs_5_) | copy-start | bytes 442372
  293.1 22.1 %collective-permute-start.12 = (f32[2,3072]{1,0:T(2,128)S(1)}, f32[2,3072]{1,0:T(2,128)S(1)}, u32[]{:S(2)}, u32[]{:S(2)}) collective-permute-start(f32[2,3072]{1,0:T(2,128)S(1)} %copy-done.20), channel_id=1, source_target_pairs={{0,1},{1,0},{2,3},{3,2},{4,5},{5,4},{6,7},{7,6},{8,9},{9,8},{10,11... | collective-permute-start | bytes 73736 | tf_op jit(solution)/shard_map/ppermute | solution.py:40
  300.3 0.7 copy-start.19
  304.0 11.9 %collective-permute-start.33 = (bf16[24,1536]{1,0:T(8,128)(2,1)}, bf16[24,1536]{1,0:T(8,128)(2,1)S(1)}, u32[]{:S(2)}, u32[]{:S(2)}) collective-permute-start(bf16[24,1536]{1,0:T(8,128)(2,1)} %get-tuple-element.122), channel_id=1, source_target_pairs={{0,0},{1,64},{2,1},{3,65},{4,2},{5,66},{6,3},{7,67},{8,4},{9,68},{... | collective-permute-start | bytes 221192 | tf_op jit(solution)/shard_map/ppermute | solution.py:532
  305.9 9.9 %collective-permute-start.34 = (bf16[24,1536]{1,0:T(8,128)(2,1)}, bf16[24,1536]{1,0:T(8,128)(2,1)S(1)}, u32[]{:S(2)}, u32[]{:S(2)}) collective-permute-start(bf16[24,1536]{1,0:T(8,128)(2,1)} %get-tuple-element.123), channel_id=1, source_target_pairs={{0,1},{1,65},{2,0},{3,64},{4,3},{5,67},{6,2},{7,66},{8,5},{9,69},{... | collective-permute-start | bytes 221192 | tf_op jit(solution)/shard_map/ppermute | solution.py:532
  308.2 7.6 %collective-permute-start.35 = (bf16[24,1536]{1,0:T(8,128)(2,1)}, bf16[24,1536]{1,0:T(8,128)(2,1)S(1)}, u32[]{:S(2)}, u32[]{:S(2)}) collective-permute-start(bf16[24,1536]{1,0:T(8,128)(2,1)} %get-tuple-element.124), channel_id=1, source_target_pairs={{0,2},{1,66},{2,3},{3,67},{4,0},{5,64},{6,1},{7,65},{8,6},{9,70},{... | collective-permute-start | bytes 221192 | tf_op jit(solution)/shard_map/ppermute | solution.py:532
  312.5 5.9 %collective-permute-start.36 = (bf16[24,1536]{1,0:T(8,128)(2,1)}, bf16[24,1536]{1,0:T(8,128)(2,1)S(1)}, u32[]{:S(2)}, u32[]{:S(2)}) collective-permute-start(bf16[24,1536]{1,0:T(8,128)(2,1)} %get-tuple-element.125), channel_id=1, source_target_pairs={{0,3},{1,67},{2,2},{3,66},{4,1},{5,65},{6,0},{7,64},{8,7},{9,71},{... | collective-permute-start | bytes 221192 | tf_op jit(solution)/shard_map/ppermute | solution.py:532
  (1 other events, 0.7 us)

commit v5 on v4

--- a/solution.py
+++ b/solution.py
@@ -217,7 +217,7 @@
                 piece(2),
                 pl.BlockSpec((heads, 8, 2 * ROWS), lambda h, sp: (h, 0, 0)),
                 d_own_spec,
-                piece(1),
+                d_own_spec,
             ],
             out_specs=[piece(3), piece(3), piece(2), piece(2)],
         ),
@@ -566,11 +566,9 @@
     place = jnp.stack([core, z_place]).astype(jnp.int32)[:, None]
     plane = jnp.stack([group_index >> 3, (group_index >> 1) & 3]).astype(jnp.int32)[:, None]
     sp = jnp.concatenate([place, limits.astype(jnp.int32), plane], axis=1)
-    first = core == 0
 
     def to_core(rows):
-        other = jnp.where(first, rows[:, HALF:], rows[:, :HALF])
-        return swap(other[None], 1)
+        return swap(rows[None], 1)
 
     received = [None, None]
     d_own, d_peer = [None, None], [None, None]
@@ -578,18 +576,18 @@
 
     cp = core.astype(jnp.int32).reshape(1, 1)
     s1, s2, s3 = prep(cp, qkv, 1)
-    received[1] = (swap(s1, 1), swap(s2, 2), swap(s3, 3))
+    near_keys = (swap(s1, 1), swap(s3, 3))
+    received[1] = (near_keys[0], swap(s2, 2), near_keys[1])
     send_1, keep_1, away = scaled_rows(after(cp, s2), 1, cotangent, gate, out_weight)
     d_spread = spread_out(away)
-    s1, s2, s3 = prep(after(cp, away), qkv, 0)
-    near_keys = (swap(s1, 1), swap(s3, 3))
-    received[0] = (near_keys[0], swap(s2, 2), near_keys[1])
-    send_0, keep_0, near = scaled_rows(after(cp, s2), 0, cotangent, gate, out_weight)
+    send_0, keep_0, near = scaled_rows(after(cp, away), 0, cotangent, gate, out_weight)
     d_own[0], d_peer[0] = near[None], to_core(near)
     scaled = (keep_0, swap(send_0, 1), keep_1, swap(send_1, 1))
-    d_picked = pick(d_spread, after(plan, near))
+    d_picked = pick(d_spread, after(plan, near, sp))
     landed = land(d_picked, (ROWS, WIDTH))
-    sp = after(sp, d_picked)
+    s1, s2, s3 = prep(after(cp, d_picked), qkv, 0)
+    received[0] = (swap(s1, 1), swap(s2, 2), swap(s3, 3))
+    sp = after(sp, s2)
     att[1], lse[1] = attend(sp, 1, qkv, received[1])
     d_own[1], d_peer[1] = landed[None], to_core(landed)
     att_spread = spread_out(after(att[1], landed).reshape(2 * ROWS, HALF))

time: 324 us -> 313 us (0.966)
  the two profiles are of different devices: /device:TPU:1 before, /device:TPU:18 now
where the time goes in v5:
time: 313 us; the launch traced here: 312 us
  waiting for transfers between devices  116 us (37%)
  Pallas kernels  112 us (36%)
  starting transfers between devices  74.1 us (24%)
  local copies, waits for them, and re-layouts  5.71 us (2%)
    ppermute x21, waiting for transfers between devices, swap(): return lax.ppermute(x, 'seq', [(i, i ^ step) for i in range(4)])  51.7 us
    ppermute x6, waiting for transfers between devices, along_x(): return lax.ppermute(x, 'dp', [(g, g ^ step << 3) for g in range(32)])  24.6 us
    pallas_call x2, Pallas kernels, attend_back(): pl.pallas_call(functools.partial(bwd_kernel, slot), grid_spec=pltpu.Prefe...  24.2 us
    pallas_call x2, Pallas kernels, attend(): pl.pallas_call(functools.partial(fwd_kernel, slot), grid_spec=pltpu.Prefe...  16.8 us
    pallas_call x2, Pallas kernels, scaled_rows(): pl.pallas_call(functools.partial(rows_kernel, slot), grid_spec=pltpu.Pref...  16.7 us
    all_to_all x2, starting transfers between devices, spread_out(): lax.all_to_all(portions, 'dp', split_axis=0, concat_axis=0, tiled=True)  16.7 us
    ppermute x4, starting transfers between devices, finish_weights(): lax.ppermute(quarter, ('dp', 'seq'), final_moves(step)).astype(jnp.float32)  15.6 us
    all_to_all x2, starting transfers between devices, land(): lax.all_to_all(arranged, 'dp', split_axis=0, concat_axis=0, tiled=True)  14.9 us
  transfers between devices with their start and end apart: 41, of which 15 were waited for; matrix products, arithmetic and copies ran while one was open for 1% of the time, Pallas kernels for 34%

profile of v5, /device:TPU:18, one launch (start us, length us, event | category | flops | bytes accessed | tf_op | source)
XLA Modules:
  0.0 312.0 jit_solution(12434101875954506120)
XLA Ops:
  0.6 3.0 shard_map.102
  3.6 8.4 %shard_map.103 = (bf16[256,1536]{1,0:T(8,128)(2,1)}, bf16[256,1536]{1,0:T(8,128)(2,1)}, bf16[256,1536]{1,0:T(8,128)(2,1)}) custom-call(s32[1,1]{1,0:T(1,128)} %bitcast.6.sp, bf16[2,256,3072]{2,1,0:T(8,128)(2,1)} %cotangent.5, f32[2,3072]{1,0:T(2,128)} %gate.5, bf16[1536,3072]{1,0:T(8,128)(2,1)} %w_other.1), custom_call_target="tpu_custom_call" | custom-call | flops 2415919104 | bytes 13000000 | tf_op jit(solution)/shard_map/pallas_call | solution.py:329
  12.0 8.8 %all-to-all-start = ((bf16[32,8,1536]{2,1,0:T(8,128)(2,1)}), bf16[32,8,1536]{2,1,0:T(8,128)(2,1)S(1)}, u32[]{:S(2)}, u32[]{:S(2)}) async-start(bf16[32,8,1536]{2,1,0:T(8,128)(2,1)} %bitcast.22), calls=%async_computation | async-start | bytes 1572864 | tf_op jit(solution)/shard_map/all_to_all | solution.py:545
  21.4 8.4 %shard_map.104 = (bf16[256,1536]{1,0:T(8,128)(2,1)}, bf16[256,1536]{1,0:T(8,128)(2,1)}, bf16[256,1536]{1,0:T(8,128)(2,1)}) custom-call(s32[1,1]{1,0:T(1,128)} %bitcast.6.sp, bf16[2,256,3072]{2,1,0:T(8,128)(2,1)} %cotangent.5, f32[2,3072]{1,0:T(2,128)} %gate.5, bf16[1536,3072]{1,0:T(8,128)(2,1)} %w_other.1), custom_call_target="tpu_custom_call" | custom-call | flops 2415919104 | bytes 13000000 | tf_op jit(solution)/shard_map/pallas_call | solution.py:329
  29.7 0.6 pad_add_fusion.sp
  30.4 2.8 all-to-all-done.rows
  33.2 0.9 copy-done.5
  34.1 2.9 pick.2
  36.9 7.5 %all-to-all-start.1 = ((bf16[32,8,1536]{2,1,0:T(8,128)(2,1)}), bf16[32,8,1536]{2,1,0:T(8,128)(2,1)}, u32[]{:S(2)}, u32[]{:S(2)}) async-start(bf16[32,8,1536]{2,1,0:T(8,128)(2,1)} %pick.2), calls=%async_computation.1 | async-start | bytes 1572864 | tf_op jit(solution)/shard_map/all_to_all | solution.py:549
  44.4 1.6 collective-permute-start.2
  46.0 2.2 collective-permute-start.1
  48.2 2.9 shard_map.105
  51.2 4.2 %all-to-all-done.1 = bf16[32,8,1536]{2,1,0:T(8,128)(2,1)} async-done(((bf16[32,8,1536]{2,1,0:T(8,128)(2,1)}), bf16[32,8,1536]{2,1,0:T(8,128)(2,1)}, u32[]{:S(2)}, u32[]{:S(2)}) %all-to-all-start.1) | async-done | bytes 786464 | tf_op jit(solution)/shard_map/all_to_all | solution.py:549
  55.4 17.1 %collective-permute-done.2.k3.v3 = bf16[2,256,768]{2,1,0:T(8,128)(2,1)S(1)} collective-permute-done((bf16[2,256,768]{2,1,0:T(8,128)(2,1)}, bf16[2,256,768]{2,1,0:T(8,128)(2,1)S(1)}, u32[]{:S(2)}, u32[]{:S(2)}) %collective-permute-start.2) | collective-permute-done | bytes 786464 | tf_op jit(solution)/shard_map/ppermute | solution.py:40
  72.5 0.9 copy-done.3
  73.4 16.6 %collective-permute-done.1.k2.v2 = bf16[2,256,768]{2,1,0:T(8,128)(2,1)} collective-permute-done((bf16[2,256,768]{2,1,0:T(8,128)(2,1)}, bf16[2,256,768]{2,1,0:T(8,128)(2,1)}, u32[]{:S(2)}, u32[]{:S(2)}) %collective-permute-start.1) | collective-permute-done | bytes 786464 | tf_op jit(solution)/shard_map/ppermute | solution.py:40
  90.0 1.0 copy-done
  91.0 8.4 %shard_map.106 = (bf16[2,256,768]{2,1,0:T(8,128)(2,1)}, f32[6,8,512]{2,1,0:T(8,128)}) custom-call(s32[2,6]{1,0:T(2,128)} %pad_add_fusion.sp, bf16[2,256,4608]{2,1,0:T(8,128)(2,1)} %v0.7, bf16[2,256,4608]{2,1,0:T(8,128)(2,1)} %v0.7, bf16[2,256,4608]{2,1,0:T(8,128)(2,1)} %v0.7, bf16[3,256,768]{2,1,0:T(8,128)(2,1)} %copy-done, bf16[3,256,768]{2,1,0:T(8,128)(2,1)} %copy-done, ...), custom_call_target="tpu_custom_call" | custom-call | flops 1610612736 | bytes 5000000 | tf_op jit(solution)/shard_map/pallas_call | solution.py:179
  99.4 7.9 %all-to-all-start.2 = ((bf16[32,16,768]{2,1,0:T(8,128)(2,1)}), bf16[32,16,768]{2,1,0:T(8,128)(2,1)}, u32[]{:S(2)}, u32[]{:S(2)}) async-start(bf16[32,16,768]{2,1,0:T(8,128)(2,1)} %bitcast.16), calls=%async_computation.2 | async-start | bytes 1572864 | tf_op jit(solution)/shard_map/all_to_all | solution.py:545
  108.0 12.1 %shard_map.107 = (f32[3,256,768]{2,1,0:T(8,128)}, bf16[3,256,768]{2,1,0:T(8,128)(2,1)}, bf16[2,256,768]{2,1,0:T(8,128)(2,1)}, bf16[2,256,768]{2,1,0:T(8,128)(2,1)}) custom-call(s32[2,6]{1,0:T(2,128)} %pad_add_fusion.sp, bf16[2,256,4608]{2,1,0:T(8,128)(2,1)} %v0.7, bf16[2,256,4608]{2,1,0:T(8,128)(2,1)} %v0.7, bf16[2,256,4608]{2,1,0:T(8,128)(2,1)} %v0.7, ...), custom_call_target="tpu_custom_call" | custom-call | flops 4026531840 | bytes 10000000 | tf_op jit(solution)/shard_map/pallas_call | solution.py:210
  120.1 11.5 %collective-permute-done.5.k2.v2 = bf16[2,256,768]{2,1,0:T(8,128)(2,1)} collective-permute-done((bf16[2,256,768]{2,1,0:T(8,128)(2,1)}, bf16[2,256,768]{2,1,0:T(8,128)(2,1)}, u32[]{:S(2)}, u32[]{:S(2)}) %collective-permute-start.5) | collective-permute-done | bytes 786464 | tf_op jit(solution)/shard_map/ppermute | solution.py:40
  131.6 1.0 copy-done.1
  132.6 8.4 %shard_map.108 = (bf16[2,256,768]{2,1,0:T(8,128)(2,1)}, f32[6,8,512]{2,1,0:T(8,128)}) custom-call(s32[2,6]{1,0:T(2,128)} %pad_add_fusion.sp, bf16[2,256,4608]{2,1,0:T(8,128)(2,1)} %v0.7, bf16[2,256,4608]{2,1,0:T(8,128)(2,1)} %v0.7, bf16[2,256,4608]{2,1,0:T(8,128)(2,1)} %v0.7, bf16[3,256,768]{2,1,0:T(8,128)(2,1)} %copy-done.1, ...), custom_call_target="tpu_custom_call" | custom-call | flops 1610612736 | bytes 5000000 | tf_op jit(solution)/shard_map/pallas_call | solution.py:179
  141.0 3.0 pick.3
  144.0 7.4 %all-to-all-start.3 = ((bf16[32,16,768]{2,1,0:T(8,128)(2,1)}), bf16[32,16,768]{2,1,0:T(8,128)(2,1)S(1)}, u32[]{:S(2)}, u32[]{:S(2)}) async-start(bf16[32,16,768]{2,1,0:T(8,128)(2,1)} %pick.3), calls=%async_computation.3 | async-start | bytes 1572864 | tf_op jit(solution)/shard_map/all_to_all | solution.py:549
  152.6 10.4 %all-to-all-done.3 = bf16[32,16,768]{2,1,0:T(8,128)(2,1)S(1)} async-done(((bf16[32,16,768]{2,1,0:T(8,128)(2,1)}), bf16[32,16,768]{2,1,0:T(8,128)(2,1)S(1)}, u32[]{:S(2)}, u32[]{:S(2)}) %all-to-all-start.3) | async-done | bytes 786464 | tf_op jit(solution)/shard_map/all_to_all | solution.py:549
  163.5 1.2 collective-permute-start.16
  164.8 1.7 collective-permute-start.17
  166.5 12.1 %shard_map.109 = (f32[3,256,768]{2,1,0:T(8,128)}, bf16[3,256,768]{2,1,0:T(8,128)(2,1)}, bf16[2,256,768]{2,1,0:T(8,128)(2,1)}, bf16[2,256,768]{2,1,0:T(8,128)(2,1)}) custom-call(s32[2,6]{1,0:T(2,128)} %pad_add_fusion.sp, bf16[2,256,4608]{2,1,0:T(8,128)(2,1)} %v0.7, bf16[2,256,4608]{2,1,0:T(8,128)(2,1)} %v0.7, bf16[2,256,4608]{2,1,0:T(8,128)(2,1)} %v0.7, ...), custom_call_target="tpu_custom_call" | custom-call | flops 4026531840 | bytes 10000000 | tf_op jit(solution)/shard_map/pallas_call | solution.py:210
  178.6 13.4 %weigh.1 = (bf16[384,768]{1,0:T(8,128)(2,1)}, bf16[384,768]{1,0:T(8,128)(2,1)}, bf16[384,768]{1,0:T(8,128)(2,1)}, bf16[384,768]{1,0:T(8,128)(2,1)}, bf16[4,96,76...) custom-call(s32[2,6]{1,0:T(2,128)} %pad_add_fusion.sp, ...), custom_call_target="tpu_custom_call" | custom-call | flops 4831838208 | bytes 12000000 | tf_op jit(solution)/shard_map/weigh/pallas_call | solution.py:421
  192.0 1.1 collective-permute-start.18
  193.1 1.2 collective-permute-start.19
  194.3 6.5 %collective-permute-done.17.p3 = bf16[2,256,768]{2,1,0:T(8,128)(2,1)S(1)} collective-permute-done((bf16[2,256,768]{2,1,0:T(8,128)(2,1)}, bf16[2,256,768]{2,1,0:T(8,128)(2,1)S(1)}, u32[]{:S(2)}, u32[]{:S(2)}) %collective-permute-start.17) | collective-permute-done | bytes 786464 | tf_op jit(solution)/shard_map/ppermute | solution.py:40
  200.8 0.8 collective-permute-start.20
  201.6 0.8 collective-permute-start.21
  202.5 5.9 %collective-permute-done.18.refs_1_ = bf16[384,768]{1,0:T(8,128)(2,1)S(1)} collective-permute-done((bf16[384,768]{1,0:T(8,128)(2,1)}, bf16[384,768]{1,0:T(8,128)(2,1)S(1)}, u32[]{:S(2)}, u32[]{:S(2)}) %collective-permute-start.18) | collective-permute-done | bytes 589856 | tf_op jit(solution)/shard_map/ppermute | solution.py:439
  208.4 0.8 copy-done.12
  209.7 11.5 %collective-permute-done.19.refs_2_ = bf16[384,768]{1,0:T(8,128)(2,1)} collective-permute-done((bf16[384,768]{1,0:T(8,128)(2,1)}, bf16[384,768]{1,0:T(8,128)(2,1)}, u32[]{:S(2)}, u32[]{:S(2)}) %collective-permute-start.19) | collective-permute-done | bytes 589856 | tf_op jit(solution)/shard_map/ppermute | solution.py:439
  221.2 1.2 collective-permute-start.25
  222.5 7.2 %collective-permute-done.20.refs_3_ = bf16[384,768]{1,0:T(8,128)(2,1)} collective-permute-done((bf16[384,768]{1,0:T(8,128)(2,1)}, bf16[384,768]{1,0:T(8,128)(2,1)}, u32[]{:S(2)}, u32[]{:S(2)}) %collective-permute-start.20) | collective-permute-done | bytes 589856 | tf_op jit(solution)/shard_map/ppermute | solution.py:439
  229.7 1.0 collective-permute-start.22
  230.7 1.2 collective-permute-start.23
  231.9 11.0 %project.1 = (bf16[2,256,3072]{2,1,0:T(8,128)(2,1)}, f32[2,3072]{1,0:T(2,128)}) custom-call(s32[2,6]{1,0:T(2,128)} %pad_add_fusion.sp, bf16[2,256,768]{2,1,0:T(8,128)(2,1)} %get-tuple-element.84.att.a0, bf16[2,256,768]{2,1,0:T(8,128)(2,1)} %bitcast.19, bf16[2,256,768]{2,1,0:T(8,128)(2,1)} %collective-permute-done.10.b0, ...), custom_call_target="tpu_custom_call" | custom-call | flops 4831838208 | bytes 16000000 | tf_op jit(solution)/shard_map/project/pallas_call | solution.py:371
  243.0 5.7 %shard_map.110.rest_0_ = bf16[2,256,4608]{2,1,0:T(8,128)(2,1)} custom-call(s32[2,6]{1,0:T(2,128)} %pad_add_fusion.sp, f32[3,256,768]{2,1,0:T(8,128)} %get-tuple-element.96.own, bf16[3,256,768]{2,1,0:T(8,128)(2,1)} %copy-done.8, bf16[2,256,768]{2,1,0:T(8,128)(2,1)} %collective-permute-done.16.p2, bf16[2,256,768]{2,1,0:T(8,128)(2,1)} %copy-done.11), custom_call_target="tpu_custom_call" | custom-call | flops 1000000 | bytes 10000000 | tf_op jit(solution)/shard_map/pallas_call | solution.py:257
  248.7 9.8 %collective-permute-done.23.refs_7_ = bf16[4,96,768]{2,1,0:T(8,128)(2,1)} collective-permute-done((bf16[4,96,768]{2,1,0:T(8,128)(2,1)}, bf16[4,96,768]{2,1,0:T(8,128)(2,1)}, u32[]{:S(2)}, u32[]{:S(2)}) %collective-permute-start.23) | collective-permute-done | bytes 589856 | tf_op jit(solution)/shard_map/ppermute | solution.py:443
  258.5 4.2 %sum_parts.1 = (bf16[96,768]{1,0:T(8,128)(2,1)}, bf16[96,768]{1,0:T(8,128)(2,1)}, bf16[96,768]{1,0:T(8,128)(2,1)}, bf16[96,768]{1,0:T(8,128)(2,1)}, bf16[96,768]...) custom-call(s32[2,6]{1,0:T(2,128)} %pad_add_fusion.sp, ...), custom_call_target="tpu_custom_call" | custom-call | flops 5000000 | bytes 6000000 | tf_op jit(solution)/shard_map/sum_parts/pallas_call | solution.py:470
  262.6 1.6 collective-permute-start.27
  264.3 1.1 collective-permute-start.28
  265.4 0.8 collective-permute-start.29
  266.2 3.1 collective-permute-start.30
  269.6 1.5 collective-permute-start.32
  271.2 1.4 collective-permute-done.28.refs_2_
  272.6 1.4 collective-permute-done.29.refs_3_
  274.0 1.1 collective-permute-start.13
  275.1 0.9 collective-permute-start.12
  276.0 5.7 %shard_map.111 = bf16[2,256,4608]{2,1,0:T(8,128)(2,1)} custom-call(s32[2,6]{1,0:T(2,128)} %pad_add_fusion.sp, f32[3,256,768]{2,1,0:T(8,128)} %get-tuple-element.109.own, bf16[3,256,768]{2,1,0:T(8,128)(2,1)} %copy-done.7, bf16[2,256,768]{2,1,0:T(8,128)(2,1)} %collective-permute-done.25.p2, ...), custom_call_target="tpu_custom_call", output_to_operand_aliasing={{}: (5, {})} | custom-call | flops 1000000 | bytes 10000000 | tf_op jit(solution)/shard_map/pallas_call | solution.py:257
  281.7 0.6 copy-done.17
  282.4 3.0 sum_weights.1
  285.4 7.3 %collective-permute-start.33 = (bf16[24,1536]{1,0:T(8,128)(2,1)}, bf16[24,1536]{1,0:T(8,128)(2,1)S(1)}, u32[]{:S(2)}, u32[]{:S(2)}) collective-permute-start(bf16[24,1536]{1,0:T(8,128)(2,1)} %get-tuple-element.120), channel_id=1, source_target_pairs={{0,0},{1,64},{2,1},{3,65},{4,2},{5,66},{6,3},{7,67},{8,4},{9,68},{... | collective-permute-start | bytes 221192 | tf_op jit(solution)/shard_map/ppermute | solution.py:532
  292.8 6.0 %collective-permute-start.35 = (bf16[24,1536]{1,0:T(8,128)(2,1)}, bf16[24,1536]{1,0:T(8,128)(2,1)S(1)}, u32[]{:S(2)}, u32[]{:S(2)}) collective-permute-start(bf16[24,1536]{1,0:T(8,128)(2,1)} %get-tuple-element.122), channel_id=1, source_target_pairs={{0,2},{1,66},{2,3},{3,67},{4,0},{5,64},{6,1},{7,65},{8,6},{9,70},{... | collective-permute-start | bytes 221192 | tf_op jit(solution)/shard_map/ppermute | solution.py:532
  298.8 2.1 collective-permute-start.36
  301.6 2.4 collective-permute-done.34
  304.0 7.3 %collective-permute-done.36 = bf16[24,1536]{1,0:T(8,128)(2,1)S(1)} collective-permute-done((bf16[24,1536]{1,0:T(8,128)(2,1)}, bf16[24,1536]{1,0:T(8,128)(2,1)S(1)}, u32[]{:S(2)}, u32[]{:S(2)}) %collective-permute-start.36) | collective-permute-done | bytes 73760 | tf_op jit(solution)/shard_map/ppermute | solution.py:532
  311.3 0.7 add_bitcast_fusion
  (95 shorter events, 4.9 us)
Async XLA Ops:
  3.6 86.4 %collective-permute-start = (bf16[3,256,768]{2,1,0:T(8,128)(2,1)}, bf16[3,256,768]{2,1,0:T(8,128)(2,1)S(1)}, u32[]{:S(2)}, u32[]{:S(2)}) collective-permute-start(bf16[3,256,768]{2,1,0:T(8,128)(2,1)} %get-tuple-element.73), channel_id=1, source_target_pairs={{0,1},{1,0},{2,3},{3,2},{4,5},{5,4},{6,7},{7,6},{8,9},{9,8},{10,11... | collective-permute-start | bytes 3538952 | tf_op jit(solution)/shard_map/ppermute | solution.py:40
  3.6 17.2 %copy-start.22 = (s32[64]{0:T(128)S(1)}, s32[64]{0:T(128)}, u32[]{:S(2)}) copy-start(s32[64]{0:T(128)} %param.11) | copy-start | bytes 772
  3.6 17.3 %copy-start.23 = (s32[64]{0:T(128)S(1)}, s32[64]{0:T(128)}, u32[]{:S(2)}) copy-start(s32[64]{0:T(128)} %param.12) | copy-start | bytes 772
  12.0 21.2 %all-to-all-start = ((bf16[32,8,1536]{2,1,0:T(8,128)(2,1)}), bf16[32,8,1536]{2,1,0:T(8,128)(2,1)S(1)}, u32[]{:S(2)}, u32[]{:S(2)}) async-start(bf16[32,8,1536]{2,1,0:T(8,128)(2,1)} %bitcast.22), calls=%async_computation | async-start | bytes 1572864 | tf_op jit(solution)/shard_map/all_to_all | solution.py:545
  33.2 0.9 copy-start.5
  36.9 18.4 %all-to-all-start.1 = ((bf16[32,8,1536]{2,1,0:T(8,128)(2,1)}), bf16[32,8,1536]{2,1,0:T(8,128)(2,1)}, u32[]{:S(2)}, u32[]{:S(2)}) async-start(bf16[32,8,1536]{2,1,0:T(8,128)(2,1)} %pick.2), calls=%async_computation.1 | async-start | bytes 1572864 | tf_op jit(solution)/shard_map/all_to_all | solution.py:549
  44.4 28.0 %collective-permute-start.2 = (bf16[2,256,768]{2,1,0:T(8,128)(2,1)}, bf16[2,256,768]{2,1,0:T(8,128)(2,1)S(1)}, u32[]{:S(2)}, u32[]{:S(2)}) collective-permute-start(bf16[2,256,768]{2,1,0:T(8,128)(2,1)} %get-tuple-element.74), channel_id=1, source_target_pairs={{0,3},{1,2},{2,1},{3,0},{4,7},{5,6},{6,5},{7,4},{8,11},{9,10},{10,... | collective-permute-start | bytes 2359304 | tf_op jit(solution)/shard_map/ppermute | solution.py:40
  46.0 43.9 %collective-permute-start.1 = (bf16[2,256,768]{2,1,0:T(8,128)(2,1)}, bf16[2,256,768]{2,1,0:T(8,128)(2,1)}, u32[]{:S(2)}, u32[]{:S(2)}) collective-permute-start(bf16[2,256,768]{2,1,0:T(8,128)(2,1)} %get-tuple-element.64), channel_id=1, source_target_pairs={{0,2},{1,3},{2,0},{3,1},{4,6},{5,7},{6,4},{7,5},{8,10},{9,11},{10,... | collective-permute-start | bytes 2359304 | tf_op jit(solution)/shard_map/ppermute | solution.py:40
  51.1 80.4 %collective-permute-start.4 = (bf16[3,256,768]{2,1,0:T(8,128)(2,1)}, bf16[3,256,768]{2,1,0:T(8,128)(2,1)S(1)}, u32[]{:S(2)}, u32[]{:S(2)}) collective-permute-start(bf16[3,256,768]{2,1,0:T(8,128)(2,1)} %get-tuple-element.79), channel_id=1, source_target_pairs={{0,1},{1,0},{2,3},{3,2},{4,5},{5,4},{6,7},{7,6},{8,9},{9,8},{10,11... | collective-permute-start | bytes 3538952 | tf_op jit(solution)/shard_map/ppermute | solution.py:40
  55.3 52.6 %collective-permute-start.3 = (bf16[1,256,1536]{2,1,0:T(8,128)(2,1)}, bf16[1,256,1536]{2,1,0:T(8,128)(2,1)}, u32[]{:S(2)}, u32[]{:S(2)}) collective-permute-start(bf16[1,256,1536]{2,1,0:T(8,128)(2,1)} %bitcast.8.do0), channel_id=1, source_target_pairs={{0,1},{1,0},{2,3},{3,2},{4,5},{5,4},{6,7},{7,6},{8,9},{9,8},{10,11... | collective-permute-start | bytes 2359304 | tf_op jit(solution)/shard_map/ppermute | solution.py:40
  72.5 0.9 copy-start.3
  73.4 46.7 %collective-permute-start.6 = (bf16[2,256,768]{2,1,0:T(8,128)(2,1)}, bf16[2,256,768]{2,1,0:T(8,128)(2,1)S(1)}, u32[]{:S(2)}, u32[]{:S(2)}) collective-permute-start(bf16[2,256,768]{2,1,0:T(8,128)(2,1)} %get-tuple-element.80), channel_id=1, source_target_pairs={{0,3},{1,2},{2,1},{3,0},{4,7},{5,6},{6,5},{7,4},{8,11},{9,10},{10,... | collective-permute-start | bytes 2359304 | tf_op jit(solution)/shard_map/ppermute | solution.py:40
  89.9 17.4 %copy-start.20 = (s32[32]{0:T(128)S(1)}, s32[32]{0:T(128)}, u32[]{:S(2)}) copy-start(s32[32]{0:T(128)} %order) | copy-start | bytes 388
  89.9 41.6 %collective-permute-start.5 = (bf16[2,256,768]{2,1,0:T(8,128)(2,1)}, bf16[2,256,768]{2,1,0:T(8,128)(2,1)}, u32[]{:S(2)}, u32[]{:S(2)}) collective-permute-start(bf16[2,256,768]{2,1,0:T(8,128)(2,1)} %get-tuple-element.71), channel_id=1, source_target_pairs={{0,2},{1,3},{2,0},{3,1},{4,6},{5,7},{6,4},{7,5},{8,10},{9,11},{10,... | collective-permute-start | bytes 2359304 | tf_op jit(solution)/shard_map/ppermute | solution.py:40
  90.0 1.0 copy-start
  99.4 41.6 %all-to-all-start.2 = ((bf16[32,16,768]{2,1,0:T(8,128)(2,1)}), bf16[32,16,768]{2,1,0:T(8,128)(2,1)}, u32[]{:S(2)}, u32[]{:S(2)}) async-start(bf16[32,16,768]{2,1,0:T(8,128)(2,1)} %bitcast.16), calls=%async_computation.2 | async-start | bytes 1572864 | tf_op jit(solution)/shard_map/all_to_all | solution.py:545
  120.1 11.5 %copy-start.2 = (bf16[2,256,768]{2,1,0:T(8,128)(2,1)}, bf16[2,256,768]{2,1,0:T(8,128)(2,1)S(1)}, u32[]{:S(2)}) copy-start(bf16[2,256,768]{2,1,0:T(8,128)(2,1)S(1)} %collective-permute-done.6.k3.v3) | copy-start | bytes 2359300
  131.6 1.0 copy-start.1
  141.0 10.5 %copy-start.21 = (bf16[256,1536]{1,0:T(8,128)(2,1)S(1)}, bf16[256,1536]{1,0:T(8,128)(2,1)}, u32[]{:S(2)}) copy-start(bf16[256,1536]{1,0:T(8,128)(2,1)} %get-tuple-element.90) | copy-start | bytes 2359300
  141.0 11.1 %copy-start.9 = (bf16[256,1536]{1,0:T(8,128)(2,1)S(1)}, bf16[256,1536]{1,0:T(8,128)(2,1)}, u32[]{:S(2)}) copy-start(bf16[256,1536]{1,0:T(8,128)(2,1)} %get-tuple-element.68) | copy-start | bytes 2359300
  141.0 11.2 %copy-start.4 = (bf16[2,256,768]{2,1,0:T(8,128)(2,1)S(1)}, bf16[2,256,768]{2,1,0:T(8,128)(2,1)}, u32[]{:S(2)}) copy-start(bf16[2,256,768]{2,1,0:T(8,128)(2,1)} %get-tuple-element.84.att.a0) | copy-start | bytes 2359300
  144.0 19.0 %all-to-all-start.3 = ((bf16[32,16,768]{2,1,0:T(8,128)(2,1)}), bf16[32,16,768]{2,1,0:T(8,128)(2,1)S(1)}, u32[]{:S(2)}, u32[]{:S(2)}) async-start(bf16[32,16,768]{2,1,0:T(8,128)(2,1)} %pick.3), calls=%async_computation.3 | async-start | bytes 1572864 | tf_op jit(solution)/shard_map/all_to_all | solution.py:549
  151.5 11.6 %collective-permute-start.9 = (bf16[256,1536]{1,0:T(8,128)(2,1)S(1)}, bf16[256,1536]{1,0:T(8,128)(2,1)}, u32[]{:S(2)}, u32[]{:S(2)}) collective-permute-start(bf16[256,1536]{1,0:T(8,128)(2,1)S(1)} %copy-done.21), channel_id=1, source_target_pairs={{0,1},{1,0},{2,3},{3,2},{4,5},{5,4},{6,7},{7,6},{8,9},{9,8},{10,11... | collective-permute-start | bytes 2359304 | tf_op jit(solution)/shard_map/ppermute | solution.py:40
  151.6 12.0 %collective-permute-start.8 = (bf16[256,1536]{1,0:T(8,128)(2,1)}, bf16[256,1536]{1,0:T(8,128)(2,1)}, u32[]{:S(2)}, u32[]{:S(2)}) collective-permute-start(bf16[256,1536]{1,0:T(8,128)(2,1)} %get-tuple-element.88), channel_id=1, source_target_pairs={{0,1},{1,0},{2,3},{3,2},{4,5},{5,4},{6,7},{7,6},{8,9},{9,8},{10,11... | collective-permute-start | bytes 2359304 | tf_op jit(solution)/shard_map/ppermute | solution.py:40
  152.1 12.7 %collective-permute-start.7 = (bf16[1,256,1536]{2,1,0:T(8,128)(2,1)S(1)}, bf16[1,256,1536]{2,1,0:T(8,128)(2,1)}, u32[]{:S(2)}, u32[]{:S(2)}) collective-permute-start(bf16[1,256,1536]{2,1,0:T(8,128)(2,1)S(1)} %bitcast.21), channel_id=1, source_target_pairs={{0,1},{1,0},{2,3},{3,2},{4,5},{5,4},{6,7},{7,6},{8,9},{9,8},{10,11... | collective-permute-start | bytes 2359304 | tf_op jit(solution)/shard_map/ppermute | solution.py:40
  152.2 26.4 %collective-permute-start.10 = (bf16[2,256,768]{2,1,0:T(8,128)(2,1)S(1)}, bf16[2,256,768]{2,1,0:T(8,128)(2,1)}, u32[]{:S(2)}, u32[]{:S(2)}) collective-permute-start(bf16[2,256,768]{2,1,0:T(8,128)(2,1)S(1)} %copy-done.4), channel_id=1, source_target_pairs={{0,1},{1,0},{2,3},{3,2},{4,5},{5,4},{6,7},{7,6},{8,9},{9,8},{10,11... | collective-permute-start | bytes 2359304 | tf_op jit(solution)/shard_map/ppermute | solution.py:40
  163.0 15.6 %copy-start.6 = (bf16[32,16,768]{2,1,0:T(8,128)(2,1)}, bf16[32,16,768]{2,1,0:T(8,128)(2,1)S(1)}, u32[]{:S(2)}) copy-start(bf16[32,16,768]{2,1,0:T(8,128)(2,1)S(1)} %all-to-all-done.3) | copy-start | bytes 2359300
  163.0 15.6 %collective-permute-start.11 = (bf16[2,256,768]{2,1,0:T(8,128)(2,1)S(1)}, bf16[2,256,768]{2,1,0:T(8,128)(2,1)}, u32[]{:S(2)}, u32[]{:S(2)}) collective-permute-start(bf16[2,256,768]{2,1,0:T(8,128)(2,1)S(1)} %bitcast.17), channel_id=1, source_target_pairs={{0,1},{1,0},{2,3},{3,2},{4,5},{5,4},{6,7},{7,6},{8,9},{9,8},{10,11... | collective-permute-start | bytes 2359304 | tf_op jit(solution)/shard_map/ppermute | solution.py:40
  163.0 39.3 %collective-permute-start.15 = (bf16[3,256,768]{2,1,0:T(8,128)(2,1)}, bf16[3,256,768]{2,1,0:T(8,128)(2,1)S(1)}, u32[]{:S(2)}, u32[]{:S(2)}) collective-permute-start(bf16[3,256,768]{2,1,0:T(8,128)(2,1)} %get-tuple-element.97), channel_id=1, source_target_pairs={{0,1},{1,0},{2,3},{3,2},{4,5},{5,4},{6,7},{7,6},{8,9},{9,8},{10,11... | collective-permute-start | bytes 3538952 | tf_op jit(solution)/shard_map/ppermute | solution.py:40
  163.5 38.0 %collective-permute-start.16 = (bf16[2,256,768]{2,1,0:T(8,128)(2,1)}, bf16[2,256,768]{2,1,0:T(8,128)(2,1)}, u32[]{:S(2)}, u32[]{:S(2)}) collective-permute-start(bf16[2,256,768]{2,1,0:T(8,128)(2,1)} %get-tuple-element.77), channel_id=1, source_target_pairs={{0,2},{1,3},{2,0},{3,1},{4,6},{5,7},{6,4},{7,5},{8,10},{9,11},{10,... | collective-permute-start | bytes 2359304 | tf_op jit(solution)/shard_map/ppermute | solution.py:40
  164.8 36.0 %collective-permute-start.17 = (bf16[2,256,768]{2,1,0:T(8,128)(2,1)}, bf16[2,256,768]{2,1,0:T(8,128)(2,1)S(1)}, u32[]{:S(2)}, u32[]{:S(2)}) collective-permute-start(bf16[2,256,768]{2,1,0:T(8,128)(2,1)} %get-tuple-element.98), channel_id=1, source_target_pairs={{0,3},{1,2},{2,1},{3,0},{4,7},{5,6},{6,5},{7,4},{8,11},{9,10},{10,... | collective-permute-start | bytes 2359304 | tf_op jit(solution)/shard_map/ppermute | solution.py:40
  192.0 16.4 %collective-permute-start.18 = (bf16[384,768]{1,0:T(8,128)(2,1)}, bf16[384,768]{1,0:T(8,128)(2,1)S(1)}, u32[]{:S(2)}, u32[]{:S(2)}) collective-permute-start(bf16[384,768]{1,0:T(8,128)(2,1)} %get-tuple-element.100), channel_id=1, source_target_pairs={{0,32},{4,36},{8,40},{12,44},{16,48},{20,52},{24,56},{28,60},{32,0... | collective-permute-start | bytes 1769480 | tf_op jit(solution)/shard_map/ppermute | solution.py:439
  193.1 28.1 %collective-permute-start.19 = (bf16[384,768]{1,0:T(8,128)(2,1)}, bf16[384,768]{1,0:T(8,128)(2,1)}, u32[]{:S(2)}, u32[]{:S(2)}) collective-permute-start(bf16[384,768]{1,0:T(8,128)(2,1)} %get-tuple-element.101), channel_id=1, source_target_pairs={{0,64},{4,68},{8,72},{12,76},{16,80},{20,84},{24,88},{28,92},{32,9... | collective-permute-start | bytes 1769480 | tf_op jit(solution)/shard_map/ppermute | solution.py:439
  200.8 7.6 %copy-start.11 = (bf16[2,256,768]{2,1,0:T(8,128)(2,1)}, bf16[2,256,768]{2,1,0:T(8,128)(2,1)S(1)}, u32[]{:S(2)}) copy-start(bf16[2,256,768]{2,1,0:T(8,128)(2,1)S(1)} %collective-permute-done.17.p3) | copy-start | bytes 2359300
  200.8 28.9 %collective-permute-start.20 = (bf16[384,768]{1,0:T(8,128)(2,1)}, bf16[384,768]{1,0:T(8,128)(2,1)}, u32[]{:S(2)}, u32[]{:S(2)}) collective-permute-start(bf16[384,768]{1,0:T(8,128)(2,1)} %get-tuple-element.102), channel_id=1, source_target_pairs={{0,96},{4,100},{8,104},{12,108},{16,112},{20,116},{24,120},{28,124... | collective-permute-start | bytes 1769480 | tf_op jit(solution)/shard_map/ppermute | solution.py:439
  201.6 29.1 %collective-permute-start.21 = (bf16[4,96,768]{2,1,0:T(8,128)(2,1)}, bf16[4,96,768]{2,1,0:T(8,128)(2,1)}, u32[]{:S(2)}, u32[]{:S(2)}) collective-permute-start(bf16[4,96,768]{2,1,0:T(8,128)(2,1)} %get-tuple-element.104), channel_id=1, source_target_pairs={{0,8},{4,12},{8,0},{12,4},{16,24},{20,28},{24,16},{28,20},{32,40},... | collective-permute-start | bytes 1769480 | tf_op jit(solution)/shard_map/ppermute | solution.py:443
  202.4 40.6 %copy-start.8 = (bf16[3,256,768]{2,1,0:T(8,128)(2,1)}, bf16[3,256,768]{2,1,0:T(8,128)(2,1)S(1)}, u32[]{:S(2)}) copy-start(bf16[3,256,768]{2,1,0:T(8,128)(2,1)S(1)} %collective-permute-done.15.p1) | copy-start | bytes 3538948
  202.4 67.0 %collective-permute-start.24 = (bf16[3,256,768]{2,1,0:T(8,128)(2,1)}, bf16[3,256,768]{2,1,0:T(8,128)(2,1)S(1)}, u32[]{:S(2)}, u32[]{:S(2)}) collective-permute-start(bf16[3,256,768]{2,1,0:T(8,128)(2,1)} %get-tuple-element.110), channel_id=1, source_target_pairs={{0,1},{1,0},{2,3},{3,2},{4,5},{5,4},{6,7},{7,6},{8,9},{9,8},{10,11... | collective-permute-start | bytes 3538952 | tf_op jit(solution)/shard_map/ppermute | solution.py:40
  208.4 0.8 copy-start.12
  209.2 56.2 %collective-permute-start.26 = (bf16[2,256,768]{2,1,0:T(8,128)(2,1)}, bf16[2,256,768]{2,1,0:T(8,128)(2,1)S(1)}, u32[]{:S(2)}, u32[]{:S(2)}) collective-permute-start(bf16[2,256,768]{2,1,0:T(8,128)(2,1)} %get-tuple-element.111), channel_id=1, source_target_pairs={{0,3},{1,2},{2,1},{3,0},{4,7},{5,6},{6,5},{7,4},{8,11},{9,10},{10,... | collective-permute-start | bytes 2359304 | tf_op jit(solution)/shard_map/ppermute | solution.py:40
  221.2 45.0 %collective-permute-start.25 = (bf16[2,256,768]{2,1,0:T(8,128)(2,1)}, bf16[2,256,768]{2,1,0:T(8,128)(2,1)}, u32[]{:S(2)}, u32[]{:S(2)}) collective-permute-start(bf16[2,256,768]{2,1,0:T(8,128)(2,1)} %get-tuple-element.85), channel_id=1, source_target_pairs={{0,2},{1,3},{2,0},{3,1},{4,6},{5,7},{6,4},{7,5},{8,10},{9,11},{10,... | collective-permute-start | bytes 2359304 | tf_op jit(solution)/shard_map/ppermute | solution.py:40
  229.7 19.0 %collective-permute-start.22 = (bf16[4,96,768]{2,1,0:T(8,128)(2,1)}, bf16[4,96,768]{2,1,0:T(8,128)(2,1)}, u32[]{:S(2)}, u32[]{:S(2)}) collective-permute-start(bf16[4,96,768]{2,1,0:T(8,128)(2,1)} %get-tuple-element.105), channel_id=1, source_target_pairs={{0,16},{4,20},{8,24},{12,28},{16,0},{20,4},{24,8},{28,12},{32,48},... | collective-permute-start | bytes 1769480 | tf_op jit(solution)/shard_map/ppermute | solution.py:443
  230.7 27.8 %collective-permute-start.23 = (bf16[4,96,768]{2,1,0:T(8,128)(2,1)}, bf16[4,96,768]{2,1,0:T(8,128)(2,1)}, u32[]{:S(2)}, u32[]{:S(2)}) collective-permute-start(bf16[4,96,768]{2,1,0:T(8,128)(2,1)} %get-tuple-element.106), channel_id=1, source_target_pairs={{0,24},{4,28},{8,16},{12,20},{16,8},{20,12},{24,0},{28,4},{32,56},... | collective-permute-start | bytes 1769480 | tf_op jit(solution)/shard_map/ppermute | solution.py:443
  258.5 14.1 %copy-start.19 = (f32[2,3072]{1,0:T(2,128)S(1)}, f32[2,3072]{1,0:T(2,128)}, u32[]{:S(2)}) copy-start(f32[2,3072]{1,0:T(2,128)} %get-tuple-element.94) | copy-start | bytes 73732
  262.6 7.0 %collective-permute-start.27 = (bf16[96,768]{1,0:T(8,128)(2,1)}, bf16[96,768]{1,0:T(8,128)(2,1)S(1)}, u32[]{:S(2)}, u32[]{:S(2)}) collective-permute-start(bf16[96,768]{1,0:T(8,128)(2,1)} %get-tuple-element.113), channel_id=1, source_target_pairs={{0,8},{4,12},{8,0},{12,4},{16,24},{20,28},{24,16},{28,20},{32,40},... | collective-permute-start | bytes 442376 | tf_op jit(solution)/shard_map/ppermute | solution.py:443
  264.3 8.3 %collective-permute-start.28 = (bf16[96,768]{1,0:T(8,128)(2,1)}, bf16[96,768]{1,0:T(8,128)(2,1)S(1)}, u32[]{:S(2)}, u32[]{:S(2)}) collective-permute-start(bf16[96,768]{1,0:T(8,128)(2,1)} %get-tuple-element.114), channel_id=1, source_target_pairs={{0,16},{4,20},{8,24},{12,28},{16,0},{20,4},{24,8},{28,12},{32,48},... | collective-permute-start | bytes 442376 | tf_op jit(solution)/shard_map/ppermute | solution.py:443
  265.4 10.5 %copy-start.10 = (bf16[2,256,768]{2,1,0:T(8,128)(2,1)}, bf16[2,256,768]{2,1,0:T(8,128)(2,1)S(1)}, u32[]{:S(2)}) copy-start(bf16[2,256,768]{2,1,0:T(8,128)(2,1)S(1)} %collective-permute-done.26.p3) | copy-start | bytes 2359300
  265.4 8.5 %collective-permute-start.29 = (bf16[96,768]{1,0:T(8,128)(2,1)}, bf16[96,768]{1,0:T(8,128)(2,1)S(1)}, u32[]{:S(2)}, u32[]{:S(2)}) collective-permute-start(bf16[96,768]{1,0:T(8,128)(2,1)} %get-tuple-element.115), channel_id=1, source_target_pairs={{0,24},{4,28},{8,16},{12,20},{16,8},{20,12},{24,0},{28,4},{32,56},... | collective-permute-start | bytes 442376 | tf_op jit(solution)/shard_map/ppermute | solution.py:443
  266.2 8.9 %collective-permute-start.30 = (bf16[96,768]{1,0:T(8,128)(2,1)}, bf16[96,768]{1,0:T(8,128)(2,1)S(1)}, u32[]{:S(2)}, u32[]{:S(2)}) collective-permute-start(bf16[96,768]{1,0:T(8,128)(2,1)} %get-tuple-element.117), channel_id=1, source_target_pairs={{0,32},{4,36},{8,40},{12,44},{16,48},{20,52},{24,56},{28,60},{32,0... | collective-permute-start | bytes 442376 | tf_op jit(solution)/shard_map/ppermute | solution.py:439
  269.3 6.6 %copy-start.7 = (bf16[3,256,768]{2,1,0:T(8,128)(2,1)}, bf16[3,256,768]{2,1,0:T(8,128)(2,1)S(1)}, u32[]{:S(2)}) copy-start(bf16[3,256,768]{2,1,0:T(8,128)(2,1)S(1)} %collective-permute-done.24.p1) | copy-start | bytes 3538948
  269.3 12.4 %collective-permute-start.31 = (bf16[96,768]{1,0:T(8,128)(2,1)}, bf16[96,768]{1,0:T(8,128)(2,1)S(1)}, u32[]{:S(2)}, u32[]{:S(2)}) collective-permute-start(bf16[96,768]{1,0:T(8,128)(2,1)} %get-tuple-element.118), channel_id=1, source_target_pairs={{0,64},{4,68},{8,72},{12,76},{16,80},{20,84},{24,88},{28,92},{32,9... | collective-permute-start | bytes 442376 | tf_op jit(solution)/shard_map/ppermute | solution.py:439
  269.6 12.0 %copy-start.13 = (bf16[96,768]{1,0:T(8,128)(2,1)}, bf16[96,768]{1,0:T(8,128)(2,1)S(1)}, u32[]{:S(2)}) copy-start(bf16[96,768]{1,0:T(8,128)(2,1)S(1)} %collective-permute-done.27.refs_1_) | copy-start | bytes 442372
  269.6 12.1 %collective-permute-start.32 = (bf16[96,768]{1,0:T(8,128)(2,1)}, bf16[96,768]{1,0:T(8,128)(2,1)S(1)}, u32[]{:S(2)}, u32[]{:S(2)}) collective-permute-start(bf16[96,768]{1,0:T(8,128)(2,1)} %get-tuple-element.119), channel_id=1, source_target_pairs={{0,96},{4,100},{8,104},{12,108},{16,112},{20,116},{24,120},{28,124... | collective-permute-start | bytes 442376 | tf_op jit(solution)/shard_map/ppermute | solution.py:439
  272.6 9.1 %copy-start.14 = (bf16[96,768]{1,0:T(8,128)(2,1)}, bf16[96,768]{1,0:T(8,128)(2,1)S(1)}, u32[]{:S(2)}) copy-start(bf16[96,768]{1,0:T(8,128)(2,1)S(1)} %collective-permute-done.28.refs_2_) | copy-start | bytes 442372
  272.6 20.3 %collective-permute-start.14 = (f32[2,3072]{1,0:T(2,128)S(1)}, f32[2,3072]{1,0:T(2,128)S(1)}, u32[]{:S(2)}, u32[]{:S(2)}) collective-permute-start(f32[2,3072]{1,0:T(2,128)S(1)} %copy-done.19), channel_id=1, source_target_pairs={{0,3},{1,2},{2,1},{3,0},{4,7},{5,6},{6,5},{7,4},{8,11},{9,10},{10,... | collective-permute-start | bytes 73736 | tf_op jit(solution)/shard_map/ppermute | solution.py:40
  274.0 7.7 %copy-start.15 = (bf16[96,768]{1,0:T(8,128)(2,1)}, bf16[96,768]{1,0:T(8,128)(2,1)S(1)}, u32[]{:S(2)}) copy-start(bf16[96,768]{1,0:T(8,128)(2,1)S(1)} %collective-permute-done.29.refs_3_) | copy-start | bytes 442372
  274.0 24.9 %collective-permute-start.13 = (f32[2,3072]{1,0:T(2,128)S(1)}, f32[2,3072]{1,0:T(2,128)S(1)}, u32[]{:S(2)}, u32[]{:S(2)}) collective-permute-start(f32[2,3072]{1,0:T(2,128)S(1)} %copy-done.19), channel_id=1, source_target_pairs={{0,2},{1,3},{2,0},{3,1},{4,6},{5,7},{6,4},{7,5},{8,10},{9,11},{10,... | collective-permute-start | bytes 73736 | tf_op jit(solution)/shard_map/ppermute | solution.py:40
  275.1 6.6 %copy-start.16 = (bf16[96,768]{1,0:T(8,128)(2,1)}, bf16[96,768]{1,0:T(8,128)(2,1)S(1)}, u32[]{:S(2)}) copy-start(bf16[96,768]{1,0:T(8,128)(2,1)S(1)} %collective-permute-done.30.refs_5_) | copy-start | bytes 442372
  275.1 25.8 %collective-permute-start.12 = (f32[2,3072]{1,0:T(2,128)S(1)}, f32[2,3072]{1,0:T(2,128)S(1)}, u32[]{:S(2)}, u32[]{:S(2)}) collective-permute-start(f32[2,3072]{1,0:T(2,128)S(1)} %copy-done.19), channel_id=1, source_target_pairs={{0,1},{1,0},{2,3},{3,2},{4,5},{5,4},{6,7},{7,6},{8,9},{9,8},{10,11... | collective-permute-start | bytes 73736 | tf_op jit(solution)/shard_map/ppermute | solution.py:40
  281.7 0.7 copy-start.18
  285.4 16.2 %collective-permute-start.33 = (bf16[24,1536]{1,0:T(8,128)(2,1)}, bf16[24,1536]{1,0:T(8,128)(2,1)S(1)}, u32[]{:S(2)}, u32[]{:S(2)}) collective-permute-start(bf16[24,1536]{1,0:T(8,128)(2,1)} %get-tuple-element.120), channel_id=1, source_target_pairs={{0,0},{1,64},{2,1},{3,65},{4,2},{5,66},{6,3},{7,67},{8,4},{9,68},{... | collective-permute-start | bytes 221192 | tf_op jit(solution)/shard_map/ppermute | solution.py:532
  292.7 11.3 %collective-permute-start.34 = (bf16[24,1536]{1,0:T(8,128)(2,1)}, bf16[24,1536]{1,0:T(8,128)(2,1)S(1)}, u32[]{:S(2)}, u32[]{:S(2)}) collective-permute-start(bf16[24,1536]{1,0:T(8,128)(2,1)} %get-tuple-element.121), channel_id=1, source_target_pairs={{0,1},{1,65},{2,0},{3,64},{4,3},{5,67},{6,2},{7,66},{8,5},{9,69},{... | collective-permute-start | bytes 221192 | tf_op jit(solution)/shard_map/ppermute | solution.py:532
  292.8 11.1 %collective-permute-start.35 = (bf16[24,1536]{1,0:T(8,128)(2,1)}, bf16[24,1536]{1,0:T(8,128)(2,1)S(1)}, u32[]{:S(2)}, u32[]{:S(2)}) collective-permute-start(bf16[24,1536]{1,0:T(8,128)(2,1)} %get-tuple-element.122), channel_id=1, source_target_pairs={{0,2},{1,66},{2,3},{3,67},{4,0},{5,64},{6,1},{7,65},{8,6},{9,70},{... | collective-permute-start | bytes 221192 | tf_op jit(solution)/shard_map/ppermute | solution.py:532
  298.8 12.5 %collective-permute-start.36 = (bf16[24,1536]{1,0:T(8,128)(2,1)}, bf16[24,1536]{1,0:T(8,128)(2,1)S(1)}, u32[]{:S(2)}, u32[]{:S(2)}) collective-permute-start(bf16[24,1536]{1,0:T(8,128)(2,1)} %get-tuple-element.123), channel_id=1, source_target_pairs={{0,3},{1,67},{2,2},{3,66},{4,1},{5,65},{6,0},{7,64},{8,7},{9,71},{... | collective-permute-start | bytes 221192 | tf_op jit(solution)/shard_map/ppermute | solution.py:532
  (1 other events, 0.7 us)

commit v6 on v5

--- a/solution.py
+++ b/solution.py
@@ -285,7 +285,6 @@
         ),
         out_shape=jax.ShapeDtypeStruct(rows.shape, rows.dtype),
         cost_estimate=cost(1e6, 2 * rows.size * 2),
-        name="pick",
     )(order, rows)
 
 
@@ -390,7 +389,6 @@
             jax.ShapeDtypeStruct((2, D), jnp.float32),
         ],
         cost_estimate=cost(2 * 512 * WIDTH * D, 1.6e7),
-        name="project",
     )(sp, mine[0], mine[1], other[0], other[1], out_weight, out_weight, gate, cotangent)
 
 
@@ -431,7 +429,6 @@
         out_shape=[jax.ShapeDtypeStruct((rows, HALF), jnp.bfloat16)] * 4
         + [jax.ShapeDtypeStruct((4, SHARE, HALF), jnp.bfloat16)] * 4,
         cost_estimate=cost(2 * 1024 * WIDTH * D // 2, 1.2e7),
-        name="weigh",
     )(sp, *scaled, mine[0], mine[1], other[0], other[1])
 
 
@@ -479,7 +476,6 @@
         ),
         out_shape=[jax.ShapeDtypeStruct((SHARE, HALF), jnp.bfloat16)] * 8,
         cost_estimate=cost(5e6, 6e6),
-        name="sum_parts",
     )(sp, *by_x, *by_y)
 
 
@@ -523,7 +519,6 @@
         ),
         out_shape=[jax.ShapeDtypeStruct((SHARE // 4, WIDTH), jnp.bfloat16)] * 4,
         cost_estimate=cost(1e6, 2e6),
-        name="sum_weights",
     )(sp, *low, *high)
 
 
@@ -586,7 +581,8 @@
     d_picked = pick(d_spread, after(plan, near, sp))
     landed = land(d_picked, (ROWS, WIDTH))
     s1, s2, s3 = prep(after(cp, d_picked), qkv, 0)
-    received[0] = (swap(s1, 1), swap(s2, 2), swap(s3, 3))
+    near_keys = (swap(s1, 1), swap(s3, 3))
+    received[0] = (near_keys[0], swap(s2, 2), near_keys[1])
     sp = after(sp, s2)
     att[1], lse[1] = attend(sp, 1, qkv, received[1])
     d_own[1], d_peer[1] = landed[None], to_core(landed)
@@ -598,13 +594,12 @@
         )
 
     own_1, r1, r2, r3 = back(sp, 1)
-    pieces_1 = (swap(r1, 1), swap(r3, 3))
-    pieces_1 = (pieces_1[0], swap(r2, 2), pieces_1[1])
-    att[0], lse[0] = attend(after(sp, r2), 0, qkv, received[0])
+    picked = pick(att_spread, after(inverse, r2))
+    moved = land(picked, (2, ROWS, HALF))
+    pieces_1 = (swap(r1, 1), swap(r2, 2), swap(r3, 3))
+    att[0], lse[0] = attend(after(sp, picked), 0, qkv, received[0])
     att_other = [swap(att[0], 1)]
-    picked = pick(att_spread, after(inverse, lse[0]))
-    moved = land(picked, (2, ROWS, HALF))
-    own_0, *sent_0 = back(after(sp, picked), 0)
+    own_0, *sent_0 = back(after(sp, lse[0]), 0)
     pieces_0 = [swap(rows, 1 + i) for i, rows in enumerate(sent_0)]
     balanced = [att[0], moved]
     att_other.append(swap(moved, 1))

time: 313 us -> 320 us (1.022)
  starting transfers between devices: 74.1 us -> 82.4 us
  waiting for transfers between devices: 116 us -> 112 us
    ppermute x21, waiting for transfers between devices: 51.7 us -> 60.5 us  [swap(): return lax.ppermute(x, 'seq', [(i, i ^ step) for i in range(4)])]
    all_to_all x2, waiting for transfers between devices: 14.6 us -> 7.13 us  [land(): lax.all_to_all(arranged, 'dp', split_axis=0, concat_axis=0, tiled=True)]
    ppermute x21, starting transfers between devices: 12.3 us -> 19.2 us  [swap(): return lax.ppermute(x, 'seq', [(i, i ^ step) for i in range(4)])]
    unnamed x48 -> x50, local copies, waits for them, and re-layouts: 5.37 us -> 7.09 us
where the time goes in v6:
time: 320 us; the launch traced here: 318 us
  Pallas kernels  113 us (35%)
  waiting for transfers between devices  112 us (35%)
  starting transfers between devices  82.4 us (26%)
  local copies, waits for them, and re-layouts  7.43 us (2%)
    ppermute x21, waiting for transfers between devices, swap(): return lax.ppermute(x, 'seq', [(i, i ^ step) for i in range(4)])  60.5 us
    pallas_call x2, Pallas kernels, attend_back(): pl.pallas_call(functools.partial(bwd_kernel, slot), grid_spec=pltpu.Prefe...  24.3 us
    ppermute x6, waiting for transfers between devices, along_x(): return lax.ppermute(x, 'dp', [(g, g ^ step << 3) for g in range(32)])  22.1 us
    ppermute x21, starting transfers between devices, swap(): return lax.ppermute(x, 'seq', [(i, i ^ step) for i in range(4)])  19.2 us
    pallas_call x2, Pallas kernels, attend(): pl.pallas_call(functools.partial(fwd_kernel, slot), grid_spec=pltpu.Prefe...  16.8 us
    pallas_call x2, Pallas kernels, scaled_rows(): pl.pallas_call(functools.partial(rows_kernel, slot), grid_spec=pltpu.Pref...  16.8 us
    all_to_all x2, starting transfers between devices, spread_out(): lax.all_to_all(portions, 'dp', split_axis=0, concat_axis=0, tiled=True)  16.2 us
    all_to_all x2, starting transfers between devices, land(): lax.all_to_all(arranged, 'dp', split_axis=0, concat_axis=0, tiled=True)  15.8 us
  transfers between devices with their start and end apart: 41, of which 15 were waited for; matrix products, arithmetic and copies ran while one was open for 1% of the time, Pallas kernels for 34%

profile of v6, /device:TPU:18, one launch (start us, length us, event | category | flops | bytes accessed | tf_op | source)
XLA Modules:
  0.0 318.3 jit_solution(13963286715827313249)
XLA Ops:
  0.6 2.9 shard_map.102
  3.6 8.4 %shard_map.103 = (bf16[256,1536]{1,0:T(8,128)(2,1)}, bf16[256,1536]{1,0:T(8,128)(2,1)}, bf16[256,1536]{1,0:T(8,128)(2,1)}) custom-call(s32[1,1]{1,0:T(1,128)} %bitcast.6.sp, bf16[2,256,3072]{2,1,0:T(8,128)(2,1)} %cotangent.5, f32[2,3072]{1,0:T(2,128)} %gate.5, bf16[1536,3072]{1,0:T(8,128)(2,1)} %w_other.1), custom_call_target="tpu_custom_call" | custom-call | flops 2415919104 | bytes 13000000 | tf_op jit(solution)/shard_map/pallas_call | solution.py:328
  12.0 8.8 %all-to-all-start = ((bf16[32,8,1536]{2,1,0:T(8,128)(2,1)}), bf16[32,8,1536]{2,1,0:T(8,128)(2,1)S(1)}, u32[]{:S(2)}, u32[]{:S(2)}) async-start(bf16[32,8,1536]{2,1,0:T(8,128)(2,1)} %bitcast.22), calls=%async_computation | async-start | bytes 1572864 | tf_op jit(solution)/shard_map/all_to_all | solution.py:540
  21.1 8.4 %shard_map.104 = (bf16[256,1536]{1,0:T(8,128)(2,1)}, bf16[256,1536]{1,0:T(8,128)(2,1)}, bf16[256,1536]{1,0:T(8,128)(2,1)}) custom-call(s32[1,1]{1,0:T(1,128)} %bitcast.6.sp, bf16[2,256,3072]{2,1,0:T(8,128)(2,1)} %cotangent.5, f32[2,3072]{1,0:T(2,128)} %gate.5, bf16[1536,3072]{1,0:T(8,128)(2,1)} %w_other.1), custom_call_target="tpu_custom_call" | custom-call | flops 2415919104 | bytes 13000000 | tf_op jit(solution)/shard_map/pallas_call | solution.py:328
  30.4 2.8 all-to-all-done.rows
  33.2 0.9 copy-done.6
  34.1 2.9 shard_map.105
  37.0 7.5 %all-to-all-start.1 = ((bf16[32,8,1536]{2,1,0:T(8,128)(2,1)}), bf16[32,8,1536]{2,1,0:T(8,128)(2,1)}, u32[]{:S(2)}, u32[]{:S(2)}) async-start(bf16[32,8,1536]{2,1,0:T(8,128)(2,1)} %shard_map.105), calls=%async_computation.1 | async-start | bytes 1572864 | tf_op jit(solution)/shard_map/all_to_all | solution.py:544
  44.5 1.6 collective-permute-start.2
  46.1 2.2 collective-permute-start.1
  48.3 7.1 %all-to-all-done.1 = bf16[32,8,1536]{2,1,0:T(8,128)(2,1)} async-done(((bf16[32,8,1536]{2,1,0:T(8,128)(2,1)}), bf16[32,8,1536]{2,1,0:T(8,128)(2,1)}, u32[]{:S(2)}, u32[]{:S(2)}) %all-to-all-start.1) | async-done | bytes 786464 | tf_op jit(solution)/shard_map/all_to_all | solution.py:544
  55.4 3.0 shard_map.106
  58.4 14.1 %collective-permute-done.2.k3.v3 = bf16[2,256,768]{2,1,0:T(8,128)(2,1)S(1)} collective-permute-done((bf16[2,256,768]{2,1,0:T(8,128)(2,1)}, bf16[2,256,768]{2,1,0:T(8,128)(2,1)S(1)}, u32[]{:S(2)}, u32[]{:S(2)}) %collective-permute-start.2) | collective-permute-done | bytes 786464 | tf_op jit(solution)/shard_map/ppermute | solution.py:40
  72.5 17.1 %collective-permute-done.1.k2.v2 = bf16[2,256,768]{2,1,0:T(8,128)(2,1)S(1)} collective-permute-done((bf16[2,256,768]{2,1,0:T(8,128)(2,1)S(1)}, bf16[2,256,768]{2,1,0:T(8,128)(2,1)S(1)}, u32[]{:S(2)}, u32[]{:S(2)}) %collective-permute-start.1) | collective-permute-done | bytes 786464 | tf_op jit(solution)/shard_map/ppermute | solution.py:40
  89.6 0.9 copy-done.5
  90.5 1.0 copy-done
  91.5 8.4 %shard_map.107 = (bf16[2,256,768]{2,1,0:T(8,128)(2,1)}, f32[6,8,512]{2,1,0:T(8,128)}) custom-call(s32[2,6]{1,0:T(2,128)} %pad_add_fusion.sp, bf16[2,256,4608]{2,1,0:T(8,128)(2,1)} %v0.7, bf16[2,256,4608]{2,1,0:T(8,128)(2,1)} %v0.7, bf16[2,256,4608]{2,1,0:T(8,128)(2,1)} %v0.7, bf16[3,256,768]{2,1,0:T(8,128)(2,1)} %copy-done, bf16[3,256,768]{2,1,0:T(8,128)(2,1)} %copy-done, ...), custom_call_target="tpu_custom_call" | custom-call | flops 1610612736 | bytes 5000000 | tf_op jit(solution)/shard_map/pallas_call | solution.py:179
  99.9 7.5 %all-to-all-start.2 = ((bf16[32,16,768]{2,1,0:T(8,128)(2,1)}), bf16[32,16,768]{2,1,0:T(8,128)(2,1)S(1)}, u32[]{:S(2)}, u32[]{:S(2)}) async-start(bf16[32,16,768]{2,1,0:T(8,128)(2,1)} %bitcast.16), calls=%async_computation.2 | async-start | bytes 1572864 | tf_op jit(solution)/shard_map/all_to_all | solution.py:540
  107.5 1.3 collective-permute-start.6
  109.4 2.4 collective-permute-start.5
  111.8 12.2 %shard_map.108 = (f32[3,256,768]{2,1,0:T(8,128)}, bf16[3,256,768]{2,1,0:T(8,128)(2,1)}, bf16[2,256,768]{2,1,0:T(8,128)(2,1)}, bf16[2,256,768]{2,1,0:T(8,128)(2,1)}) custom-call(s32[2,6]{1,0:T(2,128)} %pad_add_fusion.sp, bf16[2,256,4608]{2,1,0:T(8,128)(2,1)} %v0.7, bf16[2,256,4608]{2,1,0:T(8,128)(2,1)} %v0.7, bf16[2,256,4608]{2,1,0:T(8,128)(2,1)} %v0.7, ...), custom_call_target="tpu_custom_call" | custom-call | flops 4026531840 | bytes 10000000 | tf_op jit(solution)/shard_map/pallas_call | solution.py:210
  124.0 0.9 copy-done.7
  124.8 2.9 shard_map.109
  127.7 8.3 %all-to-all-start.3 = ((bf16[32,16,768]{2,1,0:T(8,128)(2,1)}), bf16[32,16,768]{2,1,0:T(8,128)(2,1)S(1)}, u32[]{:S(2)}, u32[]{:S(2)}) async-start(bf16[32,16,768]{2,1,0:T(8,128)(2,1)} %shard_map.109), calls=%async_computation.3 | async-start | bytes 1572864 | tf_op jit(solution)/shard_map/all_to_all | solution.py:544
  136.9 22.5 %collective-permute-done.5.k2.v2 = bf16[2,256,768]{2,1,0:T(8,128)(2,1)S(1)} collective-permute-done((bf16[2,256,768]{2,1,0:T(8,128)(2,1)}, bf16[2,256,768]{2,1,0:T(8,128)(2,1)S(1)}, u32[]{:S(2)}, u32[]{:S(2)}) %collective-permute-start.5) | collective-permute-done | bytes 786464 | tf_op jit(solution)/shard_map/ppermute | solution.py:40
  159.4 0.9 copy-done.3
  160.3 1.0 copy-done.1
  161.3 8.4 %shard_map.110 = (bf16[2,256,768]{2,1,0:T(8,128)(2,1)}, f32[6,8,512]{2,1,0:T(8,128)}) custom-call(s32[2,6]{1,0:T(2,128)} %pad_add_fusion.sp, bf16[2,256,4608]{2,1,0:T(8,128)(2,1)} %v0.7, bf16[2,256,4608]{2,1,0:T(8,128)(2,1)} %v0.7, bf16[2,256,4608]{2,1,0:T(8,128)(2,1)} %v0.7, bf16[3,256,768]{2,1,0:T(8,128)(2,1)} %copy-done.1, ...), custom_call_target="tpu_custom_call" | custom-call | flops 1610612736 | bytes 5000000 | tf_op jit(solution)/shard_map/pallas_call | solution.py:179
  170.5 2.2 collective-permute-start.16
  172.7 1.0 collective-permute-start.17
  173.7 12.1 %shard_map.111 = (f32[3,256,768]{2,1,0:T(8,128)}, bf16[3,256,768]{2,1,0:T(8,128)(2,1)}, bf16[2,256,768]{2,1,0:T(8,128)(2,1)}, bf16[2,256,768]{2,1,0:T(8,128)(2,1)}) custom-call(s32[2,6]{1,0:T(2,128)} %pad_add_fusion.sp, bf16[2,256,4608]{2,1,0:T(8,128)(2,1)} %v0.7, bf16[2,256,4608]{2,1,0:T(8,128)(2,1)} %v0.7, bf16[2,256,4608]{2,1,0:T(8,128)(2,1)} %v0.7, ...), custom_call_target="tpu_custom_call" | custom-call | flops 4026531840 | bytes 10000000 | tf_op jit(solution)/shard_map/pallas_call | solution.py:210
  185.9 13.4 %shard_map.112 = (bf16[384,768]{1,0:T(8,128)(2,1)}, bf16[384,768]{1,0:T(8,128)(2,1)}, bf16[384,768]{1,0:T(8,128)(2,1)}, bf16[384,768]{1,0:T(8,128)(2,1)}, bf16[4...) custom-call(s32[2,6]{1,0:T(2,128)} %pad_add_fusion.sp, ...), custom_call_target="tpu_custom_call" | custom-call | flops 4831838208 | bytes 12000000 | tf_op jit(solution)/shard_map/pallas_call | solution.py:419
  199.6 2.1 collective-permute-start.19
  201.7 6.7 %collective-permute-done.17.p3 = bf16[2,256,768]{2,1,0:T(8,128)(2,1)} collective-permute-done((bf16[2,256,768]{2,1,0:T(8,128)(2,1)}, bf16[2,256,768]{2,1,0:T(8,128)(2,1)}, u32[]{:S(2)}, u32[]{:S(2)}) %collective-permute-start.17) | collective-permute-done | bytes 786464 | tf_op jit(solution)/shard_map/ppermute | solution.py:40
  208.4 1.0 collective-permute-start.20
  209.4 1.3 collective-permute-start.21
  210.7 5.0 %collective-permute-done.18.refs_1_ = bf16[384,768]{1,0:T(8,128)(2,1)S(1)} collective-permute-done((bf16[384,768]{1,0:T(8,128)(2,1)}, bf16[384,768]{1,0:T(8,128)(2,1)S(1)}, u32[]{:S(2)}, u32[]{:S(2)}) %collective-permute-start.18) | collective-permute-done | bytes 589856 | tf_op jit(solution)/shard_map/ppermute | solution.py:436
  216.5 0.9 collective-permute-start.26
  217.4 11.0 %collective-permute-done.19.refs_2_ = bf16[384,768]{1,0:T(8,128)(2,1)} collective-permute-done((bf16[384,768]{1,0:T(8,128)(2,1)}, bf16[384,768]{1,0:T(8,128)(2,1)}, u32[]{:S(2)}, u32[]{:S(2)}) %collective-permute-start.19) | collective-permute-done | bytes 589856 | tf_op jit(solution)/shard_map/ppermute | solution.py:436
  228.3 2.4 collective-permute-start.25
  230.8 6.2 %collective-permute-done.20.refs_3_ = bf16[384,768]{1,0:T(8,128)(2,1)} collective-permute-done((bf16[384,768]{1,0:T(8,128)(2,1)}, bf16[384,768]{1,0:T(8,128)(2,1)}, u32[]{:S(2)}, u32[]{:S(2)}) %collective-permute-start.20) | collective-permute-done | bytes 589856 | tf_op jit(solution)/shard_map/ppermute | solution.py:436
  237.0 1.3 collective-permute-start.22
  238.3 1.2 collective-permute-start.23
  239.5 11.0 %shard_map.113 = (bf16[2,256,3072]{2,1,0:T(8,128)(2,1)}, f32[2,3072]{1,0:T(2,128)}) custom-call(s32[2,6]{1,0:T(2,128)} %pad_add_fusion.sp, bf16[2,256,768]{2,1,0:T(8,128)(2,1)} %get-tuple-element.84.att.a0, bf16[2,256,768]{2,1,0:T(8,128)(2,1)} %bitcast.19, bf16[2,256,768]{2,1,0:T(8,128)(2,1)} %collective-permute-done.10.b0, ...), custom_call_target="tpu_custom_call" | custom-call | flops 4831838208 | bytes 16000000 | tf_op jit(solution)/shard_map/pallas_call | solution.py:370
  250.5 5.7 %shard_map.114.rest_0_ = bf16[2,256,4608]{2,1,0:T(8,128)(2,1)} custom-call(s32[2,6]{1,0:T(2,128)} %pad_add_fusion.sp, f32[3,256,768]{2,1,0:T(8,128)} %get-tuple-element.96.own, bf16[3,256,768]{2,1,0:T(8,128)(2,1)} %copy-done.10, bf16[2,256,768]{2,1,0:T(8,128)(2,1)} %copy-done.12, bf16[2,256,768]{2,1,0:T(8,128)(2,1)} %collective-permute-done.17.p3), custom_call_target="tpu_custom_call" | custom-call | flops 1000000 | bytes 10000000 | tf_op jit(solution)/shard_map/pallas_call | solution.py:257
  256.2 9.5 %collective-permute-done.23.refs_7_ = bf16[4,96,768]{2,1,0:T(8,128)(2,1)} collective-permute-done((bf16[4,96,768]{2,1,0:T(8,128)(2,1)}, bf16[4,96,768]{2,1,0:T(8,128)(2,1)}, u32[]{:S(2)}, u32[]{:S(2)}) %collective-permute-start.23) | collective-permute-done | bytes 589856 | tf_op jit(solution)/shard_map/ppermute | solution.py:440
  265.7 4.2 %shard_map.115 = (bf16[96,768]{1,0:T(8,128)(2,1)}, bf16[96,768]{1,0:T(8,128)(2,1)}, bf16[96,768]{1,0:T(8,128)(2,1)}, bf16[96,768]{1,0:T(8,128)(2,1)}, bf16[96,76...) custom-call(s32[2,6]{1,0:T(2,128)} %pad_add_fusion.sp, ...), custom_call_target="tpu_custom_call" | custom-call | flops 5000000 | bytes 6000000 | tf_op jit(solution)/shard_map/pallas_call | solution.py:467
  269.9 1.6 collective-permute-start.27
  271.5 1.0 collective-permute-start.28
  272.5 1.0 collective-permute-start.29
  273.5 2.0 collective-permute-start.30
  275.5 1.2 collective-permute-start.31
  276.8 1.6 collective-permute-start.32
  278.4 1.3 collective-permute-done.28.refs_2_
  279.7 1.2 collective-permute-start.14
  281.1 2.4 collective-permute-start.13
  283.5 5.7 %shard_map.116 = bf16[2,256,4608]{2,1,0:T(8,128)(2,1)} custom-call(s32[2,6]{1,0:T(2,128)} %pad_add_fusion.sp, f32[3,256,768]{2,1,0:T(8,128)} %get-tuple-element.109.own, bf16[3,256,768]{2,1,0:T(8,128)(2,1)} %copy-done.9, bf16[2,256,768]{2,1,0:T(8,128)(2,1)} %collective-permute-done.25.p2, ...), custom_call_target="tpu_custom_call", output_to_operand_aliasing={{}: (5, {})} | custom-call | flops 1000000 | bytes 10000000 | tf_op jit(solution)/shard_map/pallas_call | solution.py:257
  289.9 3.0 shard_map.117
  292.9 6.1 %collective-permute-start.33 = (bf16[24,1536]{1,0:T(8,128)(2,1)}, bf16[24,1536]{1,0:T(8,128)(2,1)S(1)}, u32[]{:S(2)}, u32[]{:S(2)}) collective-permute-start(bf16[24,1536]{1,0:T(8,128)(2,1)} %get-tuple-element.120), channel_id=1, source_target_pairs={{0,0},{1,64},{2,1},{3,65},{4,2},{5,66},{6,3},{7,67},{8,4},{9,68},{... | collective-permute-start | bytes 221192 | tf_op jit(solution)/shard_map/ppermute | solution.py:527
  299.0 2.0 collective-permute-start.34
  301.0 4.1 %collective-permute-start.35 = (bf16[24,1536]{1,0:T(8,128)(2,1)}, bf16[24,1536]{1,0:T(8,128)(2,1)S(1)}, u32[]{:S(2)}, u32[]{:S(2)}) collective-permute-start(bf16[24,1536]{1,0:T(8,128)(2,1)} %get-tuple-element.122), channel_id=1, source_target_pairs={{0,2},{1,66},{2,3},{3,67},{4,0},{5,64},{6,1},{7,65},{8,6},{9,70},{... | collective-permute-start | bytes 221192 | tf_op jit(solution)/shard_map/ppermute | solution.py:527
  305.1 3.3 %collective-permute-start.36 = (bf16[24,1536]{1,0:T(8,128)(2,1)}, bf16[24,1536]{1,0:T(8,128)(2,1)S(1)}, u32[]{:S(2)}, u32[]{:S(2)}) collective-permute-start(bf16[24,1536]{1,0:T(8,128)(2,1)} %get-tuple-element.123), channel_id=1, source_target_pairs={{0,3},{1,67},{2,2},{3,66},{4,1},{5,65},{6,0},{7,64},{8,7},{9,71},{... | collective-permute-start | bytes 221192 | tf_op jit(solution)/shard_map/ppermute | solution.py:527
  309.1 0.9 collective-permute-done.34
  310.4 7.2 %collective-permute-done.36 = bf16[24,1536]{1,0:T(8,128)(2,1)S(1)} collective-permute-done((bf16[24,1536]{1,0:T(8,128)(2,1)}, bf16[24,1536]{1,0:T(8,128)(2,1)S(1)}, u32[]{:S(2)}, u32[]{:S(2)}) %collective-permute-start.36) | collective-permute-done | bytes 73760 | tf_op jit(solution)/shard_map/ppermute | solution.py:527
  (97 shorter events, 7.4 us)
Async XLA Ops:
  3.6 86.1 %collective-permute-start = (bf16[3,256,768]{2,1,0:T(8,128)(2,1)}, bf16[3,256,768]{2,1,0:T(8,128)(2,1)S(1)}, u32[]{:S(2)}, u32[]{:S(2)}) collective-permute-start(bf16[3,256,768]{2,1,0:T(8,128)(2,1)} %get-tuple-element.73), channel_id=1, source_target_pairs={{0,1},{1,0},{2,3},{3,2},{4,5},{5,4},{6,7},{7,6},{8,9},{9,8},{10,11... | collective-permute-start | bytes 3538952 | tf_op jit(solution)/shard_map/ppermute | solution.py:40
  3.6 17.2 %copy-start.23 = (s32[64]{0:T(128)S(1)}, s32[64]{0:T(128)}, u32[]{:S(2)}) copy-start(s32[64]{0:T(128)} %param.11) | copy-start | bytes 772
  3.6 17.3 %copy-start.24 = (s32[64]{0:T(128)S(1)}, s32[64]{0:T(128)}, u32[]{:S(2)}) copy-start(s32[64]{0:T(128)} %param.12) | copy-start | bytes 772
  12.0 21.2 %all-to-all-start = ((bf16[32,8,1536]{2,1,0:T(8,128)(2,1)}), bf16[32,8,1536]{2,1,0:T(8,128)(2,1)S(1)}, u32[]{:S(2)}, u32[]{:S(2)}) async-start(bf16[32,8,1536]{2,1,0:T(8,128)(2,1)} %bitcast.22), calls=%async_computation | async-start | bytes 1572864 | tf_op jit(solution)/shard_map/all_to_all | solution.py:540
  29.5 16.6 %copy-start.22 = (bf16[2,256,768]{2,1,0:T(8,128)(2,1)S(1)}, bf16[2,256,768]{2,1,0:T(8,128)(2,1)}, u32[]{:S(2)}) copy-start(bf16[2,256,768]{2,1,0:T(8,128)(2,1)} %get-tuple-element.64) | copy-start | bytes 2359300
  33.2 0.9 copy-start.6
  37.0 18.4 %all-to-all-start.1 = ((bf16[32,8,1536]{2,1,0:T(8,128)(2,1)}), bf16[32,8,1536]{2,1,0:T(8,128)(2,1)}, u32[]{:S(2)}, u32[]{:S(2)}) async-start(bf16[32,8,1536]{2,1,0:T(8,128)(2,1)} %shard_map.105), calls=%async_computation.1 | async-start | bytes 1572864 | tf_op jit(solution)/shard_map/all_to_all | solution.py:544
  44.5 28.0 %collective-permute-start.2 = (bf16[2,256,768]{2,1,0:T(8,128)(2,1)}, bf16[2,256,768]{2,1,0:T(8,128)(2,1)S(1)}, u32[]{:S(2)}, u32[]{:S(2)}) collective-permute-start(bf16[2,256,768]{2,1,0:T(8,128)(2,1)} %get-tuple-element.74), channel_id=1, source_target_pairs={{0,3},{1,2},{2,1},{3,0},{4,7},{5,6},{6,5},{7,4},{8,11},{9,10},{10,... | collective-permute-start | bytes 2359304 | tf_op jit(solution)/shard_map/ppermute | solution.py:40
  46.1 43.5 %collective-permute-start.1 = (bf16[2,256,768]{2,1,0:T(8,128)(2,1)S(1)}, bf16[2,256,768]{2,1,0:T(8,128)(2,1)S(1)}, u32[]{:S(2)}, u32[]{:S(2)}) collective-permute-start(bf16[2,256,768]{2,1,0:T(8,128)(2,1)S(1)} %copy-done.22), channel_id=1, source_target_pairs={{0,2},{1,3},{2,0},{3,1},{4,6},{5,7},{6,4},{7,5},{8,10},{9,11},{10,... | collective-permute-start | bytes 2359304 | tf_op jit(solution)/shard_map/ppermute | solution.py:40
  55.4 56.3 %collective-permute-start.3 = (bf16[1,256,1536]{2,1,0:T(8,128)(2,1)}, bf16[1,256,1536]{2,1,0:T(8,128)(2,1)}, u32[]{:S(2)}, u32[]{:S(2)}) collective-permute-start(bf16[1,256,1536]{2,1,0:T(8,128)(2,1)} %bitcast.8.do0), channel_id=1, source_target_pairs={{0,1},{1,0},{2,3},{3,2},{4,5},{5,4},{6,7},{7,6},{8,9},{9,8},{10,11... | collective-permute-start | bytes 2359304 | tf_op jit(solution)/shard_map/ppermute | solution.py:40
  58.4 50.4 %copy-start.21 = (s32[32]{0:T(128)S(1)}, s32[32]{0:T(128)}, u32[]{:S(2)}) copy-start(s32[32]{0:T(128)} %order) | copy-start | bytes 388
  72.5 17.1 %copy-start.4 = (bf16[2,256,768]{2,1,0:T(8,128)(2,1)}, bf16[2,256,768]{2,1,0:T(8,128)(2,1)S(1)}, u32[]{:S(2)}) copy-start(bf16[2,256,768]{2,1,0:T(8,128)(2,1)S(1)} %collective-permute-done.2.k3.v3) | copy-start | bytes 2359300
  89.6 0.9 copy-start.5
  90.5 1.0 copy-start
  99.9 24.0 %all-to-all-start.2 = ((bf16[32,16,768]{2,1,0:T(8,128)(2,1)}), bf16[32,16,768]{2,1,0:T(8,128)(2,1)S(1)}, u32[]{:S(2)}, u32[]{:S(2)}) async-start(bf16[32,16,768]{2,1,0:T(8,128)(2,1)} %bitcast.16), calls=%async_computation.2 | async-start | bytes 1572864 | tf_op jit(solution)/shard_map/all_to_all | solution.py:540
  107.4 52.0 %collective-permute-start.4 = (bf16[3,256,768]{2,1,0:T(8,128)(2,1)}, bf16[3,256,768]{2,1,0:T(8,128)(2,1)S(1)}, u32[]{:S(2)}, u32[]{:S(2)}) collective-permute-start(bf16[3,256,768]{2,1,0:T(8,128)(2,1)} %get-tuple-element.80), channel_id=1, source_target_pairs={{0,1},{1,0},{2,3},{3,2},{4,5},{5,4},{6,7},{7,6},{8,9},{9,8},{10,11... | collective-permute-start | bytes 3538952 | tf_op jit(solution)/shard_map/ppermute | solution.py:40
  107.5 29.3 %collective-permute-start.6 = (bf16[2,256,768]{2,1,0:T(8,128)(2,1)}, bf16[2,256,768]{2,1,0:T(8,128)(2,1)S(1)}, u32[]{:S(2)}, u32[]{:S(2)}) collective-permute-start(bf16[2,256,768]{2,1,0:T(8,128)(2,1)} %get-tuple-element.81), channel_id=1, source_target_pairs={{0,3},{1,2},{2,1},{3,0},{4,7},{5,6},{6,5},{7,4},{8,11},{9,10},{10,... | collective-permute-start | bytes 2359304 | tf_op jit(solution)/shard_map/ppermute | solution.py:40
  109.4 50.1 %collective-permute-start.5 = (bf16[2,256,768]{2,1,0:T(8,128)(2,1)}, bf16[2,256,768]{2,1,0:T(8,128)(2,1)S(1)}, u32[]{:S(2)}, u32[]{:S(2)}) collective-permute-start(bf16[2,256,768]{2,1,0:T(8,128)(2,1)} %get-tuple-element.71), channel_id=1, source_target_pairs={{0,2},{1,3},{2,0},{3,1},{4,6},{5,7},{6,4},{7,5},{8,10},{9,11},{10,... | collective-permute-start | bytes 2359304 | tf_op jit(solution)/shard_map/ppermute | solution.py:40
  123.9 0.9 copy-start.7
  127.7 42.1 %all-to-all-start.3 = ((bf16[32,16,768]{2,1,0:T(8,128)(2,1)}), bf16[32,16,768]{2,1,0:T(8,128)(2,1)S(1)}, u32[]{:S(2)}, u32[]{:S(2)}) async-start(bf16[32,16,768]{2,1,0:T(8,128)(2,1)} %shard_map.109), calls=%async_computation.3 | async-start | bytes 1572864 | tf_op jit(solution)/shard_map/all_to_all | solution.py:544
  136.0 34.3 %collective-permute-start.9 = (bf16[256,1536]{1,0:T(8,128)(2,1)}, bf16[256,1536]{1,0:T(8,128)(2,1)}, u32[]{:S(2)}, u32[]{:S(2)}) collective-permute-start(bf16[256,1536]{1,0:T(8,128)(2,1)} %get-tuple-element.90), channel_id=1, source_target_pairs={{0,1},{1,0},{2,3},{3,2},{4,5},{5,4},{6,7},{7,6},{8,9},{9,8},{10,11... | collective-permute-start | bytes 2359304 | tf_op jit(solution)/shard_map/ppermute | solution.py:40
  136.3 34.1 %collective-permute-start.8 = (bf16[256,1536]{1,0:T(8,128)(2,1)}, bf16[256,1536]{1,0:T(8,128)(2,1)}, u32[]{:S(2)}, u32[]{:S(2)}) collective-permute-start(bf16[256,1536]{1,0:T(8,128)(2,1)} %get-tuple-element.88), channel_id=1, source_target_pairs={{0,1},{1,0},{2,3},{3,2},{4,5},{5,4},{6,7},{7,6},{8,9},{9,8},{10,11... | collective-permute-start | bytes 2359304 | tf_op jit(solution)/shard_map/ppermute | solution.py:40
  136.8 22.6 %copy-start.2 = (bf16[2,256,768]{2,1,0:T(8,128)(2,1)}, bf16[2,256,768]{2,1,0:T(8,128)(2,1)S(1)}, u32[]{:S(2)}) copy-start(bf16[2,256,768]{2,1,0:T(8,128)(2,1)S(1)} %collective-permute-done.6.k3.v3) | copy-start | bytes 2359300
  136.8 35.9 %collective-permute-start.7 = (bf16[1,256,1536]{2,1,0:T(8,128)(2,1)}, bf16[1,256,1536]{2,1,0:T(8,128)(2,1)}, u32[]{:S(2)}, u32[]{:S(2)}) collective-permute-start(bf16[1,256,1536]{2,1,0:T(8,128)(2,1)} %bitcast.20), channel_id=1, source_target_pairs={{0,1},{1,0},{2,3},{3,2},{4,5},{5,4},{6,7},{7,6},{8,9},{9,8},{10,11... | collective-permute-start | bytes 2359304 | tf_op jit(solution)/shard_map/ppermute | solution.py:40
  159.4 0.9 copy-start.3
  160.3 1.0 copy-start.1
  169.7 16.1 %collective-permute-start.10 = (bf16[2,256,768]{2,1,0:T(8,128)(2,1)}, bf16[2,256,768]{2,1,0:T(8,128)(2,1)}, u32[]{:S(2)}, u32[]{:S(2)}) collective-permute-start(bf16[2,256,768]{2,1,0:T(8,128)(2,1)} %get-tuple-element.84.att.a0), channel_id=1, source_target_pairs={{0,1},{1,0},{2,3},{3,2},{4,5},{5,4},{6,7},{7,6},{8,9},{9,8},{10,11... | collective-permute-start | bytes 2359304 | tf_op jit(solution)/shard_map/ppermute | solution.py:40
  169.9 16.0 %copy-start.8 = (bf16[32,16,768]{2,1,0:T(8,128)(2,1)}, bf16[32,16,768]{2,1,0:T(8,128)(2,1)S(1)}, u32[]{:S(2)}) copy-start(bf16[32,16,768]{2,1,0:T(8,128)(2,1)S(1)} %all-to-all-done.3) | copy-start | bytes 2359300
  169.9 16.0 %collective-permute-start.11 = (bf16[2,256,768]{2,1,0:T(8,128)(2,1)S(1)}, bf16[2,256,768]{2,1,0:T(8,128)(2,1)}, u32[]{:S(2)}, u32[]{:S(2)}) collective-permute-start(bf16[2,256,768]{2,1,0:T(8,128)(2,1)S(1)} %bitcast.17), channel_id=1, source_target_pairs={{0,1},{1,0},{2,3},{3,2},{4,5},{5,4},{6,7},{7,6},{8,9},{9,8},{10,11... | collective-permute-start | bytes 2359304 | tf_op jit(solution)/shard_map/ppermute | solution.py:40
  170.3 40.3 %collective-permute-start.15 = (bf16[3,256,768]{2,1,0:T(8,128)(2,1)}, bf16[3,256,768]{2,1,0:T(8,128)(2,1)S(1)}, u32[]{:S(2)}, u32[]{:S(2)}) collective-permute-start(bf16[3,256,768]{2,1,0:T(8,128)(2,1)} %get-tuple-element.97), channel_id=1, source_target_pairs={{0,1},{1,0},{2,3},{3,2},{4,5},{5,4},{6,7},{7,6},{8,9},{9,8},{10,11... | collective-permute-start | bytes 3538952 | tf_op jit(solution)/shard_map/ppermute | solution.py:40
  170.5 38.9 %collective-permute-start.16 = (bf16[2,256,768]{2,1,0:T(8,128)(2,1)}, bf16[2,256,768]{2,1,0:T(8,128)(2,1)S(1)}, u32[]{:S(2)}, u32[]{:S(2)}) collective-permute-start(bf16[2,256,768]{2,1,0:T(8,128)(2,1)} %get-tuple-element.77), channel_id=1, source_target_pairs={{0,2},{1,3},{2,0},{3,1},{4,6},{5,7},{6,4},{7,5},{8,10},{9,11},{10,... | collective-permute-start | bytes 2359304 | tf_op jit(solution)/shard_map/ppermute | solution.py:40
  172.7 35.7 %collective-permute-start.17 = (bf16[2,256,768]{2,1,0:T(8,128)(2,1)}, bf16[2,256,768]{2,1,0:T(8,128)(2,1)}, u32[]{:S(2)}, u32[]{:S(2)}) collective-permute-start(bf16[2,256,768]{2,1,0:T(8,128)(2,1)} %get-tuple-element.98), channel_id=1, source_target_pairs={{0,3},{1,2},{2,1},{3,0},{4,7},{5,6},{6,5},{7,4},{8,11},{9,10},{10,... | collective-permute-start | bytes 2359304 | tf_op jit(solution)/shard_map/ppermute | solution.py:40
  199.2 16.4 %collective-permute-start.18 = (bf16[384,768]{1,0:T(8,128)(2,1)}, bf16[384,768]{1,0:T(8,128)(2,1)S(1)}, u32[]{:S(2)}, u32[]{:S(2)}) collective-permute-start(bf16[384,768]{1,0:T(8,128)(2,1)} %get-tuple-element.100), channel_id=1, source_target_pairs={{0,32},{4,36},{8,40},{12,44},{16,48},{20,52},{24,56},{28,60},{32,0... | collective-permute-start | bytes 1769480 | tf_op jit(solution)/shard_map/ppermute | solution.py:436
  199.6 28.8 %collective-permute-start.19 = (bf16[384,768]{1,0:T(8,128)(2,1)}, bf16[384,768]{1,0:T(8,128)(2,1)}, u32[]{:S(2)}, u32[]{:S(2)}) collective-permute-start(bf16[384,768]{1,0:T(8,128)(2,1)} %get-tuple-element.101), channel_id=1, source_target_pairs={{0,64},{4,68},{8,72},{12,76},{16,80},{20,84},{24,88},{28,92},{32,9... | collective-permute-start | bytes 1769480 | tf_op jit(solution)/shard_map/ppermute | solution.py:436
  208.4 28.6 %collective-permute-start.20 = (bf16[384,768]{1,0:T(8,128)(2,1)}, bf16[384,768]{1,0:T(8,128)(2,1)}, u32[]{:S(2)}, u32[]{:S(2)}) collective-permute-start(bf16[384,768]{1,0:T(8,128)(2,1)} %get-tuple-element.102), channel_id=1, source_target_pairs={{0,96},{4,100},{8,104},{12,108},{16,112},{20,116},{24,120},{28,124... | collective-permute-start | bytes 1769480 | tf_op jit(solution)/shard_map/ppermute | solution.py:436
  209.4 6.2 %copy-start.12 = (bf16[2,256,768]{2,1,0:T(8,128)(2,1)}, bf16[2,256,768]{2,1,0:T(8,128)(2,1)S(1)}, u32[]{:S(2)}) copy-start(bf16[2,256,768]{2,1,0:T(8,128)(2,1)S(1)} %collective-permute-done.16.p2) | copy-start | bytes 2359300
  209.4 28.9 %collective-permute-start.21 = (bf16[4,96,768]{2,1,0:T(8,128)(2,1)}, bf16[4,96,768]{2,1,0:T(8,128)(2,1)}, u32[]{:S(2)}, u32[]{:S(2)}) collective-permute-start(bf16[4,96,768]{2,1,0:T(8,128)(2,1)} %get-tuple-element.104), channel_id=1, source_target_pairs={{0,8},{4,12},{8,0},{12,4},{16,24},{20,28},{24,16},{28,20},{32,40},... | collective-permute-start | bytes 1769480 | tf_op jit(solution)/shard_map/ppermute | solution.py:440
  210.7 39.8 %copy-start.10 = (bf16[3,256,768]{2,1,0:T(8,128)(2,1)}, bf16[3,256,768]{2,1,0:T(8,128)(2,1)S(1)}, u32[]{:S(2)}) copy-start(bf16[3,256,768]{2,1,0:T(8,128)(2,1)S(1)} %collective-permute-done.15.p1) | copy-start | bytes 3538948
  210.7 64.9 %collective-permute-start.24 = (bf16[3,256,768]{2,1,0:T(8,128)(2,1)}, bf16[3,256,768]{2,1,0:T(8,128)(2,1)S(1)}, u32[]{:S(2)}, u32[]{:S(2)}) collective-permute-start(bf16[3,256,768]{2,1,0:T(8,128)(2,1)} %get-tuple-element.110), channel_id=1, source_target_pairs={{0,1},{1,0},{2,3},{3,2},{4,5},{5,4},{6,7},{7,6},{8,9},{9,8},{10,11... | collective-permute-start | bytes 3538952 | tf_op jit(solution)/shard_map/ppermute | solution.py:40
  215.6 0.8 copy-start.13
  216.5 56.0 %collective-permute-start.26 = (bf16[2,256,768]{2,1,0:T(8,128)(2,1)}, bf16[2,256,768]{2,1,0:T(8,128)(2,1)S(1)}, u32[]{:S(2)}, u32[]{:S(2)}) collective-permute-start(bf16[2,256,768]{2,1,0:T(8,128)(2,1)} %get-tuple-element.111), channel_id=1, source_target_pairs={{0,3},{1,2},{2,1},{3,0},{4,7},{5,6},{6,5},{7,4},{8,11},{9,10},{10,... | collective-permute-start | bytes 2359304 | tf_op jit(solution)/shard_map/ppermute | solution.py:40
  228.3 45.2 %collective-permute-start.25 = (bf16[2,256,768]{2,1,0:T(8,128)(2,1)}, bf16[2,256,768]{2,1,0:T(8,128)(2,1)}, u32[]{:S(2)}, u32[]{:S(2)}) collective-permute-start(bf16[2,256,768]{2,1,0:T(8,128)(2,1)} %get-tuple-element.85), channel_id=1, source_target_pairs={{0,2},{1,3},{2,0},{3,1},{4,6},{5,7},{6,4},{7,5},{8,10},{9,11},{10,... | collective-permute-start | bytes 2359304 | tf_op jit(solution)/shard_map/ppermute | solution.py:40
  237.0 19.2 %collective-permute-start.22 = (bf16[4,96,768]{2,1,0:T(8,128)(2,1)}, bf16[4,96,768]{2,1,0:T(8,128)(2,1)}, u32[]{:S(2)}, u32[]{:S(2)}) collective-permute-start(bf16[4,96,768]{2,1,0:T(8,128)(2,1)} %get-tuple-element.105), channel_id=1, source_target_pairs={{0,16},{4,20},{8,24},{12,28},{16,0},{20,4},{24,8},{28,12},{32,48},... | collective-permute-start | bytes 1769480 | tf_op jit(solution)/shard_map/ppermute | solution.py:440
  238.3 27.4 %collective-permute-start.23 = (bf16[4,96,768]{2,1,0:T(8,128)(2,1)}, bf16[4,96,768]{2,1,0:T(8,128)(2,1)}, u32[]{:S(2)}, u32[]{:S(2)}) collective-permute-start(bf16[4,96,768]{2,1,0:T(8,128)(2,1)} %get-tuple-element.106), channel_id=1, source_target_pairs={{0,24},{4,28},{8,16},{12,20},{16,8},{20,12},{24,0},{28,4},{32,56},... | collective-permute-start | bytes 1769480 | tf_op jit(solution)/shard_map/ppermute | solution.py:440
  265.7 14.0 %copy-start.20 = (f32[2,3072]{1,0:T(2,128)S(1)}, f32[2,3072]{1,0:T(2,128)}, u32[]{:S(2)}) copy-start(f32[2,3072]{1,0:T(2,128)} %get-tuple-element.94) | copy-start | bytes 73732
  269.9 6.8 %collective-permute-start.27 = (bf16[96,768]{1,0:T(8,128)(2,1)}, bf16[96,768]{1,0:T(8,128)(2,1)S(1)}, u32[]{:S(2)}, u32[]{:S(2)}) collective-permute-start(bf16[96,768]{1,0:T(8,128)(2,1)} %get-tuple-element.113), channel_id=1, source_target_pairs={{0,8},{4,12},{8,0},{12,4},{16,24},{20,28},{24,16},{28,20},{32,40},... | collective-permute-start | bytes 442376 | tf_op jit(solution)/shard_map/ppermute | solution.py:440
  271.5 8.2 %collective-permute-start.28 = (bf16[96,768]{1,0:T(8,128)(2,1)}, bf16[96,768]{1,0:T(8,128)(2,1)S(1)}, u32[]{:S(2)}, u32[]{:S(2)}) collective-permute-start(bf16[96,768]{1,0:T(8,128)(2,1)} %get-tuple-element.114), channel_id=1, source_target_pairs={{0,16},{4,20},{8,24},{12,28},{16,0},{20,4},{24,8},{28,12},{32,48},... | collective-permute-start | bytes 442376 | tf_op jit(solution)/shard_map/ppermute | solution.py:440
  272.5 11.0 %copy-start.11 = (bf16[2,256,768]{2,1,0:T(8,128)(2,1)}, bf16[2,256,768]{2,1,0:T(8,128)(2,1)S(1)}, u32[]{:S(2)}) copy-start(bf16[2,256,768]{2,1,0:T(8,128)(2,1)S(1)} %collective-permute-done.26.p3) | copy-start | bytes 2359300
  272.5 8.6 %collective-permute-start.29 = (bf16[96,768]{1,0:T(8,128)(2,1)}, bf16[96,768]{1,0:T(8,128)(2,1)S(1)}, u32[]{:S(2)}, u32[]{:S(2)}) collective-permute-start(bf16[96,768]{1,0:T(8,128)(2,1)} %get-tuple-element.115), channel_id=1, source_target_pairs={{0,24},{4,28},{8,16},{12,20},{16,8},{20,12},{24,0},{28,4},{32,56},... | collective-permute-start | bytes 442376 | tf_op jit(solution)/shard_map/ppermute | solution.py:440
  273.5 9.9 %collective-permute-start.30 = (bf16[96,768]{1,0:T(8,128)(2,1)}, bf16[96,768]{1,0:T(8,128)(2,1)S(1)}, u32[]{:S(2)}, u32[]{:S(2)}) collective-permute-start(bf16[96,768]{1,0:T(8,128)(2,1)} %get-tuple-element.117), channel_id=1, source_target_pairs={{0,32},{4,36},{8,40},{12,44},{16,48},{20,52},{24,56},{28,60},{32,0... | collective-permute-start | bytes 442376 | tf_op jit(solution)/shard_map/ppermute | solution.py:436
  275.5 7.9 %copy-start.9 = (bf16[3,256,768]{2,1,0:T(8,128)(2,1)}, bf16[3,256,768]{2,1,0:T(8,128)(2,1)S(1)}, u32[]{:S(2)}) copy-start(bf16[3,256,768]{2,1,0:T(8,128)(2,1)S(1)} %collective-permute-done.24.p1) | copy-start | bytes 3538948
  275.5 13.6 %collective-permute-start.31 = (bf16[96,768]{1,0:T(8,128)(2,1)}, bf16[96,768]{1,0:T(8,128)(2,1)S(1)}, u32[]{:S(2)}, u32[]{:S(2)}) collective-permute-start(bf16[96,768]{1,0:T(8,128)(2,1)} %get-tuple-element.118), channel_id=1, source_target_pairs={{0,64},{4,68},{8,72},{12,76},{16,80},{20,84},{24,88},{28,92},{32,9... | collective-permute-start | bytes 442376 | tf_op jit(solution)/shard_map/ppermute | solution.py:436
  276.8 12.4 %copy-start.14 = (bf16[96,768]{1,0:T(8,128)(2,1)}, bf16[96,768]{1,0:T(8,128)(2,1)S(1)}, u32[]{:S(2)}) copy-start(bf16[96,768]{1,0:T(8,128)(2,1)S(1)} %collective-permute-done.27.refs_1_) | copy-start | bytes 442372
  276.8 12.5 %collective-permute-start.32 = (bf16[96,768]{1,0:T(8,128)(2,1)}, bf16[96,768]{1,0:T(8,128)(2,1)S(1)}, u32[]{:S(2)}, u32[]{:S(2)}) collective-permute-start(bf16[96,768]{1,0:T(8,128)(2,1)} %get-tuple-element.119), channel_id=1, source_target_pairs={{0,96},{4,100},{8,104},{12,108},{16,112},{20,116},{24,120},{28,124... | collective-permute-start | bytes 442376 | tf_op jit(solution)/shard_map/ppermute | solution.py:436
  279.7 9.5 %copy-start.15 = (bf16[96,768]{1,0:T(8,128)(2,1)}, bf16[96,768]{1,0:T(8,128)(2,1)S(1)}, u32[]{:S(2)}) copy-start(bf16[96,768]{1,0:T(8,128)(2,1)S(1)} %collective-permute-done.28.refs_2_) | copy-start | bytes 442372
  279.7 21.3 %collective-permute-start.14 = (f32[2,3072]{1,0:T(2,128)S(1)}, f32[2,3072]{1,0:T(2,128)S(1)}, u32[]{:S(2)}, u32[]{:S(2)}) collective-permute-start(f32[2,3072]{1,0:T(2,128)S(1)} %copy-done.20), channel_id=1, source_target_pairs={{0,3},{1,2},{2,1},{3,0},{4,7},{5,6},{6,5},{7,4},{8,11},{9,10},{10,... | collective-permute-start | bytes 73736 | tf_op jit(solution)/shard_map/ppermute | solution.py:40
  281.1 8.1 %copy-start.16 = (bf16[96,768]{1,0:T(8,128)(2,1)}, bf16[96,768]{1,0:T(8,128)(2,1)S(1)}, u32[]{:S(2)}) copy-start(bf16[96,768]{1,0:T(8,128)(2,1)S(1)} %collective-permute-done.29.refs_3_) | copy-start | bytes 442372
  281.1 24.1 %collective-permute-start.13 = (f32[2,3072]{1,0:T(2,128)S(1)}, f32[2,3072]{1,0:T(2,128)S(1)}, u32[]{:S(2)}, u32[]{:S(2)}) collective-permute-start(f32[2,3072]{1,0:T(2,128)S(1)} %copy-done.20), channel_id=1, source_target_pairs={{0,2},{1,3},{2,0},{3,1},{4,6},{5,7},{6,4},{7,5},{8,10},{9,11},{10,... | collective-permute-start | bytes 73736 | tf_op jit(solution)/shard_map/ppermute | solution.py:40
  283.5 5.7 %copy-start.17 = (bf16[96,768]{1,0:T(8,128)(2,1)}, bf16[96,768]{1,0:T(8,128)(2,1)S(1)}, u32[]{:S(2)}) copy-start(bf16[96,768]{1,0:T(8,128)(2,1)S(1)} %collective-permute-done.30.refs_5_) | copy-start | bytes 442372
  283.5 25.0 %collective-permute-start.12 = (f32[2,3072]{1,0:T(2,128)S(1)}, f32[2,3072]{1,0:T(2,128)S(1)}, u32[]{:S(2)}, u32[]{:S(2)}) collective-permute-start(f32[2,3072]{1,0:T(2,128)S(1)} %copy-done.20), channel_id=1, source_target_pairs={{0,1},{1,0},{2,3},{3,2},{4,5},{5,4},{6,7},{7,6},{8,9},{9,8},{10,11... | collective-permute-start | bytes 73736 | tf_op jit(solution)/shard_map/ppermute | solution.py:40
  292.9 16.2 %collective-permute-start.33 = (bf16[24,1536]{1,0:T(8,128)(2,1)}, bf16[24,1536]{1,0:T(8,128)(2,1)S(1)}, u32[]{:S(2)}, u32[]{:S(2)}) collective-permute-start(bf16[24,1536]{1,0:T(8,128)(2,1)} %get-tuple-element.120), channel_id=1, source_target_pairs={{0,0},{1,64},{2,1},{3,65},{4,2},{5,66},{6,3},{7,67},{8,4},{9,68},{... | collective-permute-start | bytes 221192 | tf_op jit(solution)/shard_map/ppermute | solution.py:527
  299.0 10.9 %collective-permute-start.34 = (bf16[24,1536]{1,0:T(8,128)(2,1)}, bf16[24,1536]{1,0:T(8,128)(2,1)S(1)}, u32[]{:S(2)}, u32[]{:S(2)}) collective-permute-start(bf16[24,1536]{1,0:T(8,128)(2,1)} %get-tuple-element.121), channel_id=1, source_target_pairs={{0,1},{1,65},{2,0},{3,64},{4,3},{5,67},{6,2},{7,66},{8,5},{9,69},{... | collective-permute-start | bytes 221192 | tf_op jit(solution)/shard_map/ppermute | solution.py:527
  301.0 9.4 %collective-permute-start.35 = (bf16[24,1536]{1,0:T(8,128)(2,1)}, bf16[24,1536]{1,0:T(8,128)(2,1)S(1)}, u32[]{:S(2)}, u32[]{:S(2)}) collective-permute-start(bf16[24,1536]{1,0:T(8,128)(2,1)} %get-tuple-element.122), channel_id=1, source_target_pairs={{0,2},{1,66},{2,3},{3,67},{4,0},{5,64},{6,1},{7,65},{8,6},{9,70},{... | collective-permute-start | bytes 221192 | tf_op jit(solution)/shard_map/ppermute | solution.py:527
  305.1 12.5 %collective-permute-start.36 = (bf16[24,1536]{1,0:T(8,128)(2,1)}, bf16[24,1536]{1,0:T(8,128)(2,1)S(1)}, u32[]{:S(2)}, u32[]{:S(2)}) collective-permute-start(bf16[24,1536]{1,0:T(8,128)(2,1)} %get-tuple-element.123), channel_id=1, source_target_pairs={{0,3},{1,67},{2,2},{3,66},{4,1},{5,65},{6,0},{7,64},{8,7},{9,71},{... | collective-permute-start | bytes 221192 | tf_op jit(solution)/shard_map/ppermute | solution.py:527
  (2 other events, 1.3 us)

commit v7 on v6

--- a/solution.py
+++ b/solution.py
@@ -140,12 +140,12 @@
             grad_v = v_part if block == 0 else grad_v + v_part
             grad_q = (mm(keys, d_scores, TN) * SCALE).T
             if block == 0:
-                own[0, :, cols] = grad_q
+                own[0, :, cols] = grad_q.astype(low)
             else:
                 r1[0, :, cols] = grad_q.astype(low)
         grad_k = grad_k * SCALE
-        own[1, :, cols] = grad_k[:ROWS]
-        own[2, :, cols] = grad_v[:ROWS]
+        own[1, :, cols] = grad_k[:ROWS].astype(low)
+        own[2, :, cols] = grad_v[:ROWS].astype(low)
         r1[1, :, cols] = grad_k[ROWS : 2 * ROWS].astype(low)
         r1[2, :, cols] = grad_v[ROWS : 2 * ROWS].astype(low)
         r2[0, :, cols] = grad_k[2 * ROWS : 3 * ROWS].astype(low)
@@ -222,7 +222,7 @@
             out_specs=[piece(3), piece(3), piece(2), piece(2)],
         ),
         out_shape=[
-            shape(3, jnp.float32),
+            shape(3, jnp.bfloat16),
             shape(3, jnp.bfloat16),
             shape(2, jnp.bfloat16),
             shape(2, jnp.bfloat16),
@@ -236,7 +236,7 @@
     core = sp[0, 0]
     member = pl.program_id(0)
     crossing = jnp.where(member > 0, 1.0, 0.0)
-    mine = own[0] + crossing * p2[0].astype(jnp.float32)
+    mine = own[0].astype(jnp.float32) + crossing * p2[0].astype(jnp.float32)
     other = p1[0].astype(jnp.float32) + crossing * p3[0].astype(jnp.float32)
     first = core == 0
     out[0, :, :HALF] = jnp.where(first, mine, other).astype(jnp.bfloat16)

time: 320 us -> 320 us (level)
    unnamed x50 -> x46, local copies, waits for them, and re-layouts: 7.09 us -> 6.28 us
where the time goes in v7:
time: 320 us; the launch traced here: 318 us
  waiting for transfers between devices  114 us (36%)
  Pallas kernels  112 us (35%)
  starting transfers between devices  82.6 us (26%)
  local copies, waits for them, and re-layouts  6.62 us (2%)
    ppermute x21, waiting for transfers between devices, swap(): return lax.ppermute(x, 'seq', [(i, i ^ step) for i in range(4)])  61.1 us
    pallas_call x2, Pallas kernels, attend_back(): pl.pallas_call(functools.partial(bwd_kernel, slot), grid_spec=pltpu.Prefe...  23.8 us
    ppermute x6, waiting for transfers between devices, along_x(): return lax.ppermute(x, 'dp', [(g, g ^ step << 3) for g in range(32)])  23 us
    ppermute x21, starting transfers between devices, swap(): return lax.ppermute(x, 'seq', [(i, i ^ step) for i in range(4)])  19.2 us
    pallas_call x2, Pallas kernels, scaled_rows(): pl.pallas_call(functools.partial(rows_kernel, slot), grid_spec=pltpu.Pref...  16.8 us
    pallas_call x2, Pallas kernels, attend(): pl.pallas_call(functools.partial(fwd_kernel, slot), grid_spec=pltpu.Prefe...  16.8 us
    all_to_all x2, starting transfers between devices, spread_out(): lax.all_to_all(portions, 'dp', split_axis=0, concat_axis=0, tiled=True)  16.3 us
    all_to_all x2, starting transfers between devices, land(): lax.all_to_all(arranged, 'dp', split_axis=0, concat_axis=0, tiled=True)  15.9 us
  transfers between devices with their start and end apart: 41, of which 15 were waited for; matrix products, arithmetic and copies ran while one was open for 1% of the time, Pallas kernels for 34%

profile of v7, /device:TPU:18, one launch (start us, length us, event | category | flops | bytes accessed | tf_op | source)
XLA Modules:
  0.0 318.4 jit_solution(6042218379087322353)
XLA Ops:
  0.6 2.9 shard_map.102
  3.6 8.4 %shard_map.103 = (bf16[256,1536]{1,0:T(8,128)(2,1)}, bf16[256,1536]{1,0:T(8,128)(2,1)}, bf16[256,1536]{1,0:T(8,128)(2,1)}) custom-call(s32[1,1]{1,0:T(1,128)} %bitcast.6.sp, bf16[2,256,3072]{2,1,0:T(8,128)(2,1)} %cotangent.5, f32[2,3072]{1,0:T(2,128)} %gate.5, bf16[1536,3072]{1,0:T(8,128)(2,1)} %w_other.1), custom_call_target="tpu_custom_call" | custom-call | flops 2415919104 | bytes 13000000 | tf_op jit(solution)/shard_map/pallas_call | solution.py:328
  12.0 8.9 %all-to-all-start = ((bf16[32,8,1536]{2,1,0:T(8,128)(2,1)}), bf16[32,8,1536]{2,1,0:T(8,128)(2,1)S(1)}, u32[]{:S(2)}, u32[]{:S(2)}) async-start(bf16[32,8,1536]{2,1,0:T(8,128)(2,1)} %bitcast.22), calls=%async_computation | async-start | bytes 1572864 | tf_op jit(solution)/shard_map/all_to_all | solution.py:540
  21.3 8.4 %shard_map.104 = (bf16[256,1536]{1,0:T(8,128)(2,1)}, bf16[256,1536]{1,0:T(8,128)(2,1)}, bf16[256,1536]{1,0:T(8,128)(2,1)}) custom-call(s32[1,1]{1,0:T(1,128)} %bitcast.6.sp, bf16[2,256,3072]{2,1,0:T(8,128)(2,1)} %cotangent.5, f32[2,3072]{1,0:T(2,128)} %gate.5, bf16[1536,3072]{1,0:T(8,128)(2,1)} %w_other.1), custom_call_target="tpu_custom_call" | custom-call | flops 2415919104 | bytes 13000000 | tf_op jit(solution)/shard_map/pallas_call | solution.py:328
  30.6 2.7 all-to-all-done.rows
  33.3 0.9 copy-done.6
  34.2 2.9 shard_map.105
  37.1 7.6 %all-to-all-start.1 = ((bf16[32,8,1536]{2,1,0:T(8,128)(2,1)}), bf16[32,8,1536]{2,1,0:T(8,128)(2,1)}, u32[]{:S(2)}, u32[]{:S(2)}) async-start(bf16[32,8,1536]{2,1,0:T(8,128)(2,1)} %shard_map.105), calls=%async_computation.1 | async-start | bytes 1572864 | tf_op jit(solution)/shard_map/all_to_all | solution.py:544
  44.8 1.6 collective-permute-start.2
  46.3 2.2 collective-permute-start.1
  48.5 7.1 %all-to-all-done.1 = bf16[32,8,1536]{2,1,0:T(8,128)(2,1)} async-done(((bf16[32,8,1536]{2,1,0:T(8,128)(2,1)}), bf16[32,8,1536]{2,1,0:T(8,128)(2,1)}, u32[]{:S(2)}, u32[]{:S(2)}) %all-to-all-start.1) | async-done | bytes 786464 | tf_op jit(solution)/shard_map/all_to_all | solution.py:544
  55.7 2.9 shard_map.106
  58.6 14.2 %collective-permute-done.2.k3.v3 = bf16[2,256,768]{2,1,0:T(8,128)(2,1)S(1)} collective-permute-done((bf16[2,256,768]{2,1,0:T(8,128)(2,1)}, bf16[2,256,768]{2,1,0:T(8,128)(2,1)S(1)}, u32[]{:S(2)}, u32[]{:S(2)}) %collective-permute-start.2) | collective-permute-done | bytes 786464 | tf_op jit(solution)/shard_map/ppermute | solution.py:40
  72.8 17.1 %collective-permute-done.1.k2.v2 = bf16[2,256,768]{2,1,0:T(8,128)(2,1)S(1)} collective-permute-done((bf16[2,256,768]{2,1,0:T(8,128)(2,1)S(1)}, bf16[2,256,768]{2,1,0:T(8,128)(2,1)S(1)}, u32[]{:S(2)}, u32[]{:S(2)}) %collective-permute-start.1) | collective-permute-done | bytes 786464 | tf_op jit(solution)/shard_map/ppermute | solution.py:40
  89.9 0.9 copy-done.5
  90.8 1.0 copy-done
  91.8 8.4 %shard_map.107 = (bf16[2,256,768]{2,1,0:T(8,128)(2,1)}, f32[6,8,512]{2,1,0:T(8,128)}) custom-call(s32[2,6]{1,0:T(2,128)} %pad_add_fusion.sp, bf16[2,256,4608]{2,1,0:T(8,128)(2,1)} %v0.7, bf16[2,256,4608]{2,1,0:T(8,128)(2,1)} %v0.7, bf16[2,256,4608]{2,1,0:T(8,128)(2,1)} %v0.7, bf16[3,256,768]{2,1,0:T(8,128)(2,1)} %copy-done, bf16[3,256,768]{2,1,0:T(8,128)(2,1)} %copy-done, ...), custom_call_target="tpu_custom_call" | custom-call | flops 1610612736 | bytes 5000000 | tf_op jit(solution)/shard_map/pallas_call | solution.py:179
  100.2 7.5 %all-to-all-start.2 = ((bf16[32,16,768]{2,1,0:T(8,128)(2,1)}), bf16[32,16,768]{2,1,0:T(8,128)(2,1)S(1)}, u32[]{:S(2)}, u32[]{:S(2)}) async-start(bf16[32,16,768]{2,1,0:T(8,128)(2,1)} %bitcast.16), calls=%async_computation.2 | async-start | bytes 1572864 | tf_op jit(solution)/shard_map/all_to_all | solution.py:540
  107.8 1.2 collective-permute-start.6
  109.6 2.4 collective-permute-start.5
  112.0 12.0 %shard_map.108 = (bf16[3,256,768]{2,1,0:T(8,128)(2,1)}, bf16[3,256,768]{2,1,0:T(8,128)(2,1)}, bf16[2,256,768]{2,1,0:T(8,128)(2,1)}, bf16[2,256,768]{2,1,0:T(8,128)(2,1)}) custom-call(s32[2,6]{1,0:T(2,128)} %pad_add_fusion.sp, bf16[2,256,4608]{2,1,0:T(8,128)(2,1)} %v0.7, bf16[2,256,4608]{2,1,0:T(8,128)(2,1)} %v0.7, bf16[2,256,4608]{2,1,0:T(8,128)(2,1)} %v0.7, ...), custom_call_target="tpu_custom_call" | custom-call | flops 4026531840 | bytes 10000000 | tf_op jit(solution)/shard_map/pallas_call | solution.py:210
  124.0 0.9 copy-done.7
  124.9 2.9 shard_map.109
  127.8 8.3 %all-to-all-start.3 = ((bf16[32,16,768]{2,1,0:T(8,128)(2,1)}), bf16[32,16,768]{2,1,0:T(8,128)(2,1)S(1)}, u32[]{:S(2)}, u32[]{:S(2)}) async-start(bf16[32,16,768]{2,1,0:T(8,128)(2,1)} %shard_map.109), calls=%async_computation.3 | async-start | bytes 1572864 | tf_op jit(solution)/shard_map/all_to_all | solution.py:544
  136.9 22.7 %collective-permute-done.5.k2.v2 = bf16[2,256,768]{2,1,0:T(8,128)(2,1)S(1)} collective-permute-done((bf16[2,256,768]{2,1,0:T(8,128)(2,1)}, bf16[2,256,768]{2,1,0:T(8,128)(2,1)S(1)}, u32[]{:S(2)}, u32[]{:S(2)}) %collective-permute-start.5) | collective-permute-done | bytes 786464 | tf_op jit(solution)/shard_map/ppermute | solution.py:40
  159.7 0.9 copy-done.3
  160.6 1.0 copy-done.1
  161.6 8.4 %shard_map.110 = (bf16[2,256,768]{2,1,0:T(8,128)(2,1)}, f32[6,8,512]{2,1,0:T(8,128)}) custom-call(s32[2,6]{1,0:T(2,128)} %pad_add_fusion.sp, bf16[2,256,4608]{2,1,0:T(8,128)(2,1)} %v0.7, bf16[2,256,4608]{2,1,0:T(8,128)(2,1)} %v0.7, bf16[2,256,4608]{2,1,0:T(8,128)(2,1)} %v0.7, bf16[3,256,768]{2,1,0:T(8,128)(2,1)} %copy-done.1, ...), custom_call_target="tpu_custom_call" | custom-call | flops 1610612736 | bytes 5000000 | tf_op jit(solution)/shard_map/pallas_call | solution.py:179
  170.7 2.3 collective-permute-start.16
  173.0 1.0 collective-permute-start.17
  174.0 11.9 %shard_map.111 = (bf16[3,256,768]{2,1,0:T(8,128)(2,1)}, bf16[3,256,768]{2,1,0:T(8,128)(2,1)}, bf16[2,256,768]{2,1,0:T(8,128)(2,1)}, bf16[2,256,768]{2,1,0:T(8,128)(2,1)}) custom-call(s32[2,6]{1,0:T(2,128)} %pad_add_fusion.sp, bf16[2,256,4608]{2,1,0:T(8,128)(2,1)} %v0.7, bf16[2,256,4608]{2,1,0:T(8,128)(2,1)} %v0.7, bf16[2,256,4608]{2,1,0:T(8,128)(2,1)} %v0.7, ...), custom_call_target="tpu_custom_call" | custom-call | flops 4026531840 | bytes 10000000 | tf_op jit(solution)/shard_map/pallas_call | solution.py:210
  185.9 13.4 %shard_map.112 = (bf16[384,768]{1,0:T(8,128)(2,1)}, bf16[384,768]{1,0:T(8,128)(2,1)}, bf16[384,768]{1,0:T(8,128)(2,1)}, bf16[384,768]{1,0:T(8,128)(2,1)}, bf16[4...) custom-call(s32[2,6]{1,0:T(2,128)} %pad_add_fusion.sp, ...), custom_call_target="tpu_custom_call" | custom-call | flops 4831838208 | bytes 12000000 | tf_op jit(solution)/shard_map/pallas_call | solution.py:419
  199.6 2.1 collective-permute-start.19
  201.7 7.0 %collective-permute-done.17.p3 = bf16[2,256,768]{2,1,0:T(8,128)(2,1)} collective-permute-done((bf16[2,256,768]{2,1,0:T(8,128)(2,1)}, bf16[2,256,768]{2,1,0:T(8,128)(2,1)}, u32[]{:S(2)}, u32[]{:S(2)}) %collective-permute-start.17) | collective-permute-done | bytes 786464 | tf_op jit(solution)/shard_map/ppermute | solution.py:40
  208.7 1.0 collective-permute-start.20
  209.7 1.3 collective-permute-start.21
  211.0 4.8 %collective-permute-done.18.refs_1_ = bf16[384,768]{1,0:T(8,128)(2,1)} collective-permute-done((bf16[384,768]{1,0:T(8,128)(2,1)}, bf16[384,768]{1,0:T(8,128)(2,1)}, u32[]{:S(2)}, u32[]{:S(2)}) %collective-permute-start.18) | collective-permute-done | bytes 589856 | tf_op jit(solution)/shard_map/ppermute | solution.py:436
  215.8 0.9 collective-permute-start.26
  216.6 11.7 %collective-permute-done.19.refs_2_ = bf16[384,768]{1,0:T(8,128)(2,1)} collective-permute-done((bf16[384,768]{1,0:T(8,128)(2,1)}, bf16[384,768]{1,0:T(8,128)(2,1)}, u32[]{:S(2)}, u32[]{:S(2)}) %collective-permute-start.19) | collective-permute-done | bytes 589856 | tf_op jit(solution)/shard_map/ppermute | solution.py:436
  228.3 2.5 collective-permute-start.25
  230.8 6.5 %collective-permute-done.20.refs_3_ = bf16[384,768]{1,0:T(8,128)(2,1)} collective-permute-done((bf16[384,768]{1,0:T(8,128)(2,1)}, bf16[384,768]{1,0:T(8,128)(2,1)}, u32[]{:S(2)}, u32[]{:S(2)}) %collective-permute-start.20) | collective-permute-done | bytes 589856 | tf_op jit(solution)/shard_map/ppermute | solution.py:436
  237.3 1.3 collective-permute-start.22
  238.6 1.2 collective-permute-start.23
  239.7 11.1 %shard_map.113 = (bf16[2,256,3072]{2,1,0:T(8,128)(2,1)}, f32[2,3072]{1,0:T(2,128)}) custom-call(s32[2,6]{1,0:T(2,128)} %pad_add_fusion.sp, bf16[2,256,768]{2,1,0:T(8,128)(2,1)} %get-tuple-element.84.att.a0, bf16[2,256,768]{2,1,0:T(8,128)(2,1)} %bitcast.19, bf16[2,256,768]{2,1,0:T(8,128)(2,1)} %collective-permute-done.10.b0, ...), custom_call_target="tpu_custom_call" | custom-call | flops 4831838208 | bytes 16000000 | tf_op jit(solution)/shard_map/pallas_call | solution.py:370
  250.8 5.5 %shard_map.114.rest_0_ = bf16[2,256,4608]{2,1,0:T(8,128)(2,1)} custom-call(s32[2,6]{1,0:T(2,128)} %pad_add_fusion.sp, bf16[3,256,768]{2,1,0:T(8,128)(2,1)} %get-tuple-element.96.own, bf16[3,256,768]{2,1,0:T(8,128)(2,1)} %copy-done.9, bf16[2,256,768]{2,1,0:T(8,128)(2,1)} %copy-done.11, bf16[2,256,768]{2,1,0:T(8,128)(2,1)} %collective-permute-done.17.p3), custom_call_target="tpu_custom_call" | custom-call | flops 1000000 | bytes 10000000 | tf_op jit(solution)/shard_map/pallas_call | solution.py:257
  256.3 9.7 %collective-permute-done.23.refs_7_ = bf16[4,96,768]{2,1,0:T(8,128)(2,1)} collective-permute-done((bf16[4,96,768]{2,1,0:T(8,128)(2,1)}, bf16[4,96,768]{2,1,0:T(8,128)(2,1)}, u32[]{:S(2)}, u32[]{:S(2)}) %collective-permute-start.23) | collective-permute-done | bytes 589856 | tf_op jit(solution)/shard_map/ppermute | solution.py:440
  266.0 4.2 %shard_map.115 = (bf16[96,768]{1,0:T(8,128)(2,1)}, bf16[96,768]{1,0:T(8,128)(2,1)}, bf16[96,768]{1,0:T(8,128)(2,1)}, bf16[96,768]{1,0:T(8,128)(2,1)}, bf16[96,76...) custom-call(s32[2,6]{1,0:T(2,128)} %pad_add_fusion.sp, ...), custom_call_target="tpu_custom_call" | custom-call | flops 5000000 | bytes 6000000 | tf_op jit(solution)/shard_map/pallas_call | solution.py:467
  270.2 1.6 collective-permute-start.27
  271.8 1.0 collective-permute-start.28
  272.8 1.0 collective-permute-start.29
  273.8 2.0 collective-permute-start.30
  275.8 1.2 collective-permute-start.31
  277.0 1.6 collective-permute-start.32
  278.7 1.3 collective-permute-done.28.refs_2_
  280.0 1.2 collective-permute-start.14
  281.3 2.4 collective-permute-start.13
  283.8 5.5 %shard_map.116 = bf16[2,256,4608]{2,1,0:T(8,128)(2,1)} custom-call(s32[2,6]{1,0:T(2,128)} %pad_add_fusion.sp, bf16[3,256,768]{2,1,0:T(8,128)(2,1)} %get-tuple-element.109.own, bf16[3,256,768]{2,1,0:T(8,128)(2,1)} %copy-done.10, bf16[2,256,768]{2,1,0:T(8,128)(2,1)} %collective-permute-done.25.p2, ...), custom_call_target="tpu_custom_call", output_to_operand_aliasing={{}: (5, {})} | custom-call | flops 1000000 | bytes 10000000 | tf_op jit(solution)/shard_map/pallas_call | solution.py:257
  290.0 3.0 shard_map.117
  293.0 6.1 %collective-permute-start.33 = (bf16[24,1536]{1,0:T(8,128)(2,1)}, bf16[24,1536]{1,0:T(8,128)(2,1)S(1)}, u32[]{:S(2)}, u32[]{:S(2)}) collective-permute-start(bf16[24,1536]{1,0:T(8,128)(2,1)} %get-tuple-element.120), channel_id=1, source_target_pairs={{0,0},{1,64},{2,1},{3,65},{4,2},{5,66},{6,3},{7,67},{8,4},{9,68},{... | collective-permute-start | bytes 221192 | tf_op jit(solution)/shard_map/ppermute | solution.py:527
  299.1 2.0 collective-permute-start.34
  301.1 4.1 %collective-permute-start.35 = (bf16[24,1536]{1,0:T(8,128)(2,1)}, bf16[24,1536]{1,0:T(8,128)(2,1)S(1)}, u32[]{:S(2)}, u32[]{:S(2)}) collective-permute-start(bf16[24,1536]{1,0:T(8,128)(2,1)} %get-tuple-element.122), channel_id=1, source_target_pairs={{0,2},{1,66},{2,3},{3,67},{4,0},{5,64},{6,1},{7,65},{8,6},{9,70},{... | collective-permute-start | bytes 221192 | tf_op jit(solution)/shard_map/ppermute | solution.py:527
  305.2 3.3 %collective-permute-start.36 = (bf16[24,1536]{1,0:T(8,128)(2,1)}, bf16[24,1536]{1,0:T(8,128)(2,1)S(1)}, u32[]{:S(2)}, u32[]{:S(2)}) collective-permute-start(bf16[24,1536]{1,0:T(8,128)(2,1)} %get-tuple-element.123), channel_id=1, source_target_pairs={{0,3},{1,67},{2,2},{3,66},{4,1},{5,65},{6,0},{7,64},{8,7},{9,71},{... | collective-permute-start | bytes 221192 | tf_op jit(solution)/shard_map/ppermute | solution.py:527
  309.2 0.9 collective-permute-done.34
  310.4 7.2 %collective-permute-done.36 = bf16[24,1536]{1,0:T(8,128)(2,1)S(1)} collective-permute-done((bf16[24,1536]{1,0:T(8,128)(2,1)}, bf16[24,1536]{1,0:T(8,128)(2,1)S(1)}, u32[]{:S(2)}, u32[]{:S(2)}) %collective-permute-start.36) | collective-permute-done | bytes 73760 | tf_op jit(solution)/shard_map/ppermute | solution.py:527
  (93 shorter events, 6.5 us)
Async XLA Ops:
  3.6 86.3 %collective-permute-start = (bf16[3,256,768]{2,1,0:T(8,128)(2,1)}, bf16[3,256,768]{2,1,0:T(8,128)(2,1)S(1)}, u32[]{:S(2)}, u32[]{:S(2)}) collective-permute-start(bf16[3,256,768]{2,1,0:T(8,128)(2,1)} %get-tuple-element.73), channel_id=1, source_target_pairs={{0,1},{1,0},{2,3},{3,2},{4,5},{5,4},{6,7},{7,6},{8,9},{9,8},{10,11... | collective-permute-start | bytes 3538952 | tf_op jit(solution)/shard_map/ppermute | solution.py:40
  12.0 8.9 %copy-start.21 = (s32[64]{0:T(128)S(1)}, s32[64]{0:T(128)}, u32[]{:S(2)}) copy-start(s32[64]{0:T(128)} %param.11) | copy-start | bytes 772
  12.0 9.0 %copy-start.22 = (s32[64]{0:T(128)S(1)}, s32[64]{0:T(128)}, u32[]{:S(2)}) copy-start(s32[64]{0:T(128)} %param.12) | copy-start | bytes 772
  12.0 21.3 %all-to-all-start = ((bf16[32,8,1536]{2,1,0:T(8,128)(2,1)}), bf16[32,8,1536]{2,1,0:T(8,128)(2,1)S(1)}, u32[]{:S(2)}, u32[]{:S(2)}) async-start(bf16[32,8,1536]{2,1,0:T(8,128)(2,1)} %bitcast.22), calls=%async_computation | async-start | bytes 1572864 | tf_op jit(solution)/shard_map/all_to_all | solution.py:540
  33.3 0.9 copy-start.6
  37.1 9.2 %copy-start.20 = (bf16[2,256,768]{2,1,0:T(8,128)(2,1)S(1)}, bf16[2,256,768]{2,1,0:T(8,128)(2,1)}, u32[]{:S(2)}) copy-start(bf16[2,256,768]{2,1,0:T(8,128)(2,1)} %get-tuple-element.64) | copy-start | bytes 2359300
  37.1 18.5 %all-to-all-start.1 = ((bf16[32,8,1536]{2,1,0:T(8,128)(2,1)}), bf16[32,8,1536]{2,1,0:T(8,128)(2,1)}, u32[]{:S(2)}, u32[]{:S(2)}) async-start(bf16[32,8,1536]{2,1,0:T(8,128)(2,1)} %shard_map.105), calls=%async_computation.1 | async-start | bytes 1572864 | tf_op jit(solution)/shard_map/all_to_all | solution.py:544
  44.8 28.0 %collective-permute-start.2 = (bf16[2,256,768]{2,1,0:T(8,128)(2,1)}, bf16[2,256,768]{2,1,0:T(8,128)(2,1)S(1)}, u32[]{:S(2)}, u32[]{:S(2)}) collective-permute-start(bf16[2,256,768]{2,1,0:T(8,128)(2,1)} %get-tuple-element.74), channel_id=1, source_target_pairs={{0,3},{1,2},{2,1},{3,0},{4,7},{5,6},{6,5},{7,4},{8,11},{9,10},{10,... | collective-permute-start | bytes 2359304 | tf_op jit(solution)/shard_map/ppermute | solution.py:40
  46.3 43.5 %collective-permute-start.1 = (bf16[2,256,768]{2,1,0:T(8,128)(2,1)S(1)}, bf16[2,256,768]{2,1,0:T(8,128)(2,1)S(1)}, u32[]{:S(2)}, u32[]{:S(2)}) collective-permute-start(bf16[2,256,768]{2,1,0:T(8,128)(2,1)S(1)} %copy-done.20), channel_id=1, source_target_pairs={{0,2},{1,3},{2,0},{3,1},{4,6},{5,7},{6,4},{7,5},{8,10},{9,11},{10,... | collective-permute-start | bytes 2359304 | tf_op jit(solution)/shard_map/ppermute | solution.py:40
  55.7 56.4 %collective-permute-start.3 = (bf16[1,256,1536]{2,1,0:T(8,128)(2,1)}, bf16[1,256,1536]{2,1,0:T(8,128)(2,1)}, u32[]{:S(2)}, u32[]{:S(2)}) collective-permute-start(bf16[1,256,1536]{2,1,0:T(8,128)(2,1)} %bitcast.8.do0), channel_id=1, source_target_pairs={{0,1},{1,0},{2,3},{3,2},{4,5},{5,4},{6,7},{7,6},{8,9},{9,8},{10,11... | collective-permute-start | bytes 2359304 | tf_op jit(solution)/shard_map/ppermute | solution.py:40
  72.8 17.1 %copy-start.4 = (bf16[2,256,768]{2,1,0:T(8,128)(2,1)}, bf16[2,256,768]{2,1,0:T(8,128)(2,1)S(1)}, u32[]{:S(2)}) copy-start(bf16[2,256,768]{2,1,0:T(8,128)(2,1)S(1)} %collective-permute-done.2.k3.v3) | copy-start | bytes 2359300
  89.9 0.9 copy-start.5
  90.8 1.0 copy-start
  100.2 8.8 %copy-start.19 = (s32[32]{0:T(128)S(1)}, s32[32]{0:T(128)}, u32[]{:S(2)}) copy-start(s32[32]{0:T(128)} %order) | copy-start | bytes 388
  100.2 23.8 %all-to-all-start.2 = ((bf16[32,16,768]{2,1,0:T(8,128)(2,1)}), bf16[32,16,768]{2,1,0:T(8,128)(2,1)S(1)}, u32[]{:S(2)}, u32[]{:S(2)}) async-start(bf16[32,16,768]{2,1,0:T(8,128)(2,1)} %bitcast.16), calls=%async_computation.2 | async-start | bytes 1572864 | tf_op jit(solution)/shard_map/all_to_all | solution.py:540
  107.7 52.0 %collective-permute-start.4 = (bf16[3,256,768]{2,1,0:T(8,128)(2,1)}, bf16[3,256,768]{2,1,0:T(8,128)(2,1)S(1)}, u32[]{:S(2)}, u32[]{:S(2)}) collective-permute-start(bf16[3,256,768]{2,1,0:T(8,128)(2,1)} %get-tuple-element.80), channel_id=1, source_target_pairs={{0,1},{1,0},{2,3},{3,2},{4,5},{5,4},{6,7},{7,6},{8,9},{9,8},{10,11... | collective-permute-start | bytes 3538952 | tf_op jit(solution)/shard_map/ppermute | solution.py:40
  107.8 29.1 %collective-permute-start.6 = (bf16[2,256,768]{2,1,0:T(8,128)(2,1)}, bf16[2,256,768]{2,1,0:T(8,128)(2,1)S(1)}, u32[]{:S(2)}, u32[]{:S(2)}) collective-permute-start(bf16[2,256,768]{2,1,0:T(8,128)(2,1)} %get-tuple-element.81), channel_id=1, source_target_pairs={{0,3},{1,2},{2,1},{3,0},{4,7},{5,6},{6,5},{7,4},{8,11},{9,10},{10,... | collective-permute-start | bytes 2359304 | tf_op jit(solution)/shard_map/ppermute | solution.py:40
  109.6 50.1 %collective-permute-start.5 = (bf16[2,256,768]{2,1,0:T(8,128)(2,1)}, bf16[2,256,768]{2,1,0:T(8,128)(2,1)S(1)}, u32[]{:S(2)}, u32[]{:S(2)}) collective-permute-start(bf16[2,256,768]{2,1,0:T(8,128)(2,1)} %get-tuple-element.71), channel_id=1, source_target_pairs={{0,2},{1,3},{2,0},{3,1},{4,6},{5,7},{6,4},{7,5},{8,10},{9,11},{10,... | collective-permute-start | bytes 2359304 | tf_op jit(solution)/shard_map/ppermute | solution.py:40
  124.0 0.9 copy-start.7
  127.8 42.3 %all-to-all-start.3 = ((bf16[32,16,768]{2,1,0:T(8,128)(2,1)}), bf16[32,16,768]{2,1,0:T(8,128)(2,1)S(1)}, u32[]{:S(2)}, u32[]{:S(2)}) async-start(bf16[32,16,768]{2,1,0:T(8,128)(2,1)} %shard_map.109), calls=%async_computation.3 | async-start | bytes 1572864 | tf_op jit(solution)/shard_map/all_to_all | solution.py:544
  136.1 34.5 %collective-permute-start.9 = (bf16[256,1536]{1,0:T(8,128)(2,1)}, bf16[256,1536]{1,0:T(8,128)(2,1)}, u32[]{:S(2)}, u32[]{:S(2)}) collective-permute-start(bf16[256,1536]{1,0:T(8,128)(2,1)} %get-tuple-element.90), channel_id=1, source_target_pairs={{0,1},{1,0},{2,3},{3,2},{4,5},{5,4},{6,7},{7,6},{8,9},{9,8},{10,11... | collective-permute-start | bytes 2359304 | tf_op jit(solution)/shard_map/ppermute | solution.py:40
  136.4 34.4 %collective-permute-start.8 = (bf16[256,1536]{1,0:T(8,128)(2,1)}, bf16[256,1536]{1,0:T(8,128)(2,1)}, u32[]{:S(2)}, u32[]{:S(2)}) collective-permute-start(bf16[256,1536]{1,0:T(8,128)(2,1)} %get-tuple-element.88), channel_id=1, source_target_pairs={{0,1},{1,0},{2,3},{3,2},{4,5},{5,4},{6,7},{7,6},{8,9},{9,8},{10,11... | collective-permute-start | bytes 2359304 | tf_op jit(solution)/shard_map/ppermute | solution.py:40
  136.9 22.9 %copy-start.2 = (bf16[2,256,768]{2,1,0:T(8,128)(2,1)}, bf16[2,256,768]{2,1,0:T(8,128)(2,1)S(1)}, u32[]{:S(2)}) copy-start(bf16[2,256,768]{2,1,0:T(8,128)(2,1)S(1)} %collective-permute-done.6.k3.v3) | copy-start | bytes 2359300
  136.9 36.1 %collective-permute-start.7 = (bf16[1,256,1536]{2,1,0:T(8,128)(2,1)}, bf16[1,256,1536]{2,1,0:T(8,128)(2,1)}, u32[]{:S(2)}, u32[]{:S(2)}) collective-permute-start(bf16[1,256,1536]{2,1,0:T(8,128)(2,1)} %bitcast.20), channel_id=1, source_target_pairs={{0,1},{1,0},{2,3},{3,2},{4,5},{5,4},{6,7},{7,6},{8,9},{9,8},{10,11... | collective-permute-start | bytes 2359304 | tf_op jit(solution)/shard_map/ppermute | solution.py:40
  159.7 0.9 copy-start.3
  160.6 1.0 copy-start.1
  170.0 15.9 %collective-permute-start.10 = (bf16[2,256,768]{2,1,0:T(8,128)(2,1)}, bf16[2,256,768]{2,1,0:T(8,128)(2,1)}, u32[]{:S(2)}, u32[]{:S(2)}) collective-permute-start(bf16[2,256,768]{2,1,0:T(8,128)(2,1)} %get-tuple-element.84.att.a0), channel_id=1, source_target_pairs={{0,1},{1,0},{2,3},{3,2},{4,5},{5,4},{6,7},{7,6},{8,9},{9,8},{10,11... | collective-permute-start | bytes 2359304 | tf_op jit(solution)/shard_map/ppermute | solution.py:40
  170.1 15.7 %copy-start.8 = (bf16[32,16,768]{2,1,0:T(8,128)(2,1)}, bf16[32,16,768]{2,1,0:T(8,128)(2,1)S(1)}, u32[]{:S(2)}) copy-start(bf16[32,16,768]{2,1,0:T(8,128)(2,1)S(1)} %all-to-all-done.3) | copy-start | bytes 2359300
  170.1 15.8 %collective-permute-start.11 = (bf16[2,256,768]{2,1,0:T(8,128)(2,1)S(1)}, bf16[2,256,768]{2,1,0:T(8,128)(2,1)}, u32[]{:S(2)}, u32[]{:S(2)}) collective-permute-start(bf16[2,256,768]{2,1,0:T(8,128)(2,1)S(1)} %bitcast.17), channel_id=1, source_target_pairs={{0,1},{1,0},{2,3},{3,2},{4,5},{5,4},{6,7},{7,6},{8,9},{9,8},{10,11... | collective-permute-start | bytes 2359304 | tf_op jit(solution)/shard_map/ppermute | solution.py:40
  170.6 40.3 %collective-permute-start.15 = (bf16[3,256,768]{2,1,0:T(8,128)(2,1)}, bf16[3,256,768]{2,1,0:T(8,128)(2,1)S(1)}, u32[]{:S(2)}, u32[]{:S(2)}) collective-permute-start(bf16[3,256,768]{2,1,0:T(8,128)(2,1)} %get-tuple-element.97), channel_id=1, source_target_pairs={{0,1},{1,0},{2,3},{3,2},{4,5},{5,4},{6,7},{7,6},{8,9},{9,8},{10,11... | collective-permute-start | bytes 3538952 | tf_op jit(solution)/shard_map/ppermute | solution.py:40
  170.7 38.9 %collective-permute-start.16 = (bf16[2,256,768]{2,1,0:T(8,128)(2,1)}, bf16[2,256,768]{2,1,0:T(8,128)(2,1)S(1)}, u32[]{:S(2)}, u32[]{:S(2)}) collective-permute-start(bf16[2,256,768]{2,1,0:T(8,128)(2,1)} %get-tuple-element.77), channel_id=1, source_target_pairs={{0,2},{1,3},{2,0},{3,1},{4,6},{5,7},{6,4},{7,5},{8,10},{9,11},{10,... | collective-permute-start | bytes 2359304 | tf_op jit(solution)/shard_map/ppermute | solution.py:40
  173.0 35.7 %collective-permute-start.17 = (bf16[2,256,768]{2,1,0:T(8,128)(2,1)}, bf16[2,256,768]{2,1,0:T(8,128)(2,1)}, u32[]{:S(2)}, u32[]{:S(2)}) collective-permute-start(bf16[2,256,768]{2,1,0:T(8,128)(2,1)} %get-tuple-element.98), channel_id=1, source_target_pairs={{0,3},{1,2},{2,1},{3,0},{4,7},{5,6},{6,5},{7,4},{8,11},{9,10},{10,... | collective-permute-start | bytes 2359304 | tf_op jit(solution)/shard_map/ppermute | solution.py:40
  199.2 16.5 %collective-permute-start.18 = (bf16[384,768]{1,0:T(8,128)(2,1)}, bf16[384,768]{1,0:T(8,128)(2,1)}, u32[]{:S(2)}, u32[]{:S(2)}) collective-permute-start(bf16[384,768]{1,0:T(8,128)(2,1)} %get-tuple-element.100), channel_id=1, source_target_pairs={{0,32},{4,36},{8,40},{12,44},{16,48},{20,52},{24,56},{28,60},{32,0... | collective-permute-start | bytes 1769480 | tf_op jit(solution)/shard_map/ppermute | solution.py:436
  199.6 28.8 %collective-permute-start.19 = (bf16[384,768]{1,0:T(8,128)(2,1)}, bf16[384,768]{1,0:T(8,128)(2,1)}, u32[]{:S(2)}, u32[]{:S(2)}) collective-permute-start(bf16[384,768]{1,0:T(8,128)(2,1)} %get-tuple-element.101), channel_id=1, source_target_pairs={{0,64},{4,68},{8,72},{12,76},{16,80},{20,84},{24,88},{28,92},{32,9... | collective-permute-start | bytes 1769480 | tf_op jit(solution)/shard_map/ppermute | solution.py:436
  208.7 28.6 %collective-permute-start.20 = (bf16[384,768]{1,0:T(8,128)(2,1)}, bf16[384,768]{1,0:T(8,128)(2,1)}, u32[]{:S(2)}, u32[]{:S(2)}) collective-permute-start(bf16[384,768]{1,0:T(8,128)(2,1)} %get-tuple-element.102), channel_id=1, source_target_pairs={{0,96},{4,100},{8,104},{12,108},{16,112},{20,116},{24,120},{28,124... | collective-permute-start | bytes 1769480 | tf_op jit(solution)/shard_map/ppermute | solution.py:436
  209.7 41.2 %copy-start.11 = (bf16[2,256,768]{2,1,0:T(8,128)(2,1)}, bf16[2,256,768]{2,1,0:T(8,128)(2,1)S(1)}, u32[]{:S(2)}) copy-start(bf16[2,256,768]{2,1,0:T(8,128)(2,1)S(1)} %collective-permute-done.16.p2) | copy-start | bytes 2359300
  209.7 28.9 %collective-permute-start.21 = (bf16[4,96,768]{2,1,0:T(8,128)(2,1)}, bf16[4,96,768]{2,1,0:T(8,128)(2,1)}, u32[]{:S(2)}, u32[]{:S(2)}) collective-permute-start(bf16[4,96,768]{2,1,0:T(8,128)(2,1)} %get-tuple-element.104), channel_id=1, source_target_pairs={{0,8},{4,12},{8,0},{12,4},{16,24},{20,28},{24,16},{28,20},{32,40},... | collective-permute-start | bytes 1769480 | tf_op jit(solution)/shard_map/ppermute | solution.py:440
  210.9 39.9 %copy-start.9 = (bf16[3,256,768]{2,1,0:T(8,128)(2,1)}, bf16[3,256,768]{2,1,0:T(8,128)(2,1)S(1)}, u32[]{:S(2)}) copy-start(bf16[3,256,768]{2,1,0:T(8,128)(2,1)S(1)} %collective-permute-done.15.p1) | copy-start | bytes 3538948
  211.0 64.9 %collective-permute-start.24 = (bf16[3,256,768]{2,1,0:T(8,128)(2,1)}, bf16[3,256,768]{2,1,0:T(8,128)(2,1)S(1)}, u32[]{:S(2)}, u32[]{:S(2)}) collective-permute-start(bf16[3,256,768]{2,1,0:T(8,128)(2,1)} %get-tuple-element.110), channel_id=1, source_target_pairs={{0,1},{1,0},{2,3},{3,2},{4,5},{5,4},{6,7},{7,6},{8,9},{9,8},{10,11... | collective-permute-start | bytes 3538952 | tf_op jit(solution)/shard_map/ppermute | solution.py:40
  215.8 57.0 %collective-permute-start.26 = (bf16[2,256,768]{2,1,0:T(8,128)(2,1)}, bf16[2,256,768]{2,1,0:T(8,128)(2,1)}, u32[]{:S(2)}, u32[]{:S(2)}) collective-permute-start(bf16[2,256,768]{2,1,0:T(8,128)(2,1)} %get-tuple-element.111), channel_id=1, source_target_pairs={{0,3},{1,2},{2,1},{3,0},{4,7},{5,6},{6,5},{7,4},{8,11},{9,10},{10,... | collective-permute-start | bytes 2359304 | tf_op jit(solution)/shard_map/ppermute | solution.py:40
  228.3 45.4 %collective-permute-start.25 = (bf16[2,256,768]{2,1,0:T(8,128)(2,1)}, bf16[2,256,768]{2,1,0:T(8,128)(2,1)}, u32[]{:S(2)}, u32[]{:S(2)}) collective-permute-start(bf16[2,256,768]{2,1,0:T(8,128)(2,1)} %get-tuple-element.85), channel_id=1, source_target_pairs={{0,2},{1,3},{2,0},{3,1},{4,6},{5,7},{6,4},{7,5},{8,10},{9,11},{10,... | collective-permute-start | bytes 2359304 | tf_op jit(solution)/shard_map/ppermute | solution.py:40
  237.3 19.1 %collective-permute-start.22 = (bf16[4,96,768]{2,1,0:T(8,128)(2,1)}, bf16[4,96,768]{2,1,0:T(8,128)(2,1)}, u32[]{:S(2)}, u32[]{:S(2)}) collective-permute-start(bf16[4,96,768]{2,1,0:T(8,128)(2,1)} %get-tuple-element.105), channel_id=1, source_target_pairs={{0,16},{4,20},{8,24},{12,28},{16,0},{20,4},{24,8},{28,12},{32,48},... | collective-permute-start | bytes 1769480 | tf_op jit(solution)/shard_map/ppermute | solution.py:440
  238.6 27.4 %collective-permute-start.23 = (bf16[4,96,768]{2,1,0:T(8,128)(2,1)}, bf16[4,96,768]{2,1,0:T(8,128)(2,1)}, u32[]{:S(2)}, u32[]{:S(2)}) collective-permute-start(bf16[4,96,768]{2,1,0:T(8,128)(2,1)} %get-tuple-element.106), channel_id=1, source_target_pairs={{0,24},{4,28},{8,16},{12,20},{16,8},{20,12},{24,0},{28,4},{32,56},... | collective-permute-start | bytes 1769480 | tf_op jit(solution)/shard_map/ppermute | solution.py:440
  266.0 14.0 %copy-start.18 = (f32[2,3072]{1,0:T(2,128)S(1)}, f32[2,3072]{1,0:T(2,128)}, u32[]{:S(2)}) copy-start(f32[2,3072]{1,0:T(2,128)} %get-tuple-element.94) | copy-start | bytes 73732
  270.2 6.8 %collective-permute-start.27 = (bf16[96,768]{1,0:T(8,128)(2,1)}, bf16[96,768]{1,0:T(8,128)(2,1)S(1)}, u32[]{:S(2)}, u32[]{:S(2)}) collective-permute-start(bf16[96,768]{1,0:T(8,128)(2,1)} %get-tuple-element.113), channel_id=1, source_target_pairs={{0,8},{4,12},{8,0},{12,4},{16,24},{20,28},{24,16},{28,20},{32,40},... | collective-permute-start | bytes 442376 | tf_op jit(solution)/shard_map/ppermute | solution.py:440
  271.8 8.2 %collective-permute-start.28 = (bf16[96,768]{1,0:T(8,128)(2,1)}, bf16[96,768]{1,0:T(8,128)(2,1)S(1)}, u32[]{:S(2)}, u32[]{:S(2)}) collective-permute-start(bf16[96,768]{1,0:T(8,128)(2,1)} %get-tuple-element.114), channel_id=1, source_target_pairs={{0,16},{4,20},{8,24},{12,28},{16,0},{20,4},{24,8},{28,12},{32,48},... | collective-permute-start | bytes 442376 | tf_op jit(solution)/shard_map/ppermute | solution.py:440
  272.8 8.6 %collective-permute-start.29 = (bf16[96,768]{1,0:T(8,128)(2,1)}, bf16[96,768]{1,0:T(8,128)(2,1)S(1)}, u32[]{:S(2)}, u32[]{:S(2)}) collective-permute-start(bf16[96,768]{1,0:T(8,128)(2,1)} %get-tuple-element.115), channel_id=1, source_target_pairs={{0,24},{4,28},{8,16},{12,20},{16,8},{20,12},{24,0},{28,4},{32,56},... | collective-permute-start | bytes 442376 | tf_op jit(solution)/shard_map/ppermute | solution.py:440
  273.8 10.0 %collective-permute-start.30 = (bf16[96,768]{1,0:T(8,128)(2,1)}, bf16[96,768]{1,0:T(8,128)(2,1)S(1)}, u32[]{:S(2)}, u32[]{:S(2)}) collective-permute-start(bf16[96,768]{1,0:T(8,128)(2,1)} %get-tuple-element.117), channel_id=1, source_target_pairs={{0,32},{4,36},{8,40},{12,44},{16,48},{20,52},{24,56},{28,60},{32,0... | collective-permute-start | bytes 442376 | tf_op jit(solution)/shard_map/ppermute | solution.py:436
  275.8 7.9 %copy-start.10 = (bf16[3,256,768]{2,1,0:T(8,128)(2,1)}, bf16[3,256,768]{2,1,0:T(8,128)(2,1)S(1)}, u32[]{:S(2)}) copy-start(bf16[3,256,768]{2,1,0:T(8,128)(2,1)S(1)} %collective-permute-done.24.p1) | copy-start | bytes 3538948
  275.8 13.4 %collective-permute-start.31 = (bf16[96,768]{1,0:T(8,128)(2,1)}, bf16[96,768]{1,0:T(8,128)(2,1)S(1)}, u32[]{:S(2)}, u32[]{:S(2)}) collective-permute-start(bf16[96,768]{1,0:T(8,128)(2,1)} %get-tuple-element.118), channel_id=1, source_target_pairs={{0,64},{4,68},{8,72},{12,76},{16,80},{20,84},{24,88},{28,92},{32,9... | collective-permute-start | bytes 442376 | tf_op jit(solution)/shard_map/ppermute | solution.py:436
  277.0 12.2 %copy-start.12 = (bf16[96,768]{1,0:T(8,128)(2,1)}, bf16[96,768]{1,0:T(8,128)(2,1)S(1)}, u32[]{:S(2)}) copy-start(bf16[96,768]{1,0:T(8,128)(2,1)S(1)} %collective-permute-done.27.refs_1_) | copy-start | bytes 442372
  277.0 12.3 %collective-permute-start.32 = (bf16[96,768]{1,0:T(8,128)(2,1)}, bf16[96,768]{1,0:T(8,128)(2,1)S(1)}, u32[]{:S(2)}, u32[]{:S(2)}) collective-permute-start(bf16[96,768]{1,0:T(8,128)(2,1)} %get-tuple-element.119), channel_id=1, source_target_pairs={{0,96},{4,100},{8,104},{12,108},{16,112},{20,116},{24,120},{28,124... | collective-permute-start | bytes 442376 | tf_op jit(solution)/shard_map/ppermute | solution.py:436
  280.0 9.3 %copy-start.13 = (bf16[96,768]{1,0:T(8,128)(2,1)}, bf16[96,768]{1,0:T(8,128)(2,1)S(1)}, u32[]{:S(2)}) copy-start(bf16[96,768]{1,0:T(8,128)(2,1)S(1)} %collective-permute-done.28.refs_2_) | copy-start | bytes 442372
  280.0 21.1 %collective-permute-start.14 = (f32[2,3072]{1,0:T(2,128)S(1)}, f32[2,3072]{1,0:T(2,128)S(1)}, u32[]{:S(2)}, u32[]{:S(2)}) collective-permute-start(f32[2,3072]{1,0:T(2,128)S(1)} %copy-done.18), channel_id=1, source_target_pairs={{0,3},{1,2},{2,1},{3,0},{4,7},{5,6},{6,5},{7,4},{8,11},{9,10},{10,... | collective-permute-start | bytes 73736 | tf_op jit(solution)/shard_map/ppermute | solution.py:40
  281.3 7.9 %copy-start.14 = (bf16[96,768]{1,0:T(8,128)(2,1)}, bf16[96,768]{1,0:T(8,128)(2,1)S(1)}, u32[]{:S(2)}) copy-start(bf16[96,768]{1,0:T(8,128)(2,1)S(1)} %collective-permute-done.29.refs_3_) | copy-start | bytes 442372
  281.3 23.9 %collective-permute-start.13 = (f32[2,3072]{1,0:T(2,128)S(1)}, f32[2,3072]{1,0:T(2,128)S(1)}, u32[]{:S(2)}, u32[]{:S(2)}) collective-permute-start(f32[2,3072]{1,0:T(2,128)S(1)} %copy-done.18), channel_id=1, source_target_pairs={{0,2},{1,3},{2,0},{3,1},{4,6},{5,7},{6,4},{7,5},{8,10},{9,11},{10,... | collective-permute-start | bytes 73736 | tf_op jit(solution)/shard_map/ppermute | solution.py:40
  283.7 5.5 %copy-start.15 = (bf16[96,768]{1,0:T(8,128)(2,1)}, bf16[96,768]{1,0:T(8,128)(2,1)S(1)}, u32[]{:S(2)}) copy-start(bf16[96,768]{1,0:T(8,128)(2,1)S(1)} %collective-permute-done.30.refs_5_) | copy-start | bytes 442372
  283.7 24.8 %collective-permute-start.12 = (f32[2,3072]{1,0:T(2,128)S(1)}, f32[2,3072]{1,0:T(2,128)S(1)}, u32[]{:S(2)}, u32[]{:S(2)}) collective-permute-start(f32[2,3072]{1,0:T(2,128)S(1)} %copy-done.18), channel_id=1, source_target_pairs={{0,1},{1,0},{2,3},{3,2},{4,5},{5,4},{6,7},{7,6},{8,9},{9,8},{10,11... | collective-permute-start | bytes 73736 | tf_op jit(solution)/shard_map/ppermute | solution.py:40
  289.3 0.7 copy-start.16
  289.3 0.7 copy-start.17
  293.0 16.2 %collective-permute-start.33 = (bf16[24,1536]{1,0:T(8,128)(2,1)}, bf16[24,1536]{1,0:T(8,128)(2,1)S(1)}, u32[]{:S(2)}, u32[]{:S(2)}) collective-permute-start(bf16[24,1536]{1,0:T(8,128)(2,1)} %get-tuple-element.120), channel_id=1, source_target_pairs={{0,0},{1,64},{2,1},{3,65},{4,2},{5,66},{6,3},{7,67},{8,4},{9,68},{... | collective-permute-start | bytes 221192 | tf_op jit(solution)/shard_map/ppermute | solution.py:527
  299.1 10.9 %collective-permute-start.34 = (bf16[24,1536]{1,0:T(8,128)(2,1)}, bf16[24,1536]{1,0:T(8,128)(2,1)S(1)}, u32[]{:S(2)}, u32[]{:S(2)}) collective-permute-start(bf16[24,1536]{1,0:T(8,128)(2,1)} %get-tuple-element.121), channel_id=1, source_target_pairs={{0,1},{1,65},{2,0},{3,64},{4,3},{5,67},{6,2},{7,66},{8,5},{9,69},{... | collective-permute-start | bytes 221192 | tf_op jit(solution)/shard_map/ppermute | solution.py:527
  301.1 9.4 %collective-permute-start.35 = (bf16[24,1536]{1,0:T(8,128)(2,1)}, bf16[24,1536]{1,0:T(8,128)(2,1)S(1)}, u32[]{:S(2)}, u32[]{:S(2)}) collective-permute-start(bf16[24,1536]{1,0:T(8,128)(2,1)} %get-tuple-element.122), channel_id=1, source_target_pairs={{0,2},{1,66},{2,3},{3,67},{4,0},{5,64},{6,1},{7,65},{8,6},{9,70},{... | collective-permute-start | bytes 221192 | tf_op jit(solution)/shard_map/ppermute | solution.py:527
  305.2 12.5 %collective-permute-start.36 = (bf16[24,1536]{1,0:T(8,128)(2,1)}, bf16[24,1536]{1,0:T(8,128)(2,1)S(1)}, u32[]{:S(2)}, u32[]{:S(2)}) collective-permute-start(bf16[24,1536]{1,0:T(8,128)(2,1)} %get-tuple-element.123), channel_id=1, source_target_pairs={{0,3},{1,67},{2,2},{3,66},{4,1},{5,65},{6,0},{7,64},{8,7},{9,71},{... | collective-permute-start | bytes 221192 | tf_op jit(solution)/shard_map/ppermute | solution.py:527
